TPU v7x, 32 devices: a whole 2x2x4 slice. The times are simulated.
32 devices in a mesh: fsdp: 32 (over z, y, x, core).
Axes of the slice: x: 2, y: 2, z: 4, core: 2. Of those that a mesh axis runs over, the one named last changes fastest.
Arguments:
- tokens: bfloat16 [8192, 2048], P('fsdp'), may hold values from -6 to 6
- lengths: int32 [32, 3], P('fsdp'), may hold values from 1 to 128, 256 in all within a row
- ln1_gain: bfloat16 [2048], P('fsdp'), may hold values from 0.5 to 1.5
- ln1_bias: bfloat16 [2048], P('fsdp'), may hold values from -3 to 3
- w_query: bfloat16 [2048, 2048], P('fsdp'), may hold values from -0.125 to 0.125
- w_key: bfloat16 [2048, 2048], P('fsdp'), may hold values from -0.125 to 0.125
- w_value: bfloat16 [2048, 4096], P('fsdp'), may hold values from -0.125 to 0.125
- w_swish: bfloat16 [2048, 4096], P('fsdp'), may hold values from -0.125 to 0.125
- w_out: bfloat16 [4096, 2048], P('fsdp'), may hold values from -0.125 to 0.125
- ln2_gain: bfloat16 [2048], P('fsdp'), may hold values from 0.5 to 1.5
- ln2_bias: bfloat16 [2048], P('fsdp'), may hold values from -3 to 3
- w_gate: bfloat16 [2048, 4096], P('fsdp'), may hold values from -0.125 to 0.125
- w_up: bfloat16 [2048, 4096], P('fsdp'), may hold values from -0.125 to 0.125
- w_down: bfloat16 [4096, 2048], P('fsdp'), may hold values from -0.09375 to 0.09375
- cotangent: bfloat16 [8192, 2048], P('fsdp'), may hold values from -6 to 6
Outputs:
- layer_out: bfloat16 [8192, 2048], P('fsdp')
- grad_tokens: float32 [8192, 2048], P('fsdp')
- grad_ln1_gain: float32 [2048], P('fsdp')
- grad_ln1_bias: float32 [2048], P('fsdp')
- grad_query: float32 [2048, 2048], P('fsdp')
- grad_key: float32 [2048, 2048], P('fsdp')
- grad_value: float32 [2048, 4096], P('fsdp')
- grad_swish: float32 [2048, 4096], P('fsdp')
- grad_out: float32 [4096, 2048], P('fsdp')
- grad_ln2_gain: float32 [2048], P('fsdp')
- grad_ln2_bias: float32 [2048], P('fsdp')
- grad_gate: float32 [2048, 4096], P('fsdp')
- grad_up: float32 [2048, 4096], P('fsdp')
- grad_down: float32 [4096, 2048], P('fsdp')
Inputs may be any that keep to these rules, and one draw needn't show every extreme that they name: Each device's row of lengths sums to 256, and its largest entry is exactly 128.
All inputs are finite; a program needn't handle non-finite values.
Results may differ from a plain program's by a relative error of at most 0.015.
The roundings to bfloat16 on the way count: a program that leaves them out, or rounds other values in their place, can miss the bound.
Values may be sent and summed in bfloat16 or wider, within the bound.
A program may use at most 512 MiB of HBM per device.

v0:
```python
import functools
import math

import jax
import jax.numpy as jnp
from jax import lax
from jax.experimental import pallas as pl
from jax.experimental.pallas import tpu as pltpu
from jax.sharding import PartitionSpec as P

HEADS = 8
KH = 256
VH = 512
TP = 8
AXIS = "fsdp"
MESH = pl.DeviceIdType.MESH
ANY = pl.BlockSpec(memory_space=pl.ANY)
VMEM = pl.BlockSpec(memory_space=pltpu.VMEM)
bf = jnp.bfloat16
f32 = jnp.float32
SDS = jax.ShapeDtypeStruct


def place():
    me = lax.axis_index(AXIS)
    steps = [s - 2 * s * lax.rem(lax.div(me, s), 2) for s in (1, 2, 4)]

    def peer(k):
        out = me
        for bit, step in enumerate(steps):
            if k >> bit & 1:
                out = out + step
        return out

    return me, peer


def greet(peers):
    barrier = pltpu.get_barrier_semaphore()
    for p in peers:
        pl.semaphore_signal(barrier, inc=1, device_id=(p,), device_id_type=MESH)
    pl.semaphore_wait(barrier, len(peers))


def remote(src, dst, sems, i, dev):
    return pltpu.make_async_remote_copy(
        src_ref=src, dst_ref=dst, send_sem=sems[0].at[i], recv_sem=sems[1].at[i],
        device_id=(dev,), device_id_type=MESH,
    )


GATHER_SEMS = 13


def gather_blocks(own, out, sems, base, local, peer):
    h = own.shape[0] // 2
    top, bot = pl.ds(0, h), pl.ds(h, h)
    pc, px, py = peer(1), peer(2), peer(4)
    made = []

    def send(src, dst, dev):
        copy = remote(src, dst, sems, base + len(made), dev)
        copy.start()
        made.append(copy)
        return copy

    x0 = send(own.at[bot], out.at[2, bot], px)
    y0 = send(own.at[top], out.at[4, top], py)
    x1 = send(own.at[top], out.at[2, top], px)
    y1 = send(own.at[bot], out.at[4, bot], py)
    core = [send(own, out.at[1], pc)]
    keep = pltpu.make_async_copy(own, out.at[0], local)
    keep.start()
    x0.wait_recv()
    fy = send(out.at[2, bot], out.at[6, bot], py)
    core.append(send(out.at[2, bot], out.at[3, bot], pc))
    y0.wait_recv()
    fx = send(out.at[4, top], out.at[6, top], px)
    core.append(send(out.at[4, top], out.at[5, top], pc))
    x1.wait_recv()
    core.append(send(out.at[2, top], out.at[3, top], pc))
    y1.wait_recv()
    core.append(send(out.at[4, bot], out.at[5, bot], pc))
    fy.wait_recv()
    core.append(send(out.at[6, bot], out.at[7, bot], pc))
    fx.wait_recv()
    core.append(send(out.at[6, top], out.at[7, top], pc))
    for copy in core:
        copy.wait_recv()
    for copy in made:
        copy.wait_send()
    keep.wait()


def gather_kernel(x_ref, out_ref, ssem, rsem, local):
    _, peer = place()
    greet([peer(1), peer(2), peer(4)])
    gather_blocks(x_ref, out_ref, (ssem, rsem), 0, local, peer)


def plane_gather(x, cid):
    r, c = x.shape
    return pl.pallas_call(
        gather_kernel,
        out_shape=SDS((TP, r, c), x.dtype),
        in_specs=[VMEM],
        out_specs=ANY,
        scratch_shapes=[
            pltpu.SemaphoreType.DMA((GATHER_SEMS,)),
            pltpu.SemaphoreType.DMA((GATHER_SEMS,)),
            pltpu.SemaphoreType.DMA,
        ],
        compiler_params=pltpu.CompilerParams(
            collective_id=cid, has_side_effects=True, vmem_limit_bytes=8 << 20
        ),
        name=f"plane_gather_{cid}",
    )(x)


def send_columns(src, out, cols, at, sems, base, local, t, peer, tiled=True):
    copies = []

    def block(q):
        if not tiled:
            return src.at[q]
        return src.at[:, pl.ds(pl.multiple_of(q * cols, 128), cols)]

    for k in range(1, TP):
        dev = peer(k)
        copy = remote(
            block(lax.rem(dev, TP)), out.at[t, :, pl.ds(at, cols)], sems, base + k - 1, dev
        )
        copy.start()
        copies.append(copy)
    keep = pltpu.make_async_copy(block(t), out.at[t, :, pl.ds(at, cols)], local)
    keep.start()
    return copies, keep


def finish(parts):
    for copies, keep in parts:
        for copy in copies:
            copy.wait()
        keep.wait()


def first_kernel(n, wq, wk, wv, vec, qk_out, v_out, vec_out, ssem, rsem, local):
    dp = n // TP
    me, peer = place()
    t, g = lax.rem(me, TP), lax.div(me, TP)
    others = [lax.rem(me + TP * j, n) for j in range(1, dp)]
    greet([peer(k) for k in range(1, TP)] + others)
    sems = (ssem, rsem)
    kq, kv = wq.shape[1] // TP, wv.shape[1] // TP
    far = []
    keep = pltpu.make_async_copy(vec, vec_out.at[g, t], local.at[3])
    keep.start()
    for j, dev in enumerate(others):
        copy = remote(vec, vec_out.at[g, t], sems, 28 + j, dev)
        copy.start()
        far.append(copy)
    parts = [
        send_columns(wq, qk_out, kq, 0, sems, 0, local.at[0], t, peer),
        send_columns(wk, qk_out, kq, kq, sems, 7, local.at[1], t, peer),
        send_columns(wv, v_out, kv, 0, sems, 14, local.at[2], t, peer),
    ]
    for copy in far:
        copy.wait()
    keep.wait()
    near = []
    for k in range(1, TP):
        copy = remote(vec_out.at[:, t], vec_out.at[:, t], sems, 20 + k, peer(k))
        copy.start()
        near.append(copy)
    finish(parts)
    for copy in near:
        copy.wait()


def first_exchange(n, wq, wk, wv, vec, cid):
    shard = wq.shape[0]
    return pl.pallas_call(
        functools.partial(first_kernel, n),
        out_shape=(
            SDS((TP, shard, 2 * wq.shape[1] // TP), bf),
            SDS((TP, shard, wv.shape[1] // TP), bf),
            SDS((n // TP, TP) + vec.shape, f32),
        ),
        in_specs=[VMEM] * 4,
        out_specs=(ANY, ANY, ANY),
        scratch_shapes=[
            pltpu.SemaphoreType.DMA((28 + n // TP,)),
            pltpu.SemaphoreType.DMA((28 + n // TP,)),
            pltpu.SemaphoreType.DMA((4,)),
        ],
        compiler_params=pltpu.CompilerParams(
            collective_id=cid, has_side_effects=True, vmem_limit_bytes=8 << 20
        ),
        name="first_exchange",
    )(wq, wk, wv, vec)


def second_kernel(wo, ws, gu, tok, o_out, s_out, gu_out, tok_out, ssem, rsem, local):
    me, peer = place()
    t = lax.rem(me, TP)
    greet([peer(k) for k in range(1, TP)])
    sems = (ssem, rsem)
    gather_blocks(tok, tok_out, sems, 21, local.at[3], peer)
    finish([
        send_columns(wo, o_out, wo.shape[1] // TP, 0, sems, 0, local.at[0], t, peer),
        send_columns(ws, s_out, ws.shape[1] // TP, 0, sems, 7, local.at[1], t, peer),
        send_columns(gu, gu_out, gu.shape[2], 0, sems, 14, local.at[2], t, peer, tiled=False),
    ])


def second_exchange(wo, ws, gu, tok, cid):
    return pl.pallas_call(
        second_kernel,
        out_shape=(
            SDS((TP, wo.shape[0], wo.shape[1] // TP), bf),
            SDS((TP, ws.shape[0], ws.shape[1] // TP), bf),
            SDS(gu.shape, bf),
            SDS((TP,) + tok.shape, bf),
        ),
        in_specs=[VMEM] * 4,
        out_specs=(ANY, ANY, ANY, ANY),
        scratch_shapes=[
            pltpu.SemaphoreType.DMA((21 + GATHER_SEMS,)),
            pltpu.SemaphoreType.DMA((21 + GATHER_SEMS,)),
            pltpu.SemaphoreType.DMA((4,)),
        ],
        compiler_params=pltpu.CompilerParams(
            collective_id=cid, has_side_effects=True, vmem_limit_bytes=12 << 20
        ),
        name="second_exchange",
    )(wo, ws, gu, tok)


def vector_sum_kernel(n, v_ref, out_ref, near, far, part, ssem, rsem):
    dp = n // TP
    me, peer = place()
    g = lax.div(me, TP)
    width = out_ref.shape[1]
    sems = (ssem, rsem)
    others = [lax.rem(me + TP * j, n) for j in range(1, dp)]
    greet([peer(k) for k in range(1, TP)] + others)
    copies = []
    for j, dev in enumerate(others):
        at = pl.multiple_of(lax.div(dev, TP) * width, 128)
        copy = remote(v_ref.at[:, pl.ds(at, width)], far.at[j], sems, j, dev)
        copy.start()
        copies.append(copy)
    total = v_ref[:, pl.ds(pl.multiple_of(g * width, 128), width)]
    for j, copy in enumerate(copies):
        copy.wait()
        total = total + far[j]
    part[...] = total
    copies = []
    for k in range(1, TP):
        copy = remote(part, near.at[k - 1], sems, dp + k - 1, peer(k))
        copy.start()
        copies.append(copy)
    for k, copy in enumerate(copies):
        copy.wait()
        total = total + near[k]
    out_ref[...] = total


def vector_sum(n, v, cid):
    dp = n // TP
    width = v.shape[1] // dp
    return pl.pallas_call(
        functools.partial(vector_sum_kernel, n),
        out_shape=SDS((v.shape[0], width), f32),
        in_specs=[VMEM],
        out_specs=VMEM,
        scratch_shapes=[
            pltpu.VMEM((TP - 1, v.shape[0], width), f32),
            pltpu.VMEM((dp, v.shape[0], width), f32),
            pltpu.VMEM((v.shape[0], width), f32),
            pltpu.SemaphoreType.DMA((dp + TP,)),
            pltpu.SemaphoreType.DMA((dp + TP,)),
        ],
        compiler_params=pltpu.CompilerParams(
            collective_id=cid, has_side_effects=True, vmem_limit_bytes=4 << 20
        ),
        name="vector_sum",
    )(v)


REDUCE_SEMS = 10
TILE = 512


def reduce_blocks(nt, a, w, po, pe, rc, sb, xr, yr, sems, peer):
    r = a.shape[1]
    c = pe.shape[2]
    h = r // 2
    top, bot = pl.ds(0, h), pl.ds(h, h)
    pc, px, py = peer(1), peer(2), peer(4)
    sent = []

    def product(k, dst):
        @pl.loop(0, c // TILE)
        def _(j):
            at = pl.ds(pl.multiple_of(j * TILE, TILE), TILE)
            if nt:
                y = lax.dot_general(
                    a[k], w[at, :], (((1,), (1,)), ((), ())), preferred_element_type=f32
                )
            else:
                y = jnp.dot(a[k], w[:, at], preferred_element_type=f32)
            dst[:, at] = y.astype(dst.dtype)

    def send(src, dst, dev, i):
        copy = remote(src, dst, sems, i, dev)
        copy.start()
        sent.append(copy)
        return copy

    def pair(i):
        k = 2 * i
        product(k + 1, po.at[i])
        copy = send(po.at[i], rc.at[i], pc, i)
        product(k, pe.at[i])
        return copy

    def rows(ref, at):
        return pl.ds(at.start, at.size) if ref is None else at

    def add(dst, part, got, out=None):
        step = 32

        @pl.loop(0, part.size // step)
        def _(j):
            here = pl.ds(pl.multiple_of(part.start + j * step, step), step)
            there = pl.ds(pl.multiple_of(j * step, step), step)
            total = dst[here, :] + got[there, :].astype(f32)
            if out is None:
                dst[here, :] = total
            else:
                out[there, :] = total.astype(bf)

    c6 = pair(3)
    c2 = pair(1)
    c6.wait_recv()
    add(pe.at[3], top, rc.at[3, top], sb.at[0])
    x6 = send(sb.at[0], xr.at[0], px, 4)
    add(pe.at[3], bot, rc.at[3, bot], sb.at[1])
    y6 = send(sb.at[1], yr.at[0], py, 5)
    c4 = pair(2)
    c2.wait_recv()
    add(pe.at[1], top, rc.at[1, top], sb.at[2])
    x2 = send(sb.at[2], xr.at[1], px, 6)
    add(pe.at[1], bot, rc.at[1, bot])
    c0 = pair(0)
    c4.wait_recv()
    add(pe.at[2], bot, rc.at[2, bot], sb.at[3])
    y4 = send(sb.at[3], yr.at[1], py, 7)
    add(pe.at[2], top, rc.at[2, top])
    c0.wait_recv()
    x6.wait_recv()
    add(pe.at[2], top, xr.at[0], sb.at[4])
    y4b = send(sb.at[4], yr.at[2], py, 8)
    y6.wait_recv()
    add(pe.at[1], bot, yr.at[0], sb.at[5])
    x2b = send(sb.at[5], xr.at[2], px, 9)
    x2.wait_recv()
    y4.wait_recv()
    y4b.wait_recv()
    x2b.wait_recv()

    def total(at, half_at, lower):
        first, second = (yr, xr) if lower else (xr, yr)
        return (
            pe[0, at, :]
            + rc[0, at, :].astype(f32)
            + first[1, half_at, :].astype(f32)
            + second[2, half_at, :].astype(f32)
        )

    def for_rows(step, body):
        for lower in (False, True):

            @pl.loop(0, h // step)
            def _(j, lower=lower):
                half_at = pl.ds(pl.multiple_of(j * step, step), step)
                at = pl.ds(pl.multiple_of(j * step + (h if lower else 0), step), step)
                body(at, total(at, half_at, lower))

    return for_rows, sent


def reduce_scratch(r, c):
    h = r // 2
    return [
        pltpu.VMEM((4, r, c), bf),
        pltpu.VMEM((4, r, c), f32),
        pltpu.VMEM((4, r, c), bf),
        pltpu.VMEM((6, h, c), bf),
        pltpu.VMEM((3, h, c), bf),
        pltpu.VMEM((3, h, c), bf),
    ]


def reduce_kernel(nt, a, w, out_ref, po, pe, rc, sb, xr, yr, ssem, rsem):
    _, peer = place()
    greet([peer(1), peer(2), peer(4)])
    for_rows, sent = reduce_blocks(nt, a, w, po, pe, rc, sb, xr, yr, (ssem, rsem), peer)

    def body(at, value):
        out_ref[at, :] = value

    for_rows(32, body)
    for copy in sent:
        copy.wait_send()


def matmul_reduce(a, w, nt, cid):
    _, r, _ = a.shape
    c = w.shape[0] if nt else w.shape[1]
    return pl.pallas_call(
        functools.partial(reduce_kernel, nt),
        out_shape=SDS((r, c), f32),
        in_specs=[VMEM] * 2,
        out_specs=VMEM,
        scratch_shapes=reduce_scratch(r, c)
        + [pltpu.SemaphoreType.DMA((REDUCE_SEMS,)), pltpu.SemaphoreType.DMA((REDUCE_SEMS,))],
        compiler_params=pltpu.CompilerParams(
            collective_id=cid, has_side_effects=True, vmem_limit_bytes=48 << 20
        ),
        name=f"matmul_reduce_{cid}",
    )(a, w)


def forward_kernel(a, w, tok, vec, mid, out, po, pe, rc, sb, xr, yr, own, ssem, rsem, local):
    _, peer = place()
    greet([peer(1), peer(2), peer(4)])
    sems = (ssem, rsem)
    for_rows, sent = reduce_blocks(False, a, w, po, pe, rc, sb, xr, yr, sems, peer)

    def body(at, value):
        value = value + tok[at, :].astype(f32)
        mid[at, :] = value
        center = jnp.mean(value, axis=-1, keepdims=True)
        centred = value - center
        spread = jnp.mean(centred * centred, axis=-1, keepdims=True)
        own[at, :] = (
            centred * lax.rsqrt(spread + 1e-05) * vec[0:1, :] + vec[1:2, :]
        ).astype(bf)

    for_rows(16, body)
    gather_blocks(own, out, sems, REDUCE_SEMS, local, peer)
    for copy in sent:
        copy.wait_send()


def forward_exchange(a, w, tok, vec, cid):
    _, r, _ = a.shape
    c = w.shape[1]
    count = REDUCE_SEMS + GATHER_SEMS
    return pl.pallas_call(
        forward_kernel,
        out_shape=(SDS((r, c), f32), SDS((TP, r, c), bf)),
        in_specs=[VMEM] * 4,
        out_specs=(VMEM, ANY),
        scratch_shapes=reduce_scratch(r, c)
        + [
            pltpu.VMEM((r, c), bf),
            pltpu.SemaphoreType.DMA((count,)),
            pltpu.SemaphoreType.DMA((count,)),
            pltpu.SemaphoreType.DMA,
        ],
        compiler_params=pltpu.CompilerParams(
            collective_id=cid, has_side_effects=True, vmem_limit_bytes=48 << 20
        ),
        name="forward_exchange",
    )(a, w, tok, vec)


def backward_kernel(
    a, w, mid, cot, vec, gmid, out, sums, po, pe, rc, sb, xr, yr, own, acc, ssem, rsem, local
):
    _, peer = place()
    greet([peer(1), peer(2), peer(4)])
    sems = (ssem, rsem)
    acc[...] = jnp.zeros_like(acc)
    for_rows, sent = reduce_blocks(True, a, w, po, pe, rc, sb, xr, yr, sems, peer)

    def body(at, g):
        value = mid[at, :]
        center = jnp.mean(value, axis=-1, keepdims=True)
        centred = value - center
        inv = lax.rsqrt(jnp.mean(centred * centred, axis=-1, keepdims=True) + 1e-05)
        hat = centred * inv
        acc[0] += g * hat
        acc[1] += g
        scaled = g * vec[0:1, :]
        mean_g = jnp.mean(scaled, axis=-1, keepdims=True)
        mean_gh = jnp.mean(scaled * hat, axis=-1, keepdims=True)
        grad = cot[at, :].astype(f32) + inv * (scaled - mean_g - hat * mean_gh)
        gmid[at, :] = grad
        own[at, :] = grad.astype(bf)

    for_rows(16, body)
    gather_blocks(own, out, sems, REDUCE_SEMS, local, peer)
    sums[0:1, :] = jnp.sum(acc[0], axis=0, keepdims=True)
    sums[1:2, :] = jnp.sum(acc[1], axis=0, keepdims=True)
    for copy in sent:
        copy.wait_send()


def backward_exchange(a, w, mid, cot, vec, cid):
    _, r, _ = a.shape
    c = w.shape[0]
    count = REDUCE_SEMS + GATHER_SEMS
    return pl.pallas_call(
        backward_kernel,
        out_shape=(SDS((r, c), f32), SDS((TP, r, c), bf), SDS((2, c), f32)),
        in_specs=[VMEM] * 5,
        out_specs=(VMEM, ANY, VMEM),
        scratch_shapes=reduce_scratch(r, c)
        + [
            pltpu.VMEM((r, c), bf),
            pltpu.VMEM((2, 16, c), f32),
            pltpu.SemaphoreType.DMA((count,)),
            pltpu.SemaphoreType.DMA((count,)),
            pltpu.SemaphoreType.DMA,
        ],
        compiler_params=pltpu.CompilerParams(
            collective_id=cid, has_side_effects=True, vmem_limit_bytes=52 << 20
        ),
        name="backward_exchange",
    )(a, w, mid, cot, vec)


def tp_groups(n):
    return [[g * TP + t for t in range(TP)] for g in range(n // TP)]


def dp_groups(n):
    return [[g * TP + t for g in range(n // TP)] for t in range(TP)]


def plane_a2a(x, n):
    return lax.all_to_all(x, AXIS, 0, 0, axis_index_groups=tp_groups(n), tiled=True)


def dp_gather(x, n):
    return lax.all_gather(x, AXIS, axis=0, tiled=True, axis_index_groups=dp_groups(n))


def dp_reduce(x, n):
    return lax.psum_scatter(
        x, AXIS, scatter_dimension=0, tiled=True, axis_index_groups=dp_groups(n)
    )


def layer_norm(value, gain, bias):
    center = jnp.mean(value, axis=-1, keepdims=True)
    centred = value - center
    spread = jnp.mean(centred * centred, axis=-1, keepdims=True)
    return centred * lax.rsqrt(spread + 1e-05) * gain + bias


def seq_positions(lengths, rows):
    ends = jnp.cumsum(lengths, axis=1)
    starts = ends - lengths
    index = jnp.arange(rows, dtype=jnp.int32)
    segment = jnp.sum((index[None, :, None] >= ends[:, None, :]).astype(jnp.int32), axis=2)
    member = segment[:, :, None] == jnp.arange(lengths.shape[1], dtype=jnp.int32)
    offset = index[None, :] - jnp.sum(jnp.where(member, starts[:, None, :], 0), axis=2)
    return segment, offset


def rotary_tables(offset):
    half = KH // 2
    freq = jnp.exp(-math.log(10000.0) * jnp.arange(half, dtype=f32) / half)
    angle = offset.astype(f32)[..., None] * freq
    return jnp.cos(angle), jnp.sin(angle)


def rotate(value, cosine, sine):
    half = KH // 2
    u, w = value[..., :half], value[..., half:]
    return jnp.concatenate([u * cosine - w * sine, w * cosine + u * sine], axis=-1)


def rotate_back(value, cosine, sine):
    half = KH // 2
    u, w = value[..., :half], value[..., half:]
    return jnp.concatenate([u * cosine + w * sine, w * cosine - u * sine], axis=-1)


def decay_mask(segment, offset, head):
    diff = offset[:, :, None] - offset[:, None, :]
    valid = (segment[:, :, None] == segment[:, None, :]) & (diff >= 0)
    steps = jnp.where(valid, diff, 0).astype(f32)
    log = jnp.log(1.0 - jnp.exp2(-5.0 - head.astype(f32)))
    return jnp.where(valid, jnp.exp(log * steps), 0.0) / math.sqrt(KH)


def group_gate(retained, swish_in):
    center = jnp.mean(retained, axis=-1, keepdims=True)
    centred = retained - center
    spread = jnp.mean(centred * centred, axis=-1, keepdims=True)
    return jax.nn.silu(swish_in) * (centred * lax.rsqrt(jnp.maximum(spread, 0.25)))


def mlp_gate(first, second):
    return jax.nn.gelu(first, approximate=False) * second


def dot(a, b):
    return lax.dot_general(a, b, (((1,), (0,)), ((), ())), preferred_element_type=f32)


def dot_tn(a, b):
    return lax.dot_general(a, b, (((0,), (0,)), ((), ())), preferred_element_type=f32)


def dot_nt(a, b):
    return lax.dot_general(a, b, (((1,), (1,)), ((), ())), preferred_element_type=f32)


def bmm(eq, a, b):
    return jnp.einsum(eq, a, b, preferred_element_type=f32)


def col_blocks(w):
    r, c = w.shape
    return w.reshape(r, TP, c // TP).transpose(1, 0, 2).reshape(TP * r, c // TP)


def col_join(w, r):
    c = w.shape[1]
    return w.reshape(TP, r, c).transpose(1, 0, 2).reshape(r, TP * c)


def after(x, *deps):
    return lax.optimization_barrier((x,) + deps)[0]


def on_device(n, tokens, lengths, gain1, bias1, wq, wk, wv, ws, wo, gain2, bias2, wg, wu, wd, cot):
    rows, d = tokens.shape
    ff = wg.shape[1]
    dp = n // TP
    shard = d // n
    unit = ff // n
    me = lax.axis_index(AXIS)
    head = lax.rem(me, TP)

    def ff_blocks(w):
        return w.reshape(shard, dp, TP, unit).transpose(2, 0, 1, 3).reshape(TP, shard, dp * unit)

    def ff_join(w):
        return w.reshape(TP, shard, dp, unit).transpose(1, 2, 0, 3).reshape(shard, ff)

    vec = jnp.zeros((8, 128), f32)
    for i, v in enumerate((gain1, bias1, gain2, bias2)):
        vec = vec.at[i, :shard].set(v.astype(f32))
    vec = vec.at[4, :3].set(lengths[0].astype(f32))
    qk_blk, v_blk, vec_all = first_exchange(n, wq, wk, wv, vec, 1)
    gain1f, bias1f, gain2f, bias2f = (
        vec_all[:, :, i, :shard].reshape(1, d) for i in range(4)
    )
    vec2 = jnp.concatenate([gain2f, bias2f], axis=0)
    qk = dp_gather(qk_blk.reshape(TP * shard, 2 * KH), n)
    val = dp_gather(v_blk.reshape(TP * shard, VH), n)
    gu_in = jnp.concatenate([ff_blocks(wg), ff_blocks(wu)], axis=2)
    o_blk, s_blk, gu_blk, tok_all = second_exchange(after(wo, v_blk), ws, gu_in, tokens, 2)
    out = dp_gather(o_blk.reshape(TP * wo.shape[0], d // TP), n)
    out = col_join(plane_a2a(out, n), VH)
    swi = dp_gather(s_blk.reshape(TP * shard, VH), n)
    gu = dp_gather(gu_blk.reshape(TP * shard, 2 * dp * unit), n)
    down = dp_gather(after(wd, gu_blk), n)
    cot_all = plane_gather(after(cot, tok_all), 3)

    mine = lax.dynamic_slice_in_dim(vec_all, lax.div(me, TP), 1, 0)[0, :, 4, :3]
    order = jnp.arange(TP, dtype=jnp.int32)
    pick = (order[None, :] == (order[:, None] ^ head)).astype(f32)
    len_all = jnp.sum(pick[:, :, None] * mine[None], axis=1).astype(jnp.int32)
    segment, offset = seq_positions(len_all, rows)
    cosine, sine = rotary_tables(offset)
    mask = decay_mask(segment, offset, head)

    normed = layer_norm(tok_all.reshape(TP * rows, d).astype(f32), gain1f, bias1f).astype(bf)
    qk_out = dot(normed, qk).reshape(TP, rows, 2 * KH)
    query, key = qk_out[..., :KH], qk_out[..., KH:]
    v_low = dot(normed, val).reshape(TP, rows, VH).astype(bf)
    swish_in = dot(normed, swi).reshape(TP, rows, VH)
    q_rot = rotate(query, cosine, sine).astype(bf)
    k_rot = rotate(key, cosine, sine).astype(bf)
    plain = bmm("btd,bsd->bts", q_rot, k_rot)
    scores = (plain * mask).astype(bf)
    retained = bmm("bts,bsd->btd", scores, v_low)
    mixed = group_gate(retained, swish_in).astype(bf)
    middle, normed2 = forward_exchange(mixed, out, tokens, vec2, 4)
    normed2 = normed2.reshape(TP * rows, d)
    cot_all = cot_all.reshape(TP * rows, d)
    fs = dot(normed2, gu)
    first, second = fs[:, : dp * unit], fs[:, dp * unit :]
    hidden = mlp_gate(first, second).astype(bf)

    g_down = dp_reduce(dot_tn(hidden, cot_all).astype(bf), n)
    g_hidden = dot_nt(cot_all, down)
    _, pull_gate = jax.vjp(mlp_gate, first, second)
    g_first, g_second = pull_gate(g_hidden)
    g_fs = jnp.concatenate([g_first.astype(bf), g_second.astype(bf)], axis=1)
    gu_grad = dot_tn(normed2, g_fs).astype(bf)
    g_gu = dp_reduce(gu_grad, n)
    g_fs_in = after(g_fs, gu_grad)
    g_middle, g_low, sums2 = backward_exchange(
        g_fs_in.reshape(TP, rows, 2 * dp * unit), gu, middle, cot, vec2, 5
    )

    g_low = g_low.reshape(TP * rows, d)
    mixed = mixed.reshape(TP * rows, VH)
    out_grad = dot_tn(mixed, g_low).astype(bf)
    g_out = dp_reduce(plane_a2a(col_blocks(out_grad), n), n)
    g_mixed = dot_nt(g_low, out).reshape(TP, rows, VH)
    _, pull_group = jax.vjp(group_gate, retained, swish_in)
    g_retained, g_swish = pull_group(g_mixed)
    g_retained = g_retained.astype(bf)
    g_swish = g_swish.astype(bf)
    g_value = bmm("bts,btd->bsd", scores, g_retained).astype(bf)
    g_scores = bmm("btd,bsd->bts", g_retained, v_low)
    g_plain = (g_scores * mask).astype(bf)
    g_qrot = bmm("bts,bsd->btd", g_plain, k_rot)
    g_krot = bmm("bts,btd->bsd", g_plain, q_rot)
    g_query = rotate_back(g_qrot, cosine, sine).astype(bf)
    g_key = rotate_back(g_krot, cosine, sine).astype(bf)
    g_qkvs = jnp.concatenate([g_query, g_key, g_value, g_swish], axis=2)
    w_qkvs = jnp.concatenate([qk, val, swi], axis=1)
    qkvs_grad = dot_tn(normed, g_qkvs.reshape(TP * rows, 2 * KH + 2 * VH)).astype(bf)
    grad_qkvs = dp_reduce(qkvs_grad, n)
    g_qkvs = after(g_qkvs, qkvs_grad)
    g_normed = matmul_reduce(g_qkvs, w_qkvs, True, 6)
    inputs = tokens.astype(f32)
    _, pull_norm1 = jax.vjp(layer_norm, inputs, gain1f, bias1f)
    g_in_part, g_gain1, g_bias1 = pull_norm1(g_normed)
    grad_tokens = g_middle + g_in_part
    hidden = after(hidden, g_normed)
    layer_out = (middle + matmul_reduce(hidden.reshape(TP, rows, dp * unit), down, False, 7)).astype(bf)

    g_vecs = jnp.concatenate([g_gain1, g_bias1, sums2, jnp.zeros((4, d), f32)], axis=0)
    g_vecs = vector_sum(n, g_vecs, 8)
    g_vecs = lax.dynamic_slice_in_dim(g_vecs, head * shard, shard, 1)
    grad_qkvs = plane_a2a(grad_qkvs, n).astype(f32)
    grad_q = col_join(grad_qkvs[:, :KH], shard)
    grad_k = col_join(grad_qkvs[:, KH : 2 * KH], shard)
    grad_v = col_join(grad_qkvs[:, 2 * KH : 2 * KH + VH], shard)
    grad_s = col_join(grad_qkvs[:, 2 * KH + VH :], shard)
    grad_o = col_join(plane_a2a(g_out, n).astype(f32), wo.shape[0])
    g_gu = plane_a2a(g_gu, n).astype(f32)
    grad_g = ff_join(g_gu[:, : dp * unit])
    grad_u = ff_join(g_gu[:, dp * unit :])
    grad_d = g_down.astype(f32)
    return (
        layer_out, grad_tokens, g_vecs[0], g_vecs[1], grad_q, grad_k, grad_v, grad_s, grad_o,
        g_vecs[2], g_vecs[3], grad_g, grad_u, grad_d,
    )


def solution(mesh):
    n = mesh.shape[AXIS]
    row, vec = P(AXIS, None), P(AXIS)
    ins = (row, row, vec, vec, row, row, row, row, row, vec, vec, row, row, row, row)
    outs = (row, row, vec, vec, row, row, row, row, row, vec, vec, row, row, row)
    return jax.shard_map(
        lambda *a: on_device(n, *a), mesh=mesh, in_specs=ins, out_specs=outs, check_vma=False
    )
```

profile of v0, /device:TPU:14, one launch (start us, length us, event | category | flops | bytes accessed | tf_op | source)
XLA Modules:
  0.0 840.9 jit_solution(9986465331975768083)
XLA Ops:
  14.1 17.0 %first_exchange.1 = (bf16[8,64,512]{2,1,0:T(8,128)(2,1)}, bf16[8,64,512]{2,1,0:T(8,128)(2,1)}, f32[4,8,8,128]{3,2,1,0:T(8,128)S(1)}) custom-call(bf16[64,2048]{1,0:T(8,128)(2,1)S(1)} %copy-done.13, bf16[64,2048]{1,0:T(8,128)(2,1)S(1)} %copy-done.14, bf16[64,4096]{1,0:T(8,128)(2,1)S(1)} %copy-done.10, f32[8,128]{1,0:T(8,128)S(1)} %scatter.32.vec), custom_call_target="tpu_custom_call" | custom-call | tf_op jit(solution)/shard_map/first_exchange/pallas_call | solution.py:182
  37.3 65.3 %second_exchange.1 = (bf16[8,128,256]{2,1,0:T(8,128)(2,1)}, bf16[8,64,512]{2,1,0:T(8,128)(2,1)}, bf16[8,64,1024]{2,1,0:T(8,128)(2,1)}, bf16[8,256,2048]{2,1,0:T(8,128)(2,1)S(1)}) custom-call(bf16[128,2048]{1,0:T(8,128)(2,1)S(1)} %copy-done.11, bf16[64,4096]{1,0:T(8,128)(2,1)S(1)} %copy-done.12, bf16[8,64,1024]{2,1,0:T(8,128)(2,1)S(1)} %pad_maximum_fusion.2.gu, ...), custom_call_target="tpu_custom_call" | custom-call | tf_op jit(solution)/shard_map/second_exchange/pallas_call | solution.py:217
  117.0 39.2 %plane_gather_3.1 = bf16[8,256,2048]{2,1,0:T(8,128)(2,1)S(1)} custom-call(bf16[256,2048]{1,0:T(8,128)(2,1)S(1)} %copy-done.7), custom_call_target="tpu_custom_call" | custom-call | tf_op jit(solution)/shard_map/plane_gather_3/pallas_call | solution.py:103
  159.5 7.7 fusion.36
  174.9 8.2 fusion.42
  192.9 21.8 %all-gather.7.cloned.1.call-done = bf16[2048,512]{1,0:T(8,128)(2,1)} async-done(((bf16[512,512]{1,0:T(8,128)(2,1)}), bf16[2048,512]{1,0:T(8,128)(2,1)}) %all-gather.7.cloned.1.call-update) | async-done | bytes 2097168 | tf_op jit(solution)/shard_map/all_gather | solution.py:550
  214.8 10.7 %multiply_convert_fusion.2 = (bf16[8,256,512]{2,1,0:T(8,128)(2,1)}, f32[8,256,512]{2,1,0:T(8,128)}) fusion(f32[8,256,512]{2,1,0:T(8,128)} %copy-done.15, f32[8,256]{1,0:T(8,128)S(1)} %maximum_rsqrt_fusion, f32[8,256]{1,0:T(8,128)S(1)} %broadcast_multiply_fusion, bf16[2048,512]{1,0:T(8,128)(2,1)} %all-gather.7.cloned.1.call-done, ...), kind=kOutput, calls=%fused_computation.36 | convolution fusion | flops 4328521728 | bytes 21020672 | tf_op jit(solution)/shard_map/dot_general | solution.py:615
  229.0 84.6 %forward_exchange.1 = (f32[256,2048]{1,0:T(8,128)S(1)}, bf16[8,256,2048]{2,1,0:T(8,128)(2,1)}) custom-call(bf16[8,256,512]{2,1,0:T(8,128)(2,1)S(1)} %copy-done.8, bf16[512,2048]{1,0:T(8,128)(2,1)} %bitcast.138, bf16[256,2048]{1,0:T(8,128)(2,1)S(1)} %copy-done, f32[2,2048]{1,0:T(2,128)S(1)} %pad_maximum_fusion.9.vec), custom_call_target="tpu_custom_call" | custom-call | tf_op jit(solution)/shard_map/forward_exchange/pallas_call | solution.py:462
  315.0 14.7 %fusion.100 = f32[2048,1024]{0,1:T(8,128)} fusion(bf16[2048,2048]{1,0:T(8,128)(2,1)} %bitcast.168, bf16[2048,1024]{1,0:T(8,128)(2,1)} %all-gather.15.cloned.1.call-done.w), kind=kOutput, calls=%fused_computation.178 | convolution fusion | flops 8589934592 | bytes 20971520 | tf_op jit(solution)/shard_map/dot_general | solution.py:615
  329.8 11.6 %all-gather.17.cloned.1.call-done.w = bf16[512,2048]{1,0:T(8,128)(2,1)} async-done(((bf16[128,2048]{1,0:T(8,128)(2,1)}), bf16[512,2048]{1,0:T(8,128)(2,1)}) %all-gather.17.cloned.1.call-update) | async-done | bytes 2097168 | tf_op jit(solution)/shard_map/all_gather | solution.py:550
  341.4 21.8 %add_convert_fusion.1 = (bf16[2048,512]{0,1:T(8,128)(2,1)}, f32[2048,512]{0,1:T(8,128)S(1)}, f32[2048,512]{0,1:T(8,128)}) fusion(f32[2048,1024]{0,1:T(8,128)} %fusion.100, bf16[2048,2048]{1,0:T(8,128)(2,1)} %bitcast.132, bf16[512,2048]{1,0:T(8,128)(2,1)} %all-gather.17.cloned.1.call-done.w), kind=kOutput, calls=%fused_computation.22 | convolution fusion | flops 4371513344 | bytes 29360128 | tf_op jit(solution)/shard_map/dot_general | solution.py:623
  363.2 8.1 multiply_convert_fusion
  375.6 12.9 %convolution_convert_fusion = bf16[2048,1024]{1,0:T(8,128)(2,1)} fusion(bf16[2048,2048]{1,0:T(8,128)(2,1)} %bitcast.169, bf16[2048,512]{0,1:T(8,128)(2,1)S(1)} %get-tuple-element.151, bf16[2048,512]{0,1:T(8,128)(2,1)S(1)} %copy-done.26), kind=kOutput, calls=%fused_computation.42 | convolution fusion | flops 8600420352 | bytes 16777216 | tf_op jit(solution)/shard_map/dot_general | solution.py:619
  394.8 92.7 %backward_exchange.1 = (f32[256,2048]{1,0:T(8,128)}, bf16[8,256,2048]{2,1,0:T(8,128)(2,1)}, f32[2,2048]{1,0:T(2,128)S(1)}) custom-call(bf16[8,256,1024]{2,1,0:T(8,128)(2,1)} %bitcast.136, bf16[2048,1024]{1,0:T(8,128)(2,1)} %all-gather.15.cloned.1.call-done.w, f32[256,2048]{1,0:T(8,128)} %copy-done.6, bf16[256,2048]{1,0:T(8,128)(2,1)S(1)} %copy-done.7, ...), custom_call_target="tpu_custom_call" | custom-call | tf_op jit(solution)/shard_map/backward_exchange/pallas_call | solution.py:517
  487.5 8.2 bitcast_convert_fusion.1
  495.8 28.7 %all_to_all.45 = bf16[8,512,256]{2,1,0:T(8,128)(2,1)} all-to-all(bf16[8,512,256]{2,1,0:T(8,128)(2,1)S(1)} %bitcast.139), channel_id=1, replica_groups={{0,1,2,3,4,5,6,7},{8,9,10,11,12,13,14,15},{16,17,18,19,20,21,22,23},{24..., dimensions={0} | all-to-all | bytes 4194304 | tf_op jit(solution)/shard_map/all_to_all | solution.py:546
  530.7 12.3 %multiply_reduce_fusion = (f32[8,256]{1,0:T(8,128)S(1)}, f32[8,256,512]{2,1,0:T(8,128)S(1)}) fusion(f32[8,256,512]{2,1,0:T(8,128)} %copy-done.15, f32[8,256]{1,0:T(8,128)S(1)} %broadcast_multiply_fusion, f32[8,256,512]{2,1,0:T(8,128)} %get-tuple-element.174, bf16[8,256,2048]{2,1,0:T(8,128)(2,1)} %get-tuple-element.105, bf16[512,2048,1]{1,0,2:T(8,128)(2,1)} %reshape.570), kind=kOutput, calls=%fused_computation.20 | convolution fusion | flops 4303353856 | bytes 23085056 | tf_op jit(solution)/shard_map/dot_general | solution.py:623
  577.9 7.1 fusion.40.a
  585.0 20.9 %bitcast_convert_fusion = bf16[2048,1536]{1,0:T(8,128)(2,1)} fusion(bf16[8,256,1536]{2,1,0:T(8,128)(2,1)} %fusion.40.a, bf16[8,256,2048]{2,1,0:T(8,128)(2,1)} %copy-done.1, f32[2048]{0:T(1024)S(1)} %add.90, f32[2048]{0:T(1024)S(1)} %mul.300, f32[8,256]{1,0:T(8,128)S(1)} %add_rsqrt_fusion, f32[8,256]{1,0:T(8,128)S(1)} %broadcast_multiply_fusion.1), kind=kOutput, calls=%fused_computation.8 | convolution fusion | flops 12913213440 | bytes 21004288 | tf_op jit(solution)/shard_map/dot_general | solution.py:619
  612.9 51.7 %matmul_reduce_6.1 = f32[256,2048]{1,0:T(8,128)S(1)} custom-call(bf16[8,256,1536]{2,1,0:T(8,128)(2,1)} %fusion.40.a, bf16[2048,1536]{1,0:T(8,128)(2,1)} %pad_maximum_fusion.w), custom_call_target="tpu_custom_call" | custom-call | tf_op jit(solution)/shard_map/matmul_reduce_6/pallas_call | solution.py:422
  670.5 11.5 %vector_sum.1 = f32[8,512]{1,0:T(8,128)S(1)} custom-call(f32[8,2048]{1,0:T(8,128)S(1)} %maximum_maximum_fusion.v_ref), custom_call_target="tpu_custom_call" | custom-call | tf_op jit(solution)/shard_map/vector_sum/pallas_call | solution.py:272
  682.0 44.0 %matmul_reduce_7.1 = f32[256,2048]{1,0:T(8,128)S(1)} custom-call(bf16[8,256,512]{2,1,0:T(8,128)(2,1)S(1)} %bitcast.131, bf16[512,2048]{1,0:T(8,128)(2,1)} %all-gather.17.cloned.1.call-done.w), custom_call_target="tpu_custom_call" | custom-call | tf_op jit(solution)/shard_map/matmul_reduce_7/pallas_call | solution.py:422
  740.9 6.5 all-to-all-start.4
  760.6 45.9 %reduce-scatter.5.cloned.1.call-done = bf16[512,1536]{1,0:T(8,128)(2,1)} async-done(((bf16[2048,1536]{1,0:T(8,128)(2,1)}), bf16[512,1536]{1,0:T(8,128)(2,1)}) %reduce-scatter.5.cloned.1.call-update) | async-done | bytes 1572880 | tf_op jit(solution)/shard_map/reduce_scatter | solution.py:554
  (220 shorter events, 172.5 us)
Async XLA Ops:
  7.2 152.3 %all-gather.9.cloned.1.call-start = ((), (), s32[]{:S(2)}) async-start(), calls=%async_computation.10 | async-start | bytes 2621440 | tf_op jit(solution)/shard_map/all_gather | solution.py:550
  31.2 143.7 %all-gather.11.cloned.1.call-start = ((), (), s32[]{:S(2)}) async-start(), calls=%async_computation.11 | async-start | bytes 2621440 | tf_op jit(solution)/shard_map/all_gather | solution.py:550
  31.9 154.9 %all-gather.13.cloned.1.call-start = ((), (), s32[]{:S(2)}) async-start(), calls=%async_computation.12 | async-start | bytes 2621440 | tf_op jit(solution)/shard_map/all_gather | solution.py:550
  105.9 108.9 %all-gather.7.cloned.1.call-start = ((), (), s32[]{:S(2)}) async-start(), calls=%async_computation.9 | async-start | bytes 2621440 | tf_op jit(solution)/shard_map/all_gather | solution.py:550
  106.4 208.6 %all-gather.15.cloned.1.call-start = ((), (), s32[]{:S(2)}) async-start(), calls=%async_computation.13 | async-start | bytes 5242880 | tf_op jit(solution)/shard_map/all_gather | solution.py:550
  107.0 234.4 %all-gather.17.cloned.1.call-start = ((), (), s32[]{:S(2)}) async-start(), calls=%async_computation.14 | async-start | bytes 2621440 | tf_op jit(solution)/shard_map/all_gather | solution.py:550
  108.0 64.2 %copy-start.37 = (s32[8,256]{1,0:T(8,128)}, s32[8,256]{1,0:T(8,128)S(1)}, u32[]{:S(2)}) copy-start(s32[8,256]{1,0:T(8,128)S(1)} %convert_reduce_fusion.2) | copy-start | bytes 24580
  108.2 59.0 %copy-start.39 = (f32[128]{0:T(128)}, f32[128]{0:T(128)S(1)}, u32[]{:S(2)}) copy-start(f32[128]{0:T(128)S(1)} %multiply_exponential_fusion) | copy-start | bytes 1540
  108.4 58.8 %copy-start.35 = (f32[8,256]{1,0:T(8,128)}, f32[8,256]{1,0:T(8,128)S(1)}, u32[]{:S(2)}) copy-start(f32[8,256]{1,0:T(8,128)S(1)} %get-tuple-element.163) | copy-start | bytes 24580
  108.4 63.8 %copy-start.41 = (s32[8,256]{1,0:T(8,128)}, s32[8,256]{1,0:T(8,128)S(1)}, u32[]{:S(2)}) copy-start(s32[8,256]{1,0:T(8,128)S(1)} %get-tuple-element.164) | copy-start | bytes 24580
  186.8 38.6 %all-to-all-start = ((bf16[8,512,256]{2,1,0:T(8,128)(2,1)}), bf16[8,512,256]{2,1,0:T(8,128)(2,1)}, u32[]{:S(2)}, u32[]{:S(2)}) async-start(bf16[8,512,256]{2,1,0:T(8,128)(2,1)} %bitcast.147), calls=%async_computation | async-start | bytes 4194304 | tf_op jit(solution)/shard_map/all_to_all | solution.py:546
  192.7 535.2 %reduce-scatter.7.cloned.1.call-start = ((), (), s32[]{:S(2)}) async-start(), calls=%async_computation.16 | async-start | bytes 2621440 | tf_op jit(solution)/shard_map/reduce_scatter | solution.py:554
  394.8 92.7 %copy-start.9 = (bf16[8,256,512]{2,1,0:T(8,128)(2,1)S(1)}, bf16[8,256,512]{2,1,0:T(8,128)(2,1)}, u32[]{:S(2)}) copy-start(bf16[8,256,512]{2,1,0:T(8,128)(2,1)} %get-tuple-element.173.a) | copy-start | bytes 6291460
  524.6 216.3 %reduce-scatter.9.cloned.1.call-start = ((), (), s32[]{:S(2)}) async-start(), calls=%async_computation.17 | async-start | bytes 5242880 | tf_op jit(solution)/shard_map/reduce_scatter | solution.py:554
  525.3 225.8 %reduce-scatter.11.cloned.1.call-start = ((), (), s32[]{:S(2)}) async-start(), calls=%async_computation.18 | async-start | bytes 2621440 | tf_op jit(solution)/shard_map/reduce_scatter | solution.py:554
  530.7 12.3 %copy-start.16 = (f32[8,256,512]{2,1,0:T(8,128)S(1)}, f32[8,256,512]{2,1,0:T(8,128)}, u32[]{:S(2)}) copy-start(f32[8,256,512]{2,1,0:T(8,128)} %copy-done.15) | copy-start | bytes 12582916
  530.7 12.4 %copy-start.17 = (f32[8,256,512]{2,1,0:T(8,128)S(1)}, f32[8,256,512]{2,1,0:T(8,128)}, u32[]{:S(2)}) copy-start(f32[8,256,512]{2,1,0:T(8,128)} %get-tuple-element.174) | copy-start | bytes 12582916
  553.1 18.9 %slice-start = ((s8[8388608]{0:T(1024)(128)(4,1)}), s8[4194304]{0:T(1024)(128)(4,1)S(1)}, s32[]{:S(2)}) async-start(s8[8388608]{0:T(1024)(128)(4,1)} %bitcast.133), calls=%async_computation.19 | async-start | bytes 8388608
  558.1 10.4 %copy-start.22 = (bf16[8,256,256]{2,1,0:T(8,128)(2,1)S(1)}, bf16[8,256,256]{2,1,0:T(8,128)(2,1)}, u32[]{:S(2)}) copy-start(bf16[8,256,256]{2,1,0:T(8,128)(2,1)} %copy-done.21) | copy-start | bytes 3145732
  577.9 228.6 %reduce-scatter.5.cloned.1.call-start = ((), (), s32[]{:S(2)}) async-start(), calls=%async_computation.15 | async-start | bytes 7864320 | tf_op jit(solution)/shard_map/reduce_scatter | solution.py:554
  668.7 13.3 %copy-start.3 = (bf16[2048,512]{1,0:T(8,128)(2,1)S(1)}, bf16[2048,512]{1,0:T(8,128)(2,1)}, u32[]{:S(2)}) copy-start(bf16[2048,512]{1,0:T(8,128)(2,1)} %copy.99) | copy-start | bytes 6291460
  727.9 13.0 %all-to-all-start.3 = ((bf16[8,128,256]{2,1,0:T(8,128)(2,1)}), bf16[8,128,256]{2,1,0:T(8,128)(2,1)}, u32[]{:S(2)}, u32[]{:S(2)}) async-start(bf16[8,128,256]{2,1,0:T(8,128)(2,1)} %bitcast.161), calls=%async_computation.5 | async-start | bytes 1048576 | tf_op jit(solution)/shard_map/all_to_all | solution.py:546
  740.9 19.7 %all-to-all-start.4 = ((bf16[8,64,1024]{2,1,0:T(8,128)(2,1)}), bf16[8,64,1024]{2,1,0:T(8,128)(2,1)}, u32[]{:S(2)}, u32[]{:S(2)}) async-start(bf16[8,64,1024]{2,1,0:T(8,128)(2,1)} %bitcast.156), calls=%async_computation.7 | async-start | bytes 2097152 | tf_op jit(solution)/shard_map/all_to_all | solution.py:546
  806.5 22.9 %all-to-all-start.1 = ((bf16[8,64,1536]{2,1,0:T(8,128)(2,1)}), bf16[8,64,1536]{2,1,0:T(8,128)(2,1)S(1)}, u32[]{:S(2)}, u32[]{:S(2)}) async-start(bf16[8,64,1536]{2,1,0:T(8,128)(2,1)} %bitcast.155), calls=%async_computation.2 | async-start | bytes 3145728 | tf_op jit(solution)/shard_map/all_to_all | solution.py:546
  (35 other events, 115.5 us)
Sparse Core Ops, SparseCore 0:
  31.3 45.3 all-gather.8
  78.3 44.4 all-gather.10
  124.4 44.4 all-gather.12
  170.3 44.4 all-gather.6
  216.2 78.3 all-gather.14
  296.1 45.2 all-gather.16
  524.7 42.9 reduce-scatter.6
  569.9 76.8 reduce-scatter.8
  649.1 44.7 reduce-scatter.10
  696.0 110.4 reduce-scatter.4
where the time goes:
time: 849 us; the launch traced here: 841 us
  Pallas kernels  406 us (48%)
  matrix products  129 us (15%)
  waiting for transfers between devices  97.1 us (11%)
  other arithmetic  78.5 us (9%)
  local copies, waits for them, and re-layouts  63.5 us (7%)
  blocking collectives  28.7 us (3%)
  starting transfers between devices  22.9 us (3%)
  between operations  15.3 us (2%)
    pallas_call x2, Pallas kernels, matmul_reduce(): pl.pallas_call(functools.partial(reduce_kernel, nt), out_shape=SDS((r, c)...  95.6 us
    pallas_call x1, Pallas kernels, backward_exchange(): pl.pallas_call(backward_kernel, out_shape=(SDS((r, c), f32), SDS((TP, r,...  92.7 us
    pallas_call x1, Pallas kernels, forward_exchange(): pl.pallas_call(forward_kernel, out_shape=(SDS((r, c), f32), SDS((TP, r, c...  84.6 us
    pallas_call x1, Pallas kernels, second_exchange(): pl.pallas_call(second_kernel, out_shape=(SDS((TP, wo.shape[0], wo.shape[1...  65.3 us
    dot_general x4, matrix products, dot_tn(): lax.dot_general(a, b, (((0,), (0,)), ((), ())), preferred_element_type=f32)  47.8 us
    reduce_scatter x4, waiting for transfers between devices, dp_reduce(): lax.psum_scatter(x, AXIS, scatter_dimension=0, tiled=True, axis_index_gro...  45.9 us
    dot_general x4, matrix products, dot(): lax.dot_general(a, b, (((1,), (0,)), ((), ())), preferred_element_type=f32)  41.3 us
    pallas_call x1, Pallas kernels, plane_gather(): pl.pallas_call(gather_kernel, out_shape=SDS((TP, r, c), x.dtype), in_spec...  39.2 us
  transfers between devices with their start and end apart: 14, of which 6 were waited for; matrix products, arithmetic and copies ran while one was open for 21% of the time, Pallas kernels for 35%

commit v1 on v0

--- a/solution.py
+++ b/solution.py
@@ -8,7 +8,7 @@
 from jax.experimental.pallas import tpu as pltpu
 from jax.sharding import PartitionSpec as P
 
-HEADS = 8
+
 KH = 256
 VH = 512
 TP = 8
@@ -113,17 +113,17 @@
         compiler_params=pltpu.CompilerParams(
             collective_id=cid, has_side_effects=True, vmem_limit_bytes=8 << 20
         ),
-        name=f"plane_gather_{cid}",
     )(x)
 
 
-def send_columns(src, out, cols, at, sems, base, local, t, peer, tiled=True):
+def send_columns(src, out, cols, at, sems, base, local, t, peer, rows=None):
     copies = []
+    rows = slice(None) if rows is None else rows
 
     def block(q):
-        if not tiled:
+        if len(src.shape) == 3:
             return src.at[q]
-        return src.at[:, pl.ds(pl.multiple_of(q * cols, 128), cols)]
+        return src.at[rows, pl.ds(pl.multiple_of(q * cols, 128), cols)]
 
     for k in range(1, TP):
         dev = peer(k)
@@ -144,32 +144,67 @@
         keep.wait()
 
 
-def first_kernel(n, wq, wk, wv, vec, qk_out, v_out, vec_out, ssem, rsem, local):
+def exchange_call(kernel, outs, args, sems, locals_, cid):
+    return pl.pallas_call(
+        kernel,
+        out_shape=outs,
+        in_specs=[VMEM] * len(args),
+        out_specs=tuple(ANY for _ in outs),
+        scratch_shapes=[
+            pltpu.SemaphoreType.DMA((sems,)),
+            pltpu.SemaphoreType.DMA((sems,)),
+            pltpu.SemaphoreType.DMA((locals_,)),
+        ],
+        compiler_params=pltpu.CompilerParams(
+            collective_id=cid, has_side_effects=True, vmem_limit_bytes=12 << 20
+        ),
+    )(*args)
+
+
+def first_kernel(wq, wk, qk_out, ssem, rsem, local):
+    me, peer = place()
+    t = lax.rem(me, TP)
+    greet([peer(k) for k in range(1, TP)])
+    sems = (ssem, rsem)
+    cols = wq.shape[1] // TP
+    finish([
+        send_columns(wq, qk_out, cols, 0, sems, 0, local.at[0], t, peer),
+        send_columns(wk, qk_out, cols, cols, sems, 7, local.at[1], t, peer),
+    ])
+
+
+def first_exchange(wq, wk, cid):
+    outs = (SDS((TP, wq.shape[0], 2 * wq.shape[1] // TP), bf),)
+    return exchange_call(first_kernel, outs, (wq, wk), 14, 2, cid)[0]
+
+
+def second_kernel(n, wv, ws, wo, vec, out, vec_out, ssem, rsem, local):
     dp = n // TP
     me, peer = place()
     t, g = lax.rem(me, TP), lax.div(me, TP)
     others = [lax.rem(me + TP * j, n) for j in range(1, dp)]
     greet([peer(k) for k in range(1, TP)] + others)
     sems = (ssem, rsem)
-    kq, kv = wq.shape[1] // TP, wv.shape[1] // TP
+    shard, cv, co = wv.shape[0], wv.shape[1] // TP, wo.shape[1] // TP
     far = []
-    keep = pltpu.make_async_copy(vec, vec_out.at[g, t], local.at[3])
+    keep = pltpu.make_async_copy(vec, vec_out.at[g, t], local.at[4])
     keep.start()
     for j, dev in enumerate(others):
-        copy = remote(vec, vec_out.at[g, t], sems, 28 + j, dev)
+        copy = remote(vec, vec_out.at[g, t], sems, 35 + j, dev)
         copy.start()
         far.append(copy)
     parts = [
-        send_columns(wq, qk_out, kq, 0, sems, 0, local.at[0], t, peer),
-        send_columns(wk, qk_out, kq, kq, sems, 7, local.at[1], t, peer),
-        send_columns(wv, v_out, kv, 0, sems, 14, local.at[2], t, peer),
+        send_columns(wv, out, cv, 0, sems, 0, local.at[0], t, peer),
+        send_columns(ws, out, cv, cv, sems, 7, local.at[1], t, peer),
+        send_columns(wo, out, co, 2 * cv, sems, 14, local.at[2], t, peer, pl.ds(0, shard)),
+        send_columns(wo, out, co, 2 * cv + co, sems, 21, local.at[3], t, peer, pl.ds(shard, shard)),
     ]
     for copy in far:
         copy.wait()
     keep.wait()
     near = []
     for k in range(1, TP):
-        copy = remote(vec_out.at[:, t], vec_out.at[:, t], sems, 20 + k, peer(k))
+        copy = remote(vec_out.at[:, t], vec_out.at[:, t], sems, 27 + k, peer(k))
         copy.start()
         near.append(copy)
     finish(parts)
@@ -177,63 +212,25 @@
         copy.wait()
 
 
-def first_exchange(n, wq, wk, wv, vec, cid):
-    shard = wq.shape[0]
-    return pl.pallas_call(
-        functools.partial(first_kernel, n),
-        out_shape=(
-            SDS((TP, shard, 2 * wq.shape[1] // TP), bf),
-            SDS((TP, shard, wv.shape[1] // TP), bf),
-            SDS((n // TP, TP) + vec.shape, f32),
-        ),
-        in_specs=[VMEM] * 4,
-        out_specs=(ANY, ANY, ANY),
-        scratch_shapes=[
-            pltpu.SemaphoreType.DMA((28 + n // TP,)),
-            pltpu.SemaphoreType.DMA((28 + n // TP,)),
-            pltpu.SemaphoreType.DMA((4,)),
-        ],
-        compiler_params=pltpu.CompilerParams(
-            collective_id=cid, has_side_effects=True, vmem_limit_bytes=8 << 20
-        ),
-        name="first_exchange",
-    )(wq, wk, wv, vec)
-
-
-def second_kernel(wo, ws, gu, tok, o_out, s_out, gu_out, tok_out, ssem, rsem, local):
+def second_exchange(n, wv, ws, wo, vec, cid):
+    width = 2 * wv.shape[1] // TP + 2 * wo.shape[1] // TP
+    outs = (SDS((TP, wv.shape[0], width), bf), SDS((n // TP, TP) + vec.shape, f32))
+    kernel = functools.partial(second_kernel, n)
+    return exchange_call(kernel, outs, (wv, ws, wo, vec), 35 + n // TP, 5, cid)
+
+
+def third_kernel(gu, tok, gu_out, tok_out, ssem, rsem, local):
     me, peer = place()
     t = lax.rem(me, TP)
     greet([peer(k) for k in range(1, TP)])
     sems = (ssem, rsem)
-    gather_blocks(tok, tok_out, sems, 21, local.at[3], peer)
-    finish([
-        send_columns(wo, o_out, wo.shape[1] // TP, 0, sems, 0, local.at[0], t, peer),
-        send_columns(ws, s_out, ws.shape[1] // TP, 0, sems, 7, local.at[1], t, peer),
-        send_columns(gu, gu_out, gu.shape[2], 0, sems, 14, local.at[2], t, peer, tiled=False),
-    ])
-
-
-def second_exchange(wo, ws, gu, tok, cid):
-    return pl.pallas_call(
-        second_kernel,
-        out_shape=(
-            SDS((TP, wo.shape[0], wo.shape[1] // TP), bf),
-            SDS((TP, ws.shape[0], ws.shape[1] // TP), bf),
-            SDS(gu.shape, bf),
-            SDS((TP,) + tok.shape, bf),
-        ),
-        in_specs=[VMEM] * 4,
-        out_specs=(ANY, ANY, ANY, ANY),
-        scratch_shapes=[
-            pltpu.SemaphoreType.DMA((21 + GATHER_SEMS,)),
-            pltpu.SemaphoreType.DMA((21 + GATHER_SEMS,)),
-            pltpu.SemaphoreType.DMA((4,)),
-        ],
-        compiler_params=pltpu.CompilerParams(
-            collective_id=cid, has_side_effects=True, vmem_limit_bytes=12 << 20
-        ),
-        name="second_exchange",
-    )(wo, ws, gu, tok)
+    gather_blocks(tok, tok_out, sems, 7, local.at[1], peer)
+    finish([send_columns(gu, gu_out, gu.shape[2], 0, sems, 0, local.at[0], t, peer)])
+
+
+def third_exchange(gu, tok, cid):
+    outs = (SDS(gu.shape, bf), SDS((TP,) + tok.shape, bf))
+    return exchange_call(third_kernel, outs, (gu, tok), 7 + GATHER_SEMS, 2, cid)
 
 
 def vector_sum_kernel(n, v_ref, out_ref, near, far, part, ssem, rsem):
@@ -325,9 +322,6 @@
         product(k, pe.at[i])
         return copy
 
-    def rows(ref, at):
-        return pl.ds(at.start, at.size) if ref is None else at
-
     def add(dst, part, got, out=None):
         step = 32
 
@@ -429,7 +423,6 @@
         compiler_params=pltpu.CompilerParams(
             collective_id=cid, has_side_effects=True, vmem_limit_bytes=48 << 20
         ),
-        name=f"matmul_reduce_{cid}",
     )(a, w)
 
 
@@ -607,8 +600,9 @@
     return jax.nn.silu(swish_in) * (centred * lax.rsqrt(jnp.maximum(spread, 0.25)))
 
 
-def mlp_gate(first, second):
-    return jax.nn.gelu(first, approximate=False) * second
+def gelu_and_slope(x):
+    act, pull = jax.vjp(lambda v: jax.nn.gelu(v, approximate=False), x)
+    return act, pull(jnp.ones_like(x))[0]
 
 
 def dot(a, b):
@@ -660,21 +654,21 @@
     for i, v in enumerate((gain1, bias1, gain2, bias2)):
         vec = vec.at[i, :shard].set(v.astype(f32))
     vec = vec.at[4, :3].set(lengths[0].astype(f32))
-    qk_blk, v_blk, vec_all = first_exchange(n, wq, wk, wv, vec, 1)
+    qk_blk = first_exchange(wq, wk, 1)
+    qk = dp_gather(qk_blk.reshape(TP * shard, 2 * KH), n)
+    vso_blk, vec_all = second_exchange(n, after(wv, qk_blk), ws, wo, vec, 2)
+    vso = dp_gather(vso_blk.reshape(TP * shard, 3 * VH), n)
+    gu_in = jnp.concatenate([ff_blocks(wg), ff_blocks(wu)], axis=2)
+    gu_blk, tok_all = third_exchange(gu_in, after(tokens, vso_blk), 3)
+    gu = dp_gather(gu_blk.reshape(TP * shard, 2 * dp * unit), n)
+    down = dp_gather(wd, n)
+    cot_all = plane_gather(after(cot, tok_all), 4)
     gain1f, bias1f, gain2f, bias2f = (
         vec_all[:, :, i, :shard].reshape(1, d) for i in range(4)
     )
     vec2 = jnp.concatenate([gain2f, bias2f], axis=0)
-    qk = dp_gather(qk_blk.reshape(TP * shard, 2 * KH), n)
-    val = dp_gather(v_blk.reshape(TP * shard, VH), n)
-    gu_in = jnp.concatenate([ff_blocks(wg), ff_blocks(wu)], axis=2)
-    o_blk, s_blk, gu_blk, tok_all = second_exchange(after(wo, v_blk), ws, gu_in, tokens, 2)
-    out = dp_gather(o_blk.reshape(TP * wo.shape[0], d // TP), n)
-    out = col_join(plane_a2a(out, n), VH)
-    swi = dp_gather(s_blk.reshape(TP * shard, VH), n)
-    gu = dp_gather(gu_blk.reshape(TP * shard, 2 * dp * unit), n)
-    down = dp_gather(after(wd, gu_blk), n)
-    cot_all = plane_gather(after(cot, tok_all), 3)
+    out = vso[:, 2 * VH :].reshape(n, shard, 2, d // TP).transpose(0, 2, 1, 3)
+    out = col_join(plane_a2a(out.reshape(TP * VH, d // TP), n), VH)
 
     mine = lax.dynamic_slice_in_dim(vec_all, lax.div(me, TP), 1, 0)[0, :, 4, :3]
     order = jnp.arange(TP, dtype=jnp.int32)
@@ -684,45 +678,48 @@
     cosine, sine = rotary_tables(offset)
     mask = decay_mask(segment, offset, head)
 
+    cot_all = cot_all.reshape(TP * rows, d)
     normed = layer_norm(tok_all.reshape(TP * rows, d).astype(f32), gain1f, bias1f).astype(bf)
     qk_out = dot(normed, qk).reshape(TP, rows, 2 * KH)
     query, key = qk_out[..., :KH], qk_out[..., KH:]
-    v_low = dot(normed, val).reshape(TP, rows, VH).astype(bf)
-    swish_in = dot(normed, swi).reshape(TP, rows, VH)
     q_rot = rotate(query, cosine, sine).astype(bf)
     k_rot = rotate(key, cosine, sine).astype(bf)
     plain = bmm("btd,bsd->bts", q_rot, k_rot)
     scores = (plain * mask).astype(bf)
+    v_low = dot(normed, vso[:, :VH]).reshape(TP, rows, VH).astype(bf)
+    swish_in = dot(normed, vso[:, VH : 2 * VH]).reshape(TP, rows, VH)
     retained = bmm("bts,bsd->btd", scores, v_low)
     mixed = group_gate(retained, swish_in).astype(bf)
-    middle, normed2 = forward_exchange(mixed, out, tokens, vec2, 4)
+    middle, normed2 = forward_exchange(mixed, out, tokens, vec2, 5)
     normed2 = normed2.reshape(TP * rows, d)
-    cot_all = cot_all.reshape(TP * rows, d)
     fs = dot(normed2, gu)
     first, second = fs[:, : dp * unit], fs[:, dp * unit :]
-    hidden = mlp_gate(first, second).astype(bf)
-
-    g_down = dp_reduce(dot_tn(hidden, cot_all).astype(bf), n)
+    act, slope = gelu_and_slope(first)
+    hidden = (act * second).astype(bf)
+    down_grad = dot_tn(hidden, cot_all).astype(bf)
+    g_down = dp_reduce(down_grad, n)
+
     g_hidden = dot_nt(cot_all, down)
-    _, pull_gate = jax.vjp(mlp_gate, first, second)
-    g_first, g_second = pull_gate(g_hidden)
-    g_fs = jnp.concatenate([g_first.astype(bf), g_second.astype(bf)], axis=1)
+    g_first = (g_hidden * (second * slope)).astype(bf)
+    g_second = (g_hidden * act).astype(bf)
+    g_fs = jnp.concatenate([g_first, g_second], axis=1)
     gu_grad = dot_tn(normed2, g_fs).astype(bf)
     g_gu = dp_reduce(gu_grad, n)
-    g_fs_in = after(g_fs, gu_grad)
     g_middle, g_low, sums2 = backward_exchange(
-        g_fs_in.reshape(TP, rows, 2 * dp * unit), gu, middle, cot, vec2, 5
+        g_fs.reshape(TP, rows, 2 * dp * unit), gu, middle, cot, vec2, 6
     )
 
     g_low = g_low.reshape(TP * rows, d)
     mixed = mixed.reshape(TP * rows, VH)
-    out_grad = dot_tn(mixed, g_low).astype(bf)
-    g_out = dp_reduce(plane_a2a(col_blocks(out_grad), n), n)
     g_mixed = dot_nt(g_low, out).reshape(TP, rows, VH)
     _, pull_group = jax.vjp(group_gate, retained, swish_in)
     g_retained, g_swish = pull_group(g_mixed)
     g_retained = g_retained.astype(bf)
     g_swish = g_swish.astype(bf)
+    swish_grad = dot_tn(normed, g_swish.reshape(TP * rows, VH)).astype(bf)
+    g_swi = dp_reduce(swish_grad, n)
+    out_grad = dot_tn(mixed, g_low).astype(bf)
+    out_grad = plane_a2a(col_blocks(out_grad), n)
     g_value = bmm("bts,btd->bsd", scores, g_retained).astype(bf)
     g_scores = bmm("btd,bsd->bts", g_retained, v_low)
     g_plain = (g_scores * mask).astype(bf)
@@ -730,32 +727,33 @@
     g_krot = bmm("bts,btd->bsd", g_plain, q_rot)
     g_query = rotate_back(g_qrot, cosine, sine).astype(bf)
     g_key = rotate_back(g_krot, cosine, sine).astype(bf)
-    g_qkvs = jnp.concatenate([g_query, g_key, g_value, g_swish], axis=2)
-    w_qkvs = jnp.concatenate([qk, val, swi], axis=1)
-    qkvs_grad = dot_tn(normed, g_qkvs.reshape(TP * rows, 2 * KH + 2 * VH)).astype(bf)
-    grad_qkvs = dp_reduce(qkvs_grad, n)
-    g_qkvs = after(g_qkvs, qkvs_grad)
-    g_normed = matmul_reduce(g_qkvs, w_qkvs, True, 6)
+    g_qkv = jnp.concatenate([g_query, g_key, g_value], axis=2)
+    qkv_grad = dot_tn(normed, g_qkv.reshape(TP * rows, 2 * KH + VH)).astype(bf)
+    g_qkv_own = dp_reduce(qkv_grad, n)
+    g_out = dp_reduce(out_grad, n)
+    g_qkvs = jnp.concatenate([g_qkv, g_swish], axis=2)
+    w_qkvs = jnp.concatenate([qk, vso[:, : 2 * VH]], axis=1)
+    g_normed = matmul_reduce(g_qkvs, w_qkvs, True, 7)
     inputs = tokens.astype(f32)
     _, pull_norm1 = jax.vjp(layer_norm, inputs, gain1f, bias1f)
     g_in_part, g_gain1, g_bias1 = pull_norm1(g_normed)
     grad_tokens = g_middle + g_in_part
-    hidden = after(hidden, g_normed)
-    layer_out = (middle + matmul_reduce(hidden.reshape(TP, rows, dp * unit), down, False, 7)).astype(bf)
+    ffn = matmul_reduce(hidden.reshape(TP, rows, dp * unit), down, False, 8)
+    layer_out = (middle + ffn).astype(bf)
 
     g_vecs = jnp.concatenate([g_gain1, g_bias1, sums2, jnp.zeros((4, d), f32)], axis=0)
-    g_vecs = vector_sum(n, g_vecs, 8)
+    g_vecs = vector_sum(n, g_vecs, 9)
     g_vecs = lax.dynamic_slice_in_dim(g_vecs, head * shard, shard, 1)
-    grad_qkvs = plane_a2a(grad_qkvs, n).astype(f32)
-    grad_q = col_join(grad_qkvs[:, :KH], shard)
-    grad_k = col_join(grad_qkvs[:, KH : 2 * KH], shard)
-    grad_v = col_join(grad_qkvs[:, 2 * KH : 2 * KH + VH], shard)
-    grad_s = col_join(grad_qkvs[:, 2 * KH + VH :], shard)
-    grad_o = col_join(plane_a2a(g_out, n).astype(f32), wo.shape[0])
+    grad_d = g_down.astype(f32)
     g_gu = plane_a2a(g_gu, n).astype(f32)
     grad_g = ff_join(g_gu[:, : dp * unit])
     grad_u = ff_join(g_gu[:, dp * unit :])
-    grad_d = g_down.astype(f32)
+    grad_s = col_join(plane_a2a(g_swi, n).astype(f32), shard)
+    g_qkv_own = plane_a2a(g_qkv_own, n).astype(f32)
+    grad_q = col_join(g_qkv_own[:, :KH], shard)
+    grad_k = col_join(g_qkv_own[:, KH : 2 * KH], shard)
+    grad_v = col_join(g_qkv_own[:, 2 * KH :], shard)
+    grad_o = col_join(plane_a2a(g_out, n).astype(f32), wo.shape[0])
     return (
         layer_out, grad_tokens, g_vecs[0], g_vecs[1], grad_q, grad_k, grad_v, grad_s, grad_o,
         g_vecs[2], g_vecs[3], grad_g, grad_u, grad_d,
@@ -767,6 +765,8 @@
     row, vec = P(AXIS, None), P(AXIS)
     ins = (row, row, vec, vec, row, row, row, row, row, vec, vec, row, row, row, row)
     outs = (row, row, vec, vec, row, row, row, row, row, vec, vec, row, row, row)
-    return jax.shard_map(
-        lambda *a: on_device(n, *a), mesh=mesh, in_specs=ins, out_specs=outs, check_vma=False
-    )
+
+    def body(*args):
+        return on_device(n, *args)
+
+    return jax.shard_map(body, mesh=mesh, in_specs=ins, out_specs=outs, check_vma=False)

time: 849 us -> 849 us (level)
  waiting for transfers between devices: 97.1 us -> 83.2 us
    all_gather x6 -> x4, waiting for transfers between devices: 33.5 us -> 3.03 us  [dp_gather(): lax.all_gather(x, AXIS, axis=0, tiled=True, axis_index_groups=dp_groups(n))]
    reduce_scatter x4 -> x5, waiting for transfers between devices: 45.9 us -> 66.3 us  [dp_reduce(): lax.psum_scatter(x, AXIS, scatter_dimension=0, tiled=True, axis_index_gro...]
    optimization_barrier x2 -> x0, local copies, waits for them, and re-layouts: 10.5 us -> none  [after(): return lax.optimization_barrier((x,) + deps)[0]]
    dot_general x4 -> x5, matrix products: 47.8 us -> 54.5 us  [dot_tn(): lax.dot_general(a, b, (((0,), (0,)), ((), ())), preferred_element_type=f32)]
    all_to_all x4 -> x5, starting transfers between devices: 22.1 us -> 26.7 us  [plane_a2a(): lax.all_to_all(x, AXIS, 0, 0, axis_index_groups=tp_groups(n), tiled=True)]
    pallas_call x2 -> x3, Pallas kernels: 82.3 us -> 86.4 us  [exchange_call(): pl.pallas_call(kernel, out_shape=outs, in_specs=[VMEM] * len(args), out_s...]
    unnamed x93 -> x97, local copies, waits for them, and re-layouts: 25.1 us -> 26.9 us
    unnamed x5 -> x6, other arithmetic: 19.2 us -> 20.6 us
  transfers between devices with their start and end apart: 14 -> 14, of which waited for: 6 -> 5; matrix products, arithmetic and copies ran while one was open for 21% -> 18% of each run, Pallas kernels for 35% -> 37%
where the time goes in v1:
time: 849 us; the launch traced here: 836 us
  Pallas kernels  412 us (49%)
  matrix products  132 us (16%)
  waiting for transfers between devices  83.2 us (10%)
  other arithmetic  72.2 us (9%)
  local copies, waits for them, and re-layouts  64.8 us (8%)
  blocking collectives  29.2 us (3%)
  starting transfers between devices  27.5 us (3%)
  between operations  15.1 us (2%)
    pallas_call x2, Pallas kernels, matmul_reduce(): pl.pallas_call(functools.partial(reduce_kernel, nt), out_shape=SDS((r, c)...  96.6 us
    pallas_call x1, Pallas kernels, backward_exchange(): pl.pallas_call(backward_kernel, out_shape=(SDS((r, c), f32), SDS((TP, r,...  92.8 us
    pallas_call x3, Pallas kernels, exchange_call(): pl.pallas_call(kernel, out_shape=outs, in_specs=[VMEM] * len(args), out_s...  86.4 us
    pallas_call x1, Pallas kernels, forward_exchange(): pl.pallas_call(forward_kernel, out_shape=(SDS((r, c), f32), SDS((TP, r, c...  85.3 us
    reduce_scatter x5, waiting for transfers between devices, dp_reduce(): lax.psum_scatter(x, AXIS, scatter_dimension=0, tiled=True, axis_index_gro...  66.3 us
    dot_general x5, matrix products, dot_tn(): lax.dot_general(a, b, (((0,), (0,)), ((), ())), preferred_element_type=f32)  54.5 us
    dot_general x4, matrix products, dot(): lax.dot_general(a, b, (((1,), (0,)), ((), ())), preferred_element_type=f32)  40.1 us
    pallas_call x1, Pallas kernels, plane_gather(): pl.pallas_call(gather_kernel, out_shape=SDS((TP, r, c), x.dtype), in_spec...  39 us
  transfers between devices with their start and end apart: 14, of which 5 were waited for; matrix products, arithmetic and copies ran while one was open for 18% of the time, Pallas kernels for 37%

profile of v1, /device:TPU:14, one launch (start us, length us, event | category | flops | bytes accessed | tf_op | source)
XLA Modules:
  0.0 835.8 jit_solution(8997271476246598134)
XLA Ops:
  9.1 9.5 %shard_map.254 = bf16[8,64,512]{2,1,0:T(8,128)(2,1)} custom-call(bf16[64,2048]{1,0:T(8,128)(2,1)S(1)} %copy-done.14, bf16[64,2048]{1,0:T(8,128)(2,1)S(1)} %copy-done.15), custom_call_target="tpu_custom_call" | custom-call | tf_op jit(solution)/shard_map/pallas_call | solution.py:148
  25.7 22.8 %shard_map.255 = (bf16[8,64,1536]{2,1,0:T(8,128)(2,1)}, f32[4,8,8,128]{3,2,1,0:T(8,128)S(1)}) custom-call(bf16[64,4096]{1,0:T(8,128)(2,1)S(1)} %copy-done.11, bf16[64,4096]{1,0:T(8,128)(2,1)S(1)} %copy-done.12, bf16[128,2048]{1,0:T(8,128)(2,1)S(1)} %copy-done.13, f32[8,128]{1,0:T(8,128)S(1)} %scatter.32.vec), custom_call_target="tpu_custom_call" | custom-call | tf_op jit(solution)/shard_map/pallas_call | solution.py:148
  49.8 54.0 %shard_map.256 = (bf16[8,64,1024]{2,1,0:T(8,128)(2,1)}, bf16[8,256,2048]{2,1,0:T(8,128)(2,1)S(1)}) custom-call(bf16[8,64,1024]{2,1,0:T(8,128)(2,1)S(1)} %pad_maximum_fusion.2.gu, bf16[256,2048]{1,0:T(8,128)(2,1)S(1)} %copy-done), custom_call_target="tpu_custom_call" | custom-call | tf_op jit(solution)/shard_map/pallas_call | solution.py:148
  117.1 39.0 %shard_map.258 = bf16[8,256,2048]{2,1,0:T(8,128)(2,1)S(1)} custom-call(bf16[256,2048]{1,0:T(8,128)(2,1)S(1)} %copy-done.8), custom_call_target="tpu_custom_call" | custom-call | tf_op jit(solution)/shard_map/pallas_call | solution.py:103
  159.4 7.7 fusion.35
  190.5 8.1 fusion.38
  201.4 9.7 %multiply_convert_fusion.3 = (bf16[8,256,512]{2,1,0:T(8,128)(2,1)S(1)}, f32[8,256,512]{2,1,0:T(8,128)}) fusion(f32[8,256,512]{2,1,0:T(8,128)S(1)} %get-tuple-element.170, f32[8,256]{1,0:T(8,128)S(1)} %maximum_rsqrt_fusion, f32[8,256]{1,0:T(8,128)S(1)} %broadcast_multiply_fusion, bf16[2048,1536]{1,0:T(8,128)(2,1)} %all-gather.5.cloned.1.call-done, ...), kind=kOutput, calls=%fused_computation.38 | convolution fusion | flops 4328521728 | bytes 21020672 | tf_op jit(solution)/shard_map/dot_general | solution.py:609
  226.5 85.3 %forward_exchange.1 = (f32[256,2048]{1,0:T(8,128)S(1)}, bf16[8,256,2048]{2,1,0:T(8,128)(2,1)}) custom-call(bf16[8,256,512]{2,1,0:T(8,128)(2,1)S(1)} %get-tuple-element.171.a, bf16[512,2048]{1,0:T(8,128)(2,1)} %bitcast.142, bf16[256,2048]{1,0:T(8,128)(2,1)S(1)} %copy-done, f32[2,2048]{1,0:T(2,128)S(1)} %pad_maximum_fusion.9.vec), custom_call_target="tpu_custom_call" | custom-call | tf_op jit(solution)/shard_map/forward_exchange/pallas_call | solution.py:455
  313.1 14.6 %fusion.95 = f32[2048,1024]{1,0:T(8,128)} fusion(bf16[2048,2048]{1,0:T(8,128)(2,1)} %bitcast.170, bf16[2048,1024]{1,0:T(8,128)(2,1)} %all-gather.9.cloned.1.call-done.w), kind=kOutput, calls=%fused_computation.184 | convolution fusion | flops 8589934592 | bytes 20971520 | tf_op jit(solution)/shard_map/dot_general | solution.py:609
  327.7 18.5 %multiply_convert_fusion.1 = (bf16[2048,512]{1,0:T(8,128)(2,1)}, f32[2048,512]{1,0:T(8,128)S(1)}, f32[2048,512]{1,0:T(8,128)}) fusion(f32[2048,1024]{1,0:T(8,128)} %fusion.95, bf16[2048,2048]{1,0:T(8,128)(2,1)} %bitcast.137, bf16[512,2048]{1,0:T(8,128)(2,1)} %all-gather.11.cloned.1.call-done.w), kind=kOutput, calls=%fused_computation.23 | convolution fusion | flops 4369416192 | bytes 29360128 | tf_op jit(solution)/shard_map/dot_general | solution.py:617
  346.2 7.0 multiply_convert_fusion
  359.0 92.8 %backward_exchange.1 = (f32[256,2048]{1,0:T(8,128)}, bf16[8,256,2048]{2,1,0:T(8,128)(2,1)}, f32[2,2048]{1,0:T(2,128)S(1)}) custom-call(bf16[8,256,1024]{2,1,0:T(8,128)(2,1)} %bitcast.139, bf16[2048,1024]{1,0:T(8,128)(2,1)} %all-gather.9.cloned.1.call-done.w, f32[256,2048]{1,0:T(8,128)} %copy-done.7, bf16[256,2048]{1,0:T(8,128)(2,1)S(1)} %copy-done.9, ...), custom_call_target="tpu_custom_call" | custom-call | tf_op jit(solution)/shard_map/backward_exchange/pallas_call | solution.py:510
  451.8 10.7 %multiply_reduce_fusion = (f32[8,256]{1,0:T(8,128)S(1)}, f32[8,256,512]{2,1,0:T(8,128)S(1)}) fusion(f32[8,256,512]{2,1,0:T(8,128)S(1)} %copy-done.17, f32[8,256]{1,0:T(8,128)S(1)} %broadcast_multiply_fusion, f32[8,256,512]{2,1,0:T(8,128)} %get-tuple-element.172, bf16[8,256,2048]{2,1,0:T(8,128)(2,1)} %get-tuple-element.96, ...), kind=kOutput, calls=%fused_computation.21 | convolution fusion | flops 4303353856 | bytes 23085056 | tf_op jit(solution)/shard_map/dot_general | solution.py:617
  497.5 7.3 bitcast_convert_fusion.2
  504.9 8.6 %bitcast_convert_fusion.1 = bf16[512,2048]{1,0:T(8,128)(2,1)S(1)} fusion(bf16[8,256,512]{2,1,0:T(8,128)(2,1)} %copy-done.10, bf16[8,256,2048]{2,1,0:T(8,128)(2,1)} %get-tuple-element.96), kind=kOutput, calls=%fused_computation.18 | convolution fusion | flops 4296015872 | bytes 12582912 | tf_op jit(solution)/shard_map/dot_general | solution.py:613
  513.7 29.2 %all_to_all.54 = bf16[8,512,256]{2,1,0:T(8,128)(2,1)} all-to-all(bf16[8,512,256]{2,1,0:T(8,128)(2,1)S(1)} %bitcast.143), channel_id=1, replica_groups={{0,1,2,3,4,5,6,7},{8,9,10,11,12,13,14,15},{16,17,18,19,20,21,22,23},{24..., dimensions={0} | all-to-all | bytes 4194304 | tf_op jit(solution)/shard_map/all_to_all | solution.py:539
  542.9 15.3 %bitcast_convert_fusion = bf16[2048,1024]{1,0:T(8,128)(2,1)} fusion(bf16[8,256,1024]{2,1,0:T(8,128)(2,1)} %get-tuple-element.159, bf16[8,256,2048]{2,1,0:T(8,128)(2,1)} %copy-done.1, f32[2048]{0:T(1024)S(1)} %add.93, f32[2048]{0:T(1024)S(1)} %mul.296, f32[8,256]{1,0:T(8,128)S(1)} %add_rsqrt_fusion, f32[8,256]{1,0:T(8,128)S(1)} %broadcast_multiply_fusion.1), kind=kOutput, calls=%fused_computation.8 | convolution fusion | flops 8617197568 | bytes 16809984 | tf_op jit(solution)/shard_map/dot_general | solution.py:613
  558.3 9.1 %convolution_convert_fusion.1 = bf16[512,2048]{1,0:T(8,128)(2,1)} fusion(bf16[2048,512]{1,0:T(8,128)(2,1)S(1)} %get-tuple-element.150, bf16[2048,2048]{1,0:T(8,128)(2,1)} %bitcast.138), kind=kOutput, calls=%fused_computation.47 | convolution fusion | flops 4296015872 | bytes 12582912 | tf_op jit(solution)/shard_map/dot_general | solution.py:613
  568.0 14.1 %convolution_convert_fusion = bf16[2048,1024]{1,0:T(8,128)(2,1)} fusion(bf16[2048,2048]{1,0:T(8,128)(2,1)} %bitcast.171, bf16[2048,512]{1,0:T(8,128)(2,1)} %copy-done.20, bf16[2048,512]{1,0:T(8,128)(2,1)} %get-tuple-element.147), kind=kOutput, calls=%fused_computation.43 | convolution fusion | flops 8600420352 | bytes 16777216 | tf_op jit(solution)/shard_map/dot_general | solution.py:613
  588.5 51.7 %shard_map.259 = f32[256,2048]{1,0:T(8,128)S(1)} custom-call(bf16[8,256,1536]{2,1,0:T(8,128)(2,1)} %copy-done.21, bf16[2048,1536]{1,0:T(8,128)(2,1)} %pad_maximum_fusion.w), custom_call_target="tpu_custom_call" | custom-call | tf_op jit(solution)/shard_map/pallas_call | solution.py:416
  647.5 11.6 %vector_sum.1 = f32[8,512]{1,0:T(8,128)S(1)} custom-call(f32[8,2048]{1,0:T(8,128)S(1)} %maximum_maximum_fusion.v_ref), custom_call_target="tpu_custom_call" | custom-call | tf_op jit(solution)/shard_map/vector_sum/pallas_call | solution.py:269
  660.7 44.9 %shard_map.257 = f32[256,2048]{1,0:T(8,128)S(1)} custom-call(bf16[8,256,512]{2,1,0:T(8,128)(2,1)S(1)} %bitcast.136, bf16[512,2048]{1,0:T(8,128)(2,1)} %all-gather.11.cloned.1.call-done.w), custom_call_target="tpu_custom_call" | custom-call | tf_op jit(solution)/shard_map/pallas_call | solution.py:416
  720.1 6.5 all-to-all-start.1
  733.1 66.3 %reduce-scatter.12.cloned.1.call-done = bf16[512,1024]{1,0:T(8,128)(2,1)} async-done(((bf16[2048,1024]{1,0:T(8,128)(2,1)}), bf16[512,1024]{1,0:T(8,128)(2,1)}) %reduce-scatter.12.cloned.1.call-update) | async-done | bytes 1048592 | tf_op jit(solution)/shard_map/reduce_scatter | solution.py:547
  (231 shorter events, 176.2 us)
Async XLA Ops:
  7.2 152.2 %all-gather.7.cloned.1.call-start = ((), (), s32[]{:S(2)}) async-start(), calls=%async_computation.12 | async-start | bytes 2621440 | tf_op jit(solution)/shard_map/all_gather | solution.py:543
  9.1 39.4 %copy-start.36 = (bf16[64,4096]{1,0:T(8,128)(2,1)S(1)}, bf16[64,4096]{1,0:T(8,128)(2,1)}, u32[]{:S(2)}) copy-start(bf16[64,4096]{1,0:T(8,128)(2,1)} %param.36) | copy-start | bytes 1572868
  9.1 40.0 %copy-start.37 = (bf16[64,4096]{1,0:T(8,128)(2,1)S(1)}, bf16[64,4096]{1,0:T(8,128)(2,1)}, u32[]{:S(2)}) copy-start(bf16[64,4096]{1,0:T(8,128)(2,1)} %param.37) | copy-start | bytes 1572868
  18.7 160.1 %all-gather.5.cloned.1.call-start = ((), (), s32[]{:S(2)}) async-start(), calls=%async_computation.11 | async-start | bytes 7864320 | tf_op jit(solution)/shard_map/all_gather | solution.py:543
  48.5 264.6 %all-gather.9.cloned.1.call-start = ((), (), s32[]{:S(2)}) async-start(), calls=%async_computation.13 | async-start | bytes 5242880 | tf_op jit(solution)/shard_map/all_gather | solution.py:543
  107.1 220.6 %all-gather.11.cloned.1.call-start = ((), (), s32[]{:S(2)}) async-start(), calls=%async_computation.14 | async-start | bytes 2621440 | tf_op jit(solution)/shard_map/all_gather | solution.py:543
  107.7 59.4 %copy-start.41 = (f32[128]{0:T(128)}, f32[128]{0:T(128)S(1)}, u32[]{:S(2)}) copy-start(f32[128]{0:T(128)S(1)} %multiply_exponential_fusion) | copy-start | bytes 1540
  108.8 58.3 %copy-start.38 = (f32[8,256]{1,0:T(8,128)}, f32[8,256]{1,0:T(8,128)S(1)}, u32[]{:S(2)}) copy-start(f32[8,256]{1,0:T(8,128)S(1)} %get-tuple-element.161) | copy-start | bytes 24580
  185.8 29.2 %all-to-all-start = ((bf16[8,512,256]{2,1,0:T(8,128)(2,1)}), bf16[8,512,256]{2,1,0:T(8,128)(2,1)}, u32[]{:S(2)}, u32[]{:S(2)}) async-start(bf16[8,512,256]{2,1,0:T(8,128)(2,1)} %bitcast.13), calls=%async_computation | async-start | bytes 4194304 | tf_op jit(solution)/shard_map/all_to_all | solution.py:539
  190.5 8.1 copy-start.22
  190.5 451.4 %reduce-scatter.8.cloned.1.call-start = ((), (), s32[]{:S(2)}) async-start(), calls=%async_computation.16 | async-start | bytes 2621440 | tf_op jit(solution)/shard_map/reduce_scatter | solution.py:547
  211.1 15.4 %copy-start.10 = (bf16[8,256,512]{2,1,0:T(8,128)(2,1)}, bf16[8,256,512]{2,1,0:T(8,128)(2,1)S(1)}, u32[]{:S(2)}) copy-start(bf16[8,256,512]{2,1,0:T(8,128)(2,1)S(1)} %get-tuple-element.171.a) | copy-start | bytes 6291460
  353.2 205.1 %copy-start.3 = (bf16[2048,512]{1,0:T(8,128)(2,1)}, bf16[2048,512]{1,0:T(8,128)(2,1)S(1)}, u32[]{:S(2)}) copy-start(bf16[2048,512]{1,0:T(8,128)(2,1)S(1)} %get-tuple-element.150) | copy-start | bytes 6291460
  359.0 92.8 %copy-start.17 = (f32[8,256,512]{2,1,0:T(8,128)S(1)}, f32[8,256,512]{2,1,0:T(8,128)}, u32[]{:S(2)}) copy-start(f32[8,256,512]{2,1,0:T(8,128)} %copy-done.16) | copy-start | bytes 12582916
  359.0 92.9 %copy-start.24 = (bf16[512,2048,1]{1,0,2:T(8,128)(2,1)S(1)}, bf16[512,2048,1]{1,0,2:T(8,128)(2,1)}, u32[]{:S(2)}) copy-start(bf16[512,2048,1]{1,0,2:T(8,128)(2,1)} %reshape.596) | copy-start | bytes 6291460
  451.8 10.8 %copy-start.18 = (f32[8,256,512]{2,1,0:T(8,128)S(1)}, f32[8,256,512]{2,1,0:T(8,128)}, u32[]{:S(2)}) copy-start(f32[8,256,512]{2,1,0:T(8,128)} %get-tuple-element.172) | copy-start | bytes 12582916
  504.9 202.1 %reduce-scatter.10.cloned.1.call-start = ((), (), s32[]{:S(2)}) async-start(), calls=%async_computation.17 | async-start | bytes 2621440 | tf_op jit(solution)/shard_map/reduce_scatter | solution.py:547
  542.8 177.3 %reduce-scatter.6.cloned.1.call-start = ((), (), s32[]{:S(2)}) async-start(), calls=%async_computation.15 | async-start | bytes 5242880 | tf_op jit(solution)/shard_map/reduce_scatter | solution.py:547
  558.3 172.7 %reduce-scatter.14.cloned.1.call-start = ((), (), s32[]{:S(2)}) async-start(), calls=%async_computation.19 | async-start | bytes 2621440 | tf_op jit(solution)/shard_map/reduce_scatter | solution.py:547
  567.5 231.8 %reduce-scatter.12.cloned.1.call-start = ((), (), s32[]{:S(2)}) async-start(), calls=%async_computation.18 | async-start | bytes 5242880 | tf_op jit(solution)/shard_map/reduce_scatter | solution.py:547
  641.9 65.1 %all-to-all-start.2 = ((bf16[8,64,512]{2,1,0:T(8,128)(2,1)}), bf16[8,64,512]{2,1,0:T(8,128)(2,1)}, u32[]{:S(2)}, u32[]{:S(2)}) async-start(bf16[8,64,512]{2,1,0:T(8,128)(2,1)} %bitcast.162), calls=%async_computation.4 | async-start | bytes 1048576 | tf_op jit(solution)/shard_map/all_to_all | solution.py:539
  707.0 13.1 %all-to-all-start.4 = ((bf16[8,128,256]{2,1,0:T(8,128)(2,1)}), bf16[8,128,256]{2,1,0:T(8,128)(2,1)}, u32[]{:S(2)}, u32[]{:S(2)}) async-start(bf16[8,128,256]{2,1,0:T(8,128)(2,1)} %bitcast.163), calls=%async_computation.7 | async-start | bytes 1048576 | tf_op jit(solution)/shard_map/all_to_all | solution.py:539
  720.1 79.2 %all-to-all-start.1 = ((bf16[8,64,1024]{2,1,0:T(8,128)(2,1)}), bf16[8,64,1024]{2,1,0:T(8,128)(2,1)}, u32[]{:S(2)}, u32[]{:S(2)}) async-start(bf16[8,64,1024]{2,1,0:T(8,128)(2,1)} %bitcast.156), calls=%async_computation.2 | async-start | bytes 2097152 | tf_op jit(solution)/shard_map/all_to_all | solution.py:539
  799.3 17.3 %all-to-all-start.5 = ((bf16[8,64,1024]{2,1,0:T(8,128)(2,1)}), bf16[8,64,1024]{2,1,0:T(8,128)(2,1)S(1)}, u32[]{:S(2)}, u32[]{:S(2)}) async-start(bf16[8,64,1024]{2,1,0:T(8,128)(2,1)} %bitcast.157), calls=%async_computation.9 | async-start | bytes 2097152 | tf_op jit(solution)/shard_map/all_to_all | solution.py:539
  (38 other events, 101.6 us)
Sparse Core Ops, SparseCore 0:
  18.8 45.4 all-gather.6
  65.9 112.9 all-gather.4
  180.4 79.2 all-gather.8
  261.1 45.2 all-gather.10
  505.0 44.3 reduce-scatter.7
  551.5 42.8 reduce-scatter.9
  596.7 78.2 reduce-scatter.5
  677.2 42.9 reduce-scatter.13
  722.5 76.7 reduce-scatter.11

commit v2 on v1

--- a/solution.py
+++ b/solution.py
@@ -161,50 +161,52 @@
     )(*args)
 
 
-def first_kernel(wq, wk, qk_out, ssem, rsem, local):
+def first_kernel(wq, wk, wo, out, ssem, rsem, local):
     me, peer = place()
     t = lax.rem(me, TP)
     greet([peer(k) for k in range(1, TP)])
     sems = (ssem, rsem)
-    cols = wq.shape[1] // TP
+    shard, cq, co = wq.shape[0], wq.shape[1] // TP, wo.shape[1] // TP
+    low, high = pl.ds(0, shard), pl.ds(shard, shard)
     finish([
-        send_columns(wq, qk_out, cols, 0, sems, 0, local.at[0], t, peer),
-        send_columns(wk, qk_out, cols, cols, sems, 7, local.at[1], t, peer),
+        send_columns(wq, out, cq, 0, sems, 0, local.at[0], t, peer),
+        send_columns(wk, out, cq, cq, sems, 7, local.at[1], t, peer),
+        send_columns(wo, out, co, 2 * cq, sems, 14, local.at[2], t, peer, low),
+        send_columns(wo, out, co, 2 * cq + co, sems, 21, local.at[3], t, peer, high),
     ])
 
 
-def first_exchange(wq, wk, cid):
-    outs = (SDS((TP, wq.shape[0], 2 * wq.shape[1] // TP), bf),)
-    return exchange_call(first_kernel, outs, (wq, wk), 14, 2, cid)[0]
-
-
-def second_kernel(n, wv, ws, wo, vec, out, vec_out, ssem, rsem, local):
+def first_exchange(wq, wk, wo, cid):
+    width = 2 * wq.shape[1] // TP + 2 * wo.shape[1] // TP
+    outs = (SDS((TP, wq.shape[0], width), bf),)
+    return exchange_call(first_kernel, outs, (wq, wk, wo), 28, 4, cid)[0]
+
+
+def second_kernel(n, wv, ws, vec, out, vec_out, ssem, rsem, local):
     dp = n // TP
     me, peer = place()
     t, g = lax.rem(me, TP), lax.div(me, TP)
     others = [lax.rem(me + TP * j, n) for j in range(1, dp)]
     greet([peer(k) for k in range(1, TP)] + others)
     sems = (ssem, rsem)
-    shard, cv, co = wv.shape[0], wv.shape[1] // TP, wo.shape[1] // TP
+    cols = wv.shape[1] // TP
     far = []
-    keep = pltpu.make_async_copy(vec, vec_out.at[g, t], local.at[4])
+    keep = pltpu.make_async_copy(vec, vec_out.at[g, t], local.at[2])
     keep.start()
     for j, dev in enumerate(others):
-        copy = remote(vec, vec_out.at[g, t], sems, 35 + j, dev)
+        copy = remote(vec, vec_out.at[g, t], sems, 21 + j, dev)
         copy.start()
         far.append(copy)
     parts = [
-        send_columns(wv, out, cv, 0, sems, 0, local.at[0], t, peer),
-        send_columns(ws, out, cv, cv, sems, 7, local.at[1], t, peer),
-        send_columns(wo, out, co, 2 * cv, sems, 14, local.at[2], t, peer, pl.ds(0, shard)),
-        send_columns(wo, out, co, 2 * cv + co, sems, 21, local.at[3], t, peer, pl.ds(shard, shard)),
+        send_columns(wv, out, cols, 0, sems, 0, local.at[0], t, peer),
+        send_columns(ws, out, cols, cols, sems, 7, local.at[1], t, peer),
     ]
     for copy in far:
         copy.wait()
     keep.wait()
     near = []
     for k in range(1, TP):
-        copy = remote(vec_out.at[:, t], vec_out.at[:, t], sems, 27 + k, peer(k))
+        copy = remote(vec_out.at[:, t], vec_out.at[:, t], sems, 13 + k, peer(k))
         copy.start()
         near.append(copy)
     finish(parts)
@@ -212,11 +214,13 @@
         copy.wait()
 
 
-def second_exchange(n, wv, ws, wo, vec, cid):
-    width = 2 * wv.shape[1] // TP + 2 * wo.shape[1] // TP
-    outs = (SDS((TP, wv.shape[0], width), bf), SDS((n // TP, TP) + vec.shape, f32))
+def second_exchange(n, wv, ws, vec, cid):
+    outs = (
+        SDS((TP, wv.shape[0], 2 * wv.shape[1] // TP), bf),
+        SDS((n // TP, TP) + vec.shape, f32),
+    )
     kernel = functools.partial(second_kernel, n)
-    return exchange_call(kernel, outs, (wv, ws, wo, vec), 35 + n // TP, 5, cid)
+    return exchange_call(kernel, outs, (wv, ws, vec), 21 + n // TP, 3, cid)
 
 
 def third_kernel(gu, tok, gu_out, tok_out, ssem, rsem, local):
@@ -289,25 +293,12 @@
 TILE = 512
 
 
-def reduce_blocks(nt, a, w, po, pe, rc, sb, xr, yr, sems, peer):
-    r = a.shape[1]
-    c = pe.shape[2]
+def reduce_blocks(product, po, pe, rc, sb, xr, yr, sems, peer, prepare=None):
+    r = pe.shape[1]
     h = r // 2
     top, bot = pl.ds(0, h), pl.ds(h, h)
     pc, px, py = peer(1), peer(2), peer(4)
     sent = []
-
-    def product(k, dst):
-        @pl.loop(0, c // TILE)
-        def _(j):
-            at = pl.ds(pl.multiple_of(j * TILE, TILE), TILE)
-            if nt:
-                y = lax.dot_general(
-                    a[k], w[at, :], (((1,), (1,)), ((), ())), preferred_element_type=f32
-                )
-            else:
-                y = jnp.dot(a[k], w[:, at], preferred_element_type=f32)
-            dst[:, at] = y.astype(dst.dtype)
 
     def send(src, dst, dev, i):
         copy = remote(src, dst, sems, i, dev)
@@ -317,6 +308,8 @@
 
     def pair(i):
         k = 2 * i
+        if prepare is not None:
+            prepare(k)
         product(k + 1, po.at[i])
         copy = send(po.at[i], rc.at[i], pc, i)
         product(k, pe.at[i])
@@ -397,10 +390,27 @@
     ]
 
 
+def times(a, w, nt):
+    def product(k, dst):
+        @pl.loop(0, dst.shape[1] // TILE)
+        def _(j):
+            at = pl.ds(pl.multiple_of(j * TILE, TILE), TILE)
+            if nt:
+                y = lax.dot_general(
+                    a[k], w[at, :], (((1,), (1,)), ((), ())), preferred_element_type=f32
+                )
+            else:
+                y = jnp.dot(a[k], w[:, at], preferred_element_type=f32)
+            dst[:, at] = y.astype(dst.dtype)
+
+    return product
+
+
 def reduce_kernel(nt, a, w, out_ref, po, pe, rc, sb, xr, yr, ssem, rsem):
     _, peer = place()
     greet([peer(1), peer(2), peer(4)])
-    for_rows, sent = reduce_blocks(nt, a, w, po, pe, rc, sb, xr, yr, (ssem, rsem), peer)
+    product = times(a, w, nt)
+    for_rows, sent = reduce_blocks(product, po, pe, rc, sb, xr, yr, (ssem, rsem), peer)
 
     def body(at, value):
         out_ref[at, :] = value
@@ -426,11 +436,61 @@
     )(a, w)
 
 
-def forward_kernel(a, w, tok, vec, mid, out, po, pe, rc, sb, xr, yr, own, ssem, rsem, local):
+def forward_kernel(
+    nrm, wvs, sco, w, tok, vec, v_out, mix_out, ret_out, swi_out, mid, out,
+    v_buf, mix_buf, ret_buf, swi_buf, po, pe, rc, sb, xr, yr, own, ssem, rsem, local,
+):
     _, peer = place()
     greet([peer(1), peer(2), peer(4)])
     sems = (ssem, rsem)
-    for_rows, sent = reduce_blocks(False, a, w, po, pe, rc, sb, xr, yr, sems, peer)
+    r, width = v_buf.shape[1:]
+    kept = []
+
+    def prepare(first):
+        @pl.loop(0, 2)
+        def _(i):
+            k = first + i
+
+            @pl.loop(0, width // 256)
+            def _(j):
+                at = pl.ds(pl.multiple_of(j * 256, 256), 256)
+                behind = pl.ds(pl.multiple_of(j * 256 + width, 256), 256)
+                v = jnp.dot(nrm[k], wvs[:, at], preferred_element_type=f32).astype(bf)
+                v_buf[k, :, at] = v
+                swi_buf[k, :, at] = jnp.dot(nrm[k], wvs[:, behind], preferred_element_type=f32)
+                ret_buf[k, :, at] = jnp.dot(sco[k], v, preferred_element_type=f32)
+
+            @pl.loop(0, r // 32)
+            def _(j):
+                at = pl.ds(pl.multiple_of(j * 32, 32), 32)
+                value = ret_buf[k, at, :]
+                centred = value - jnp.mean(value, axis=-1, keepdims=True)
+                spread = jnp.mean(centred * centred, axis=-1, keepdims=True)
+                gate = swi_buf[k, at, :]
+                gate = gate / (1.0 + jnp.exp(-gate))
+                mix_buf[k, at, :] = (
+                    gate * (centred * lax.rsqrt(jnp.maximum(spread, 0.25)))
+                ).astype(bf)
+
+        two = pl.ds(first, 2)
+        for i, (src, dst) in enumerate(
+            ((v_buf, v_out), (mix_buf, mix_out), (ret_buf, ret_out), (swi_buf, swi_out))
+        ):
+            copy = pltpu.make_async_copy(
+                src.at[two], dst.at[two], local.at[1 + 2 * first + i]
+            )
+            copy.start()
+            kept.append(copy)
+
+    def product(k, dst):
+        step = w.shape[2]
+
+        @pl.loop(0, w.shape[0])
+        def _(j):
+            at = pl.ds(pl.multiple_of(j * step, step), step)
+            dst[:, at] = jnp.dot(mix_buf[k], w[j], preferred_element_type=f32).astype(dst.dtype)
+
+    for_rows, sent = reduce_blocks(product, po, pe, rc, sb, xr, yr, sems, peer, prepare)
 
     def body(at, value):
         value = value + tok[at, :].astype(f32)
@@ -443,32 +503,113 @@
         ).astype(bf)
 
     for_rows(16, body)
-    gather_blocks(own, out, sems, REDUCE_SEMS, local, peer)
+    gather_blocks(own, out, sems, REDUCE_SEMS, local.at[0], peer)
     for copy in sent:
         copy.wait_send()
-
-
-def forward_exchange(a, w, tok, vec, cid):
-    _, r, _ = a.shape
-    c = w.shape[1]
+    for copy in kept:
+        copy.wait()
+
+
+def forward_exchange(nrm, wvs, sco, w, tok, vec, cid):
+    _, r, d = nrm.shape
+    width = w.shape[1]
     count = REDUCE_SEMS + GATHER_SEMS
+    blocks = [((TP, r, width), t) for t in (bf, bf, f32, f32)]
     return pl.pallas_call(
         forward_kernel,
-        out_shape=(SDS((r, c), f32), SDS((TP, r, c), bf)),
-        in_specs=[VMEM] * 4,
-        out_specs=(VMEM, ANY),
-        scratch_shapes=reduce_scratch(r, c)
+        out_shape=tuple(SDS(*b) for b in blocks) + (SDS((r, d), f32), SDS((TP, r, d), bf)),
+        in_specs=[VMEM] * 6,
+        out_specs=(ANY,) * 4 + (VMEM, ANY),
+        scratch_shapes=[pltpu.VMEM(*b) for b in blocks]
+        + reduce_scratch(r, d)
         + [
-            pltpu.VMEM((r, c), bf),
+            pltpu.VMEM((r, d), bf),
             pltpu.SemaphoreType.DMA((count,)),
             pltpu.SemaphoreType.DMA((count,)),
-            pltpu.SemaphoreType.DMA,
+            pltpu.SemaphoreType.DMA((17,)),
         ],
         compiler_params=pltpu.CompilerParams(
-            collective_id=cid, has_side_effects=True, vmem_limit_bytes=48 << 20
+            collective_id=cid, has_side_effects=True, vmem_limit_bytes=60 << 20
         ),
         name="forward_exchange",
-    )(a, w, tok, vec)
+    )(nrm, wvs, sco, w, tok, vec)
+
+
+def hidden_kernel(x, gu, hid, act_out, slope_out):
+    width = hid.shape[2]
+    step = 256
+
+    @pl.loop(0, width // step)
+    def _(j):
+        at = pl.ds(pl.multiple_of(j * step, step), step)
+        behind = pl.ds(pl.multiple_of(j * step + width, step), step)
+        first = jnp.dot(x[0], gu[:, at], preferred_element_type=f32)
+        second = jnp.dot(x[0], gu[:, behind], preferred_element_type=f32)
+        share = 0.5 * (1.0 + lax.erf(first * math.sqrt(0.5)))
+        act = first * share
+        slope = share + first * (jnp.exp(-0.5 * first * first) * (1.0 / math.sqrt(2.0 * math.pi)))
+        hid[0, :, at] = (act * second).astype(bf)
+        act_out[0, :, at] = act
+        slope_out[0, :, at] = slope * second
+
+
+def hidden_units(x, gu):
+    _, r, d = x.shape
+    width = gu.shape[1] // 2
+    row = pl.BlockSpec((1, r, width), lambda k: (k, 0, 0))
+    return pl.pallas_call(
+        hidden_kernel,
+        grid=(TP,),
+        out_shape=tuple(SDS((TP, r, width), t) for t in (bf, f32, f32)),
+        in_specs=[
+            pl.BlockSpec((1, r, d), lambda k: (k, 0, 0)),
+            pl.BlockSpec(gu.shape, lambda k: (0, 0)),
+        ],
+        out_specs=(row, row, row),
+        compiler_params=pltpu.CompilerParams(vmem_limit_bytes=32 << 20),
+        cost_estimate=pl.CostEstimate(
+            flops=4 * TP * r * d * width, bytes_accessed=24 << 20, transcendentals=2 * TP * r * width
+        ),
+        name="hidden_units",
+    )(x, gu)
+
+
+def hidden_back_kernel(cot, down, act, slope, out):
+    width = act.shape[2]
+    step = 256
+
+    @pl.loop(0, width // step)
+    def _(j):
+        at = pl.ds(pl.multiple_of(j * step, step), step)
+        behind = pl.ds(pl.multiple_of(j * step + width, step), step)
+        grad = lax.dot_general(
+            cot[0], down[at, :], (((1,), (1,)), ((), ())), preferred_element_type=f32
+        )
+        out[0, :, at] = (grad * slope[0, :, at]).astype(bf)
+        out[0, :, behind] = (grad * act[0, :, at]).astype(bf)
+
+
+def hidden_back(cot, down, act, slope):
+    _, r, d = cot.shape
+    width = act.shape[2]
+    row = pl.BlockSpec((1, r, width), lambda k: (k, 0, 0))
+    return pl.pallas_call(
+        hidden_back_kernel,
+        grid=(TP,),
+        out_shape=SDS((TP, r, 2 * width), bf),
+        in_specs=[
+            pl.BlockSpec((1, r, d), lambda k: (k, 0, 0)),
+            pl.BlockSpec(down.shape, lambda k: (0, 0)),
+            row,
+            row,
+        ],
+        out_specs=pl.BlockSpec((1, r, 2 * width), lambda k: (k, 0, 0)),
+        compiler_params=pltpu.CompilerParams(vmem_limit_bytes=32 << 20),
+        cost_estimate=pl.CostEstimate(
+            flops=2 * TP * r * d * width, bytes_accessed=24 << 20, transcendentals=0
+        ),
+        name="hidden_back",
+    )(cot, down, act, slope)
 
 
 def backward_kernel(
@@ -478,7 +619,7 @@
     greet([peer(1), peer(2), peer(4)])
     sems = (ssem, rsem)
     acc[...] = jnp.zeros_like(acc)
-    for_rows, sent = reduce_blocks(True, a, w, po, pe, rc, sb, xr, yr, sems, peer)
+    for_rows, sent = reduce_blocks(times(a, w, True), po, pe, rc, sb, xr, yr, sems, peer)
 
     def body(at, g):
         value = mid[at, :]
@@ -600,11 +741,6 @@
     return jax.nn.silu(swish_in) * (centred * lax.rsqrt(jnp.maximum(spread, 0.25)))
 
 
-def gelu_and_slope(x):
-    act, pull = jax.vjp(lambda v: jax.nn.gelu(v, approximate=False), x)
-    return act, pull(jnp.ones_like(x))[0]
-
-
 def dot(a, b):
     return lax.dot_general(a, b, (((1,), (0,)), ((), ())), preferred_element_type=f32)
 
@@ -629,6 +765,37 @@
 def col_join(w, r):
     c = w.shape[1]
     return w.reshape(TP, r, c).transpose(1, 0, 2).reshape(r, TP * c)
+
+
+def join_kernel(widths, parts, x, *outs):
+    at = 0
+    for out, width in zip(outs, widths):
+        piece = width // parts
+        for t in range(TP):
+            for p in range(parts):
+                to = (p * TP + t) * piece
+                out[:, to : to + piece] = x[t, :, at + p * piece : at + (p + 1) * piece].astype(f32)
+        at += width
+
+
+def join(x, widths, parts=1):
+    r = x.shape[1]
+    if any(width // parts % 128 for width in widths):
+        made, at = [], 0
+        for width in widths:
+            part = x[:, :, at : at + width].reshape(TP, r, parts, width // parts)
+            made.append(part.transpose(1, 2, 0, 3).reshape(r, TP * width).astype(f32))
+            at += width
+        return made
+    return pl.pallas_call(
+        functools.partial(join_kernel, widths, parts),
+        out_shape=tuple(SDS((r, TP * width), f32) for width in widths),
+        in_specs=[VMEM],
+        out_specs=tuple(VMEM for _ in widths),
+        compiler_params=pltpu.CompilerParams(vmem_limit_bytes=8 << 20),
+        cost_estimate=pl.CostEstimate(flops=0, bytes_accessed=6 * x.size, transcendentals=0),
+        name="join",
+    )(x)
 
 
 def after(x, *deps):
@@ -647,19 +814,16 @@
     def ff_blocks(w):
         return w.reshape(shard, dp, TP, unit).transpose(2, 0, 1, 3).reshape(TP, shard, dp * unit)
 
-    def ff_join(w):
-        return w.reshape(TP, shard, dp, unit).transpose(1, 2, 0, 3).reshape(shard, ff)
-
     vec = jnp.zeros((8, 128), f32)
     for i, v in enumerate((gain1, bias1, gain2, bias2)):
         vec = vec.at[i, :shard].set(v.astype(f32))
     vec = vec.at[4, :3].set(lengths[0].astype(f32))
-    qk_blk = first_exchange(wq, wk, 1)
-    qk = dp_gather(qk_blk.reshape(TP * shard, 2 * KH), n)
-    vso_blk, vec_all = second_exchange(n, after(wv, qk_blk), ws, wo, vec, 2)
-    vso = dp_gather(vso_blk.reshape(TP * shard, 3 * VH), n)
+    qko_blk = first_exchange(wq, wk, wo, 1)
+    qko = dp_gather(qko_blk.reshape(TP * shard, 4 * KH), n)
+    vs_blk, vec_all = second_exchange(n, after(wv, qko_blk), ws, vec, 2)
+    vs = dp_gather(vs_blk.reshape(TP * shard, 2 * VH), n)
     gu_in = jnp.concatenate([ff_blocks(wg), ff_blocks(wu)], axis=2)
-    gu_blk, tok_all = third_exchange(gu_in, after(tokens, vso_blk), 3)
+    gu_blk, tok_all = third_exchange(gu_in, after(tokens, vs_blk), 3)
     gu = dp_gather(gu_blk.reshape(TP * shard, 2 * dp * unit), n)
     down = dp_gather(wd, n)
     cot_all = plane_gather(after(cot, tok_all), 4)
@@ -667,8 +831,8 @@
         vec_all[:, :, i, :shard].reshape(1, d) for i in range(4)
     )
     vec2 = jnp.concatenate([gain2f, bias2f], axis=0)
-    out = vso[:, 2 * VH :].reshape(n, shard, 2, d // TP).transpose(0, 2, 1, 3)
-    out = col_join(plane_a2a(out.reshape(TP * VH, d // TP), n), VH)
+    out = qko[:, 2 * KH :].reshape(n, shard, 2, d // TP).transpose(0, 2, 1, 3)
+    out_blk = plane_a2a(out.reshape(TP * VH, d // TP), n)
 
     mine = lax.dynamic_slice_in_dim(vec_all, lax.div(me, TP), 1, 0)[0, :, 4, :3]
     order = jnp.arange(TP, dtype=jnp.int32)
@@ -678,36 +842,26 @@
     cosine, sine = rotary_tables(offset)
     mask = decay_mask(segment, offset, head)
 
-    cot_all = cot_all.reshape(TP * rows, d)
     normed = layer_norm(tok_all.reshape(TP * rows, d).astype(f32), gain1f, bias1f).astype(bf)
-    qk_out = dot(normed, qk).reshape(TP, rows, 2 * KH)
+    qk_out = dot(normed, qko[:, : 2 * KH]).reshape(TP, rows, 2 * KH)
     query, key = qk_out[..., :KH], qk_out[..., KH:]
     q_rot = rotate(query, cosine, sine).astype(bf)
     k_rot = rotate(key, cosine, sine).astype(bf)
     plain = bmm("btd,bsd->bts", q_rot, k_rot)
     scores = (plain * mask).astype(bf)
-    v_low = dot(normed, vso[:, :VH]).reshape(TP, rows, VH).astype(bf)
-    swish_in = dot(normed, vso[:, VH : 2 * VH]).reshape(TP, rows, VH)
-    retained = bmm("bts,bsd->btd", scores, v_low)
-    mixed = group_gate(retained, swish_in).astype(bf)
-    middle, normed2 = forward_exchange(mixed, out, tokens, vec2, 5)
+    v_low, mixed, retained, swish_in, middle, normed2 = forward_exchange(
+        normed.reshape(TP, rows, d), vs, scores, out_blk.reshape(TP, VH, d // TP), tokens, vec2, 5
+    )
+    out = col_join(out_blk, VH)
+    hidden, act, slope = hidden_units(normed2, gu)
     normed2 = normed2.reshape(TP * rows, d)
-    fs = dot(normed2, gu)
-    first, second = fs[:, : dp * unit], fs[:, dp * unit :]
-    act, slope = gelu_and_slope(first)
-    hidden = (act * second).astype(bf)
-    down_grad = dot_tn(hidden, cot_all).astype(bf)
+    down_grad = dot_tn(hidden.reshape(TP * rows, dp * unit), cot_all.reshape(TP * rows, d)).astype(bf)
     g_down = dp_reduce(down_grad, n)
 
-    g_hidden = dot_nt(cot_all, down)
-    g_first = (g_hidden * (second * slope)).astype(bf)
-    g_second = (g_hidden * act).astype(bf)
-    g_fs = jnp.concatenate([g_first, g_second], axis=1)
-    gu_grad = dot_tn(normed2, g_fs).astype(bf)
+    g_fs = hidden_back(cot_all, down, act, slope)
+    gu_grad = dot_tn(normed2, g_fs.reshape(TP * rows, 2 * dp * unit)).astype(bf)
     g_gu = dp_reduce(gu_grad, n)
-    g_middle, g_low, sums2 = backward_exchange(
-        g_fs.reshape(TP, rows, 2 * dp * unit), gu, middle, cot, vec2, 6
-    )
+    g_middle, g_low, sums2 = backward_exchange(g_fs, gu, middle, cot, vec2, 6)
 
     g_low = g_low.reshape(TP * rows, d)
     mixed = mixed.reshape(TP * rows, VH)
@@ -732,28 +886,27 @@
     g_qkv_own = dp_reduce(qkv_grad, n)
     g_out = dp_reduce(out_grad, n)
     g_qkvs = jnp.concatenate([g_qkv, g_swish], axis=2)
-    w_qkvs = jnp.concatenate([qk, vso[:, : 2 * VH]], axis=1)
+    w_qkvs = jnp.concatenate([qko[:, : 2 * KH], vs], axis=1)
     g_normed = matmul_reduce(g_qkvs, w_qkvs, True, 7)
     inputs = tokens.astype(f32)
     _, pull_norm1 = jax.vjp(layer_norm, inputs, gain1f, bias1f)
     g_in_part, g_gain1, g_bias1 = pull_norm1(g_normed)
     grad_tokens = g_middle + g_in_part
-    ffn = matmul_reduce(hidden.reshape(TP, rows, dp * unit), down, False, 8)
+    ffn = matmul_reduce(hidden, down, False, 8)
     layer_out = (middle + ffn).astype(bf)
 
     g_vecs = jnp.concatenate([g_gain1, g_bias1, sums2, jnp.zeros((4, d), f32)], axis=0)
     g_vecs = vector_sum(n, g_vecs, 9)
     g_vecs = lax.dynamic_slice_in_dim(g_vecs, head * shard, shard, 1)
     grad_d = g_down.astype(f32)
-    g_gu = plane_a2a(g_gu, n).astype(f32)
-    grad_g = ff_join(g_gu[:, : dp * unit])
-    grad_u = ff_join(g_gu[:, dp * unit :])
-    grad_s = col_join(plane_a2a(g_swi, n).astype(f32), shard)
-    g_qkv_own = plane_a2a(g_qkv_own, n).astype(f32)
-    grad_q = col_join(g_qkv_own[:, :KH], shard)
-    grad_k = col_join(g_qkv_own[:, KH : 2 * KH], shard)
-    grad_v = col_join(g_qkv_own[:, 2 * KH :], shard)
-    grad_o = col_join(plane_a2a(g_out, n).astype(f32), wo.shape[0])
+    g_gu = plane_a2a(g_gu, n)
+    grad_g, grad_u = join(g_gu.reshape(TP, shard, 2 * dp * unit), (dp * unit,) * 2, dp)
+    g_swi = plane_a2a(g_swi, n)
+    (grad_s,) = join(g_swi.reshape(TP, shard, VH), (VH,))
+    g_qkv_own = plane_a2a(g_qkv_own, n)
+    grad_q, grad_k, grad_v = join(g_qkv_own.reshape(TP, shard, 2 * KH + VH), (KH, KH, VH))
+    g_out = plane_a2a(g_out, n)
+    (grad_o,) = join(g_out.reshape(TP, wo.shape[0], d // TP), (d // TP,))
     return (
         layer_out, grad_tokens, g_vecs[0], g_vecs[1], grad_q, grad_k, grad_v, grad_s, grad_o,
         g_vecs[2], g_vecs[3], grad_g, grad_u, grad_d,

time: 849 us -> 842 us (level)
  Pallas kernels: 412 us -> 500 us
  matrix products: 132 us -> 73 us
  local copies, waits for them, and re-layouts: 64.8 us -> 50.6 us
  waiting for transfers between devices: 83.2 us -> 70 us
    pallas_call x1 -> x7, Pallas kernels: 85.3 us -> 150 us  [the longest x1 116 us: forward_exchange(): pl.pallas_call(forward_kernel, out_shape=tuple((SDS(*b) for b in blocks))...]
    dot_general x4 -> x1, matrix products: 40.1 us -> 6.87 us  [dot(): lax.dot_general(a, b, (((1,), (0,)), ((), ())), preferred_element_type=f32)]
    reshape x12 -> x1, local copies, waits for them, and re-layouts: 23.9 us -> 2.55 us  [on_device(): out = qko[:, 2 * KH:].reshape(n, shard, 2, d // TP).transpose(0, 2, 1, 3)]
    pallas_call x1, Pallas kernels: 39 us -> 60.1 us  [plane_gather(): pl.pallas_call(gather_kernel, out_shape=SDS((TP, r, c), x.dtype), in_spec...]
    dot_general x2 -> x1, matrix products: 29.2 us -> 8.52 us  [dot_nt(): lax.dot_general(a, b, (((1,), (1,)), ((), ())), preferred_element_type=f32)]
    unnamed x97 -> x96, local copies, waits for them, and re-layouts: 26.9 us -> 36.5 us
    unnamed x6 -> x5, other arithmetic: 20.6 us -> 19.2 us
  transfers between devices with their start and end apart: 14 -> 14, of which waited for: 5 -> 4; matrix products, arithmetic and copies ran while one was open for 18% -> 13% of each run, Pallas kernels for 37% -> 46%
where the time goes in v2:
time: 842 us; the launch traced here: 831 us
  Pallas kernels  500 us (59%)
  matrix products  73 us (9%)
  waiting for transfers between devices  70 us (8%)
  other arithmetic  64.3 us (8%)
  local copies, waits for them, and re-layouts  50.6 us (6%)
  blocking collectives  28.8 us (3%)
  starting transfers between devices  28.4 us (3%)
  between operations  15 us (2%)
    pallas_call x1, Pallas kernels, forward_exchange(): pl.pallas_call(forward_kernel, out_shape=tuple((SDS(*b) for b in blocks))...  116 us
    pallas_call x2, Pallas kernels, matmul_reduce(): pl.pallas_call(functools.partial(reduce_kernel, nt), out_shape=SDS((r, c)...  96.6 us
    pallas_call x1, Pallas kernels, backward_exchange(): pl.pallas_call(backward_kernel, out_shape=(SDS((r, c), f32), SDS((TP, r,...  93.4 us
    pallas_call x3, Pallas kernels, exchange_call(): pl.pallas_call(kernel, out_shape=outs, in_specs=[VMEM] * len(args), out_s...  86.4 us
    reduce_scatter x5, waiting for transfers between devices, dp_reduce(): lax.psum_scatter(x, AXIS, scatter_dimension=0, tiled=True, axis_index_gro...  62.9 us
    pallas_call x1, Pallas kernels, plane_gather(): pl.pallas_call(gather_kernel, out_shape=SDS((TP, r, c), x.dtype), in_spec...  60.1 us
    dot_general x5, matrix products, dot_tn(): lax.dot_general(a, b, (((0,), (0,)), ((), ())), preferred_element_type=f32)  51.8 us
    unnamed x96, local copies, waits for them, and re-layouts  36.5 us
  transfers between devices with their start and end apart: 14, of which 4 were waited for; matrix products, arithmetic and copies ran while one was open for 13% of the time, Pallas kernels for 46%

profile of v2, /device:TPU:14, one launch (start us, length us, event | category | flops | bytes accessed | tf_op | source)
XLA Modules:
  0.0 830.5 jit_solution(12833476604227506384)
XLA Ops:
  10.2 15.4 %shard_map.254 = bf16[8,64,1024]{2,1,0:T(8,128)(2,1)} custom-call(bf16[64,2048]{1,0:T(8,128)(2,1)S(1)} %copy-done.18, bf16[64,2048]{1,0:T(8,128)(2,1)S(1)} %copy-done.19, bf16[128,2048]{1,0:T(8,128)(2,1)S(1)} %copy-done.17), custom_call_target="tpu_custom_call" | custom-call | tf_op jit(solution)/shard_map/pallas_call | solution.py:148
  31.5 16.9 %shard_map.255 = (bf16[8,64,1024]{2,1,0:T(8,128)(2,1)}, f32[4,8,8,128]{3,2,1,0:T(8,128)S(1)}) custom-call(bf16[64,4096]{1,0:T(8,128)(2,1)S(1)} %copy-done.15, bf16[64,4096]{1,0:T(8,128)(2,1)S(1)} %copy-done.16, f32[8,128]{1,0:T(8,128)S(1)} %scatter.32.vec), custom_call_target="tpu_custom_call" | custom-call | tf_op jit(solution)/shard_map/pallas_call | solution.py:148
  49.8 54.0 %shard_map.256 = (bf16[8,64,1024]{2,1,0:T(8,128)(2,1)}, bf16[8,256,2048]{2,1,0:T(8,128)(2,1)S(1)}) custom-call(bf16[8,64,1024]{2,1,0:T(8,128)(2,1)S(1)} %pad_maximum_fusion.1.gu, bf16[256,2048]{1,0:T(8,128)(2,1)S(1)} %copy-done.2), custom_call_target="tpu_custom_call" | custom-call | tf_op jit(solution)/shard_map/pallas_call | solution.py:148
  137.1 60.1 %shard_map.258.cot = bf16[8,256,2048]{2,1,0:T(8,128)(2,1)S(1)} custom-call(bf16[256,2048]{1,0:T(8,128)(2,1)S(1)} %copy-done.12), custom_call_target="tpu_custom_call" | custom-call | tf_op jit(solution)/shard_map/pallas_call | solution.py:103
  200.4 6.9 fusion.26
  218.7 115.9 %forward_exchange.1 = (bf16[8,256,512]{2,1,0:T(8,128)(2,1)}, bf16[8,256,512]{2,1,0:T(8,128)(2,1)}, f32[8,256,512]{2,1,0:T(8,128)}, f32[8,256,512]{2,1,0:T(8,128)...) custom-call(bf16[8,256,2048]{2,1,0:T(8,128)(2,1)} %fusion.5.nrm, ...), custom_call_target="tpu_custom_call" | custom-call | tf_op jit(solution)/shard_map/forward_exchange/pallas_call | solution.py:518
  339.3 14.4 %hidden_units.1 = (bf16[8,256,512]{2,1,0:T(8,128)(2,1)S(1)}, f32[8,256,512]{2,1,0:T(8,128)S(1)}, f32[8,256,512]{2,1,0:T(8,128)S(1)}) custom-call(bf16[8,256,2048]{2,1,0:T(8,128)(2,1)} %get-tuple-element.104.x, bf16[2048,1024]{1,0:T(8,128)(2,1)S(1)} %copy-done.7), custom_call_target="tpu_custom_call" | custom-call | flops 8589934592 | bytes 25165824 | tf_op jit(solution)/shard_map/hidden_units/pallas_call | solution.py:560
  364.5 10.0 %hidden_back.1.a = bf16[8,256,1024]{2,1,0:T(8,128)(2,1)S(1)} custom-call(bf16[8,256,2048]{2,1,0:T(8,128)(2,1)} %copy-done.4, bf16[512,2048]{1,0:T(8,128)(2,1)S(1)} %copy-done.6, f32[8,256,512]{2,1,0:T(8,128)S(1)} %copy-done.9, f32[8,256,512]{2,1,0:T(8,128)S(1)} %copy-done.11), custom_call_target="tpu_custom_call" | custom-call | flops 4294967296 | bytes 25165824 | tf_op jit(solution)/shard_map/hidden_back/pallas_call | solution.py:596
  376.6 93.4 %backward_exchange.1 = (f32[256,2048]{1,0:T(8,128)}, bf16[8,256,2048]{2,1,0:T(8,128)(2,1)}, f32[2,2048]{1,0:T(2,128)S(1)}) custom-call(bf16[8,256,1024]{2,1,0:T(8,128)(2,1)} %copy-done.5, bf16[2048,1024]{1,0:T(8,128)(2,1)} %all-gather.9.cloned.1.call-done.gu.w, f32[256,2048]{1,0:T(8,128)} %get-tuple-element.103.mid, bf16[256,2048]{1,0:T(8,128)(2,1)S(1)} %copy-done.12, ...), custom_call_target="tpu_custom_call" | custom-call | tf_op jit(solution)/shard_map/backward_exchange/pallas_call | solution.py:651
  470.0 8.5 %multiply_reduce_fusion.1 = (f32[8,256]{1,0:T(8,128)S(1)}, f32[8,256]{1,0:T(8,128)S(1)}, f32[8,256,512]{2,1,0:T(8,128)S(1)}) fusion(f32[8,256,512]{2,1,0:T(8,128)S(1)} %copy-done.21, f32[8,256]{1,0:T(8,128)S(1)} %broadcast_multiply_fusion, f32[8,256,512]{2,1,0:T(8,128)S(1)} %copy-done.22, bf16[8,256,2048]{2,1,0:T(8,128)(2,1)} %get-tuple-element.112, ...), kind=kOutput, calls=%fused_computation.21 | convolution fusion | flops 4305448960 | bytes 23093248 | tf_op jit(solution)/shard_map/dot_general | solution.py:753
  513.7 5.8 bitcast_convert_fusion.4
  519.9 8.6 %bitcast_convert_fusion.3 = bf16[512,2048]{1,0:T(8,128)(2,1)S(1)} fusion(bf16[8,256,512]{2,1,0:T(8,128)(2,1)} %get-tuple-element.119, bf16[8,256,2048]{2,1,0:T(8,128)(2,1)} %get-tuple-element.112), kind=kOutput, calls=%fused_computation.17 | convolution fusion | flops 4296015872 | bytes 12582912 | tf_op jit(solution)/shard_map/dot_general | solution.py:749
  528.6 28.8 %all_to_all.54 = bf16[8,512,256]{2,1,0:T(8,128)(2,1)} all-to-all(bf16[8,512,256]{2,1,0:T(8,128)(2,1)S(1)} %bitcast.92), channel_id=1, replica_groups={{0,1,2,3,4,5,6,7},{8,9,10,11,12,13,14,15},{16,17,18,19,20,21,22,23},{24..., dimensions={0} | all-to-all | bytes 4194304 | tf_op jit(solution)/shard_map/all_to_all | solution.py:680
  557.6 14.1 %bitcast_convert_fusion = bf16[2048,1024]{1,0:T(8,128)(2,1)} fusion(bf16[8,256,2048]{2,1,0:T(8,128)(2,1)} %get-tuple-element.104.x, bf16[8,256,1024]{2,1,0:T(8,128)(2,1)} %copy-done.5), kind=kOutput, calls=%fused_computation.8 | convolution fusion | flops 8592031744 | bytes 16777216 | tf_op jit(solution)/shard_map/dot_general | solution.py:749
  571.9 14.0 %bitcast_convert_fusion.1 = bf16[2048,1024]{1,0:T(8,128)(2,1)} fusion(bf16[8,256,2048]{2,1,0:T(8,128)(2,1)} %fusion.5.nrm, bf16[8,256,1024]{2,1,0:T(8,128)(2,1)} %copy-done.41), kind=kOutput, calls=%fused_computation.9 | convolution fusion | flops 8592031744 | bytes 16777216 | tf_op jit(solution)/shard_map/dot_general | solution.py:749
  586.0 9.4 %bitcast_convert_fusion.2 = bf16[512,2048]{1,0:T(8,128)(2,1)} fusion(bf16[8,256,512]{2,1,0:T(8,128)(2,1)S(1)} %get-tuple-element.106.a, bf16[8,256,2048]{2,1,0:T(8,128)(2,1)} %copy-done.4), kind=kOutput, calls=%fused_computation.16 | convolution fusion | flops 4296015872 | bytes 12582912 | tf_op jit(solution)/shard_map/dot_general | solution.py:749
  595.7 6.5 all-to-all-start.2
  607.5 51.6 %shard_map.259 = f32[256,2048]{1,0:T(8,128)S(1)} custom-call(bf16[8,256,1536]{2,1,0:T(8,128)(2,1)} %copy-done.26, bf16[2048,1536]{1,0:T(8,128)(2,1)} %pad_maximum_fusion.w), custom_call_target="tpu_custom_call" | custom-call | tf_op jit(solution)/shard_map/pallas_call | solution.py:426
  666.4 6.4 all-to-all-done.4.x
  672.8 13.8 %reduce-scatter.12.cloned.1.call-done = bf16[512,1024]{1,0:T(8,128)(2,1)} async-done(((bf16[2048,1024]{1,0:T(8,128)(2,1)}), bf16[512,1024]{1,0:T(8,128)(2,1)}) %reduce-scatter.12.cloned.1.call-update) | async-done | bytes 1048592 | tf_op jit(solution)/shard_map/reduce_scatter | solution.py:688
  691.5 14.2 %vector_sum.1 = f32[8,512]{1,0:T(8,128)S(1)} custom-call(f32[8,2048]{1,0:T(8,128)S(1)} %maximum_maximum_fusion.v_ref), custom_call_target="tpu_custom_call" | custom-call | tf_op jit(solution)/shard_map/vector_sum/pallas_call | solution.py:273
  707.4 45.0 %shard_map.257 = f32[256,2048]{1,0:T(8,128)S(1)} custom-call(bf16[8,256,512]{2,1,0:T(8,128)(2,1)S(1)} %copy-done.14, bf16[512,2048]{1,0:T(8,128)(2,1)} %all-gather.11.cloned.1.call-done.w.down), custom_call_target="tpu_custom_call" | custom-call | tf_op jit(solution)/shard_map/pallas_call | solution.py:426
  753.6 12.6 %reduce-scatter.6.cloned.1.call-done = bf16[512,1024]{1,0:T(8,128)(2,1)} async-done(((bf16[2048,1024]{1,0:T(8,128)(2,1)}), bf16[512,1024]{1,0:T(8,128)(2,1)}) %reduce-scatter.6.cloned.1.call-update) | async-done | bytes 1048592 | tf_op jit(solution)/shard_map/reduce_scatter | solution.py:688
  775.7 36.5 %reduce-scatter.14.cloned.1.call-done = bf16[128,2048]{1,0:T(8,128)(2,1)} async-done(((bf16[512,2048]{1,0:T(8,128)(2,1)}), bf16[128,2048]{1,0:T(8,128)(2,1)}) %reduce-scatter.14.cloned.1.call-update) | async-done | bytes 524304 | tf_op jit(solution)/shard_map/reduce_scatter | solution.py:688
  (207 shorter events, 152.8 us)
Async XLA Ops:
  7.2 115.7 %all-gather.7.cloned.1.call-start = ((), (), s32[]{:S(2)}) async-start(), calls=%async_computation.12 | async-start | bytes 5242880 | tf_op jit(solution)/shard_map/all_gather | solution.py:684
  10.2 38.4 %copy-start.37 = (bf16[64,4096]{1,0:T(8,128)(2,1)S(1)}, bf16[64,4096]{1,0:T(8,128)(2,1)}, u32[]{:S(2)}) copy-start(bf16[64,4096]{1,0:T(8,128)(2,1)} %param.36) | copy-start | bytes 1572868
  10.2 38.9 %copy-start.38 = (bf16[64,4096]{1,0:T(8,128)(2,1)S(1)}, bf16[64,4096]{1,0:T(8,128)(2,1)}, u32[]{:S(2)}) copy-start(bf16[64,4096]{1,0:T(8,128)(2,1)} %param.37) | copy-start | bytes 1572868
  25.6 193.1 %all-gather.5.cloned.1.call-start = ((), (), s32[]{:S(2)}) async-start(), calls=%async_computation.11 | async-start | bytes 5242880 | tf_op jit(solution)/shard_map/all_gather | solution.py:684
  48.5 288.6 %all-gather.9.cloned.1.call-start = ((), (), s32[]{:S(2)}) async-start(), calls=%async_computation.13 | async-start | bytes 5242880 | tf_op jit(solution)/shard_map/all_gather | solution.py:684
  107.1 250.7 %all-gather.11.cloned.1.call-start = ((), (), s32[]{:S(2)}) async-start(), calls=%async_computation.14 | async-start | bytes 2621440 | tf_op jit(solution)/shard_map/all_gather | solution.py:684
  131.7 84.3 %all-to-all-start = ((bf16[8,512,256]{2,1,0:T(8,128)(2,1)}), bf16[8,512,256]{2,1,0:T(8,128)(2,1)S(1)}, u32[]{:S(2)}, u32[]{:S(2)}) async-start(bf16[8,512,256]{2,1,0:T(8,128)(2,1)} %bitcast.90), calls=%async_computation | async-start | bytes 4194304 | tf_op jit(solution)/shard_map/all_to_all | solution.py:680
  136.9 458.8 %reduce-scatter.8.cloned.1.call-start = ((), (), s32[]{:S(2)}) async-start(), calls=%async_computation.16 | async-start | bytes 2621440 | tf_op jit(solution)/shard_map/reduce_scatter | solution.py:688
  137.0 63.4 %copy-start.28 = (bf16[2048,1024]{1,0:T(8,128)(2,1)S(1)}, bf16[2048,1024]{1,0:T(8,128)(2,1)}, u32[]{:S(2)}) copy-start(bf16[2048,1024]{1,0:T(8,128)(2,1)} %all-gather.7.cloned.1.call-done) | copy-start | bytes 12582916
  357.8 228.2 %copy-start.13 = (bf16[8,256,512]{2,1,0:T(8,128)(2,1)}, bf16[8,256,512]{2,1,0:T(8,128)(2,1)S(1)}, u32[]{:S(2)}) copy-start(bf16[8,256,512]{2,1,0:T(8,128)(2,1)S(1)} %get-tuple-element.106.a) | copy-start | bytes 6291460
  364.5 12.1 %copy-start.20 = (f32[2,2048]{1,0:T(2,128)S(1)}, f32[2,2048]{1,0:T(2,128)}, u32[]{:S(2)}) copy-start(f32[2,2048]{1,0:T(2,128)} %pad_maximum_fusion.8.vec) | copy-start | bytes 49156
  376.6 93.4 %copy-start.21 = (f32[8,256,512]{2,1,0:T(8,128)S(1)}, f32[8,256,512]{2,1,0:T(8,128)}, u32[]{:S(2)}) copy-start(f32[8,256,512]{2,1,0:T(8,128)} %get-tuple-element.113) | copy-start | bytes 12582916
  376.6 93.4 %copy-start.22 = (f32[8,256,512]{2,1,0:T(8,128)S(1)}, f32[8,256,512]{2,1,0:T(8,128)}, u32[]{:S(2)}) copy-start(f32[8,256,512]{2,1,0:T(8,128)} %get-tuple-element.111) | copy-start | bytes 12582916
  519.5 140.3 %reduce-scatter.10.cloned.1.call-start = ((), (), s32[]{:S(2)}) async-start(), calls=%async_computation.17 | async-start | bytes 2621440 | tf_op jit(solution)/shard_map/reduce_scatter | solution.py:688
  557.5 129.1 %reduce-scatter.12.cloned.1.call-start = ((), (), s32[]{:S(2)}) async-start(), calls=%async_computation.18 | async-start | bytes 5242880 | tf_op jit(solution)/shard_map/reduce_scatter | solution.py:688
  571.7 194.5 %reduce-scatter.6.cloned.1.call-start = ((), (), s32[]{:S(2)}) async-start(), calls=%async_computation.15 | async-start | bytes 5242880 | tf_op jit(solution)/shard_map/reduce_scatter | solution.py:688
  585.9 226.3 %reduce-scatter.14.cloned.1.call-start = ((), (), s32[]{:S(2)}) async-start(), calls=%async_computation.19 | async-start | bytes 2621440 | tf_op jit(solution)/shard_map/reduce_scatter | solution.py:688
  586.0 9.5 %copy-start.3 = (bf16[256,2048]{1,0:T(8,128)(2,1)S(1)}, bf16[256,2048]{1,0:T(8,128)(2,1)}, u32[]{:S(2)}) copy-start(bf16[256,2048]{1,0:T(8,128)(2,1)} %tok.2) | copy-start | bytes 3145732
  595.7 64.0 %all-to-all-start.2 = ((bf16[8,64,512]{2,1,0:T(8,128)(2,1)}), bf16[8,64,512]{2,1,0:T(8,128)(2,1)}, u32[]{:S(2)}, u32[]{:S(2)}) async-start(bf16[8,64,512]{2,1,0:T(8,128)(2,1)} %bitcast.104), calls=%async_computation.4 | async-start | bytes 1048576 | tf_op jit(solution)/shard_map/all_to_all | solution.py:680
  607.5 51.6 %copy-start.40 = (f32[2048]{0:T(1024)S(1)}, f32[2048]{0:T(1024)}, u32[]{:S(2)}) copy-start(f32[2048]{0:T(1024)} %copy-done.39) | copy-start | bytes 24580
  659.8 13.0 %all-to-all-start.4 = ((bf16[8,128,256]{2,1,0:T(8,128)(2,1)}), bf16[8,128,256]{2,1,0:T(8,128)(2,1)}, u32[]{:S(2)}, u32[]{:S(2)}) async-start(bf16[8,128,256]{2,1,0:T(8,128)(2,1)} %bitcast.103), calls=%async_computation.7 | async-start | bytes 1048576 | tf_op jit(solution)/shard_map/all_to_all | solution.py:680
  686.6 79.6 %all-to-all-start.5 = ((bf16[8,64,1024]{2,1,0:T(8,128)(2,1)}), bf16[8,64,1024]{2,1,0:T(8,128)(2,1)}, u32[]{:S(2)}, u32[]{:S(2)}) async-start(bf16[8,64,1024]{2,1,0:T(8,128)(2,1)} %bitcast.100), calls=%async_computation.9 | async-start | bytes 2097152 | tf_op jit(solution)/shard_map/all_to_all | solution.py:680
  707.4 45.0 %copy-start.24 = (f32[256,2048]{1,0:T(8,128)S(1)}, f32[256,2048]{1,0:T(8,128)}, u32[]{:S(2)}) copy-start(f32[256,2048]{1,0:T(8,128)} %get-tuple-element.103.mid) | copy-start | bytes 6291460
  766.2 55.0 %all-to-all-start.1 = ((bf16[8,64,1024]{2,1,0:T(8,128)(2,1)}), bf16[8,64,1024]{2,1,0:T(8,128)(2,1)}, u32[]{:S(2)}, u32[]{:S(2)}) async-start(bf16[8,64,1024]{2,1,0:T(8,128)(2,1)} %bitcast.99), calls=%async_computation.2 | async-start | bytes 2097152 | tf_op jit(solution)/shard_map/all_to_all | solution.py:680
  (35 other events, 95.4 us)
Sparse Core Ops, SparseCore 0:
  25.7 79.4 all-gather.6
  106.9 79.0 all-gather.4
  187.6 79.2 all-gather.8
  268.3 45.2 all-gather.10
  519.6 42.8 reduce-scatter.7
  564.6 42.8 reduce-scatter.9
  609.7 76.8 reduce-scatter.11
  688.9 77.2 reduce-scatter.5
  768.5 43.7 reduce-scatter.13

commit v3 on v2

--- a/solution.py
+++ b/solution.py
@@ -52,44 +52,63 @@
 GATHER_SEMS = 13
 
 
+class Gather:
+    def __init__(self, own, out, start, size, sems, base, local, peer):
+        self.own, self.out, self.sems, self.base, self.local = own, out, sems, base, local
+        h = size // 2
+        self.all, self.top, self.bot = pl.ds(start, size), pl.ds(start, h), pl.ds(start + h, h)
+        self.pc, self.px, self.py = peer(1), peer(2), peer(4)
+        self.made = []
+
+    def send(self, src, dst, dev):
+        copy = remote(src, dst, self.sems, self.base + len(self.made), dev)
+        copy.start()
+        self.made.append(copy)
+        return copy
+
+    def pass_on(self, k, at):
+        self.core.append(self.send(self.out.at[k, at], self.out.at[k + 1, at], self.pc))
+
+    def start(self):
+        own, out, top, bot = self.own, self.out, self.top, self.bot
+        self.x0 = self.send(own.at[bot], out.at[2, bot], self.px)
+        self.y0 = self.send(own.at[top], out.at[4, top], self.py)
+        self.x1 = self.send(own.at[top], out.at[2, top], self.px)
+        self.y1 = self.send(own.at[bot], out.at[4, bot], self.py)
+        self.core = [self.send(own.at[self.all], out.at[1, self.all], self.pc)]
+        self.keep = pltpu.make_async_copy(own.at[self.all], out.at[0, self.all], self.local)
+        self.keep.start()
+
+    def forward(self):
+        out, top, bot = self.out, self.top, self.bot
+        self.x0.wait_recv()
+        self.fy = self.send(out.at[2, bot], out.at[6, bot], self.py)
+        self.pass_on(2, bot)
+        self.y0.wait_recv()
+        self.fx = self.send(out.at[4, top], out.at[6, top], self.px)
+        self.pass_on(4, top)
+        self.x1.wait_recv()
+        self.pass_on(2, top)
+        self.y1.wait_recv()
+        self.pass_on(4, bot)
+
+    def finish(self):
+        self.fy.wait_recv()
+        self.pass_on(6, self.bot)
+        self.fx.wait_recv()
+        self.pass_on(6, self.top)
+        for copy in self.core:
+            copy.wait_recv()
+        for copy in self.made:
+            copy.wait_send()
+        self.keep.wait()
+
+
 def gather_blocks(own, out, sems, base, local, peer):
-    h = own.shape[0] // 2
-    top, bot = pl.ds(0, h), pl.ds(h, h)
-    pc, px, py = peer(1), peer(2), peer(4)
-    made = []
-
-    def send(src, dst, dev):
-        copy = remote(src, dst, sems, base + len(made), dev)
-        copy.start()
-        made.append(copy)
-        return copy
-
-    x0 = send(own.at[bot], out.at[2, bot], px)
-    y0 = send(own.at[top], out.at[4, top], py)
-    x1 = send(own.at[top], out.at[2, top], px)
-    y1 = send(own.at[bot], out.at[4, bot], py)
-    core = [send(own, out.at[1], pc)]
-    keep = pltpu.make_async_copy(own, out.at[0], local)
-    keep.start()
-    x0.wait_recv()
-    fy = send(out.at[2, bot], out.at[6, bot], py)
-    core.append(send(out.at[2, bot], out.at[3, bot], pc))
-    y0.wait_recv()
-    fx = send(out.at[4, top], out.at[6, top], px)
-    core.append(send(out.at[4, top], out.at[5, top], pc))
-    x1.wait_recv()
-    core.append(send(out.at[2, top], out.at[3, top], pc))
-    y1.wait_recv()
-    core.append(send(out.at[4, bot], out.at[5, bot], pc))
-    fy.wait_recv()
-    core.append(send(out.at[6, bot], out.at[7, bot], pc))
-    fx.wait_recv()
-    core.append(send(out.at[6, top], out.at[7, top], pc))
-    for copy in core:
-        copy.wait_recv()
-    for copy in made:
-        copy.wait_send()
-    keep.wait()
+    gather = Gather(own, out, 0, own.shape[0], sems, base, local, peer)
+    gather.start()
+    gather.forward()
+    gather.finish()
 
 
 def gather_kernel(x_ref, out_ref, ssem, rsem, local):
@@ -237,203 +256,172 @@
     return exchange_call(third_kernel, outs, (gu, tok), 7 + GATHER_SEMS, 2, cid)
 
 
-def vector_sum_kernel(n, v_ref, out_ref, near, far, part, ssem, rsem):
-    dp = n // TP
-    me, peer = place()
-    g = lax.div(me, TP)
-    width = out_ref.shape[1]
-    sems = (ssem, rsem)
-    others = [lax.rem(me + TP * j, n) for j in range(1, dp)]
-    greet([peer(k) for k in range(1, TP)] + others)
-    copies = []
-    for j, dev in enumerate(others):
-        at = pl.multiple_of(lax.div(dev, TP) * width, 128)
-        copy = remote(v_ref.at[:, pl.ds(at, width)], far.at[j], sems, j, dev)
+REDUCE_SEMS = 16
+TILE = 512
+
+
+class Reduce:
+    def __init__(self, product, bufs, sems, base, peer, prepare=None):
+        self.product, self.prepare, self.sems, self.base = product, prepare, sems, base
+        self.po, self.pe, self.rc, self.sb, self.xr, self.yr = bufs
+        self.pc, self.px, self.py = peer(1), peer(2), peer(4)
+        self.q = self.pe.shape[1] // 4
+        self.sent, self.core, self.got = [], {}, ({}, {})
+
+    def send(self, src, dst, dev, i):
+        copy = remote(src, dst, self.sems, self.base + i, dev)
         copy.start()
-        copies.append(copy)
-    total = v_ref[:, pl.ds(pl.multiple_of(g * width, 128), width)]
-    for j, copy in enumerate(copies):
-        copy.wait()
-        total = total + far[j]
-    part[...] = total
-    copies = []
-    for k in range(1, TP):
-        copy = remote(part, near.at[k - 1], sems, dp + k - 1, peer(k))
-        copy.start()
-        copies.append(copy)
-    for k, copy in enumerate(copies):
-        copy.wait()
-        total = total + near[k]
-    out_ref[...] = total
-
-
-def vector_sum(n, v, cid):
-    dp = n // TP
-    width = v.shape[1] // dp
-    return pl.pallas_call(
-        functools.partial(vector_sum_kernel, n),
-        out_shape=SDS((v.shape[0], width), f32),
-        in_specs=[VMEM],
-        out_specs=VMEM,
-        scratch_shapes=[
-            pltpu.VMEM((TP - 1, v.shape[0], width), f32),
-            pltpu.VMEM((dp, v.shape[0], width), f32),
-            pltpu.VMEM((v.shape[0], width), f32),
-            pltpu.SemaphoreType.DMA((dp + TP,)),
-            pltpu.SemaphoreType.DMA((dp + TP,)),
-        ],
-        compiler_params=pltpu.CompilerParams(
-            collective_id=cid, has_side_effects=True, vmem_limit_bytes=4 << 20
-        ),
-        name="vector_sum",
-    )(v)
-
-
-REDUCE_SEMS = 10
-TILE = 512
-
-
-def reduce_blocks(product, po, pe, rc, sb, xr, yr, sems, peer, prepare=None):
-    r = pe.shape[1]
-    h = r // 2
-    top, bot = pl.ds(0, h), pl.ds(h, h)
-    pc, px, py = peer(1), peer(2), peer(4)
-    sent = []
-
-    def send(src, dst, dev, i):
-        copy = remote(src, dst, sems, i, dev)
-        copy.start()
-        sent.append(copy)
+        self.sent.append(copy)
         return copy
 
-    def pair(i):
-        k = 2 * i
-        if prepare is not None:
-            prepare(k)
-        product(k + 1, po.at[i])
-        copy = send(po.at[i], rc.at[i], pc, i)
-        product(k, pe.at[i])
-        return copy
-
-    def add(dst, part, got, out=None):
+    def pair(self, i):
+        if self.prepare is not None:
+            self.prepare(2 * i)
+        self.product(i, self.po.at[i], self.pe.at[i])
+        self.core[i] = self.send(self.po.at[i], self.rc.at[i], self.pc, i)
+
+    def add(self, c, i, lower, out, more=None):
         step = 32
 
-        @pl.loop(0, part.size // step)
+        @pl.loop(0, self.q // step)
         def _(j):
-            here = pl.ds(pl.multiple_of(part.start + j * step, step), step)
             there = pl.ds(pl.multiple_of(j * step, step), step)
-            total = dst[here, :] + got[there, :].astype(f32)
-            if out is None:
-                dst[here, :] = total
-            else:
-                out[there, :] = total.astype(bf)
-
-    c6 = pair(3)
-    c2 = pair(1)
-    c6.wait_recv()
-    add(pe.at[3], top, rc.at[3, top], sb.at[0])
-    x6 = send(sb.at[0], xr.at[0], px, 4)
-    add(pe.at[3], bot, rc.at[3, bot], sb.at[1])
-    y6 = send(sb.at[1], yr.at[0], py, 5)
-    c4 = pair(2)
-    c2.wait_recv()
-    add(pe.at[1], top, rc.at[1, top], sb.at[2])
-    x2 = send(sb.at[2], xr.at[1], px, 6)
-    add(pe.at[1], bot, rc.at[1, bot])
-    c0 = pair(0)
-    c4.wait_recv()
-    add(pe.at[2], bot, rc.at[2, bot], sb.at[3])
-    y4 = send(sb.at[3], yr.at[1], py, 7)
-    add(pe.at[2], top, rc.at[2, top])
-    c0.wait_recv()
-    x6.wait_recv()
-    add(pe.at[2], top, xr.at[0], sb.at[4])
-    y4b = send(sb.at[4], yr.at[2], py, 8)
-    y6.wait_recv()
-    add(pe.at[1], bot, yr.at[0], sb.at[5])
-    x2b = send(sb.at[5], xr.at[2], px, 9)
-    x2.wait_recv()
-    y4.wait_recv()
-    y4b.wait_recv()
-    x2b.wait_recv()
-
-    def total(at, half_at, lower):
-        first, second = (yr, xr) if lower else (xr, yr)
-        return (
-            pe[0, at, :]
-            + rc[0, at, :].astype(f32)
-            + first[1, half_at, :].astype(f32)
-            + second[2, half_at, :].astype(f32)
+            here = pl.ds(pl.multiple_of(j * step + (2 * c + lower) * self.q, step), step)
+            total = self.pe[i, here, :].astype(f32) + self.rc[i, here, :].astype(f32)
+            if more is not None:
+                total = total + more[there, :].astype(f32)
+            self.sb[c, out, there, :] = total.astype(bf)
+
+    def link(self, c, slot, name, ring, at, dev):
+        self.got[c][name] = self.send(
+            self.sb.at[c, slot], ring.at[c, at], dev, 4 + 6 * c + slot
         )
 
-    def for_rows(step, body):
-        for lower in (False, True):
-
-            @pl.loop(0, h // step)
-            def _(j, lower=lower):
-                half_at = pl.ds(pl.multiple_of(j * step, step), step)
-                at = pl.ds(pl.multiple_of(j * step + (h if lower else 0), step), step)
-                body(at, total(at, half_at, lower))
-
-    return for_rows, sent
-
-
-def reduce_scratch(r, c):
-    h = r // 2
+    def six(self, c):
+        self.add(c, 3, 0, 0)
+        self.link(c, 0, "x6", self.xr, 0, self.px)
+        self.add(c, 3, 1, 1)
+        self.link(c, 1, "y6", self.yr, 0, self.py)
+
+    def two(self, c):
+        self.add(c, 1, 0, 2)
+        self.link(c, 2, "x2", self.xr, 1, self.px)
+
+    def four(self, c):
+        self.add(c, 2, 1, 3)
+        self.link(c, 3, "y4", self.yr, 1, self.py)
+
+    def onward(self, c):
+        self.got[c]["x6"].wait_recv()
+        self.add(c, 2, 0, 4, self.xr.at[c, 0])
+        self.link(c, 4, "y4b", self.yr, 2, self.py)
+        self.got[c]["y6"].wait_recv()
+        self.add(c, 1, 1, 5, self.yr.at[c, 0])
+        self.link(c, 5, "x2b", self.xr, 2, self.px)
+
+    def first(self):
+        self.pair(3)
+        self.pair(1)
+        self.core[3].wait_recv()
+        self.six(0)
+        self.pair(2)
+        self.core[1].wait_recv()
+        self.two(0)
+        self.core[2].wait_recv()
+        self.four(0)
+        self.pair(0)
+        self.onward(0)
+
+    def second(self):
+        self.six(1)
+        self.two(1)
+        self.four(1)
+        self.onward(1)
+
+    def rows(self, c, step, body):
+        if c == 0:
+            self.core[0].wait_recv()
+        for name in ("x2", "y4", "y4b", "x2b"):
+            self.got[c][name].wait_recv()
+        for lower in (0, 1):
+            near, far = (self.yr, self.xr) if lower else (self.xr, self.yr)
+
+            @pl.loop(0, self.q // step)
+            def _(j, lower=lower, near=near, far=far):
+                there = pl.ds(pl.multiple_of(j * step, step), step)
+                here = pl.ds(pl.multiple_of(j * step + (2 * c + lower) * self.q, step), step)
+                body(
+                    here,
+                    self.pe[0, here, :].astype(f32)
+                    + self.rc[0, here, :].astype(f32)
+                    + near[c, 1, there, :].astype(f32)
+                    + far[c, 2, there, :].astype(f32),
+                )
+
+    def finish(self):
+        for copy in self.sent:
+            copy.wait_send()
+
+
+def reduce_scratch(r, c, even=f32):
+    q = r // 4
     return [
         pltpu.VMEM((4, r, c), bf),
-        pltpu.VMEM((4, r, c), f32),
+        pltpu.VMEM((4, r, c), even),
         pltpu.VMEM((4, r, c), bf),
-        pltpu.VMEM((6, h, c), bf),
-        pltpu.VMEM((3, h, c), bf),
-        pltpu.VMEM((3, h, c), bf),
+        pltpu.VMEM((2, 6, q, c), bf),
+        pltpu.VMEM((2, 3, q, c), bf),
+        pltpu.VMEM((2, 3, q, c), bf),
     ]
 
 
+def rows_of_pair(a, i):
+    two, r, k = 2, a.shape[1], a.shape[2]
+    return a[pl.ds(2 * i, two)].reshape(two * r, k)
+
+
 def times(a, w, nt):
-    def product(k, dst):
-        @pl.loop(0, dst.shape[1] // TILE)
+    def product(i, odd, even):
+        r = a.shape[1]
+
+        @pl.loop(0, even.shape[1] // TILE)
         def _(j):
             at = pl.ds(pl.multiple_of(j * TILE, TILE), TILE)
+            x = rows_of_pair(a, i)
             if nt:
                 y = lax.dot_general(
-                    a[k], w[at, :], (((1,), (1,)), ((), ())), preferred_element_type=f32
+                    x, w[at, :], (((1,), (1,)), ((), ())), preferred_element_type=f32
                 )
             else:
-                y = jnp.dot(a[k], w[:, at], preferred_element_type=f32)
-            dst[:, at] = y.astype(dst.dtype)
+                y = jnp.dot(x, w[:, at], preferred_element_type=f32)
+            even[:, at] = y[:r].astype(even.dtype)
+            odd[:, at] = y[r:].astype(odd.dtype)
 
     return product
 
 
-def reduce_kernel(nt, a, w, out_ref, po, pe, rc, sb, xr, yr, ssem, rsem):
-    _, peer = place()
-    greet([peer(1), peer(2), peer(4)])
-    product = times(a, w, nt)
-    for_rows, sent = reduce_blocks(product, po, pe, rc, sb, xr, yr, (ssem, rsem), peer)
-
-    def body(at, value):
-        out_ref[at, :] = value
-
-    for_rows(32, body)
-    for copy in sent:
-        copy.wait_send()
-
-
-def matmul_reduce(a, w, nt, cid):
-    _, r, _ = a.shape
-    c = w.shape[0] if nt else w.shape[1]
-    return pl.pallas_call(
-        functools.partial(reduce_kernel, nt),
-        out_shape=SDS((r, c), f32),
-        in_specs=[VMEM] * 2,
-        out_specs=VMEM,
-        scratch_shapes=reduce_scratch(r, c)
-        + [pltpu.SemaphoreType.DMA((REDUCE_SEMS,)), pltpu.SemaphoreType.DMA((REDUCE_SEMS,))],
-        compiler_params=pltpu.CompilerParams(
-            collective_id=cid, has_side_effects=True, vmem_limit_bytes=48 << 20
-        ),
-    )(a, w)
+def exchange_and_gather(reduce, gathers, step, body):
+    reduce.first()
+    reduce.second()
+    for c in (0, 1):
+        reduce.rows(c, step, body)
+        gathers[c].start()
+    for c in (0, 1):
+        gathers[c].forward()
+    for c in (0, 1):
+        gathers[c].finish()
+    reduce.finish()
+
+
+def both_gathers(own, out, sems, local, peer):
+    half = own.shape[0] // 2
+    return [
+        Gather(own, out, c * half, half, sems, REDUCE_SEMS + c * GATHER_SEMS, local.at[c], peer)
+        for c in (0, 1)
+    ]
+
+
+EXCHANGE_SEMS = REDUCE_SEMS + 2 * GATHER_SEMS
 
 
 def forward_kernel(
@@ -447,50 +435,54 @@
     kept = []
 
     def prepare(first):
-        @pl.loop(0, 2)
-        def _(i):
-            k = first + i
-
-            @pl.loop(0, width // 256)
-            def _(j):
-                at = pl.ds(pl.multiple_of(j * 256, 256), 256)
-                behind = pl.ds(pl.multiple_of(j * 256 + width, 256), 256)
-                v = jnp.dot(nrm[k], wvs[:, at], preferred_element_type=f32).astype(bf)
-                v_buf[k, :, at] = v
-                swi_buf[k, :, at] = jnp.dot(nrm[k], wvs[:, behind], preferred_element_type=f32)
-                ret_buf[k, :, at] = jnp.dot(sco[k], v, preferred_element_type=f32)
-
-            @pl.loop(0, r // 32)
-            def _(j):
-                at = pl.ds(pl.multiple_of(j * 32, 32), 32)
-                value = ret_buf[k, at, :]
-                centred = value - jnp.mean(value, axis=-1, keepdims=True)
-                spread = jnp.mean(centred * centred, axis=-1, keepdims=True)
-                gate = swi_buf[k, at, :]
-                gate = gate / (1.0 + jnp.exp(-gate))
-                mix_buf[k, at, :] = (
-                    gate * (centred * lax.rsqrt(jnp.maximum(spread, 0.25)))
-                ).astype(bf)
-
         two = pl.ds(first, 2)
+        x = nrm[two].reshape(2 * r, nrm.shape[2])
+
+        @pl.loop(0, width // 256)
+        def _(j):
+            at = pl.ds(pl.multiple_of(j * 256, 256), 256)
+            behind = pl.ds(pl.multiple_of(j * 256 + width, 256), 256)
+            v = jnp.dot(x, wvs[:, at], preferred_element_type=f32).astype(bf)
+            s = jnp.dot(x, wvs[:, behind], preferred_element_type=f32)
+            for i in (0, 1):
+                mine = v[i * r : (i + 1) * r]
+                v_buf[first + i, :, at] = mine
+                swi_buf[first + i, :, at] = s[i * r : (i + 1) * r]
+                ret_buf[first + i, :, at] = jnp.dot(
+                    sco[first + i], mine, preferred_element_type=f32
+                )
+
+        @pl.loop(0, 2 * r // 32)
+        def _(j):
+            k = first + lax.div(j, r // 32)
+            at = pl.ds(pl.multiple_of(lax.rem(j, r // 32) * 32, 32), 32)
+            value = ret_buf[k, at, :]
+            centred = value - jnp.mean(value, axis=-1, keepdims=True)
+            spread = jnp.mean(centred * centred, axis=-1, keepdims=True)
+            gate = swi_buf[k, at, :]
+            gate = gate / (1.0 + jnp.exp(-gate))
+            mix_buf[k, at, :] = (
+                gate * (centred * lax.rsqrt(jnp.maximum(spread, 0.25)))
+            ).astype(bf)
+
         for i, (src, dst) in enumerate(
             ((v_buf, v_out), (mix_buf, mix_out), (ret_buf, ret_out), (swi_buf, swi_out))
         ):
             copy = pltpu.make_async_copy(
-                src.at[two], dst.at[two], local.at[1 + 2 * first + i]
+                src.at[two], dst.at[two], local.at[2 + 2 * first + i]
             )
             copy.start()
             kept.append(copy)
 
-    def product(k, dst):
+    def product(i, odd, even):
         step = w.shape[2]
 
         @pl.loop(0, w.shape[0])
         def _(j):
             at = pl.ds(pl.multiple_of(j * step, step), step)
-            dst[:, at] = jnp.dot(mix_buf[k], w[j], preferred_element_type=f32).astype(dst.dtype)
-
-    for_rows, sent = reduce_blocks(product, po, pe, rc, sb, xr, yr, sems, peer, prepare)
+            y = jnp.dot(rows_of_pair(mix_buf, i), w[j], preferred_element_type=f32)
+            even[:, at] = y[:r].astype(even.dtype)
+            odd[:, at] = y[r:].astype(odd.dtype)
 
     def body(at, value):
         value = value + tok[at, :].astype(f32)
@@ -502,10 +494,8 @@
             centred * lax.rsqrt(spread + 1e-05) * vec[0:1, :] + vec[1:2, :]
         ).astype(bf)
 
-    for_rows(16, body)
-    gather_blocks(own, out, sems, REDUCE_SEMS, local.at[0], peer)
-    for copy in sent:
-        copy.wait_send()
+    reduce = Reduce(product, (po, pe, rc, sb, xr, yr), sems, 0, peer, prepare)
+    exchange_and_gather(reduce, both_gathers(own, out, sems, local, peer), 16, body)
     for copy in kept:
         copy.wait()
 
@@ -513,7 +503,7 @@
 def forward_exchange(nrm, wvs, sco, w, tok, vec, cid):
     _, r, d = nrm.shape
     width = w.shape[1]
-    count = REDUCE_SEMS + GATHER_SEMS
+    count = EXCHANGE_SEMS
     blocks = [((TP, r, width), t) for t in (bf, bf, f32, f32)]
     return pl.pallas_call(
         forward_kernel,
@@ -526,7 +516,7 @@
             pltpu.VMEM((r, d), bf),
             pltpu.SemaphoreType.DMA((count,)),
             pltpu.SemaphoreType.DMA((count,)),
-            pltpu.SemaphoreType.DMA((17,)),
+            pltpu.SemaphoreType.DMA((18,)),
         ],
         compiler_params=pltpu.CompilerParams(
             collective_id=cid, has_side_effects=True, vmem_limit_bytes=60 << 20
@@ -566,7 +556,7 @@
             pl.BlockSpec(gu.shape, lambda k: (0, 0)),
         ],
         out_specs=(row, row, row),
-        compiler_params=pltpu.CompilerParams(vmem_limit_bytes=32 << 20),
+        compiler_params=pltpu.CompilerParams(vmem_limit_bytes=56 << 20),
         cost_estimate=pl.CostEstimate(
             flops=4 * TP * r * d * width, bytes_accessed=24 << 20, transcendentals=2 * TP * r * width
         ),
@@ -604,7 +594,7 @@
             row,
         ],
         out_specs=pl.BlockSpec((1, r, 2 * width), lambda k: (k, 0, 0)),
-        compiler_params=pltpu.CompilerParams(vmem_limit_bytes=32 << 20),
+        compiler_params=pltpu.CompilerParams(vmem_limit_bytes=56 << 20),
         cost_estimate=pl.CostEstimate(
             flops=2 * TP * r * d * width, bytes_accessed=24 << 20, transcendentals=0
         ),
@@ -619,7 +609,6 @@
     greet([peer(1), peer(2), peer(4)])
     sems = (ssem, rsem)
     acc[...] = jnp.zeros_like(acc)
-    for_rows, sent = reduce_blocks(times(a, w, True), po, pe, rc, sb, xr, yr, sems, peer)
 
     def body(at, g):
         value = mid[at, :]
@@ -636,18 +625,16 @@
         gmid[at, :] = grad
         own[at, :] = grad.astype(bf)
 
-    for_rows(16, body)
-    gather_blocks(own, out, sems, REDUCE_SEMS, local, peer)
+    reduce = Reduce(times(a, w, True), (po, pe, rc, sb, xr, yr), sems, 0, peer)
+    exchange_and_gather(reduce, both_gathers(own, out, sems, local, peer), 16, body)
     sums[0:1, :] = jnp.sum(acc[0], axis=0, keepdims=True)
     sums[1:2, :] = jnp.sum(acc[1], axis=0, keepdims=True)
-    for copy in sent:
-        copy.wait_send()
 
 
 def backward_exchange(a, w, mid, cot, vec, cid):
     _, r, _ = a.shape
     c = w.shape[0]
-    count = REDUCE_SEMS + GATHER_SEMS
+    count = EXCHANGE_SEMS
     return pl.pallas_call(
         backward_kernel,
         out_shape=(SDS((r, c), f32), SDS((TP, r, c), bf), SDS((2, c), f32)),
@@ -659,13 +646,114 @@
             pltpu.VMEM((2, 16, c), f32),
             pltpu.SemaphoreType.DMA((count,)),
             pltpu.SemaphoreType.DMA((count,)),
-            pltpu.SemaphoreType.DMA,
+            pltpu.SemaphoreType.DMA((2,)),
         ],
         compiler_params=pltpu.CompilerParams(
             collective_id=cid, has_side_effects=True, vmem_limit_bytes=52 << 20
         ),
         name="backward_exchange",
     )(a, w, mid, cot, vec)
+
+
+def last_kernel(
+    n, a1, w1, a2, w2, tok, gmid, gain, sums2, gtok, ffn, vec_out,
+    po, pe, rc, sb, xr, yr, pe2, rc2, sb2, xr2, yr2, acc, vecs, near, far, part, ssem, rsem,
+):
+    dp = n // TP
+    me, peer = place()
+    g = lax.div(me, TP)
+    width = vec_out.shape[1]
+    others = [lax.rem(me + TP * j, n) for j in range(1, dp)]
+    greet([peer(k) for k in range(1, TP)] + others)
+    sems = (ssem, rsem)
+    acc[...] = jnp.zeros_like(acc)
+    one = Reduce(times(a1, w1, True), (po, pe, rc, sb, xr, yr), sems, 0, peer)
+    one.first()
+    one.second()
+    for copy in one.core.values():
+        copy.wait_send()
+    one.sent = [copy for copy in one.sent if all(copy is not c for c in one.core.values())]
+    two = Reduce(times(a2, w2, False), (po, pe2, rc2, sb2, xr2, yr2), sems, REDUCE_SEMS, peer)
+    two.first()
+    two.second()
+
+    def body(at, grad):
+        value = tok[at, :].astype(f32)
+        center = jnp.mean(value, axis=-1, keepdims=True)
+        centred = value - center
+        inv = lax.rsqrt(jnp.mean(centred * centred, axis=-1, keepdims=True) + 1e-05)
+        hat = centred * inv
+        acc[0] += grad * hat
+        acc[1] += grad
+        scaled = grad * gain[...]
+        mean_g = jnp.mean(scaled, axis=-1, keepdims=True)
+        mean_gh = jnp.mean(scaled * hat, axis=-1, keepdims=True)
+        gtok[at, :] = gmid[at, :] + inv * (scaled - mean_g - hat * mean_gh)
+
+    for c in (0, 1):
+        one.rows(c, 16, body)
+    vecs[...] = jnp.zeros_like(vecs)
+    vecs[0:1, :] = jnp.sum(acc[0], axis=0, keepdims=True)
+    vecs[1:2, :] = jnp.sum(acc[1], axis=0, keepdims=True)
+    vecs[2:4, :] = sums2[...]
+    base = 2 * REDUCE_SEMS
+    copies = []
+    for j, dev in enumerate(others):
+        at = pl.multiple_of(lax.div(dev, TP) * width, 128)
+        copy = remote(vecs.at[:, pl.ds(at, width)], far.at[j], sems, base + j, dev)
+        copy.start()
+        copies.append(copy)
+
+    def keep(at, value):
+        ffn[at, :] = value
+
+    two.rows(0, 32, keep)
+    total = vecs[:, pl.ds(pl.multiple_of(g * width, 128), width)]
+    for j, copy in enumerate(copies):
+        copy.wait()
+        total = total + far[j]
+    part[...] = total
+    copies = []
+    for k in range(1, TP):
+        copy = remote(part, near.at[k - 1], sems, base + dp + k - 1, peer(k))
+        copy.start()
+        copies.append(copy)
+    two.rows(1, 32, keep)
+    for k, copy in enumerate(copies):
+        copy.wait()
+        total = total + near[k]
+    vec_out[...] = total
+    one.finish()
+    two.finish()
+
+
+def last_exchange(n, a1, w1, a2, w2, tok, gmid, gain, sums2, cid):
+    dp = n // TP
+    _, r, _ = a1.shape
+    c = w1.shape[0]
+    width = c // dp
+    count = 2 * REDUCE_SEMS + dp + TP
+    return pl.pallas_call(
+        functools.partial(last_kernel, n),
+        out_shape=(SDS((r, c), f32), SDS((r, c), f32), SDS((8, width), f32)),
+        in_specs=[VMEM] * 8,
+        out_specs=(VMEM,) * 3,
+        scratch_shapes=reduce_scratch(r, c)
+        + reduce_scratch(r, c, bf)[1:]
+        + [
+            pltpu.VMEM((2, 16, c), f32),
+            pltpu.VMEM((8, c), f32),
+            pltpu.VMEM((TP - 1, 8, width), f32),
+            pltpu.VMEM((dp, 8, width), f32),
+            pltpu.VMEM((8, width), f32),
+            pltpu.SemaphoreType.DMA((count,)),
+            pltpu.SemaphoreType.DMA((count,)),
+        ],
+        compiler_params=pltpu.CompilerParams(
+            collective_id=cid, has_side_effects=True, vmem_limit_bytes=67043328
+        ),
+        name="last_exchange",
+    )(a1, w1, a2, w2, tok, gmid, gain, sums2)
 
 
 def tp_groups(n):
@@ -887,16 +975,11 @@
     g_out = dp_reduce(out_grad, n)
     g_qkvs = jnp.concatenate([g_qkv, g_swish], axis=2)
     w_qkvs = jnp.concatenate([qko[:, : 2 * KH], vs], axis=1)
-    g_normed = matmul_reduce(g_qkvs, w_qkvs, True, 7)
-    inputs = tokens.astype(f32)
-    _, pull_norm1 = jax.vjp(layer_norm, inputs, gain1f, bias1f)
-    g_in_part, g_gain1, g_bias1 = pull_norm1(g_normed)
-    grad_tokens = g_middle + g_in_part
-    ffn = matmul_reduce(hidden, down, False, 8)
+    grad_tokens, ffn, g_vecs = last_exchange(
+        n, g_qkvs, w_qkvs, hidden, down, tokens, g_middle, gain1f, sums2, 7
+    )
     layer_out = (middle + ffn).astype(bf)
 
-    g_vecs = jnp.concatenate([g_gain1, g_bias1, sums2, jnp.zeros((4, d), f32)], axis=0)
-    g_vecs = vector_sum(n, g_vecs, 9)
     g_vecs = lax.dynamic_slice_in_dim(g_vecs, head * shard, shard, 1)
     grad_d = g_down.astype(f32)
     g_gu = plane_a2a(g_gu, n)

time: 842 us -> 815 us (0.968)
  Pallas kernels: 500 us -> 466 us
  blocking collectives: 28.8 us -> 56.6 us
  starting transfers between devices: 28.4 us -> 16 us
  local copies, waits for them, and re-layouts: 50.6 us -> 40.6 us
    all_to_all x1 -> x3, blocking collectives: 28.8 us -> 56.6 us  [plane_a2a(): lax.all_to_all(x, AXIS, 0, 0, axis_index_groups=tp_groups(n), tiled=True)]
    pallas_call x3 -> x1, Pallas kernels: 111 us -> 92.8 us  [last_exchange(): pl.pallas_call(functools.partial(last_kernel, n), out_shape=(SDS((r, c),...]
    reduce_scatter x5, waiting for transfers between devices: 62.9 us -> 75.5 us  [dp_reduce(): lax.psum_scatter(x, AXIS, scatter_dimension=0, tiled=True, axis_index_gro...]
    all_to_all x5 -> x3, starting transfers between devices: 27.5 us -> 15.5 us  [plane_a2a(): lax.all_to_all(x, AXIS, 0, 0, axis_index_groups=tp_groups(n), tiled=True)]
    unnamed x96 -> x85, local copies, waits for them, and re-layouts: 36.5 us -> 24.7 us
    pallas_call x1, Pallas kernels: 116 us -> 105 us  [forward_exchange(): pl.pallas_call(forward_kernel, out_shape=tuple((SDS(*b) for b in blocks))...]
  transfers between devices with their start and end apart: 14 -> 12, of which waited for: 4 -> 2; matrix products, arithmetic and copies ran while one was open for 13% -> 13% of each run, Pallas kernels for 46% -> 44%
where the time goes in v3:
time: 815 us; the launch traced here: 804 us
  Pallas kernels  466 us (57%)
  waiting for transfers between devices  76.2 us (9%)
  matrix products  72 us (9%)
  other arithmetic  61.5 us (8%)
  blocking collectives  56.6 us (7%)
  local copies, waits for them, and re-layouts  40.6 us (5%)
  starting transfers between devices  16 us (2%)
  between operations  14.9 us (2%)
    pallas_call x1, Pallas kernels, forward_exchange(): pl.pallas_call(forward_kernel, out_shape=tuple((SDS(*b) for b in blocks))...  105 us
    pallas_call x1, Pallas kernels, last_exchange(): pl.pallas_call(functools.partial(last_kernel, n), out_shape=(SDS((r, c),...  92.8 us
    pallas_call x3, Pallas kernels, exchange_call(): pl.pallas_call(kernel, out_shape=outs, in_specs=[VMEM] * len(args), out_s...  86.4 us
    pallas_call x1, Pallas kernels, backward_exchange(): pl.pallas_call(backward_kernel, out_shape=(SDS((r, c), f32), SDS((TP, r,...  85 us
    reduce_scatter x5, waiting for transfers between devices, dp_reduce(): lax.psum_scatter(x, AXIS, scatter_dimension=0, tiled=True, axis_index_gro...  75.5 us
    pallas_call x1, Pallas kernels, plane_gather(): pl.pallas_call(gather_kernel, out_shape=SDS((TP, r, c), x.dtype), in_spec...  59.9 us
    all_to_all x3, blocking collectives, plane_a2a(): lax.all_to_all(x, AXIS, 0, 0, axis_index_groups=tp_groups(n), tiled=True)  56.6 us
    dot_general x5, matrix products, dot_tn(): lax.dot_general(a, b, (((0,), (0,)), ((), ())), preferred_element_type=f32)  51.4 us
  transfers between devices with their start and end apart: 12, of which 2 were waited for; matrix products, arithmetic and copies ran while one was open for 13% of the time, Pallas kernels for 44%

profile of v3, /device:TPU:14, one launch (start us, length us, event | category | flops | bytes accessed | tf_op | source)
XLA Modules:
  0.0 804.2 jit_solution(12743709164865470307)
XLA Ops:
  10.2 15.4 %shard_map.254 = bf16[8,64,1024]{2,1,0:T(8,128)(2,1)} custom-call(bf16[64,2048]{1,0:T(8,128)(2,1)S(1)} %copy-done.10, bf16[64,2048]{1,0:T(8,128)(2,1)S(1)} %copy-done.11, bf16[128,2048]{1,0:T(8,128)(2,1)S(1)} %copy-done.9), custom_call_target="tpu_custom_call" | custom-call | tf_op jit(solution)/shard_map/pallas_call | solution.py:167
  31.5 16.9 %shard_map.255 = (bf16[8,64,1024]{2,1,0:T(8,128)(2,1)}, f32[4,8,8,128]{3,2,1,0:T(8,128)S(1)}) custom-call(bf16[64,4096]{1,0:T(8,128)(2,1)S(1)} %copy-done.7, bf16[64,4096]{1,0:T(8,128)(2,1)S(1)} %copy-done.8, f32[8,128]{1,0:T(8,128)S(1)} %scatter.32.vec), custom_call_target="tpu_custom_call" | custom-call | tf_op jit(solution)/shard_map/pallas_call | solution.py:167
  49.8 54.0 %shard_map.256 = (bf16[8,64,1024]{2,1,0:T(8,128)(2,1)}, bf16[8,256,2048]{2,1,0:T(8,128)(2,1)S(1)}) custom-call(bf16[8,64,1024]{2,1,0:T(8,128)(2,1)S(1)} %pad_maximum_fusion.1.gu, bf16[256,2048]{1,0:T(8,128)(2,1)S(1)} %copy-done.3), custom_call_target="tpu_custom_call" | custom-call | tf_op jit(solution)/shard_map/pallas_call | solution.py:167
  118.0 5.4 fusion.5.nrm
  137.7 59.9 %shard_map.257.cot = bf16[8,256,2048]{2,1,0:T(8,128)(2,1)S(1)} custom-call(bf16[256,2048]{1,0:T(8,128)(2,1)S(1)} %copy-done.4), custom_call_target="tpu_custom_call" | custom-call | tf_op jit(solution)/shard_map/pallas_call | solution.py:122
  200.9 6.9 fusion.18
  219.2 105.4 %forward_exchange.1 = (bf16[8,256,512]{2,1,0:T(8,128)(2,1)}, bf16[8,256,512]{2,1,0:T(8,128)(2,1)}, f32[8,256,512]{2,1,0:T(8,128)}, f32[8,256,512]{2,1,0:T(8,128)...) custom-call(bf16[8,256,2048]{2,1,0:T(8,128)(2,1)} %fusion.5.nrm, ...), custom_call_target="tpu_custom_call" | custom-call | tf_op jit(solution)/shard_map/forward_exchange/pallas_call | solution.py:508
  327.2 17.0 %hidden_units.1 = (bf16[8,256,512]{2,1,0:T(8,128)(2,1)}, f32[8,256,512]{2,1,0:T(8,128)}, f32[8,256,512]{2,1,0:T(8,128)}) custom-call(bf16[8,256,2048]{2,1,0:T(8,128)(2,1)} %get-tuple-element.109.x, bf16[2048,1024]{1,0:T(8,128)(2,1)} %all-gather.11.cloned.1.call-done.gu.w), custom_call_target="tpu_custom_call" | custom-call | flops 8589934592 | bytes 25165824 | tf_op jit(solution)/shard_map/hidden_units/pallas_call | solution.py:550
  344.2 13.7 %hidden_back.1.a = bf16[8,256,1024]{2,1,0:T(8,128)(2,1)} custom-call(bf16[8,256,2048]{2,1,0:T(8,128)(2,1)} %copy-done.2, bf16[512,2048]{1,0:T(8,128)(2,1)} %all-gather.9.cloned.1.call-done.down.w2, f32[8,256,512]{2,1,0:T(8,128)} %get-tuple-element.111.act, f32[8,256,512]{2,1,0:T(8,128)} %get-tuple-element.112.slope), custom_call_target="tpu_custom_call" | custom-call | flops 4294967296 | bytes 25165824 | tf_op jit(solution)/shard_map/hidden_back/pallas_call | solution.py:586
  357.9 85.0 %backward_exchange.1 = (f32[256,2048]{1,0:T(8,128)}, bf16[8,256,2048]{2,1,0:T(8,128)(2,1)}, f32[2,2048]{1,0:T(2,128)S(1)}) custom-call(bf16[8,256,1024]{2,1,0:T(8,128)(2,1)} %hidden_back.1.a, bf16[2048,1024]{1,0:T(8,128)(2,1)} %all-gather.11.cloned.1.call-done.gu.w, f32[256,2048]{1,0:T(8,128)} %get-tuple-element.106.mid, bf16[256,2048]{1,0:T(8,128)(2,1)S(1)} %copy-done.4, ...), custom_call_target="tpu_custom_call" | custom-call | tf_op jit(solution)/shard_map/backward_exchange/pallas_call | solution.py:638
  443.0 7.8 multiply_reduce_fusion.1
  472.9 5.3 constant_dynamic-update-slice_fusion.7
  486.4 5.8 bitcast_convert_fusion.4
  492.3 8.2 %bitcast_convert_fusion.3 = bf16[512,2048]{1,0:T(8,128)(2,1)S(1)} fusion(bf16[8,256,512]{2,1,0:T(8,128)(2,1)S(1)} %copy-done.35, bf16[8,256,2048]{2,1,0:T(8,128)(2,1)} %get-tuple-element.113), kind=kOutput, calls=%fused_computation.17 | convolution fusion | flops 4296015872 | bytes 12582912 | tf_op jit(solution)/shard_map/dot_general | solution.py:837
  500.6 28.8 %all_to_all.54 = bf16[8,512,256]{2,1,0:T(8,128)(2,1)} all-to-all(bf16[8,512,256]{2,1,0:T(8,128)(2,1)S(1)} %bitcast.91), channel_id=1, replica_groups={{0,1,2,3,4,5,6,7},{8,9,10,11,12,13,14,15},{16,17,18,19,20,21,22,23},{24..., dimensions={0} | all-to-all | bytes 4194304 | tf_op jit(solution)/shard_map/all_to_all | solution.py:768
  529.5 14.0 %bitcast_convert_fusion = bf16[2048,1024]{1,0:T(8,128)(2,1)} fusion(bf16[8,256,2048]{2,1,0:T(8,128)(2,1)} %get-tuple-element.109.x, bf16[8,256,1024]{2,1,0:T(8,128)(2,1)} %hidden_back.1.a), kind=kOutput, calls=%fused_computation.8 | convolution fusion | flops 8592031744 | bytes 16777216 | tf_op jit(solution)/shard_map/dot_general | solution.py:837
  543.6 14.2 %bitcast_convert_fusion.1 = bf16[2048,1024]{1,0:T(8,128)(2,1)} fusion(bf16[8,256,2048]{2,1,0:T(8,128)(2,1)} %fusion.5.nrm, bf16[8,256,1024]{2,1,0:T(8,128)(2,1)} %copy-done.34), kind=kOutput, calls=%fused_computation.9 | convolution fusion | flops 8592031744 | bytes 16777216 | tf_op jit(solution)/shard_map/dot_general | solution.py:837
  559.4 9.2 %bitcast_convert_fusion.2 = bf16[512,2048]{1,0:T(8,128)(2,1)} fusion(bf16[8,256,512]{2,1,0:T(8,128)(2,1)S(1)} %copy-done.30, bf16[8,256,2048]{2,1,0:T(8,128)(2,1)} %copy-done.2), kind=kOutput, calls=%fused_computation.16 | convolution fusion | flops 4296015872 | bytes 12582912 | tf_op jit(solution)/shard_map/dot_general | solution.py:837
  568.8 13.9 %all_to_all.55.x = bf16[8,64,512]{2,1,0:T(8,128)(2,1)} all-to-all(bf16[8,64,512]{2,1,0:T(8,128)(2,1)} %bitcast.102), channel_id=1, replica_groups={{0,1,2,3,4,5,6,7},{8,9,10,11,12,13,14,15},{16,17,18,19,20,21,22,23},{24..., dimensions={0} | all-to-all | bytes 1048576 | tf_op jit(solution)/shard_map/all_to_all | solution.py:768
  582.7 13.9 %all_to_all.56.x = bf16[8,128,256]{2,1,0:T(8,128)(2,1)} all-to-all(bf16[8,128,256]{2,1,0:T(8,128)(2,1)} %bitcast.103), channel_id=1, replica_groups={{0,1,2,3,4,5,6,7},{8,9,10,11,12,13,14,15},{16,17,18,19,20,21,22,23},{24..., dimensions={0} | all-to-all | bytes 1048576 | tf_op jit(solution)/shard_map/all_to_all | solution.py:768
  596.6 62.8 %reduce-scatter.12.cloned.1.call-done = bf16[512,1024]{1,0:T(8,128)(2,1)} async-done(((bf16[2048,1024]{1,0:T(8,128)(2,1)}), bf16[512,1024]{1,0:T(8,128)(2,1)}) %reduce-scatter.12.cloned.1.call-update) | async-done | bytes 1048592 | tf_op jit(solution)/shard_map/reduce_scatter | solution.py:776
  665.1 5.4 pad_maximum_fusion.w1
  670.5 92.8 %last_exchange.1 = (f32[256,2048]{1,0:T(8,128)}, f32[256,2048]{1,0:T(8,128)}, f32[8,512]{1,0:T(8,128)}) custom-call(bf16[8,256,1536]{2,1,0:T(8,128)(2,1)} %copy-done.18, bf16[2048,1536]{1,0:T(8,128)(2,1)} %pad_maximum_fusion.w1, bf16[8,256,512]{2,1,0:T(8,128)(2,1)} %get-tuple-element.116.a2, bf16[512,2048]{1,0:T(8,128)(2,1)} %all-gather.9.cloned.1.call-done.down.w2, ...), custom_call_target="tpu_custom_call" | custom-call | tf_op jit(solution)/shard_map/last_exchange/pallas_call | solution.py:736
  773.4 12.6 %reduce-scatter.14.cloned.1.call-done = bf16[128,2048]{1,0:T(8,128)(2,1)} async-done(((bf16[512,2048]{1,0:T(8,128)(2,1)}), bf16[128,2048]{1,0:T(8,128)(2,1)}) %reduce-scatter.14.cloned.1.call-update) | async-done | bytes 524304 | tf_op jit(solution)/shard_map/reduce_scatter | solution.py:776
  (183 shorter events, 114.7 us)
Async XLA Ops:
  7.2 116.2 %all-gather.7.cloned.1.call-start = ((), (), s32[]{:S(2)}) async-start(), calls=%async_computation.12 | async-start | bytes 5242880 | tf_op jit(solution)/shard_map/all_gather | solution.py:772
  10.2 38.4 %copy-start.31 = (bf16[64,4096]{1,0:T(8,128)(2,1)S(1)}, bf16[64,4096]{1,0:T(8,128)(2,1)}, u32[]{:S(2)}) copy-start(bf16[64,4096]{1,0:T(8,128)(2,1)} %param.36) | copy-start | bytes 1572868
  10.2 38.9 %copy-start.32 = (bf16[64,4096]{1,0:T(8,128)(2,1)S(1)}, bf16[64,4096]{1,0:T(8,128)(2,1)}, u32[]{:S(2)}) copy-start(bf16[64,4096]{1,0:T(8,128)(2,1)} %param.37) | copy-start | bytes 1572868
  25.6 193.6 %all-gather.5.cloned.1.call-start = ((), (), s32[]{:S(2)}) async-start(), calls=%async_computation.11 | async-start | bytes 5242880 | tf_op jit(solution)/shard_map/all_gather | solution.py:772
  48.5 278.7 %all-gather.11.cloned.1.call-start = ((), (), s32[]{:S(2)}) async-start(), calls=%async_computation.14 | async-start | bytes 5242880 | tf_op jit(solution)/shard_map/all_gather | solution.py:772
  107.1 237.1 %all-gather.9.cloned.1.call-start = ((), (), s32[]{:S(2)}) async-start(), calls=%async_computation.13 | async-start | bytes 2621440 | tf_op jit(solution)/shard_map/all_gather | solution.py:772
  132.2 84.3 %all-to-all-start = ((bf16[8,512,256]{2,1,0:T(8,128)(2,1)}), bf16[8,512,256]{2,1,0:T(8,128)(2,1)S(1)}, u32[]{:S(2)}, u32[]{:S(2)}) async-start(bf16[8,512,256]{2,1,0:T(8,128)(2,1)} %bitcast.89), calls=%async_computation | async-start | bytes 4194304 | tf_op jit(solution)/shard_map/all_to_all | solution.py:768
  137.4 431.3 %reduce-scatter.8.cloned.1.call-start = ((), (), s32[]{:S(2)}) async-start(), calls=%async_computation.16 | async-start | bytes 2621440 | tf_op jit(solution)/shard_map/reduce_scatter | solution.py:776
  137.7 63.2 %copy-start.20 = (bf16[2048,1024]{1,0:T(8,128)(2,1)S(1)}, bf16[2048,1024]{1,0:T(8,128)(2,1)}, u32[]{:S(2)}) copy-start(bf16[2048,1024]{1,0:T(8,128)(2,1)} %all-gather.7.cloned.1.call-done) | copy-start | bytes 12582916
  344.2 13.7 %copy-start.12 = (f32[2,2048]{1,0:T(2,128)S(1)}, f32[2,2048]{1,0:T(2,128)}, u32[]{:S(2)}) copy-start(f32[2,2048]{1,0:T(2,128)} %pad_maximum_fusion.8.vec) | copy-start | bytes 49156
  357.9 85.1 %copy-start.14 = (f32[8,256,512]{2,1,0:T(8,128)S(1)}, f32[8,256,512]{2,1,0:T(8,128)}, u32[]{:S(2)}) copy-start(f32[8,256,512]{2,1,0:T(8,128)} %get-tuple-element.114) | copy-start | bytes 12582916
  357.9 85.1 %copy-start.15 = (f32[8,256,512]{2,1,0:T(8,128)S(1)}, f32[8,256,512]{2,1,0:T(8,128)}, u32[]{:S(2)}) copy-start(f32[8,256,512]{2,1,0:T(8,128)} %get-tuple-element.107) | copy-start | bytes 12582916
  357.9 85.1 %copy-start.21 = (bf16[512,8,256]{0,2,1:T(8,128)(2,1)S(1)}, bf16[512,8,256]{0,2,1:T(8,128)(2,1)}, u32[]{:S(2)}) copy-start(bf16[512,8,256]{0,2,1:T(8,128)(2,1)} %copy.91) | copy-start | bytes 6291460
  443.0 7.9 copy-start.13
  492.2 90.5 %reduce-scatter.10.cloned.1.call-start = ((), (), s32[]{:S(2)}) async-start(), calls=%async_computation.17 | async-start | bytes 2621440 | tf_op jit(solution)/shard_map/reduce_scatter | solution.py:776
  529.5 130.0 %reduce-scatter.12.cloned.1.call-start = ((), (), s32[]{:S(2)}) async-start(), calls=%async_computation.18 | async-start | bytes 5242880 | tf_op jit(solution)/shard_map/reduce_scatter | solution.py:776
  543.6 219.8 %reduce-scatter.6.cloned.1.call-start = ((), (), s32[]{:S(2)}) async-start(), calls=%async_computation.15 | async-start | bytes 5242880 | tf_op jit(solution)/shard_map/reduce_scatter | solution.py:776
  557.9 228.2 %reduce-scatter.14.cloned.1.call-start = ((), (), s32[]{:S(2)}) async-start(), calls=%async_computation.19 | async-start | bytes 2621440 | tf_op jit(solution)/shard_map/reduce_scatter | solution.py:776
  568.7 95.7 %copy-start.33 = (f32[4,8,1,64]{3,2,1,0:T(1,128)S(1)}, f32[4,8,1,64]{3,2,1,0:T(1,128)}, u32[]{:S(2)}) copy-start(f32[4,8,1,64]{3,2,1,0:T(1,128)} %get-tuple-element.152) | copy-start | bytes 24580
  568.7 96.4 %copy-start.17 = (bf16[2048,512]{1,0:T(8,128)(2,1)S(1)}, bf16[2048,512]{1,0:T(8,128)(2,1)}, u32[]{:S(2)}) copy-start(bf16[2048,512]{1,0:T(8,128)(2,1)} %get-tuple-element.148) | copy-start | bytes 6291460
  659.4 103.9 %all-to-all-start.5 = ((bf16[8,64,1024]{2,1,0:T(8,128)(2,1)}), bf16[8,64,1024]{2,1,0:T(8,128)(2,1)}, u32[]{:S(2)}, u32[]{:S(2)}) async-start(bf16[8,64,1024]{2,1,0:T(8,128)(2,1)} %bitcast.99), calls=%async_computation.9 | async-start | bytes 2097152 | tf_op jit(solution)/shard_map/all_to_all | solution.py:768
  763.3 24.9 %copy-start.5 = (bf16[8,64,512]{2,1,0:T(8,128)(2,1)S(1)}, bf16[8,64,512]{2,1,0:T(8,128)(2,1)}, u32[]{:S(2)}) copy-start(bf16[8,64,512]{2,1,0:T(8,128)(2,1)} %all_to_all.55.x) | copy-start | bytes 1572868
  763.4 29.6 %all-to-all-start.1 = ((bf16[8,64,1024]{2,1,0:T(8,128)(2,1)}), bf16[8,64,1024]{2,1,0:T(8,128)(2,1)S(1)}, u32[]{:S(2)}, u32[]{:S(2)}) async-start(bf16[8,64,1024]{2,1,0:T(8,128)(2,1)} %bitcast.98), calls=%async_computation.2 | async-start | bytes 2097152 | tf_op jit(solution)/shard_map/all_to_all | solution.py:768
  769.9 19.3 %copy-start.6 = (bf16[8,128,256]{2,1,0:T(8,128)(2,1)S(1)}, bf16[8,128,256]{2,1,0:T(8,128)(2,1)}, u32[]{:S(2)}) copy-start(bf16[8,128,256]{2,1,0:T(8,128)(2,1)} %all_to_all.56.x) | copy-start | bytes 1572868
  (27 other events, 71.0 us)
Sparse Core Ops, SparseCore 0:
  25.7 79.4 all-gather.6
  106.9 79.1 all-gather.4
  187.6 79.2 all-gather.10
  268.3 45.2 all-gather.8
  492.4 42.8 reduce-scatter.7
  537.4 42.8 reduce-scatter.9
  582.6 76.8 reduce-scatter.11
  661.7 77.2 reduce-scatter.5
  741.3 44.6 reduce-scatter.13

commit v4 on v3

--- a/solution.py
+++ b/solution.py
@@ -109,30 +109,6 @@
     gather.start()
     gather.forward()
     gather.finish()
-
-
-def gather_kernel(x_ref, out_ref, ssem, rsem, local):
-    _, peer = place()
-    greet([peer(1), peer(2), peer(4)])
-    gather_blocks(x_ref, out_ref, (ssem, rsem), 0, local, peer)
-
-
-def plane_gather(x, cid):
-    r, c = x.shape
-    return pl.pallas_call(
-        gather_kernel,
-        out_shape=SDS((TP, r, c), x.dtype),
-        in_specs=[VMEM],
-        out_specs=ANY,
-        scratch_shapes=[
-            pltpu.SemaphoreType.DMA((GATHER_SEMS,)),
-            pltpu.SemaphoreType.DMA((GATHER_SEMS,)),
-            pltpu.SemaphoreType.DMA,
-        ],
-        compiler_params=pltpu.CompilerParams(
-            collective_id=cid, has_side_effects=True, vmem_limit_bytes=8 << 20
-        ),
-    )(x)
 
 
 def send_columns(src, out, cols, at, sems, base, local, t, peer, rows=None):
@@ -201,59 +177,74 @@
     return exchange_call(first_kernel, outs, (wq, wk, wo), 28, 4, cid)[0]
 
 
-def second_kernel(n, wv, ws, vec, out, vec_out, ssem, rsem, local):
+def second_kernel(n, tok, vec, tok_out, vec_out, ssem, rsem, local):
     dp = n // TP
     me, peer = place()
     t, g = lax.rem(me, TP), lax.div(me, TP)
     others = [lax.rem(me + TP * j, n) for j in range(1, dp)]
     greet([peer(k) for k in range(1, TP)] + others)
     sems = (ssem, rsem)
-    cols = wv.shape[1] // TP
+    base = GATHER_SEMS
     far = []
-    keep = pltpu.make_async_copy(vec, vec_out.at[g, t], local.at[2])
+    keep = pltpu.make_async_copy(vec, vec_out.at[g, t], local.at[1])
     keep.start()
     for j, dev in enumerate(others):
-        copy = remote(vec, vec_out.at[g, t], sems, 21 + j, dev)
+        copy = remote(vec, vec_out.at[g, t], sems, base + TP + j, dev)
         copy.start()
         far.append(copy)
-    parts = [
-        send_columns(wv, out, cols, 0, sems, 0, local.at[0], t, peer),
-        send_columns(ws, out, cols, cols, sems, 7, local.at[1], t, peer),
-    ]
+    gather = Gather(tok, tok_out, 0, tok.shape[0], sems, 0, local.at[0], peer)
+    gather.start()
     for copy in far:
         copy.wait()
     keep.wait()
     near = []
     for k in range(1, TP):
-        copy = remote(vec_out.at[:, t], vec_out.at[:, t], sems, 13 + k, peer(k))
+        copy = remote(vec_out.at[:, t], vec_out.at[:, t], sems, base + k, peer(k))
         copy.start()
         near.append(copy)
-    finish(parts)
+    gather.forward()
+    gather.finish()
     for copy in near:
         copy.wait()
 
 
-def second_exchange(n, wv, ws, vec, cid):
-    outs = (
-        SDS((TP, wv.shape[0], 2 * wv.shape[1] // TP), bf),
-        SDS((n // TP, TP) + vec.shape, f32),
-    )
+def second_exchange(n, tok, vec, cid):
+    outs = (SDS((TP,) + tok.shape, bf), SDS((n // TP, TP) + vec.shape, f32))
     kernel = functools.partial(second_kernel, n)
-    return exchange_call(kernel, outs, (wv, ws, vec), 21 + n // TP, 3, cid)
-
-
-def third_kernel(gu, tok, gu_out, tok_out, ssem, rsem, local):
+    sems = GATHER_SEMS + TP + n // TP
+    return exchange_call(kernel, outs, (tok, vec), sems, 2, cid)
+
+
+def third_kernel(wv, ws, out, ssem, rsem, local):
     me, peer = place()
     t = lax.rem(me, TP)
     greet([peer(k) for k in range(1, TP)])
     sems = (ssem, rsem)
-    gather_blocks(tok, tok_out, sems, 7, local.at[1], peer)
-    finish([send_columns(gu, gu_out, gu.shape[2], 0, sems, 0, local.at[0], t, peer)])
-
-
-def third_exchange(gu, tok, cid):
-    outs = (SDS(gu.shape, bf), SDS((TP,) + tok.shape, bf))
-    return exchange_call(third_kernel, outs, (gu, tok), 7 + GATHER_SEMS, 2, cid)
+    cols = wv.shape[1] // TP
+    finish([
+        send_columns(wv, out, cols, 0, sems, 0, local.at[0], t, peer),
+        send_columns(ws, out, cols, cols, sems, 7, local.at[1], t, peer),
+    ])
+
+
+def third_exchange(wv, ws, cid):
+    outs = (SDS((TP, wv.shape[0], 2 * wv.shape[1] // TP), bf),)
+    return exchange_call(third_kernel, outs, (wv, ws), 14, 2, cid)[0]
+
+
+def fourth_kernel(gu, cot, gu_out, cot_out, ssem, rsem, local):
+    me, peer = place()
+    t = lax.rem(me, TP)
+    greet([peer(k) for k in range(1, TP)])
+    sems = (ssem, rsem)
+    parts = [send_columns(gu, gu_out, gu.shape[2], 0, sems, 0, local.at[0], t, peer)]
+    gather_blocks(cot, cot_out, sems, 7, local.at[1], peer)
+    finish(parts)
+
+
+def fourth_exchange(gu, cot, cid):
+    outs = (SDS(gu.shape, bf), SDS((TP,) + cot.shape, bf))
+    return exchange_call(fourth_kernel, outs, (gu, cot), 7 + GATHER_SEMS, 2, cid)
 
 
 REDUCE_SEMS = 16
@@ -274,9 +265,11 @@
         self.sent.append(copy)
         return copy
 
-    def pair(self, i):
+    def ready(self, i):
         if self.prepare is not None:
             self.prepare(2 * i)
+
+    def pair(self, i):
         self.product(i, self.po.at[i], self.pe.at[i])
         self.core[i] = self.send(self.po.at[i], self.rc.at[i], self.pc, i)
 
@@ -319,24 +312,21 @@
         self.add(c, 1, 1, 5, self.yr.at[c, 0])
         self.link(c, 5, "x2b", self.xr, 2, self.px)
 
-    def first(self):
+    def run(self):
+        self.ready(3)
         self.pair(3)
-        self.pair(1)
-        self.core[3].wait_recv()
-        self.six(0)
-        self.pair(2)
-        self.core[1].wait_recv()
-        self.two(0)
-        self.core[2].wait_recv()
-        self.four(0)
-        self.pair(0)
-        self.onward(0)
-
-    def second(self):
-        self.six(1)
-        self.two(1)
-        self.four(1)
-        self.onward(1)
+        stages = ((1, 3, self.six), (2, 1, self.two), (0, 2, self.four))
+        for following, now, stage in stages:
+            self.ready(following)
+            if self.prepare is None:
+                self.pair(following)
+            self.core[now].wait_recv()
+            for c in (0, 1):
+                stage(c)
+            if self.prepare is not None:
+                self.pair(following)
+        for c in (0, 1):
+            self.onward(c)
 
     def rows(self, c, step, body):
         if c == 0:
@@ -401,8 +391,7 @@
 
 
 def exchange_and_gather(reduce, gathers, step, body):
-    reduce.first()
-    reduce.second()
+    reduce.run()
     for c in (0, 1):
         reduce.rows(c, step, body)
         gathers[c].start()
@@ -656,7 +645,7 @@
 
 
 def last_kernel(
-    n, a1, w1, a2, w2, tok, gmid, gain, sums2, gtok, ffn, vec_out,
+    n, gqkv, gs, wqk, wvs, a2, w2, tok, gmid, gain, sums2, gtok, ffn, vec_out,
     po, pe, rc, sb, xr, yr, pe2, rc2, sb2, xr2, yr2, acc, vecs, near, far, part, ssem, rsem,
 ):
     dp = n // TP
@@ -667,15 +656,28 @@
     greet([peer(k) for k in range(1, TP)] + others)
     sems = (ssem, rsem)
     acc[...] = jnp.zeros_like(acc)
-    one = Reduce(times(a1, w1, True), (po, pe, rc, sb, xr, yr), sems, 0, peer)
-    one.first()
-    one.second()
+    nt = (((1,), (1,)), ((), ()))
+
+    def product(i, odd, even):
+        r, qk, v = gqkv.shape[1], wqk.shape[1], gs.shape[2]
+        x, y = rows_of_pair(gqkv, i), rows_of_pair(gs, i)
+
+        @pl.loop(0, even.shape[1] // TILE)
+        def _(j):
+            at = pl.ds(pl.multiple_of(j * TILE, TILE), TILE)
+            z = lax.dot_general(x[:, :qk], wqk[at, :], nt, preferred_element_type=f32)
+            z += lax.dot_general(x[:, qk:], wvs[at, :v], nt, preferred_element_type=f32)
+            z += lax.dot_general(y, wvs[at, v:], nt, preferred_element_type=f32)
+            even[:, at] = z[:r].astype(even.dtype)
+            odd[:, at] = z[r:].astype(odd.dtype)
+
+    one = Reduce(product, (po, pe, rc, sb, xr, yr), sems, 0, peer)
+    one.run()
     for copy in one.core.values():
         copy.wait_send()
     one.sent = [copy for copy in one.sent if all(copy is not c for c in one.core.values())]
     two = Reduce(times(a2, w2, False), (po, pe2, rc2, sb2, xr2, yr2), sems, REDUCE_SEMS, peer)
-    two.first()
-    two.second()
+    two.run()
 
     def body(at, grad):
         value = tok[at, :].astype(f32)
@@ -727,16 +729,16 @@
     two.finish()
 
 
-def last_exchange(n, a1, w1, a2, w2, tok, gmid, gain, sums2, cid):
+def last_exchange(n, gqkv, gs, wqk, wvs, a2, w2, tok, gmid, gain, sums2, cid):
     dp = n // TP
-    _, r, _ = a1.shape
-    c = w1.shape[0]
+    _, r, _ = a2.shape
+    c = w2.shape[1]
     width = c // dp
     count = 2 * REDUCE_SEMS + dp + TP
     return pl.pallas_call(
         functools.partial(last_kernel, n),
         out_shape=(SDS((r, c), f32), SDS((r, c), f32), SDS((8, width), f32)),
-        in_specs=[VMEM] * 8,
+        in_specs=[VMEM] * 10,
         out_specs=(VMEM,) * 3,
         scratch_shapes=reduce_scratch(r, c)
         + reduce_scratch(r, c, bf)[1:]
@@ -753,7 +755,90 @@
             collective_id=cid, has_side_effects=True, vmem_limit_bytes=67043328
         ),
         name="last_exchange",
-    )(a1, w1, a2, w2, tok, gmid, gain, sums2)
+    )(gqkv, gs, wqk, wvs, a2, w2, tok, gmid, gain, sums2)
+
+
+def gate_back_kernel(g_low, w, ret, swi, gret, gswi):
+    r, width = gret.shape[1:]
+    cols = w.shape[2]
+    nt = (((1,), (1,)), ((), ()))
+    grad = jnp.zeros((r, width), f32)
+    for j in range(w.shape[0]):
+        grad += lax.dot_general(
+            g_low[0, :, j * cols : (j + 1) * cols], w[j], nt, preferred_element_type=f32
+        )
+    value, gate = ret[0], swi[0]
+    centred = value - jnp.mean(value, axis=-1, keepdims=True)
+    spread = jnp.mean(centred * centred, axis=-1, keepdims=True)
+    inv = lax.rsqrt(jnp.maximum(spread, 0.25))
+    share = 1.0 / (1.0 + jnp.exp(-gate))
+    silu = gate * share
+    gswi[0] = (grad * (centred * inv) * (share * (1.0 + gate * (1.0 - share)))).astype(bf)
+    grad = grad * silu
+    pull = jnp.mean(grad * centred, axis=-1, keepdims=True)
+    pull = jnp.where(spread > 0.25, inv * inv * inv * pull, 0.0)
+    grad = grad * inv - centred * pull
+    gret[0] = (grad - jnp.mean(grad, axis=-1, keepdims=True)).astype(bf)
+
+
+def gate_back(g_low, w, ret, swi):
+    _, r, d = g_low.shape
+    width = ret.shape[2]
+    row = pl.BlockSpec((1, r, width), lambda k: (k, 0, 0))
+    return pl.pallas_call(
+        gate_back_kernel,
+        grid=(TP,),
+        out_shape=(SDS(ret.shape, bf), SDS(ret.shape, bf)),
+        in_specs=[
+            pl.BlockSpec((1, r, d), lambda k: (k, 0, 0)),
+            pl.BlockSpec(w.shape, lambda k: (0, 0, 0)),
+            row,
+            row,
+        ],
+        out_specs=(row, row),
+        compiler_params=pltpu.CompilerParams(vmem_limit_bytes=56 << 20),
+        cost_estimate=pl.CostEstimate(
+            flops=2 * TP * r * d * width, bytes_accessed=22 << 20, transcendentals=TP * r * width
+        ),
+        name="gate_back",
+    )(g_low, w, ret, swi)
+
+
+def scores_back_kernel(sco, mask, q, k, v, gret, cosine, sine, out):
+    nt, tn = (((1,), (1,)), ((), ())), (((0,), (0,)), ((), ()))
+    kh = q.shape[2]
+    half = kh // 2
+    out[0, :, 2 * kh :] = lax.dot_general(
+        sco[0], gret[0], tn, preferred_element_type=f32
+    ).astype(bf)
+    grad = lax.dot_general(gret[0], v[0], nt, preferred_element_type=f32)
+    grad = (grad * mask[0]).astype(bf)
+    gq = jnp.dot(grad, k[0], preferred_element_type=f32)
+    gk = lax.dot_general(grad, q[0], tn, preferred_element_type=f32)
+    for i, g in enumerate((gq, gk)):
+        u, w = g[:, :half], g[:, half:]
+        at = i * kh
+        out[0, :, at : at + half] = (u * cosine[0] + w * sine[0]).astype(bf)
+        out[0, :, at + half : at + kh] = (w * cosine[0] - u * sine[0]).astype(bf)
+
+
+def scores_back(sco, mask, q, k, v, gret, cosine, sine):
+    _, r, kh = q.shape
+    arrays = (sco, mask, q, k, v, gret, cosine, sine)
+    width = 2 * kh + v.shape[2]
+    spec = [pl.BlockSpec((1,) + x.shape[1:], lambda i: (i, 0, 0)) for x in arrays]
+    return pl.pallas_call(
+        scores_back_kernel,
+        grid=(TP,),
+        out_shape=SDS((TP, r, width), bf),
+        in_specs=spec,
+        out_specs=pl.BlockSpec((1, r, width), lambda i: (i, 0, 0)),
+        compiler_params=pltpu.CompilerParams(vmem_limit_bytes=56 << 20),
+        cost_estimate=pl.CostEstimate(
+            flops=4 * TP * r * r * (kh + v.shape[2]), bytes_accessed=16 << 20, transcendentals=0
+        ),
+        name="scores_back",
+    )(*arrays)
 
 
 def tp_groups(n):
@@ -808,12 +893,6 @@
     return jnp.concatenate([u * cosine - w * sine, w * cosine + u * sine], axis=-1)
 
 
-def rotate_back(value, cosine, sine):
-    half = KH // 2
-    u, w = value[..., :half], value[..., half:]
-    return jnp.concatenate([u * cosine + w * sine, w * cosine - u * sine], axis=-1)
-
-
 def decay_mask(segment, offset, head):
     diff = offset[:, :, None] - offset[:, None, :]
     valid = (segment[:, :, None] == segment[:, None, :]) & (diff >= 0)
@@ -822,23 +901,12 @@
     return jnp.where(valid, jnp.exp(log * steps), 0.0) / math.sqrt(KH)
 
 
-def group_gate(retained, swish_in):
-    center = jnp.mean(retained, axis=-1, keepdims=True)
-    centred = retained - center
-    spread = jnp.mean(centred * centred, axis=-1, keepdims=True)
-    return jax.nn.silu(swish_in) * (centred * lax.rsqrt(jnp.maximum(spread, 0.25)))
-
-
 def dot(a, b):
     return lax.dot_general(a, b, (((1,), (0,)), ((), ())), preferred_element_type=f32)
 
 
 def dot_tn(a, b):
     return lax.dot_general(a, b, (((0,), (0,)), ((), ())), preferred_element_type=f32)
-
-
-def dot_nt(a, b):
-    return lax.dot_general(a, b, (((1,), (1,)), ((), ())), preferred_element_type=f32)
 
 
 def bmm(eq, a, b):
@@ -848,11 +916,6 @@
 def col_blocks(w):
     r, c = w.shape
     return w.reshape(r, TP, c // TP).transpose(1, 0, 2).reshape(TP * r, c // TP)
-
-
-def col_join(w, r):
-    c = w.shape[1]
-    return w.reshape(TP, r, c).transpose(1, 0, 2).reshape(r, TP * c)
 
 
 def join_kernel(widths, parts, x, *outs):
@@ -902,25 +965,25 @@
     def ff_blocks(w):
         return w.reshape(shard, dp, TP, unit).transpose(2, 0, 1, 3).reshape(TP, shard, dp * unit)
 
-    vec = jnp.zeros((8, 128), f32)
-    for i, v in enumerate((gain1, bias1, gain2, bias2)):
-        vec = vec.at[i, :shard].set(v.astype(f32))
-    vec = vec.at[4, :3].set(lengths[0].astype(f32))
+    lens = jnp.pad(lengths[0].astype(f32), (0, shard - lengths.shape[1]))
+    vec = jnp.stack([v.astype(f32) for v in (gain1, bias1, gain2, bias2)] + [lens])
+    vec = jnp.pad(vec, ((0, 3), (0, 128 - shard)))
     qko_blk = first_exchange(wq, wk, wo, 1)
     qko = dp_gather(qko_blk.reshape(TP * shard, 4 * KH), n)
-    vs_blk, vec_all = second_exchange(n, after(wv, qko_blk), ws, vec, 2)
+    tok_all, vec_all = second_exchange(n, after(tokens, qko_blk), vec, 2)
+    vs_blk = third_exchange(after(wv, tok_all), ws, 3)
     vs = dp_gather(vs_blk.reshape(TP * shard, 2 * VH), n)
     gu_in = jnp.concatenate([ff_blocks(wg), ff_blocks(wu)], axis=2)
-    gu_blk, tok_all = third_exchange(gu_in, after(tokens, vs_blk), 3)
+    gu_blk, cot_all = fourth_exchange(gu_in, after(cot, vs_blk), 4)
     gu = dp_gather(gu_blk.reshape(TP * shard, 2 * dp * unit), n)
     down = dp_gather(wd, n)
-    cot_all = plane_gather(after(cot, tok_all), 4)
     gain1f, bias1f, gain2f, bias2f = (
         vec_all[:, :, i, :shard].reshape(1, d) for i in range(4)
     )
     vec2 = jnp.concatenate([gain2f, bias2f], axis=0)
+    qk = qko[:, : 2 * KH]
     out = qko[:, 2 * KH :].reshape(n, shard, 2, d // TP).transpose(0, 2, 1, 3)
-    out_blk = plane_a2a(out.reshape(TP * VH, d // TP), n)
+    out_blk = plane_a2a(out.reshape(TP * VH, d // TP), n).reshape(TP, VH, d // TP)
 
     mine = lax.dynamic_slice_in_dim(vec_all, lax.div(me, TP), 1, 0)[0, :, 4, :3]
     order = jnp.arange(TP, dtype=jnp.int32)
@@ -931,16 +994,15 @@
     mask = decay_mask(segment, offset, head)
 
     normed = layer_norm(tok_all.reshape(TP * rows, d).astype(f32), gain1f, bias1f).astype(bf)
-    qk_out = dot(normed, qko[:, : 2 * KH]).reshape(TP, rows, 2 * KH)
+    qk_out = dot(normed, qk).reshape(TP, rows, 2 * KH)
     query, key = qk_out[..., :KH], qk_out[..., KH:]
     q_rot = rotate(query, cosine, sine).astype(bf)
     k_rot = rotate(key, cosine, sine).astype(bf)
     plain = bmm("btd,bsd->bts", q_rot, k_rot)
     scores = (plain * mask).astype(bf)
     v_low, mixed, retained, swish_in, middle, normed2 = forward_exchange(
-        normed.reshape(TP, rows, d), vs, scores, out_blk.reshape(TP, VH, d // TP), tokens, vec2, 5
+        normed.reshape(TP, rows, d), vs, scores, out_blk, tokens, vec2, 5
     )
-    out = col_join(out_blk, VH)
     hidden, act, slope = hidden_units(normed2, gu)
     normed2 = normed2.reshape(TP * rows, d)
     down_grad = dot_tn(hidden.reshape(TP * rows, dp * unit), cot_all.reshape(TP * rows, d)).astype(bf)
@@ -951,32 +1013,18 @@
     g_gu = dp_reduce(gu_grad, n)
     g_middle, g_low, sums2 = backward_exchange(g_fs, gu, middle, cot, vec2, 6)
 
+    g_retained, g_swish = gate_back(g_low, out_blk, retained, swish_in)
     g_low = g_low.reshape(TP * rows, d)
-    mixed = mixed.reshape(TP * rows, VH)
-    g_mixed = dot_nt(g_low, out).reshape(TP, rows, VH)
-    _, pull_group = jax.vjp(group_gate, retained, swish_in)
-    g_retained, g_swish = pull_group(g_mixed)
-    g_retained = g_retained.astype(bf)
-    g_swish = g_swish.astype(bf)
     swish_grad = dot_tn(normed, g_swish.reshape(TP * rows, VH)).astype(bf)
     g_swi = dp_reduce(swish_grad, n)
-    out_grad = dot_tn(mixed, g_low).astype(bf)
+    out_grad = dot_tn(mixed.reshape(TP * rows, VH), g_low).astype(bf)
     out_grad = plane_a2a(col_blocks(out_grad), n)
-    g_value = bmm("bts,btd->bsd", scores, g_retained).astype(bf)
-    g_scores = bmm("btd,bsd->bts", g_retained, v_low)
-    g_plain = (g_scores * mask).astype(bf)
-    g_qrot = bmm("bts,bsd->btd", g_plain, k_rot)
-    g_krot = bmm("bts,btd->bsd", g_plain, q_rot)
-    g_query = rotate_back(g_qrot, cosine, sine).astype(bf)
-    g_key = rotate_back(g_krot, cosine, sine).astype(bf)
-    g_qkv = jnp.concatenate([g_query, g_key, g_value], axis=2)
+    g_qkv = scores_back(scores, mask, q_rot, k_rot, v_low, g_retained, cosine, sine)
     qkv_grad = dot_tn(normed, g_qkv.reshape(TP * rows, 2 * KH + VH)).astype(bf)
     g_qkv_own = dp_reduce(qkv_grad, n)
     g_out = dp_reduce(out_grad, n)
-    g_qkvs = jnp.concatenate([g_qkv, g_swish], axis=2)
-    w_qkvs = jnp.concatenate([qko[:, : 2 * KH], vs], axis=1)
     grad_tokens, ffn, g_vecs = last_exchange(
-        n, g_qkvs, w_qkvs, hidden, down, tokens, g_middle, gain1f, sums2, 7
+        n, g_qkv, g_swish, qk, vs, hidden, down, tokens, g_middle, gain1f, sums2, 7
     )
     layer_out = (middle + ffn).astype(bf)
 

time: 815 us -> 764 us (0.937)
  other arithmetic: 61.5 us -> 35.6 us
  local copies, waits for them, and re-layouts: 40.6 us -> 31 us
    pallas_call x3 -> x4, Pallas kernels: 86.4 us -> 123 us  [exchange_call(): pl.pallas_call(kernel, out_shape=outs, in_specs=[VMEM] * len(args), out_s...]
    pallas_call x1 -> x2, Pallas kernels: 59.9 us -> 23.8 us  [the longest x1 13.7 us: gate_back(): pl.pallas_call(gate_back_kernel, grid=(TP,), out_shape=(SDS(ret.shape, bf...]
    unnamed x5 -> x0, other arithmetic: 19.6 us -> none
    reduce_scatter x5, waiting for transfers between devices: 75.5 us -> 65.8 us  [dp_reduce(): lax.psum_scatter(x, AXIS, scatter_dimension=0, tiled=True, axis_index_gro...]
    unnamed x85 -> x67, local copies, waits for them, and re-layouts: 24.7 us -> 18.6 us
  transfers between devices with their start and end apart: 12 -> 12, of which waited for: 2 -> 3; matrix products, arithmetic and copies ran while one was open for 13% -> 14% of each run, Pallas kernels for 44% -> 44%
where the time goes in v4:
time: 764 us; the launch traced here: 754 us
  Pallas kernels  460 us (60%)
  waiting for transfers between devices  73.4 us (10%)
  matrix products  65.8 us (9%)
  blocking collectives  56.6 us (7%)
  other arithmetic  35.6 us (5%)
  local copies, waits for them, and re-layouts  31 us (4%)
  starting transfers between devices  16.5 us (2%)
  between operations  14.6 us (2%)
    pallas_call x4, Pallas kernels, exchange_call(): pl.pallas_call(kernel, out_shape=outs, in_specs=[VMEM] * len(args), out_s...  123 us
    pallas_call x1, Pallas kernels, forward_exchange(): pl.pallas_call(forward_kernel, out_shape=tuple((SDS(*b) for b in blocks))...  100 us
    pallas_call x1, Pallas kernels, last_exchange(): pl.pallas_call(functools.partial(last_kernel, n), out_shape=(SDS((r, c),...  91.2 us
    pallas_call x1, Pallas kernels, backward_exchange(): pl.pallas_call(backward_kernel, out_shape=(SDS((r, c), f32), SDS((TP, r,...  84.7 us
    reduce_scatter x5, waiting for transfers between devices, dp_reduce(): lax.psum_scatter(x, AXIS, scatter_dimension=0, tiled=True, axis_index_gro...  65.8 us
    all_to_all x3, blocking collectives, plane_a2a(): lax.all_to_all(x, AXIS, 0, 0, axis_index_groups=tp_groups(n), tiled=True)  56.6 us
    dot_general x5, matrix products, dot_tn(): lax.dot_general(a, b, (((0,), (0,)), ((), ())), preferred_element_type=f32)  55.8 us
    unnamed x67, local copies, waits for them, and re-layouts  18.6 us
  transfers between devices with their start and end apart: 12, of which 3 were waited for; matrix products, arithmetic and copies ran while one was open for 14% of the time, Pallas kernels for 44%

profile of v4, /device:TPU:14, one launch (start us, length us, event | category | flops | bytes accessed | tf_op | source)
XLA Modules:
  0.0 753.6 jit_solution(9765745060799582109)
XLA Ops:
  10.3 15.5 %shard_map.254 = bf16[8,64,1024]{2,1,0:T(8,128)(2,1)} custom-call(bf16[64,2048]{1,0:T(8,128)(2,1)S(1)} %copy-done.9, bf16[64,2048]{1,0:T(8,128)(2,1)S(1)} %copy-done.10, bf16[128,2048]{1,0:T(8,128)(2,1)S(1)} %copy-done.6), custom_call_target="tpu_custom_call" | custom-call | tf_op jit(solution)/shard_map/pallas_call | solution.py:143
  26.0 41.8 %shard_map.255 = (bf16[8,256,2048]{2,1,0:T(8,128)(2,1)S(1)}, f32[4,8,8,128]{3,2,1,0:T(8,128)S(1)}) custom-call(bf16[256,2048]{1,0:T(8,128)(2,1)S(1)} %copy-done.1, f32[8,128]{1,0:T(8,128)S(1)} %pad.9.vec), custom_call_target="tpu_custom_call" | custom-call | tf_op jit(solution)/shard_map/pallas_call | solution.py:143
  71.1 15.0 %shard_map.256 = bf16[8,64,1024]{2,1,0:T(8,128)(2,1)} custom-call(bf16[64,4096]{1,0:T(8,128)(2,1)S(1)} %copy-done.7, bf16[64,4096]{1,0:T(8,128)(2,1)S(1)} %copy-done.8), custom_call_target="tpu_custom_call" | custom-call | tf_op jit(solution)/shard_map/pallas_call | solution.py:143
  88.5 51.1 %shard_map.257 = (bf16[8,64,1024]{2,1,0:T(8,128)(2,1)}, bf16[8,256,2048]{2,1,0:T(8,128)(2,1)S(1)}) custom-call(bf16[8,64,1024]{2,1,0:T(8,128)(2,1)S(1)} %pad_maximum_fusion.2.gu, bf16[256,2048]{1,0:T(8,128)(2,1)S(1)} %copy-done.3), custom_call_target="tpu_custom_call" | custom-call | tf_op jit(solution)/shard_map/pallas_call | solution.py:143
  155.5 8.6 %fusion.5.nrm = bf16[8,256,2048]{2,1,0:T(8,128)(2,1)} fusion(bf16[8,256,2048]{2,1,0:T(8,128)(2,1)} %copy-done, f32[2048]{0:T(1024)S(1)} %add.56, f32[2048]{0:T(1024)S(1)} %mul.100, f32[8,256]{1,0:T(8,128)S(1)} %add_rsqrt_fusion, f32[8,256]{1,0:T(8,128)S(1)} %broadcast_multiply_fusion), kind=kLoop, calls=%fused_computation.7 | loop fusion | flops 25165824 | bytes 16809984 | tf_op jit(solution)/shard_map/convert_element_type | solution.py:996
  179.0 7.6 %fusion.11 = f32[8,256,512]{2,1,0:T(8,128)S(1)} fusion(bf16[8,256,2048]{2,1,0:T(8,128)(2,1)} %fusion.5.nrm, bf16[2048,1024]{1,0:T(8,128)(2,1)} %all-gather.7.cloned.1.call-done), kind=kOutput, calls=%fused_computation.21 | convolution fusion | flops 4294967296 | bytes 14680064 | tf_op jit(solution)/shard_map/dot_general | solution.py:905
  196.1 6.9 all-to-all-done.w
  204.4 100.1 %forward_exchange.1 = (bf16[8,256,512]{2,1,0:T(8,128)(2,1)}, bf16[8,256,512]{2,1,0:T(8,128)(2,1)}, f32[8,256,512]{2,1,0:T(8,128)}, f32[8,256,512]{2,1,0:T(8,128)...) custom-call(bf16[8,256,2048]{2,1,0:T(8,128)(2,1)} %fusion.5.nrm, ...), custom_call_target="tpu_custom_call" | custom-call | tf_op jit(solution)/shard_map/forward_exchange/pallas_call | solution.py:497
  304.6 17.0 %hidden_units.1 = (bf16[8,256,512]{2,1,0:T(8,128)(2,1)}, f32[8,256,512]{2,1,0:T(8,128)}, f32[8,256,512]{2,1,0:T(8,128)}) custom-call(bf16[8,256,2048]{2,1,0:T(8,128)(2,1)} %get-tuple-element.51.x, bf16[2048,1024]{1,0:T(8,128)(2,1)} %all-gather.11.cloned.1.call-done.gu.w), custom_call_target="tpu_custom_call" | custom-call | flops 8589934592 | bytes 25165824 | tf_op jit(solution)/shard_map/hidden_units/pallas_call | solution.py:539
  321.6 13.7 %hidden_back.1.a = bf16[8,256,1024]{2,1,0:T(8,128)(2,1)} custom-call(bf16[8,256,2048]{2,1,0:T(8,128)(2,1)} %copy-done.2, bf16[512,2048]{1,0:T(8,128)(2,1)} %all-gather.9.cloned.1.call-done.down.w2, f32[8,256,512]{2,1,0:T(8,128)} %get-tuple-element.53.act, f32[8,256,512]{2,1,0:T(8,128)} %get-tuple-element.54.slope), custom_call_target="tpu_custom_call" | custom-call | flops 4294967296 | bytes 25165824 | tf_op jit(solution)/shard_map/hidden_back/pallas_call | solution.py:575
  335.3 84.7 %backward_exchange.1 = (f32[256,2048]{1,0:T(8,128)}, bf16[8,256,2048]{2,1,0:T(8,128)(2,1)}, f32[2,2048]{1,0:T(2,128)S(1)}) custom-call(bf16[8,256,1024]{2,1,0:T(8,128)(2,1)} %hidden_back.1.a, bf16[2048,1024]{1,0:T(8,128)(2,1)} %all-gather.11.cloned.1.call-done.gu.w, f32[256,2048]{1,0:T(8,128)} %get-tuple-element.47.mid, bf16[256,2048]{1,0:T(8,128)(2,1)S(1)} %copy-done.3, ...), custom_call_target="tpu_custom_call" | custom-call | tf_op jit(solution)/shard_map/backward_exchange/pallas_call | solution.py:627
  420.6 13.7 %gate_back.1 = (bf16[8,256,512]{2,1,0:T(8,128)(2,1)}, bf16[8,256,512]{2,1,0:T(8,128)(2,1)}) custom-call(bf16[8,256,2048]{2,1,0:T(8,128)(2,1)} %get-tuple-element.55.g_low, bf16[8,512,256]{2,1,0:T(8,128)(2,1)} %copy-done.13, f32[8,256,512]{2,1,0:T(8,128)} %get-tuple-element.56.ret, f32[8,256,512]{2,1,0:T(8,128)} %get-tuple-element.57.swi), custom_call_target="tpu_custom_call" | custom-call | flops 4294967296 | bytes 23068672 | tf_op jit(solution)/shard_map/gate_back/pallas_call | solution.py:788
  434.3 9.9 %bitcast_convert_fusion.4 = bf16[2048,512]{1,0:T(8,128)(2,1)} fusion(bf16[8,256,2048]{2,1,0:T(8,128)(2,1)} %fusion.5.nrm, bf16[8,256,512]{2,1,0:T(8,128)(2,1)} %get-tuple-element.59.gs), kind=kOutput, calls=%fused_computation.12 | convolution fusion | flops 4296015872 | bytes 12582912 | tf_op jit(solution)/shard_map/dot_general | solution.py:909
  445.8 8.1 %bitcast_convert_fusion.3 = bf16[512,2048]{1,0:T(8,128)(2,1)S(1)} fusion(bf16[8,256,512]{2,1,0:T(8,128)(2,1)S(1)} %copy-done.30, bf16[8,256,2048]{2,1,0:T(8,128)(2,1)} %get-tuple-element.55.g_low), kind=kOutput, calls=%fused_computation.11 | convolution fusion | flops 4296015872 | bytes 12582912 | tf_op jit(solution)/shard_map/dot_general | solution.py:909
  454.1 28.8 %all_to_all.54 = bf16[8,512,256]{2,1,0:T(8,128)(2,1)} all-to-all(bf16[8,512,256]{2,1,0:T(8,128)(2,1)S(1)} %bitcast.82), channel_id=1, replica_groups={{0,1,2,3,4,5,6,7},{8,9,10,11,12,13,14,15},{16,17,18,19,20,21,22,23},{24..., dimensions={0} | all-to-all | bytes 4194304 | tf_op jit(solution)/shard_map/all_to_all | solution.py:853
  483.0 14.5 %bitcast_convert_fusion = bf16[2048,1024]{1,0:T(8,128)(2,1)} fusion(bf16[8,256,2048]{2,1,0:T(8,128)(2,1)} %get-tuple-element.51.x, bf16[8,256,1024]{2,1,0:T(8,128)(2,1)} %hidden_back.1.a), kind=kOutput, calls=%fused_computation.8 | convolution fusion | flops 8592031744 | bytes 16777216 | tf_op jit(solution)/shard_map/dot_general | solution.py:909
  501.6 10.1 %scores_back.1.gqkv = bf16[8,256,1024]{2,1,0:T(8,128)(2,1)} custom-call(bf16[8,256,256]{2,1,0:T(8,128)(2,1)} %multiply_convert_fusion.sco, f32[8,256,256]{2,1,0:T(8,128)} %fusion.10.mask, bf16[8,256,256]{2,1,0:T(8,128)(2,1)} %pad_maximum_fusion.q, bf16[8,256,256]{2,1,0:T(8,128)(2,1)} %pad_maximum_fusion.1.k, bf16[8,256,512]{2,1,0:T(8,128)(2,1)} %get-tuple-element.48.v, ...), custom_call_target="tpu_custom_call" | custom-call | flops 1610612736 | bytes 16777216 | tf_op jit(solution)/shard_map/scores_back/pallas_call | solution.py:830
  511.8 14.1 %bitcast_convert_fusion.1 = bf16[2048,1024]{1,0:T(8,128)(2,1)} fusion(bf16[8,256,2048]{2,1,0:T(8,128)(2,1)} %fusion.5.nrm, bf16[8,256,1024]{2,1,0:T(8,128)(2,1)} %scores_back.1.gqkv), kind=kOutput, calls=%fused_computation.9 | convolution fusion | flops 8592031744 | bytes 16777216 | tf_op jit(solution)/shard_map/dot_general | solution.py:909
  527.5 9.1 %bitcast_convert_fusion.2 = bf16[512,2048]{1,0:T(8,128)(2,1)} fusion(bf16[8,256,512]{2,1,0:T(8,128)(2,1)S(1)} %copy-done.23, bf16[8,256,2048]{2,1,0:T(8,128)(2,1)} %copy-done.2), kind=kOutput, calls=%fused_computation.10 | convolution fusion | flops 4296015872 | bytes 12582912 | tf_op jit(solution)/shard_map/dot_general | solution.py:909
  536.7 13.9 %all_to_all.55.x = bf16[8,64,512]{2,1,0:T(8,128)(2,1)} all-to-all(bf16[8,64,512]{2,1,0:T(8,128)(2,1)} %bitcast.92), channel_id=1, replica_groups={{0,1,2,3,4,5,6,7},{8,9,10,11,12,13,14,15},{16,17,18,19,20,21,22,23},{24..., dimensions={0} | all-to-all | bytes 1048576 | tf_op jit(solution)/shard_map/all_to_all | solution.py:853
  550.6 13.8 %all_to_all.56.x = bf16[8,128,256]{2,1,0:T(8,128)(2,1)} all-to-all(bf16[8,128,256]{2,1,0:T(8,128)(2,1)} %bitcast.93), channel_id=1, replica_groups={{0,1,2,3,4,5,6,7},{8,9,10,11,12,13,14,15},{16,17,18,19,20,21,22,23},{24..., dimensions={0} | all-to-all | bytes 1048576 | tf_op jit(solution)/shard_map/all_to_all | solution.py:853
  564.4 46.4 %reduce-scatter.12.cloned.1.call-done = bf16[512,1024]{1,0:T(8,128)(2,1)} async-done(((bf16[2048,1024]{1,0:T(8,128)(2,1)}), bf16[512,1024]{1,0:T(8,128)(2,1)}) %reduce-scatter.12.cloned.1.call-update) | async-done | bytes 1048592 | tf_op jit(solution)/shard_map/reduce_scatter | solution.py:861
  616.4 91.2 %last_exchange.1 = (f32[256,2048]{1,0:T(8,128)}, f32[256,2048]{1,0:T(8,128)}, f32[8,512]{1,0:T(8,128)}) custom-call(bf16[8,256,1024]{2,1,0:T(8,128)(2,1)} %scores_back.1.gqkv, bf16[8,256,512]{2,1,0:T(8,128)(2,1)} %get-tuple-element.59.gs, bf16[2048,512]{1,0:T(8,128)(2,1)} %get-tuple-element.80.wqk, bf16[2048,1024]{1,0:T(8,128)(2,1)} %all-gather.5.cloned.1.call-done.wvs, ...), custom_call_target="tpu_custom_call" | custom-call | tf_op jit(solution)/shard_map/last_exchange/pallas_call | solution.py:738
  717.8 19.4 %reduce-scatter.14.cloned.1.call-done = bf16[128,2048]{1,0:T(8,128)(2,1)} async-done(((bf16[512,2048]{1,0:T(8,128)(2,1)}), bf16[128,2048]{1,0:T(8,128)(2,1)}) %reduce-scatter.14.cloned.1.call-update) | async-done | bytes 524304 | tf_op jit(solution)/shard_map/reduce_scatter | solution.py:861
  (148 shorter events, 83.9 us)
Async XLA Ops:
  7.2 18.8 %copy-start.1 = (bf16[256,2048]{1,0:T(8,128)(2,1)S(1)}, bf16[256,2048]{1,0:T(8,128)(2,1)}, u32[]{:S(2)}) copy-start(bf16[256,2048]{1,0:T(8,128)(2,1)} %tok.4) | copy-start | bytes 3145732
  7.2 156.9 %all-gather.7.cloned.1.call-start = ((), (), s32[]{:S(2)}) async-start(), calls=%async_computation.12 | async-start | bytes 5242880 | tf_op jit(solution)/shard_map/all_gather | solution.py:857
  10.3 15.6 %copy-start.31 = (s32[1,3]{1,0:T(1,128)S(1)}, s32[1,3]{1,0:T(1,128)}, u32[]{:S(2)}) copy-start(s32[1,3]{1,0:T(1,128)} %param.16) | copy-start | bytes 40
  10.3 15.6 %copy-start.26 = (bf16[64]{0:T(256)(128)(2,1)S(1)}, bf16[64]{0:T(256)(128)(2,1)}, u32[]{:S(2)}) copy-start(bf16[64]{0:T(256)(128)(2,1)} %param.25) | copy-start | bytes 388
  10.3 15.6 %copy-start.27 = (bf16[64]{0:T(256)(128)(2,1)S(1)}, bf16[64]{0:T(256)(128)(2,1)}, u32[]{:S(2)}) copy-start(bf16[64]{0:T(256)(128)(2,1)} %param.24) | copy-start | bytes 388
  10.3 15.6 %copy-start.28 = (bf16[64]{0:T(256)(128)(2,1)S(1)}, bf16[64]{0:T(256)(128)(2,1)}, u32[]{:S(2)}) copy-start(bf16[64]{0:T(256)(128)(2,1)} %param.18) | copy-start | bytes 388
  10.3 15.7 %copy-start.29 = (bf16[64]{0:T(256)(128)(2,1)S(1)}, bf16[64]{0:T(256)(128)(2,1)}, u32[]{:S(2)}) copy-start(bf16[64]{0:T(256)(128)(2,1)} %param.17) | copy-start | bytes 388
  10.3 60.8 %copy-start.7 = (bf16[64,4096]{1,0:T(8,128)(2,1)S(1)}, bf16[64,4096]{1,0:T(8,128)(2,1)}, u32[]{:S(2)}) copy-start(bf16[64,4096]{1,0:T(8,128)(2,1)} %wv) | copy-start | bytes 1572868
  10.3 60.8 %copy-start.8 = (bf16[64,4096]{1,0:T(8,128)(2,1)S(1)}, bf16[64,4096]{1,0:T(8,128)(2,1)}, u32[]{:S(2)}) copy-start(bf16[64,4096]{1,0:T(8,128)(2,1)} %ws.1) | copy-start | bytes 1572868
  25.8 170.3 %all-gather.5.cloned.1.call-start = ((), (), s32[]{:S(2)}) async-start(), calls=%async_computation.11 | async-start | bytes 5242880 | tf_op jit(solution)/shard_map/all_gather | solution.py:857
  26.0 60.2 %copy-start.24 = (bf16[64,4096]{1,0:T(8,128)(2,1)S(1)}, bf16[64,4096]{1,0:T(8,128)(2,1)}, u32[]{:S(2)}) copy-start(bf16[64,4096]{1,0:T(8,128)(2,1)} %param.26) | copy-start | bytes 1572868
  86.1 218.4 %all-gather.11.cloned.1.call-start = ((), (), s32[]{:S(2)}) async-start(), calls=%async_computation.14 | async-start | bytes 5242880 | tf_op jit(solution)/shard_map/all_gather | solution.py:857
  142.9 178.6 %all-gather.9.cloned.1.call-start = ((), (), s32[]{:S(2)}) async-start(), calls=%async_computation.13 | async-start | bytes 2621440 | tf_op jit(solution)/shard_map/all_gather | solution.py:857
  173.0 30.1 %all-to-all-start = ((bf16[8,512,256]{2,1,0:T(8,128)(2,1)}), bf16[8,512,256]{2,1,0:T(8,128)(2,1)S(1)}, u32[]{:S(2)}, u32[]{:S(2)}) async-start(bf16[8,512,256]{2,1,0:T(8,128)(2,1)} %bitcast.80), calls=%async_computation | async-start | bytes 4194304 | tf_op jit(solution)/shard_map/all_to_all | solution.py:853
  178.8 357.9 %reduce-scatter.8.cloned.1.call-start = ((), (), s32[]{:S(2)}) async-start(), calls=%async_computation.16 | async-start | bytes 2621440 | tf_op jit(solution)/shard_map/reduce_scatter | solution.py:861
  321.6 13.7 %copy-start.11 = (f32[2,2048]{1,0:T(2,128)S(1)}, f32[2,2048]{1,0:T(2,128)}, u32[]{:S(2)}) copy-start(f32[2,2048]{1,0:T(2,128)} %pad_maximum_fusion.3.vec) | copy-start | bytes 49156
  444.2 106.4 %reduce-scatter.10.cloned.1.call-start = ((), (), s32[]{:S(2)}) async-start(), calls=%async_computation.17 | async-start | bytes 2621440 | tf_op jit(solution)/shard_map/reduce_scatter | solution.py:861
  483.0 127.9 %reduce-scatter.12.cloned.1.call-start = ((), (), s32[]{:S(2)}) async-start(), calls=%async_computation.18 | async-start | bytes 5242880 | tf_op jit(solution)/shard_map/reduce_scatter | solution.py:861
  497.5 210.1 %reduce-scatter.6.cloned.1.call-start = ((), (), s32[]{:S(2)}) async-start(), calls=%async_computation.15 | async-start | bytes 5242880 | tf_op jit(solution)/shard_map/reduce_scatter | solution.py:861
  525.9 211.3 %reduce-scatter.14.cloned.1.call-start = ((), (), s32[]{:S(2)}) async-start(), calls=%async_computation.19 | async-start | bytes 2621440 | tf_op jit(solution)/shard_map/reduce_scatter | solution.py:861
  610.8 96.8 %all-to-all-start.5 = ((bf16[8,64,1024]{2,1,0:T(8,128)(2,1)}), bf16[8,64,1024]{2,1,0:T(8,128)(2,1)}, u32[]{:S(2)}, u32[]{:S(2)}) async-start(bf16[8,64,1024]{2,1,0:T(8,128)(2,1)} %bitcast.89), calls=%async_computation.9 | async-start | bytes 2097152 | tf_op jit(solution)/shard_map/all_to_all | solution.py:853
  707.7 36.5 %all-to-all-start.1 = ((bf16[8,64,1024]{2,1,0:T(8,128)(2,1)}), bf16[8,64,1024]{2,1,0:T(8,128)(2,1)S(1)}, u32[]{:S(2)}, u32[]{:S(2)}) async-start(bf16[8,64,1024]{2,1,0:T(8,128)(2,1)} %bitcast.88), calls=%async_computation.2 | async-start | bytes 2097152 | tf_op jit(solution)/shard_map/all_to_all | solution.py:853
  714.2 25.1 %copy-start.4 = (bf16[8,64,512]{2,1,0:T(8,128)(2,1)S(1)}, bf16[8,64,512]{2,1,0:T(8,128)(2,1)}, u32[]{:S(2)}) copy-start(bf16[8,64,512]{2,1,0:T(8,128)(2,1)} %all_to_all.55.x) | copy-start | bytes 1572868
  717.8 22.5 %copy-start.5 = (bf16[8,128,256]{2,1,0:T(8,128)(2,1)S(1)}, bf16[8,128,256]{2,1,0:T(8,128)(2,1)}, u32[]{:S(2)}) copy-start(bf16[8,128,256]{2,1,0:T(8,128)(2,1)} %all_to_all.56.x) | copy-start | bytes 1572868
  (20 other events, 35.4 us)
Sparse Core Ops, SparseCore 0:
  25.9 79.3 all-gather.6
  106.9 79.2 all-gather.4
  187.7 79.2 all-gather.10
  268.4 45.4 all-gather.8
  444.4 42.2 reduce-scatter.7
  488.8 42.8 reduce-scatter.9
  534.0 76.8 reduce-scatter.11
  613.1 78.1 reduce-scatter.5
  693.6 43.5 reduce-scatter.13

commit v5 on v4

--- a/solution.py
+++ b/solution.py
@@ -19,6 +19,7 @@
 bf = jnp.bfloat16
 f32 = jnp.float32
 SDS = jax.ShapeDtypeStruct
+ALL_VMEM = 67043328
 
 
 def place():
@@ -104,13 +105,6 @@
         self.keep.wait()
 
 
-def gather_blocks(own, out, sems, base, local, peer):
-    gather = Gather(own, out, 0, own.shape[0], sems, base, local, peer)
-    gather.start()
-    gather.forward()
-    gather.finish()
-
-
 def send_columns(src, out, cols, at, sems, base, local, t, peer, rows=None):
     copies = []
     rows = slice(None) if rows is None else rows
@@ -139,11 +133,12 @@
         keep.wait()
 
 
-def exchange_call(kernel, outs, args, sems, locals_, cid):
+def exchange_call(kernel, outs, args, sems, locals_, cid, specs=None, aliases=None, vmem=12 << 20):
     return pl.pallas_call(
         kernel,
         out_shape=outs,
-        in_specs=[VMEM] * len(args),
+        in_specs=specs or [VMEM] * len(args),
+        input_output_aliases=aliases or {},
         out_specs=tuple(ANY for _ in outs),
         scratch_shapes=[
             pltpu.SemaphoreType.DMA((sems,)),
@@ -151,7 +146,7 @@
             pltpu.SemaphoreType.DMA((locals_,)),
         ],
         compiler_params=pltpu.CompilerParams(
-            collective_id=cid, has_side_effects=True, vmem_limit_bytes=12 << 20
+            collective_id=cid, has_side_effects=True, vmem_limit_bytes=vmem
         ),
     )(*args)
 
@@ -177,23 +172,44 @@
     return exchange_call(first_kernel, outs, (wq, wk, wo), 28, 4, cid)[0]
 
 
-def second_kernel(n, tok, vec, tok_out, vec_out, ssem, rsem, local):
+def send_along(n, src, out, sems, base, parity):
+    dp = n // TP
+    me = lax.axis_index(AXIS)
+    g = lax.div(me, TP)
+    copies = []
+    for j in range(1, dp):
+        if j % 2 == parity:
+            copy = remote(src, out.at[g], sems, base + j, lax.rem(me + TP * j, n))
+            copy.start()
+            copies.append(copy)
+    return copies
+
+
+def others_along(n):
+    me = lax.axis_index(AXIS)
+    return [lax.rem(me + TP * j, n) for j in range(1, n // TP)]
+
+
+def second_kernel(n, tok, vec, wd, tok_out, vec_out, wd_out, ssem, rsem, local):
     dp = n // TP
     me, peer = place()
     t, g = lax.rem(me, TP), lax.div(me, TP)
-    others = [lax.rem(me + TP * j, n) for j in range(1, dp)]
+    others = others_along(n)
     greet([peer(k) for k in range(1, TP)] + others)
     sems = (ssem, rsem)
     base = GATHER_SEMS
     far = []
     keep = pltpu.make_async_copy(vec, vec_out.at[g, t], local.at[1])
     keep.start()
+    mine = pltpu.make_async_copy(wd, wd_out.at[g], local.at[2])
+    mine.start()
     for j, dev in enumerate(others):
         copy = remote(vec, vec_out.at[g, t], sems, base + TP + j, dev)
         copy.start()
         far.append(copy)
     gather = Gather(tok, tok_out, 0, tok.shape[0], sems, 0, local.at[0], peer)
     gather.start()
+    along = send_along(n, wd, wd_out, sems, base + TP + dp, 1)
     for copy in far:
         copy.wait()
     keep.wait()
@@ -204,18 +220,24 @@
         near.append(copy)
     gather.forward()
     gather.finish()
-    for copy in near:
+    for copy in near + along:
         copy.wait()
-
-
-def second_exchange(n, tok, vec, cid):
-    outs = (SDS((TP,) + tok.shape, bf), SDS((n // TP, TP) + vec.shape, f32))
+    mine.wait()
+
+
+def second_exchange(n, tok, vec, wd, cid):
+    dp = n // TP
+    outs = (
+        SDS((TP,) + tok.shape, bf),
+        SDS((dp, TP) + vec.shape, f32),
+        SDS((dp,) + wd.shape, bf),
+    )
     kernel = functools.partial(second_kernel, n)
-    sems = GATHER_SEMS + TP + n // TP
-    return exchange_call(kernel, outs, (tok, vec), sems, 2, cid)
-
-
-def third_kernel(wv, ws, out, ssem, rsem, local):
+    sems = GATHER_SEMS + TP + 2 * dp
+    return exchange_call(kernel, outs, (tok, vec, wd), sems, 3, cid, vmem=ALL_VMEM)
+
+
+def third_kernel(wv, ws, gu, out, gu_out, ssem, rsem, local):
     me, peer = place()
     t = lax.rem(me, TP)
     greet([peer(k) for k in range(1, TP)])
@@ -224,27 +246,65 @@
     finish([
         send_columns(wv, out, cols, 0, sems, 0, local.at[0], t, peer),
         send_columns(ws, out, cols, cols, sems, 7, local.at[1], t, peer),
+        send_columns(gu, gu_out, gu.shape[2], 0, sems, 14, local.at[2], t, peer),
     ])
 
 
-def third_exchange(wv, ws, cid):
-    outs = (SDS((TP, wv.shape[0], 2 * wv.shape[1] // TP), bf),)
-    return exchange_call(third_kernel, outs, (wv, ws), 14, 2, cid)[0]
-
-
-def fourth_kernel(gu, cot, gu_out, cot_out, ssem, rsem, local):
+def third_exchange(wv, ws, gu, cid):
+    outs = (SDS((TP, wv.shape[0], 2 * wv.shape[1] // TP), bf), SDS(gu.shape, bf))
+    return exchange_call(third_kernel, outs, (wv, ws, gu), 21, 3, cid)
+
+
+def fourth_kernel(n, at, cot, qko, wd, _, cot_out, o_out, wd_out, ssem, rsem, local):
     me, peer = place()
     t = lax.rem(me, TP)
-    greet([peer(k) for k in range(1, TP)])
+    others = others_along(n)
+    greet([peer(k) for k in range(1, TP)] + others)
     sems = (ssem, rsem)
-    parts = [send_columns(gu, gu_out, gu.shape[2], 0, sems, 0, local.at[0], t, peer)]
-    gather_blocks(cot, cot_out, sems, 7, local.at[1], peer)
-    finish(parts)
-
-
-def fourth_exchange(gu, cot, cid):
-    outs = (SDS(gu.shape, bf), SDS((TP,) + cot.shape, bf))
-    return exchange_call(fourth_kernel, outs, (gu, cot), 7 + GATHER_SEMS, 2, cid)
+    share, cols = n // TP, o_out.shape[4]
+    base = GATHER_SEMS + 2 * TP
+    gather = Gather(cot, cot_out, 0, cot.shape[0], sems, 0, local.at[0], peer)
+    gather.start()
+    along = send_along(n, wd, wd_out, sems, base, 0)
+    copies, keeps = [], []
+
+    def part(p, half):
+        return qko.at[pl.ds(p * share, share), :, pl.ds(at + half * cols, cols)]
+
+    for half in (0, 1):
+        for k in range(1, TP):
+            dev = peer(k)
+            copy = remote(
+                part(lax.rem(dev, TP), half), o_out.at[t, :, half], sems,
+                GATHER_SEMS + half * TP + k, dev,
+            )
+            copy.start()
+            copies.append(copy)
+        keep = pltpu.make_async_copy(part(t, half), o_out.at[t, :, half], local.at[1 + half])
+        keep.start()
+        keeps.append(keep)
+    gather.forward()
+    gather.finish()
+    for copy in copies + along:
+        copy.wait()
+    for keep in keeps:
+        keep.wait()
+
+
+def fourth_exchange(n, cot, qko, at, wd, wd_all, cid):
+    _, shard, width = qko.shape
+    cols = (width - at) // 2
+    outs = (
+        SDS((TP,) + cot.shape, bf),
+        SDS((TP, n // TP, 2, shard, cols), bf),
+        SDS(wd_all.shape, bf),
+    )
+    kernel = functools.partial(fourth_kernel, n, at)
+    return exchange_call(
+        kernel, outs, (cot, qko, wd, wd_all),
+        GATHER_SEMS + 2 * TP + n // TP, 3, cid,
+        specs=[VMEM, ANY, VMEM, ANY], aliases={3: 2}, vmem=ALL_VMEM,
+    )
 
 
 REDUCE_SEMS = 16
@@ -514,6 +574,74 @@
     )(nrm, wvs, sco, w, tok, vec)
 
 
+def norm_kernel(x, gain, bias, out):
+    step = 32
+
+    @pl.loop(0, x.shape[1] // step)
+    def _(j):
+        at = pl.ds(pl.multiple_of(j * step, step), step)
+        value = x[0, at, :].astype(f32)
+        centred = value - jnp.mean(value, axis=-1, keepdims=True)
+        spread = jnp.mean(centred * centred, axis=-1, keepdims=True)
+        out[0, at, :] = (centred * lax.rsqrt(spread + 1e-05) * gain[...] + bias[...]).astype(bf)
+
+
+def norm_rows(x, gain, bias):
+    _, r, d = x.shape
+    row = pl.BlockSpec((1, r, d), lambda k: (k, 0, 0))
+    vec = pl.BlockSpec((1, d), lambda k: (0, 0))
+    return pl.pallas_call(
+        norm_kernel,
+        grid=(TP,),
+        out_shape=SDS(x.shape, bf),
+        in_specs=[row, vec, vec],
+        out_specs=row,
+        compiler_params=pltpu.CompilerParams(vmem_limit_bytes=56 << 20),
+        cost_estimate=pl.CostEstimate(
+            flops=8 * x.size, bytes_accessed=4 * x.size, transcendentals=0
+        ),
+        name="norm_rows",
+    )(x, gain, bias)
+
+
+def scores_kernel(x, w, cosine, sine, mask, q_out, k_out, sco, w_out):
+    two, r, kh = q_out.shape
+    half = kh // 2
+    w_out[...] = w[...]
+    rows = x[...].reshape(two * r, x.shape[2])
+    for j, out in enumerate((q_out, k_out)):
+        y = jnp.dot(rows, w[:, j * kh : (j + 1) * kh], preferred_element_type=f32)
+        for i in range(two):
+            u, v = y[i * r : (i + 1) * r, :half], y[i * r : (i + 1) * r, half:]
+            out[i, :, :half] = (u * cosine[i] - v * sine[i]).astype(bf)
+            out[i, :, half:] = (v * cosine[i] + u * sine[i]).astype(bf)
+    for i in range(two):
+        plain = lax.dot_general(
+            q_out[i], k_out[i], (((1,), (1,)), ((), ())), preferred_element_type=f32
+        )
+        sco[i] = (plain * mask[i]).astype(bf)
+
+
+def rotated_and_scores(x, qko, cosine, sine, mask):
+    _, r, d = x.shape
+    pair = lambda k: (k, 0, 0)
+    square = pl.BlockSpec((2, r, KH), pair)
+    angle = pl.BlockSpec((2, r, KH // 2), pair)
+    weights = pl.BlockSpec((d, 2 * KH), lambda k: (0, 0))
+    return pl.pallas_call(
+        scores_kernel,
+        grid=(TP // 2,),
+        out_shape=(SDS((TP, r, KH), bf), SDS((TP, r, KH), bf), SDS(mask.shape, bf), SDS((d, 2 * KH), bf)),
+        in_specs=[pl.BlockSpec((2, r, d), pair), weights, angle, angle, pl.BlockSpec((2, r, r), pair)],
+        out_specs=(square, square, pl.BlockSpec((2, r, r), pair), weights),
+        compiler_params=pltpu.CompilerParams(vmem_limit_bytes=56 << 20),
+        cost_estimate=pl.CostEstimate(
+            flops=4 * TP * r * d * KH, bytes_accessed=16 << 20, transcendentals=0
+        ),
+        name="rotated_and_scores",
+    )(x, qko, cosine, sine, mask)
+
+
 def hidden_kernel(x, gu, hid, act_out, slope_out):
     width = hid.shape[2]
     step = 256
@@ -522,26 +650,28 @@
     def _(j):
         at = pl.ds(pl.multiple_of(j * step, step), step)
         behind = pl.ds(pl.multiple_of(j * step + width, step), step)
-        first = jnp.dot(x[0], gu[:, at], preferred_element_type=f32)
-        second = jnp.dot(x[0], gu[:, behind], preferred_element_type=f32)
+        rows = x[...].reshape(-1, x.shape[2])
+        first = jnp.dot(rows, gu[:, at], preferred_element_type=f32)
+        second = jnp.dot(rows, gu[:, behind], preferred_element_type=f32)
         share = 0.5 * (1.0 + lax.erf(first * math.sqrt(0.5)))
         act = first * share
         slope = share + first * (jnp.exp(-0.5 * first * first) * (1.0 / math.sqrt(2.0 * math.pi)))
-        hid[0, :, at] = (act * second).astype(bf)
-        act_out[0, :, at] = act
-        slope_out[0, :, at] = slope * second
+        block = hid.shape[:2] + (step,)
+        hid[:, :, at] = (act * second).astype(bf).reshape(block)
+        act_out[:, :, at] = act.reshape(block)
+        slope_out[:, :, at] = (slope * second).reshape(block)
 
 
 def hidden_units(x, gu):
     _, r, d = x.shape
     width = gu.shape[1] // 2
-    row = pl.BlockSpec((1, r, width), lambda k: (k, 0, 0))
+    row = pl.BlockSpec((2, r, width), lambda k: (k, 0, 0))
     return pl.pallas_call(
         hidden_kernel,
-        grid=(TP,),
+        grid=(TP // 2,),
         out_shape=tuple(SDS((TP, r, width), t) for t in (bf, f32, f32)),
         in_specs=[
-            pl.BlockSpec((1, r, d), lambda k: (k, 0, 0)),
+            pl.BlockSpec((2, r, d), lambda k: (k, 0, 0)),
             pl.BlockSpec(gu.shape, lambda k: (0, 0)),
         ],
         out_specs=(row, row, row),
@@ -562,27 +692,28 @@
         at = pl.ds(pl.multiple_of(j * step, step), step)
         behind = pl.ds(pl.multiple_of(j * step + width, step), step)
         grad = lax.dot_general(
-            cot[0], down[at, :], (((1,), (1,)), ((), ())), preferred_element_type=f32
-        )
-        out[0, :, at] = (grad * slope[0, :, at]).astype(bf)
-        out[0, :, behind] = (grad * act[0, :, at]).astype(bf)
+            cot[...].reshape(-1, cot.shape[2]), down[at, :], (((1,), (1,)), ((), ())),
+            preferred_element_type=f32,
+        ).reshape(act.shape[:2] + (step,))
+        out[:, :, at] = (grad * slope[:, :, at]).astype(bf)
+        out[:, :, behind] = (grad * act[:, :, at]).astype(bf)
 
 
 def hidden_back(cot, down, act, slope):
     _, r, d = cot.shape
     width = act.shape[2]
-    row = pl.BlockSpec((1, r, width), lambda k: (k, 0, 0))
+    row = pl.BlockSpec((2, r, width), lambda k: (k, 0, 0))
     return pl.pallas_call(
         hidden_back_kernel,
-        grid=(TP,),
+        grid=(TP // 2,),
         out_shape=SDS((TP, r, 2 * width), bf),
         in_specs=[
-            pl.BlockSpec((1, r, d), lambda k: (k, 0, 0)),
+            pl.BlockSpec((2, r, d), lambda k: (k, 0, 0)),
             pl.BlockSpec(down.shape, lambda k: (0, 0)),
             row,
             row,
         ],
-        out_specs=pl.BlockSpec((1, r, 2 * width), lambda k: (k, 0, 0)),
+        out_specs=pl.BlockSpec((2, r, 2 * width), lambda k: (k, 0, 0)),
         compiler_params=pltpu.CompilerParams(vmem_limit_bytes=56 << 20),
         cost_estimate=pl.CostEstimate(
             flops=2 * TP * r * d * width, bytes_accessed=24 << 20, transcendentals=0
@@ -752,7 +883,7 @@
             pltpu.SemaphoreType.DMA((count,)),
         ],
         compiler_params=pltpu.CompilerParams(
-            collective_id=cid, has_side_effects=True, vmem_limit_bytes=67043328
+            collective_id=cid, has_side_effects=True, vmem_limit_bytes=ALL_VMEM
         ),
         name="last_exchange",
     )(gqkv, gs, wqk, wvs, a2, w2, tok, gmid, gain, sums2)
@@ -863,13 +994,6 @@
     )
 
 
-def layer_norm(value, gain, bias):
-    center = jnp.mean(value, axis=-1, keepdims=True)
-    centred = value - center
-    spread = jnp.mean(centred * centred, axis=-1, keepdims=True)
-    return centred * lax.rsqrt(spread + 1e-05) * gain + bias
-
-
 def seq_positions(lengths, rows):
     ends = jnp.cumsum(lengths, axis=1)
     starts = ends - lengths
@@ -887,12 +1011,6 @@
     return jnp.cos(angle), jnp.sin(angle)
 
 
-def rotate(value, cosine, sine):
-    half = KH // 2
-    u, w = value[..., :half], value[..., half:]
-    return jnp.concatenate([u * cosine - w * sine, w * cosine + u * sine], axis=-1)
-
-
 def decay_mask(segment, offset, head):
     diff = offset[:, :, None] - offset[:, None, :]
     valid = (segment[:, :, None] == segment[:, None, :]) & (diff >= 0)
@@ -901,16 +1019,8 @@
     return jnp.where(valid, jnp.exp(log * steps), 0.0) / math.sqrt(KH)
 
 
-def dot(a, b):
-    return lax.dot_general(a, b, (((1,), (0,)), ((), ())), preferred_element_type=f32)
-
-
 def dot_tn(a, b):
     return lax.dot_general(a, b, (((0,), (0,)), ((), ())), preferred_element_type=f32)
-
-
-def bmm(eq, a, b):
-    return jnp.einsum(eq, a, b, preferred_element_type=f32)
 
 
 def col_blocks(w):
@@ -970,21 +1080,15 @@
     vec = jnp.pad(vec, ((0, 3), (0, 128 - shard)))
     qko_blk = first_exchange(wq, wk, wo, 1)
     qko = dp_gather(qko_blk.reshape(TP * shard, 4 * KH), n)
-    tok_all, vec_all = second_exchange(n, after(tokens, qko_blk), vec, 2)
-    vs_blk = third_exchange(after(wv, tok_all), ws, 3)
+    tok_all, vec_all, wd_all = second_exchange(n, after(tokens, qko_blk), vec, wd, 2)
+    gu_in = jnp.concatenate([ff_blocks(wg), ff_blocks(wu)], axis=2)
+    vs_blk, gu_blk = third_exchange(after(wv, tok_all), ws, gu_in, 3)
     vs = dp_gather(vs_blk.reshape(TP * shard, 2 * VH), n)
-    gu_in = jnp.concatenate([ff_blocks(wg), ff_blocks(wu)], axis=2)
-    gu_blk, cot_all = fourth_exchange(gu_in, after(cot, vs_blk), 4)
     gu = dp_gather(gu_blk.reshape(TP * shard, 2 * dp * unit), n)
-    down = dp_gather(wd, n)
     gain1f, bias1f, gain2f, bias2f = (
         vec_all[:, :, i, :shard].reshape(1, d) for i in range(4)
     )
     vec2 = jnp.concatenate([gain2f, bias2f], axis=0)
-    qk = qko[:, : 2 * KH]
-    out = qko[:, 2 * KH :].reshape(n, shard, 2, d // TP).transpose(0, 2, 1, 3)
-    out_blk = plane_a2a(out.reshape(TP * VH, d // TP), n).reshape(TP, VH, d // TP)
-
     mine = lax.dynamic_slice_in_dim(vec_all, lax.div(me, TP), 1, 0)[0, :, 4, :3]
     order = jnp.arange(TP, dtype=jnp.int32)
     pick = (order[None, :] == (order[:, None] ^ head)).astype(f32)
@@ -993,18 +1097,19 @@
     cosine, sine = rotary_tables(offset)
     mask = decay_mask(segment, offset, head)
 
-    normed = layer_norm(tok_all.reshape(TP * rows, d).astype(f32), gain1f, bias1f).astype(bf)
-    qk_out = dot(normed, qk).reshape(TP, rows, 2 * KH)
-    query, key = qk_out[..., :KH], qk_out[..., KH:]
-    q_rot = rotate(query, cosine, sine).astype(bf)
-    k_rot = rotate(key, cosine, sine).astype(bf)
-    plain = bmm("btd,bsd->bts", q_rot, k_rot)
-    scores = (plain * mask).astype(bf)
+    normed = norm_rows(tok_all, gain1f, bias1f)
+    q_rot, k_rot, scores, qk = rotated_and_scores(normed, qko, cosine, sine, mask)
+    cot_all, out_blk, wd_all = fourth_exchange(
+        n, after(cot, scores), qko.reshape(n, shard, 4 * KH), 2 * KH, wd, wd_all, 4
+    )
+    out_blk = out_blk.reshape(TP, VH, d // TP)
+    down = wd_all.reshape(dp * wd.shape[0], d)
     v_low, mixed, retained, swish_in, middle, normed2 = forward_exchange(
-        normed.reshape(TP, rows, d), vs, scores, out_blk, tokens, vec2, 5
+        normed, vs, scores, out_blk, tokens, vec2, 5
     )
     hidden, act, slope = hidden_units(normed2, gu)
     normed2 = normed2.reshape(TP * rows, d)
+    normed = normed.reshape(TP * rows, d)
     down_grad = dot_tn(hidden.reshape(TP * rows, dp * unit), cot_all.reshape(TP * rows, d)).astype(bf)
     g_down = dp_reduce(down_grad, n)
 

time: 764 us -> 783 us (1.025)
  Pallas kernels: 460 us -> 521 us
  other arithmetic: 35.6 us -> 15.4 us
  local copies, waits for them, and re-layouts: 31 us -> 14.5 us
  waiting for transfers between devices: 73.4 us -> 88 us
  matrix products: 65.8 us -> 55.5 us
    pallas_call x6 -> x8, Pallas kernels: 154 us -> 215 us  [the longest x4 158 us: exchange_call(): pl.pallas_call(kernel, out_shape=outs, in_specs=specs or [VMEM] * len(arg...]
    all_gather x4 -> x3, waiting for transfers between devices: 0.03 us -> 13.3 us  [dp_gather(): lax.all_gather(x, AXIS, axis=0, tiled=True, axis_index_groups=dp_groups(n))]
    unnamed x67 -> x45, local copies, waits for them, and re-layouts: 18.6 us -> 8.24 us
    reduce_sum x2 -> x0, other arithmetic: 10.3 us -> none  [the longest x1 5.72 us: layer_norm(): spread = jnp.mean(centred * centred, axis=-1, keepdims=True)]
    dot_general x2 -> x0, matrix products: 10 us -> none  [the longest x1 7.56 us: dot(): lax.dot_general(a, b, (((1,), (0,)), ((), ())), preferred_element_type=f32)]
    convert_element_type x2 -> x0, other arithmetic: 8.6 us -> none  [the longest x1 8.59 us: on_device(): layer_norm(tok_all.reshape(TP * rows, d).astype(f32), gain1f, bias1f)]
    reduce_scatter x5, waiting for transfers between devices: 65.8 us -> 73.9 us  [dp_reduce(): lax.psum_scatter(x, AXIS, scatter_dimension=0, tiled=True, axis_index_gro...]
    all_to_all x3 -> x2, starting transfers between devices: 16 us -> 10.3 us  [plane_a2a(): lax.all_to_all(x, AXIS, 0, 0, axis_index_groups=tp_groups(n), tiled=True)]
  transfers between devices with their start and end apart: 12 -> 10, of which waited for: 3 -> 3; matrix products, arithmetic and copies ran while one was open for 14% -> 9% of each run, Pallas kernels for 44% -> 49%
where the time goes in v5:
time: 783 us; the launch traced here: 776 us
  Pallas kernels  521 us (67%)
  waiting for transfers between devices  88 us (11%)
  blocking collectives  56.4 us (7%)
  matrix products  55.5 us (7%)
  other arithmetic  15.4 us (2%)
  between operations  14.9 us (2%)
  local copies, waits for them, and re-layouts  14.5 us (2%)
  starting transfers between devices  10.6 us (1%)
    pallas_call x4, Pallas kernels, exchange_call(): pl.pallas_call(kernel, out_shape=outs, in_specs=specs or [VMEM] * len(arg...  158 us
    pallas_call x1, Pallas kernels, forward_exchange(): pl.pallas_call(forward_kernel, out_shape=tuple((SDS(*b) for b in blocks))...  100 us
    pallas_call x1, Pallas kernels, last_exchange(): pl.pallas_call(functools.partial(last_kernel, n), out_shape=(SDS((r, c),...  91.2 us
    pallas_call x1, Pallas kernels, backward_exchange(): pl.pallas_call(backward_kernel, out_shape=(SDS((r, c), f32), SDS((TP, r,...  84.8 us
    reduce_scatter x5, waiting for transfers between devices, dp_reduce(): lax.psum_scatter(x, AXIS, scatter_dimension=0, tiled=True, axis_index_gro...  73.9 us
    all_to_all x3, blocking collectives, plane_a2a(): lax.all_to_all(x, AXIS, 0, 0, axis_index_groups=tp_groups(n), tiled=True)  56.4 us
    dot_general x5, matrix products, dot_tn(): lax.dot_general(a, b, (((0,), (0,)), ((), ())), preferred_element_type=f32)  55.5 us
    pallas_call x1, Pallas kernels, norm_rows(): pl.pallas_call(norm_kernel, grid=(TP,), out_shape=SDS(x.shape, bf), in_sp...  18.2 us
  transfers between devices with their start and end apart: 10, of which 3 were waited for; matrix products, arithmetic and copies ran while one was open for 9% of the time, Pallas kernels for 49%

profile of v5, /device:TPU:14, one launch (start us, length us, event | category | flops | bytes accessed | tf_op | source)
XLA Modules:
  0.0 776.2 jit_solution(13362995263423337655)
XLA Ops:
  10.2 15.4 %shard_map.254 = bf16[8,64,1024]{2,1,0:T(8,128)(2,1)} custom-call(bf16[64,2048]{1,0:T(8,128)(2,1)S(1)} %copy-done.6, bf16[64,2048]{1,0:T(8,128)(2,1)S(1)} %copy-done.7, bf16[128,2048]{1,0:T(8,128)(2,1)S(1)} %copy-done.3), custom_call_target="tpu_custom_call" | custom-call | tf_op jit(solution)/shard_map/pallas_call | solution.py:137
  29.1 51.4 %shard_map.255 = (bf16[8,256,2048]{2,1,0:T(8,128)(2,1)}, f32[4,8,8,128]{3,2,1,0:T(8,128)}, bf16[4,128,2048]{2,1,0:T(8,128)(2,1)}) custom-call(bf16[256,2048]{1,0:T(8,128)(2,1)} %tok.4, f32[8,128]{1,0:T(8,128)} %pad.9.vec, bf16[128,2048]{1,0:T(8,128)(2,1)} %wd.3), custom_call_target="tpu_custom_call" | custom-call | tf_op jit(solution)/shard_map/pallas_call | solution.py:137
  82.0 26.4 %shard_map.256 = (bf16[8,64,1024]{2,1,0:T(8,128)(2,1)}, bf16[8,64,1024]{2,1,0:T(8,128)(2,1)}) custom-call(bf16[64,4096]{1,0:T(8,128)(2,1)S(1)} %copy-done.4, bf16[64,4096]{1,0:T(8,128)(2,1)S(1)} %copy-done.5, bf16[8,64,1024]{2,1,0:T(8,128)(2,1)S(1)} %pad_maximum_fusion.gu), custom_call_target="tpu_custom_call" | custom-call | tf_op jit(solution)/shard_map/pallas_call | solution.py:137
  111.4 18.2 %norm_rows.1.x.nrm = bf16[8,256,2048]{2,1,0:T(8,128)(2,1)} custom-call(bf16[8,256,2048]{2,1,0:T(8,128)(2,1)} %get-tuple-element.52.x, f32[1,2048]{1,0:T(1,128)} %reshape_squeeze.12.gain, f32[1,2048]{1,0:T(1,128)} %reshape_squeeze.13.bias), custom_call_target="tpu_custom_call" | custom-call | flops 33554432 | bytes 16777216 | tf_op jit(solution)/shard_map/norm_rows/pallas_call | solution.py:593
  137.7 10.9 %rotated_and_scores.1 = (bf16[8,256,256]{2,1,0:T(8,128)(2,1)}, bf16[8,256,256]{2,1,0:T(8,128)(2,1)}, bf16[8,256,256]{2,1,0:T(8,128)(2,1)}, bf16[2048,512]{1,0:T(8,128)(2,1)}) custom-call(bf16[8,256,2048]{2,1,0:T(8,128)(2,1)} %norm_rows.1.x.nrm, bf16[2048,1024]{1,0:T(8,128)(2,1)} %all-gather.6.cloned.1.call-done.w, f32[8,256,128]{2,1,0:T(8,128)} %get-tuple-element.93.cosine, ...), custom_call_target="tpu_custom_call" | custom-call | flops 4294967296 | bytes 16777216 | tf_op jit(solution)/shard_map/rotated_and_scores/pallas_call | solution.py:631
  148.6 65.0 %shard_map.257 = (bf16[8,256,2048]{2,1,0:T(8,128)(2,1)}, bf16[8,4,2,64,256]{4,3,2,1,0:T(8,128)(2,1)}, bf16[4,128,2048]{2,1,0:T(8,128)(2,1)}) custom-call(bf16[256,2048]{1,0:T(8,128)(2,1)} %cot.2, bf16[32,64,1024]{2,1,0:T(8,128)(2,1)} %bitcast.77, bf16[128,2048]{1,0:T(8,128)(2,1)} %wd.3, ...), custom_call_target="tpu_custom_call", output_to_operand_aliasing={{2}: (3, {})} | custom-call | tf_op jit(solution)/shard_map/pallas_call | solution.py:137
  213.6 13.3 %all-gather.4.cloned.1.call-done.wvs = bf16[2048,1024]{1,0:T(8,128)(2,1)} async-done(((bf16[512,1024]{1,0:T(8,128)(2,1)}), bf16[2048,1024]{1,0:T(8,128)(2,1)}) %all-gather.4.cloned.1.call-update) | async-done | bytes 4194320 | tf_op jit(solution)/shard_map/all_gather | solution.py:988
  226.8 100.0 %forward_exchange.1 = (bf16[8,256,512]{2,1,0:T(8,128)(2,1)}, bf16[8,256,512]{2,1,0:T(8,128)(2,1)}, f32[8,256,512]{2,1,0:T(8,128)}, f32[8,256,512]{2,1,0:T(8,128)...) custom-call(bf16[8,256,2048]{2,1,0:T(8,128)(2,1)} %norm_rows.1.x.nrm, ...), custom_call_target="tpu_custom_call" | custom-call | tf_op jit(solution)/shard_map/forward_exchange/pallas_call | solution.py:557
  326.9 15.7 %hidden_units.1 = (bf16[8,256,512]{2,1,0:T(8,128)(2,1)}, f32[8,256,512]{2,1,0:T(8,128)}, f32[8,256,512]{2,1,0:T(8,128)}) custom-call(bf16[8,256,2048]{2,1,0:T(8,128)(2,1)} %get-tuple-element.66.x, bf16[2048,1024]{1,0:T(8,128)(2,1)} %all-gather.8.cloned.1.call-done.gu.w), custom_call_target="tpu_custom_call" | custom-call | flops 8589934592 | bytes 25165824 | tf_op jit(solution)/shard_map/hidden_units/pallas_call | solution.py:669
  342.6 11.8 %hidden_back.1.a = bf16[8,256,1024]{2,1,0:T(8,128)(2,1)} custom-call(bf16[8,256,2048]{2,1,0:T(8,128)(2,1)} %get-tuple-element.64.cot, bf16[512,2048]{1,0:T(8,128)(2,1)} %bitcast.75, f32[8,256,512]{2,1,0:T(8,128)} %get-tuple-element.68.act, f32[8,256,512]{2,1,0:T(8,128)} %get-tuple-element.69.slope), custom_call_target="tpu_custom_call" | custom-call | flops 4294967296 | bytes 25165824 | tf_op jit(solution)/shard_map/hidden_back/pallas_call | solution.py:706
  354.4 84.8 %backward_exchange.1 = (f32[256,2048]{1,0:T(8,128)}, bf16[8,256,2048]{2,1,0:T(8,128)(2,1)}, f32[2,2048]{1,0:T(2,128)S(1)}) custom-call(bf16[8,256,1024]{2,1,0:T(8,128)(2,1)} %hidden_back.1.a, bf16[2048,1024]{1,0:T(8,128)(2,1)} %all-gather.8.cloned.1.call-done.gu.w, f32[256,2048]{1,0:T(8,128)} %get-tuple-element.60.mid, bf16[256,2048]{1,0:T(8,128)(2,1)S(1)} %copy-done, ...), custom_call_target="tpu_custom_call" | custom-call | tf_op jit(solution)/shard_map/backward_exchange/pallas_call | solution.py:758
  439.8 13.7 %gate_back.1 = (bf16[8,256,512]{2,1,0:T(8,128)(2,1)}, bf16[8,256,512]{2,1,0:T(8,128)(2,1)}) custom-call(bf16[8,256,2048]{2,1,0:T(8,128)(2,1)} %get-tuple-element.70.g_low, bf16[8,512,256]{2,1,0:T(8,128)(2,1)} %bitcast.79, f32[8,256,512]{2,1,0:T(8,128)} %get-tuple-element.71.ret, f32[8,256,512]{2,1,0:T(8,128)} %get-tuple-element.72.swi), custom_call_target="tpu_custom_call" | custom-call | flops 4294967296 | bytes 23068672 | tf_op jit(solution)/shard_map/gate_back/pallas_call | solution.py:919
  453.5 9.9 %bitcast_convert_fusion.4 = bf16[2048,512]{1,0:T(8,128)(2,1)} fusion(bf16[8,256,2048]{2,1,0:T(8,128)(2,1)} %norm_rows.1.x.nrm, bf16[8,256,512]{2,1,0:T(8,128)(2,1)} %get-tuple-element.74.gs), kind=kOutput, calls=%fused_computation.4 | convolution fusion | flops 4296015872 | bytes 12582912 | tf_op jit(solution)/shard_map/dot_general | solution.py:1023
  465.0 8.1 %bitcast_convert_fusion.3 = bf16[512,2048]{1,0:T(8,128)(2,1)S(1)} fusion(bf16[8,256,512]{2,1,0:T(8,128)(2,1)S(1)} %copy-done.19, bf16[8,256,2048]{2,1,0:T(8,128)(2,1)} %get-tuple-element.70.g_low), kind=kOutput, calls=%fused_computation.3 | convolution fusion | flops 4296015872 | bytes 12582912 | tf_op jit(solution)/shard_map/dot_general | solution.py:1023
  473.2 28.8 %all_to_all.45 = bf16[8,512,256]{2,1,0:T(8,128)(2,1)} all-to-all(bf16[8,512,256]{2,1,0:T(8,128)(2,1)S(1)} %bitcast.81), channel_id=1, replica_groups={{0,1,2,3,4,5,6,7},{8,9,10,11,12,13,14,15},{16,17,18,19,20,21,22,23},{24..., dimensions={0} | all-to-all | bytes 4194304 | tf_op jit(solution)/shard_map/all_to_all | solution.py:984
  502.2 14.2 %bitcast_convert_fusion = bf16[2048,1024]{1,0:T(8,128)(2,1)} fusion(bf16[8,256,2048]{2,1,0:T(8,128)(2,1)} %get-tuple-element.66.x, bf16[8,256,1024]{2,1,0:T(8,128)(2,1)} %hidden_back.1.a), kind=kOutput, calls=%fused_computation | convolution fusion | flops 8592031744 | bytes 16777216 | tf_op jit(solution)/shard_map/dot_general | solution.py:1023
  516.5 10.2 %scores_back.1.gqkv = bf16[8,256,1024]{2,1,0:T(8,128)(2,1)} custom-call(bf16[8,256,256]{2,1,0:T(8,128)(2,1)} %get-tuple-element.56.sco, f32[8,256,256]{2,1,0:T(8,128)} %fusion.4.mask, bf16[8,256,256]{2,1,0:T(8,128)(2,1)} %get-tuple-element.61.q, bf16[8,256,256]{2,1,0:T(8,128)(2,1)} %get-tuple-element.62.k, bf16[8,256,512]{2,1,0:T(8,128)(2,1)} %get-tuple-element.63.v, ...), custom_call_target="tpu_custom_call" | custom-call | flops 1610612736 | bytes 16777216 | tf_op jit(solution)/shard_map/scores_back/pallas_call | solution.py:961
  526.7 14.1 %bitcast_convert_fusion.1 = bf16[2048,1024]{1,0:T(8,128)(2,1)} fusion(bf16[8,256,2048]{2,1,0:T(8,128)(2,1)} %norm_rows.1.x.nrm, bf16[8,256,1024]{2,1,0:T(8,128)(2,1)} %scores_back.1.gqkv), kind=kOutput, calls=%fused_computation.1 | convolution fusion | flops 8592031744 | bytes 16777216 | tf_op jit(solution)/shard_map/dot_general | solution.py:1023
  542.4 9.1 %bitcast_convert_fusion.2 = bf16[512,2048]{1,0:T(8,128)(2,1)} fusion(bf16[8,256,512]{2,1,0:T(8,128)(2,1)S(1)} %copy-done.11, bf16[8,256,2048]{2,1,0:T(8,128)(2,1)} %get-tuple-element.64.cot), kind=kOutput, calls=%fused_computation.2 | convolution fusion | flops 4296015872 | bytes 12582912 | tf_op jit(solution)/shard_map/dot_general | solution.py:1023
  551.6 13.7 %all_to_all.46.x = bf16[8,64,512]{2,1,0:T(8,128)(2,1)} all-to-all(bf16[8,64,512]{2,1,0:T(8,128)(2,1)} %bitcast.91), channel_id=1, replica_groups={{0,1,2,3,4,5,6,7},{8,9,10,11,12,13,14,15},{16,17,18,19,20,21,22,23},{24..., dimensions={0} | all-to-all | bytes 1048576 | tf_op jit(solution)/shard_map/all_to_all | solution.py:984
  565.3 13.8 %all_to_all.47.x = bf16[8,128,256]{2,1,0:T(8,128)(2,1)} all-to-all(bf16[8,128,256]{2,1,0:T(8,128)(2,1)} %bitcast.92), channel_id=1, replica_groups={{0,1,2,3,4,5,6,7},{8,9,10,11,12,13,14,15},{16,17,18,19,20,21,22,23},{24..., dimensions={0} | all-to-all | bytes 1048576 | tf_op jit(solution)/shard_map/all_to_all | solution.py:984
  579.2 53.3 %reduce-scatter.12.cloned.1.call-done = bf16[512,1024]{1,0:T(8,128)(2,1)} async-done(((bf16[2048,1024]{1,0:T(8,128)(2,1)}), bf16[512,1024]{1,0:T(8,128)(2,1)}) %reduce-scatter.12.cloned.1.call-update) | async-done | bytes 1048592 | tf_op jit(solution)/shard_map/reduce_scatter | solution.py:992
  637.5 91.2 %last_exchange.1 = (f32[256,2048]{1,0:T(8,128)}, f32[256,2048]{1,0:T(8,128)}, f32[8,512]{1,0:T(8,128)}) custom-call(bf16[8,256,1024]{2,1,0:T(8,128)(2,1)} %scores_back.1.gqkv, bf16[8,256,512]{2,1,0:T(8,128)(2,1)} %get-tuple-element.74.gs, bf16[2048,512]{1,0:T(8,128)(2,1)} %get-tuple-element.75.wqk, bf16[2048,1024]{1,0:T(8,128)(2,1)} %all-gather.4.cloned.1.call-done.wvs, ...), custom_call_target="tpu_custom_call" | custom-call | tf_op jit(solution)/shard_map/last_exchange/pallas_call | solution.py:869
  738.7 20.6 %reduce-scatter.14.cloned.1.call-done = bf16[128,2048]{1,0:T(8,128)(2,1)} async-done(((bf16[512,2048]{1,0:T(8,128)(2,1)}), bf16[128,2048]{1,0:T(8,128)(2,1)}) %reduce-scatter.14.cloned.1.call-update) | async-done | bytes 524304 | tf_op jit(solution)/shard_map/reduce_scatter | solution.py:992
  (110 shorter events, 47.6 us)
Async XLA Ops:
  7.2 130.5 %all-gather.6.cloned.1.call-start = ((), (), s32[]{:S(2)}) async-start(), calls=%async_computation.11 | async-start | bytes 5242880 | tf_op jit(solution)/shard_map/all_gather | solution.py:988
  10.2 15.5 %copy-start.12 = (bf16[64,4096]{1,0:T(8,128)(2,1)S(1)}, bf16[64,4096]{1,0:T(8,128)(2,1)}, u32[]{:S(2)}) copy-start(bf16[64,4096]{1,0:T(8,128)(2,1)} %param.26) | copy-start | bytes 1572868
  25.6 201.2 %all-gather.4.cloned.1.call-start = ((), (), s32[]{:S(2)}) async-start(), calls=%async_computation.10 | async-start | bytes 5242880 | tf_op jit(solution)/shard_map/all_gather | solution.py:988
  26.0 2.4 copy-start.20
  26.0 2.4 copy-start.15
  26.0 2.4 copy-start.16
  26.0 2.4 copy-start.17
  26.1 2.4 copy-start.18
  82.0 27.3 %copy-start.14 = (f32[4,8,8,128]{3,2,1,0:T(8,128)S(1)}, f32[4,8,8,128]{3,2,1,0:T(8,128)}, u32[]{:S(2)}) copy-start(f32[4,8,8,128]{3,2,1,0:T(8,128)} %get-tuple-element.53) | copy-start | bytes 393220
  108.5 218.4 %all-gather.8.cloned.1.call-start = ((), (), s32[]{:S(2)}) async-start(), calls=%async_computation.12 | async-start | bytes 5242880 | tf_op jit(solution)/shard_map/all_gather | solution.py:988
  109.2 442.4 %reduce-scatter.8.cloned.1.call-start = ((), (), s32[]{:S(2)}) async-start(), calls=%async_computation.14 | async-start | bytes 2621440 | tf_op jit(solution)/shard_map/reduce_scatter | solution.py:992
  342.6 11.8 %copy-start = (bf16[256,2048]{1,0:T(8,128)(2,1)S(1)}, bf16[256,2048]{1,0:T(8,128)(2,1)}, u32[]{:S(2)}) copy-start(bf16[256,2048]{1,0:T(8,128)(2,1)} %cot.2) | copy-start | bytes 3145732
  342.6 11.8 %copy-start.8 = (f32[2,2048]{1,0:T(2,128)S(1)}, f32[2,2048]{1,0:T(2,128)}, u32[]{:S(2)}) copy-start(f32[2,2048]{1,0:T(2,128)} %pad_maximum_fusion.1.vec) | copy-start | bytes 49156
  463.4 1.6 copy-start.19
  463.4 101.9 %reduce-scatter.10.cloned.1.call-start = ((), (), s32[]{:S(2)}) async-start(), calls=%async_computation.15 | async-start | bytes 2621440 | tf_op jit(solution)/shard_map/reduce_scatter | solution.py:992
  502.1 130.3 %reduce-scatter.12.cloned.1.call-start = ((), (), s32[]{:S(2)}) async-start(), calls=%async_computation.16 | async-start | bytes 5242880 | tf_op jit(solution)/shard_map/reduce_scatter | solution.py:992
  516.4 212.3 %reduce-scatter.6.cloned.1.call-start = ((), (), s32[]{:S(2)}) async-start(), calls=%async_computation.13 | async-start | bytes 5242880 | tf_op jit(solution)/shard_map/reduce_scatter | solution.py:992
  540.8 1.6 copy-start.11
  540.9 218.5 %reduce-scatter.14.cloned.1.call-start = ((), (), s32[]{:S(2)}) async-start(), calls=%async_computation.17 | async-start | bytes 2621440 | tf_op jit(solution)/shard_map/reduce_scatter | solution.py:992
  632.4 96.3 %all-to-all-start.4 = ((bf16[8,64,1024]{2,1,0:T(8,128)(2,1)}), bf16[8,64,1024]{2,1,0:T(8,128)(2,1)}, u32[]{:S(2)}, u32[]{:S(2)}) async-start(bf16[8,64,1024]{2,1,0:T(8,128)(2,1)} %bitcast.88), calls=%async_computation.8 | async-start | bytes 2097152 | tf_op jit(solution)/shard_map/all_to_all | solution.py:984
  728.7 37.6 %all-to-all-start = ((bf16[8,64,1024]{2,1,0:T(8,128)(2,1)}), bf16[8,64,1024]{2,1,0:T(8,128)(2,1)S(1)}, u32[]{:S(2)}, u32[]{:S(2)}) async-start(bf16[8,64,1024]{2,1,0:T(8,128)(2,1)} %bitcast.87), calls=%async_computation.1 | async-start | bytes 2097152 | tf_op jit(solution)/shard_map/all_to_all | solution.py:984
  735.2 26.2 %copy-start.1 = (bf16[8,64,512]{2,1,0:T(8,128)(2,1)S(1)}, bf16[8,64,512]{2,1,0:T(8,128)(2,1)}, u32[]{:S(2)}) copy-start(bf16[8,64,512]{2,1,0:T(8,128)(2,1)} %all_to_all.46.x) | copy-start | bytes 1572868
  738.7 23.7 %copy-start.2 = (bf16[8,128,256]{2,1,0:T(8,128)(2,1)S(1)}, bf16[8,128,256]{2,1,0:T(8,128)(2,1)}, u32[]{:S(2)}) copy-start(bf16[8,128,256]{2,1,0:T(8,128)(2,1)} %all_to_all.47.x) | copy-start | bytes 1572868
  763.5 4.2 copy-start.10
  (7 other events, 8.0 us)
Sparse Core Ops, SparseCore 0:
  25.8 100.2 all-gather.5
  127.6 99.1 all-gather.3
  228.4 80.3 all-gather.7
  463.5 44.8 reduce-scatter.7
  510.6 42.8 reduce-scatter.9
  555.6 76.7 reduce-scatter.11
  634.7 78.6 reduce-scatter.5
  716.3 42.9 reduce-scatter.13

commit v6 on v5

--- a/solution.py
+++ b/solution.py
@@ -40,7 +40,11 @@
     barrier = pltpu.get_barrier_semaphore()
     for p in peers:
         pl.semaphore_signal(barrier, inc=1, device_id=(p,), device_id_type=MESH)
-    pl.semaphore_wait(barrier, len(peers))
+    return lambda: pl.semaphore_wait(barrier, len(peers))
+
+
+def meet(peers):
+    greet(peers)()
 
 
 def remote(src, dst, sems, i, dev):
@@ -133,13 +137,14 @@
         keep.wait()
 
 
-def exchange_call(kernel, outs, args, sems, locals_, cid, specs=None, aliases=None, vmem=12 << 20):
+def exchange_call(
+    kernel, outs, args, sems, locals_, cid, specs=None, out_specs=None, vmem=12 << 20
+):
     return pl.pallas_call(
         kernel,
         out_shape=outs,
         in_specs=specs or [VMEM] * len(args),
-        input_output_aliases=aliases or {},
-        out_specs=tuple(ANY for _ in outs),
+        out_specs=out_specs or tuple(ANY for _ in outs),
         scratch_shapes=[
             pltpu.SemaphoreType.DMA((sems,)),
             pltpu.SemaphoreType.DMA((sems,)),
@@ -154,7 +159,7 @@
 def first_kernel(wq, wk, wo, out, ssem, rsem, local):
     me, peer = place()
     t = lax.rem(me, TP)
-    greet([peer(k) for k in range(1, TP)])
+    meet([peer(k) for k in range(1, TP)])
     sems = (ssem, rsem)
     shard, cq, co = wq.shape[0], wq.shape[1] // TP, wo.shape[1] // TP
     low, high = pl.ds(0, shard), pl.ds(shard, shard)
@@ -172,44 +177,27 @@
     return exchange_call(first_kernel, outs, (wq, wk, wo), 28, 4, cid)[0]
 
 
-def send_along(n, src, out, sems, base, parity):
-    dp = n // TP
-    me = lax.axis_index(AXIS)
-    g = lax.div(me, TP)
-    copies = []
-    for j in range(1, dp):
-        if j % 2 == parity:
-            copy = remote(src, out.at[g], sems, base + j, lax.rem(me + TP * j, n))
-            copy.start()
-            copies.append(copy)
-    return copies
-
-
 def others_along(n):
     me = lax.axis_index(AXIS)
     return [lax.rem(me + TP * j, n) for j in range(1, n // TP)]
 
 
-def second_kernel(n, tok, vec, wd, tok_out, vec_out, wd_out, ssem, rsem, local):
-    dp = n // TP
+def second_kernel(n, tok, vec, tok_out, vec_out, ssem, rsem, local):
     me, peer = place()
     t, g = lax.rem(me, TP), lax.div(me, TP)
     others = others_along(n)
-    greet([peer(k) for k in range(1, TP)] + others)
+    meet([peer(k) for k in range(1, TP)] + others)
     sems = (ssem, rsem)
     base = GATHER_SEMS
     far = []
     keep = pltpu.make_async_copy(vec, vec_out.at[g, t], local.at[1])
     keep.start()
-    mine = pltpu.make_async_copy(wd, wd_out.at[g], local.at[2])
-    mine.start()
     for j, dev in enumerate(others):
         copy = remote(vec, vec_out.at[g, t], sems, base + TP + j, dev)
         copy.start()
         far.append(copy)
     gather = Gather(tok, tok_out, 0, tok.shape[0], sems, 0, local.at[0], peer)
     gather.start()
-    along = send_along(n, wd, wd_out, sems, base + TP + dp, 1)
     for copy in far:
         copy.wait()
     keep.wait()
@@ -220,100 +208,147 @@
         near.append(copy)
     gather.forward()
     gather.finish()
-    for copy in near + along:
+    for copy in near:
         copy.wait()
-    mine.wait()
-
-
-def second_exchange(n, tok, vec, wd, cid):
-    dp = n // TP
-    outs = (
-        SDS((TP,) + tok.shape, bf),
-        SDS((dp, TP) + vec.shape, f32),
-        SDS((dp,) + wd.shape, bf),
-    )
+
+
+def second_exchange(n, tok, vec, cid):
+    outs = (SDS((TP,) + tok.shape, bf), SDS((n // TP, TP) + vec.shape, f32))
     kernel = functools.partial(second_kernel, n)
-    sems = GATHER_SEMS + TP + 2 * dp
-    return exchange_call(kernel, outs, (tok, vec, wd), sems, 3, cid, vmem=ALL_VMEM)
-
-
-def third_kernel(wv, ws, gu, out, gu_out, ssem, rsem, local):
+    sems = GATHER_SEMS + TP + n // TP
+    return exchange_call(kernel, outs, (tok, vec), sems, 2, cid)
+
+
+def third_kernel(wv, ws, gu, tok, gain, bias, out, gu_out, nrm, ssem, rsem, local):
     me, peer = place()
     t = lax.rem(me, TP)
-    greet([peer(k) for k in range(1, TP)])
+    meet([peer(k) for k in range(1, TP)])
     sems = (ssem, rsem)
     cols = wv.shape[1] // TP
-    finish([
+    parts = [
         send_columns(wv, out, cols, 0, sems, 0, local.at[0], t, peer),
         send_columns(ws, out, cols, cols, sems, 7, local.at[1], t, peer),
         send_columns(gu, gu_out, gu.shape[2], 0, sems, 14, local.at[2], t, peer),
-    ])
-
-
-def third_exchange(wv, ws, gu, cid):
-    outs = (SDS((TP, wv.shape[0], 2 * wv.shape[1] // TP), bf), SDS(gu.shape, bf))
-    return exchange_call(third_kernel, outs, (wv, ws, gu), 21, 3, cid)
-
-
-def fourth_kernel(n, at, cot, qko, wd, _, cot_out, o_out, wd_out, ssem, rsem, local):
+    ]
+    step, r = 16, tok.shape[1]
+
+    def norm(j, _):
+        k = lax.div(j, r // step)
+        at = pl.ds(pl.multiple_of(lax.rem(j, r // step) * step, step), step)
+        value = tok[k, at, :].astype(f32)
+        centred = value - jnp.mean(value, axis=-1, keepdims=True)
+        spread = jnp.mean(centred * centred, axis=-1, keepdims=True)
+        nrm[k, at, :] = (centred * lax.rsqrt(spread + 1e-05) * gain[...] + bias[...]).astype(bf)
+        return 0
+
+    lax.fori_loop(0, TP * r // step, norm, 0, unroll=4)
+    finish(parts)
+
+
+def third_exchange(wv, ws, gu, tok, gain, bias, cid):
+    outs = (
+        SDS((TP, wv.shape[0], 2 * wv.shape[1] // TP), bf),
+        SDS(gu.shape, bf),
+        SDS(tok.shape, bf),
+    )
+    return exchange_call(
+        third_kernel, outs, (wv, ws, gu, tok, gain, bias), 21, 3, cid,
+        out_specs=(ANY, ANY, VMEM), vmem=32 << 20,
+    )
+
+
+def fourth_kernel(
+    n, cot, qko, nrm, cosine, sine, mask, cot_out, o_out, q_out, k_out, sco, w, ssem, rsem, local
+):
     me, peer = place()
     t = lax.rem(me, TP)
-    others = others_along(n)
-    greet([peer(k) for k in range(1, TP)] + others)
+    meet([peer(k) for k in range(1, TP)])
     sems = (ssem, rsem)
     share, cols = n // TP, o_out.shape[4]
-    base = GATHER_SEMS + 2 * TP
+    _, r, kh = q_out.shape
+    half = kh // 2
+    weights = pltpu.make_async_copy(qko.at[:, :, pl.ds(0, 2 * kh)], w, local.at[3])
+    weights.start()
     gather = Gather(cot, cot_out, 0, cot.shape[0], sems, 0, local.at[0], peer)
     gather.start()
-    along = send_along(n, wd, wd_out, sems, base, 0)
     copies, keeps = [], []
 
-    def part(p, half):
-        return qko.at[pl.ds(p * share, share), :, pl.ds(at + half * cols, cols)]
-
-    for half in (0, 1):
+    def part(p, which):
+        return qko.at[pl.ds(p * share, share), :, pl.ds(2 * kh + which * cols, cols)]
+
+    for which in (0, 1):
         for k in range(1, TP):
             dev = peer(k)
             copy = remote(
-                part(lax.rem(dev, TP), half), o_out.at[t, :, half], sems,
-                GATHER_SEMS + half * TP + k, dev,
+                part(lax.rem(dev, TP), which), o_out.at[t, :, which], sems,
+                GATHER_SEMS + which * TP + k, dev,
             )
             copy.start()
             copies.append(copy)
-        keep = pltpu.make_async_copy(part(t, half), o_out.at[t, :, half], local.at[1 + half])
+        keep = pltpu.make_async_copy(part(t, which), o_out.at[t, :, which], local.at[1 + which])
         keep.start()
         keeps.append(keep)
+    weights.wait()
+
+    def products(pairs):
+        @pl.loop(*pairs)
+        def _(j):
+            rows = nrm[pl.ds(2 * j, 2)].reshape(2 * r, nrm.shape[2])
+            for at, out in ((0, q_out), (kh, k_out)):
+                y = jnp.dot(
+                    rows, w[:, :, at : at + kh].reshape(nrm.shape[2], kh),
+                    preferred_element_type=f32,
+                )
+                for i in (0, 1):
+                    u, v = y[i * r : (i + 1) * r, :half], y[i * r : (i + 1) * r, half:]
+                    cos, sin = cosine[2 * j + i], sine[2 * j + i]
+                    out[2 * j + i, :, :half] = (u * cos - v * sin).astype(bf)
+                    out[2 * j + i, :, half:] = (v * cos + u * sin).astype(bf)
+            for i in (0, 1):
+                plain = lax.dot_general(
+                    q_out[2 * j + i], k_out[2 * j + i], (((1,), (1,)), ((), ())),
+                    preferred_element_type=f32,
+                )
+                sco[2 * j + i] = (plain * mask[2 * j + i]).astype(bf)
+
+    products((0, TP // 2))
     gather.forward()
     gather.finish()
-    for copy in copies + along:
+    for copy in copies:
         copy.wait()
     for keep in keeps:
         keep.wait()
 
 
-def fourth_exchange(n, cot, qko, at, wd, wd_all, cid):
+def fourth_exchange(n, cot, qko, nrm, cosine, sine, mask, cid):
     _, shard, width = qko.shape
-    cols = (width - at) // 2
+    cols = (width - 2 * KH) // 2
+    r = cot.shape[0]
     outs = (
         SDS((TP,) + cot.shape, bf),
         SDS((TP, n // TP, 2, shard, cols), bf),
-        SDS(wd_all.shape, bf),
+        SDS((TP, r, KH), bf),
+        SDS((TP, r, KH), bf),
+        SDS(mask.shape, bf),
+        SDS((n, shard, 2 * KH), bf),
     )
-    kernel = functools.partial(fourth_kernel, n, at)
+    kernel = functools.partial(fourth_kernel, n)
     return exchange_call(
-        kernel, outs, (cot, qko, wd, wd_all),
-        GATHER_SEMS + 2 * TP + n // TP, 3, cid,
-        specs=[VMEM, ANY, VMEM, ANY], aliases={3: 2}, vmem=ALL_VMEM,
+        kernel, outs, (cot, qko, nrm, cosine, sine, mask),
+        GATHER_SEMS + 2 * TP, 4, cid,
+        specs=[VMEM, ANY, VMEM, VMEM, VMEM, VMEM],
+        out_specs=(ANY, ANY, VMEM, VMEM, VMEM, VMEM), vmem=40 << 20,
     )
 
 
 REDUCE_SEMS = 16
-TILE = 512
+TILE = 256
 
 
 class Reduce:
-    def __init__(self, product, bufs, sems, base, peer, prepare=None):
+    def __init__(self, product, bufs, sems, base, peer, prepare=None, enter=None):
         self.product, self.prepare, self.sems, self.base = product, prepare, sems, base
+        self.enter = enter
         self.po, self.pe, self.rc, self.sb, self.xr, self.yr = bufs
         self.pc, self.px, self.py = peer(1), peer(2), peer(4)
         self.q = self.pe.shape[1] // 4
@@ -331,10 +366,13 @@
 
     def pair(self, i):
         self.product(i, self.po.at[i], self.pe.at[i])
+        if self.enter is not None:
+            self.enter()
+            self.enter = None
         self.core[i] = self.send(self.po.at[i], self.rc.at[i], self.pc, i)
 
     def add(self, c, i, lower, out, more=None):
-        step = 32
+        step = 16
 
         @pl.loop(0, self.q // step)
         def _(j):
@@ -478,7 +516,7 @@
     v_buf, mix_buf, ret_buf, swi_buf, po, pe, rc, sb, xr, yr, own, ssem, rsem, local,
 ):
     _, peer = place()
-    greet([peer(1), peer(2), peer(4)])
+    enter = greet([peer(1), peer(2), peer(4)])
     sems = (ssem, rsem)
     r, width = v_buf.shape[1:]
     kept = []
@@ -487,19 +525,27 @@
         two = pl.ds(first, 2)
         x = nrm[two].reshape(2 * r, nrm.shape[2])
 
-        @pl.loop(0, width // 256)
+        tiles = width // TILE
+
+        @pl.loop(0, 2 * tiles)
         def _(j):
-            at = pl.ds(pl.multiple_of(j * 256, 256), 256)
-            behind = pl.ds(pl.multiple_of(j * 256 + width, 256), 256)
-            v = jnp.dot(x, wvs[:, at], preferred_element_type=f32).astype(bf)
-            s = jnp.dot(x, wvs[:, behind], preferred_element_type=f32)
-            for i in (0, 1):
-                mine = v[i * r : (i + 1) * r]
-                v_buf[first + i, :, at] = mine
-                swi_buf[first + i, :, at] = s[i * r : (i + 1) * r]
-                ret_buf[first + i, :, at] = jnp.dot(
-                    sco[first + i], mine, preferred_element_type=f32
-                )
+            at = pl.ds(pl.multiple_of(j * TILE, TILE), TILE)
+            y = jnp.dot(x, wvs[:, at], preferred_element_type=f32)
+            y = y.reshape(2, r, TILE)
+
+            @pl.when(j < tiles)
+            def _():
+                v_buf[two, :, at] = y.astype(bf)
+
+            @pl.when(j >= tiles)
+            def _():
+                swi_buf[two, :, pl.ds(pl.multiple_of(j * TILE - width, TILE), TILE)] = y
+
+        @pl.loop(0, 2 * tiles)
+        def _(j):
+            k = first + lax.div(j, tiles)
+            at = pl.ds(pl.multiple_of(lax.rem(j, tiles) * TILE, TILE), TILE)
+            ret_buf[k, :, at] = jnp.dot(sco[k], v_buf[k, :, at], preferred_element_type=f32)
 
         @pl.loop(0, 2 * r // 32)
         def _(j):
@@ -543,7 +589,7 @@
             centred * lax.rsqrt(spread + 1e-05) * vec[0:1, :] + vec[1:2, :]
         ).astype(bf)
 
-    reduce = Reduce(product, (po, pe, rc, sb, xr, yr), sems, 0, peer, prepare)
+    reduce = Reduce(product, (po, pe, rc, sb, xr, yr), sems, 0, peer, prepare, enter)
     exchange_and_gather(reduce, both_gathers(own, out, sems, local, peer), 16, body)
     for copy in kept:
         copy.wait()
@@ -574,72 +620,40 @@
     )(nrm, wvs, sco, w, tok, vec)
 
 
-def norm_kernel(x, gain, bias, out):
-    step = 32
-
-    @pl.loop(0, x.shape[1] // step)
+def product_kernel(a, b, out, turned):
+    turned[...] = a[...].reshape(-1, a.shape[-1]).T
+    rows = turned.shape[1]
+
+    @pl.loop(0, out.shape[1] // TILE)
     def _(j):
-        at = pl.ds(pl.multiple_of(j * step, step), step)
-        value = x[0, at, :].astype(f32)
-        centred = value - jnp.mean(value, axis=-1, keepdims=True)
-        spread = jnp.mean(centred * centred, axis=-1, keepdims=True)
-        out[0, at, :] = (centred * lax.rsqrt(spread + 1e-05) * gain[...] + bias[...]).astype(bf)
-
-
-def norm_rows(x, gain, bias):
-    _, r, d = x.shape
-    row = pl.BlockSpec((1, r, d), lambda k: (k, 0, 0))
-    vec = pl.BlockSpec((1, d), lambda k: (0, 0))
+        at = pl.ds(pl.multiple_of(j * TILE, TILE), TILE)
+        out[:, at] = jnp.dot(
+            turned[...], b[:, :, at].reshape(rows, TILE), preferred_element_type=f32
+        ).astype(bf)
+
+
+def row_product(a, b):
+    _, r, m = a.shape
+    width = b.shape[2]
+    tile = 512 if m >= 2048 else 256
     return pl.pallas_call(
-        norm_kernel,
-        grid=(TP,),
-        out_shape=SDS(x.shape, bf),
-        in_specs=[row, vec, vec],
-        out_specs=row,
+        product_kernel,
+        grid=(m // tile,),
+        out_shape=SDS((m, width), bf),
+        in_specs=[
+            pl.BlockSpec((TP, r, tile), lambda i: (0, 0, i)),
+            pl.BlockSpec((TP, r, width), lambda i: (0, 0, 0)),
+        ],
+        out_specs=pl.BlockSpec((tile, width), lambda i: (i, 0)),
+        scratch_shapes=[pltpu.VMEM((tile, TP * r), bf)],
         compiler_params=pltpu.CompilerParams(vmem_limit_bytes=56 << 20),
         cost_estimate=pl.CostEstimate(
-            flops=8 * x.size, bytes_accessed=4 * x.size, transcendentals=0
+            flops=2 * TP * r * m * width,
+            bytes_accessed=2 * (a.size + b.size + m * width),
+            transcendentals=0,
         ),
-        name="norm_rows",
-    )(x, gain, bias)
-
-
-def scores_kernel(x, w, cosine, sine, mask, q_out, k_out, sco, w_out):
-    two, r, kh = q_out.shape
-    half = kh // 2
-    w_out[...] = w[...]
-    rows = x[...].reshape(two * r, x.shape[2])
-    for j, out in enumerate((q_out, k_out)):
-        y = jnp.dot(rows, w[:, j * kh : (j + 1) * kh], preferred_element_type=f32)
-        for i in range(two):
-            u, v = y[i * r : (i + 1) * r, :half], y[i * r : (i + 1) * r, half:]
-            out[i, :, :half] = (u * cosine[i] - v * sine[i]).astype(bf)
-            out[i, :, half:] = (v * cosine[i] + u * sine[i]).astype(bf)
-    for i in range(two):
-        plain = lax.dot_general(
-            q_out[i], k_out[i], (((1,), (1,)), ((), ())), preferred_element_type=f32
-        )
-        sco[i] = (plain * mask[i]).astype(bf)
-
-
-def rotated_and_scores(x, qko, cosine, sine, mask):
-    _, r, d = x.shape
-    pair = lambda k: (k, 0, 0)
-    square = pl.BlockSpec((2, r, KH), pair)
-    angle = pl.BlockSpec((2, r, KH // 2), pair)
-    weights = pl.BlockSpec((d, 2 * KH), lambda k: (0, 0))
-    return pl.pallas_call(
-        scores_kernel,
-        grid=(TP // 2,),
-        out_shape=(SDS((TP, r, KH), bf), SDS((TP, r, KH), bf), SDS(mask.shape, bf), SDS((d, 2 * KH), bf)),
-        in_specs=[pl.BlockSpec((2, r, d), pair), weights, angle, angle, pl.BlockSpec((2, r, r), pair)],
-        out_specs=(square, square, pl.BlockSpec((2, r, r), pair), weights),
-        compiler_params=pltpu.CompilerParams(vmem_limit_bytes=56 << 20),
-        cost_estimate=pl.CostEstimate(
-            flops=4 * TP * r * d * KH, bytes_accessed=16 << 20, transcendentals=0
-        ),
-        name="rotated_and_scores",
-    )(x, qko, cosine, sine, mask)
+        name="row_product",
+    )(a, b)
 
 
 def hidden_kernel(x, gu, hid, act_out, slope_out):
@@ -726,7 +740,7 @@
     a, w, mid, cot, vec, gmid, out, sums, po, pe, rc, sb, xr, yr, own, acc, ssem, rsem, local
 ):
     _, peer = place()
-    greet([peer(1), peer(2), peer(4)])
+    enter = greet([peer(1), peer(2), peer(4)])
     sems = (ssem, rsem)
     acc[...] = jnp.zeros_like(acc)
 
@@ -745,7 +759,7 @@
         gmid[at, :] = grad
         own[at, :] = grad.astype(bf)
 
-    reduce = Reduce(times(a, w, True), (po, pe, rc, sb, xr, yr), sems, 0, peer)
+    reduce = Reduce(times(a, w, True), (po, pe, rc, sb, xr, yr), sems, 0, peer, enter=enter)
     exchange_and_gather(reduce, both_gathers(own, out, sems, local, peer), 16, body)
     sums[0:1, :] = jnp.sum(acc[0], axis=0, keepdims=True)
     sums[1:2, :] = jnp.sum(acc[1], axis=0, keepdims=True)
@@ -784,7 +798,7 @@
     g = lax.div(me, TP)
     width = vec_out.shape[1]
     others = [lax.rem(me + TP * j, n) for j in range(1, dp)]
-    greet([peer(k) for k in range(1, TP)] + others)
+    enter = greet([peer(k) for k in range(1, TP)] + others)
     sems = (ssem, rsem)
     acc[...] = jnp.zeros_like(acc)
     nt = (((1,), (1,)), ((), ()))
@@ -802,7 +816,7 @@
             even[:, at] = z[:r].astype(even.dtype)
             odd[:, at] = z[r:].astype(odd.dtype)
 
-    one = Reduce(product, (po, pe, rc, sb, xr, yr), sems, 0, peer)
+    one = Reduce(product, (po, pe, rc, sb, xr, yr), sems, 0, peer, enter=enter)
     one.run()
     for copy in one.core.values():
         copy.wait_send()
@@ -840,7 +854,7 @@
     def keep(at, value):
         ffn[at, :] = value
 
-    two.rows(0, 32, keep)
+    two.rows(0, 16, keep)
     total = vecs[:, pl.ds(pl.multiple_of(g * width, 128), width)]
     for j, copy in enumerate(copies):
         copy.wait()
@@ -851,7 +865,7 @@
         copy = remote(part, near.at[k - 1], sems, base + dp + k - 1, peer(k))
         copy.start()
         copies.append(copy)
-    two.rows(1, 32, keep)
+    two.rows(1, 16, keep)
     for k, copy in enumerate(copies):
         copy.wait()
         total = total + near[k]
@@ -889,44 +903,58 @@
     )(gqkv, gs, wqk, wvs, a2, w2, tok, gmid, gain, sums2)
 
 
-def gate_back_kernel(g_low, w, ret, swi, gret, gswi):
-    r, width = gret.shape[1:]
+def gate_back_kernel(g_low, w, ret, swi, gret, gswi, whole, back):
+    two, r, _ = gret.shape
     cols = w.shape[2]
-    nt = (((1,), (1,)), ((), ()))
-    grad = jnp.zeros((r, width), f32)
-    for j in range(w.shape[0]):
-        grad += lax.dot_general(
-            g_low[0, :, j * cols : (j + 1) * cols], w[j], nt, preferred_element_type=f32
-        )
-    value, gate = ret[0], swi[0]
-    centred = value - jnp.mean(value, axis=-1, keepdims=True)
-    spread = jnp.mean(centred * centred, axis=-1, keepdims=True)
-    inv = lax.rsqrt(jnp.maximum(spread, 0.25))
-    share = 1.0 / (1.0 + jnp.exp(-gate))
-    silu = gate * share
-    gswi[0] = (grad * (centred * inv) * (share * (1.0 + gate * (1.0 - share)))).astype(bf)
-    grad = grad * silu
-    pull = jnp.mean(grad * centred, axis=-1, keepdims=True)
-    pull = jnp.where(spread > 0.25, inv * inv * inv * pull, 0.0)
-    grad = grad * inv - centred * pull
-    gret[0] = (grad - jnp.mean(grad, axis=-1, keepdims=True)).astype(bf)
+
+    @pl.when(pl.program_id(0) == 0)
+    def _():
+        for j in range(w.shape[0]):
+            whole[:, j * cols : (j + 1) * cols] = w[j]
+
+    back[...] = lax.dot_general(
+        g_low[...].reshape(two * r, g_low.shape[2]), whole[...], (((1,), (1,)), ((), ())),
+        preferred_element_type=f32,
+    )
+    step = 32
+    for i in range(two):
+
+        @pl.loop(0, r // step)
+        def _(j, i=i):
+            at = pl.ds(pl.multiple_of(j * step, step), step)
+            value, gate = ret[i, at, :], swi[i, at, :]
+            grad = back[pl.ds(pl.multiple_of(i * r + j * step, step), step), :]
+            centred = value - jnp.mean(value, axis=-1, keepdims=True)
+            spread = jnp.mean(centred * centred, axis=-1, keepdims=True)
+            inv = lax.rsqrt(jnp.maximum(spread, 0.25))
+            share = 1.0 / (1.0 + jnp.exp(-gate))
+            silu = gate * share
+            gswi[i, at, :] = (
+                grad * (centred * inv) * (share * (1.0 + gate * (1.0 - share)))
+            ).astype(bf)
+            grad = grad * silu
+            pull = jnp.mean(grad * centred, axis=-1, keepdims=True)
+            pull = jnp.where(spread > 0.25, inv * inv * inv * pull, 0.0)
+            grad = grad * inv - centred * pull
+            gret[i, at, :] = (grad - jnp.mean(grad, axis=-1, keepdims=True)).astype(bf)
 
 
 def gate_back(g_low, w, ret, swi):
     _, r, d = g_low.shape
     width = ret.shape[2]
-    row = pl.BlockSpec((1, r, width), lambda k: (k, 0, 0))
+    row = pl.BlockSpec((2, r, width), lambda k: (k, 0, 0))
     return pl.pallas_call(
         gate_back_kernel,
-        grid=(TP,),
+        grid=(TP // 2,),
         out_shape=(SDS(ret.shape, bf), SDS(ret.shape, bf)),
         in_specs=[
-            pl.BlockSpec((1, r, d), lambda k: (k, 0, 0)),
+            pl.BlockSpec((2, r, d), lambda k: (k, 0, 0)),
             pl.BlockSpec(w.shape, lambda k: (0, 0, 0)),
             row,
             row,
         ],
         out_specs=(row, row),
+        scratch_shapes=[pltpu.VMEM((width, d), bf), pltpu.VMEM((2 * r, width), f32)],
         compiler_params=pltpu.CompilerParams(vmem_limit_bytes=56 << 20),
         cost_estimate=pl.CostEstimate(
             flops=2 * TP * r * d * width, bytes_accessed=22 << 20, transcendentals=TP * r * width
@@ -1017,10 +1045,6 @@
     steps = jnp.where(valid, diff, 0).astype(f32)
     log = jnp.log(1.0 - jnp.exp2(-5.0 - head.astype(f32)))
     return jnp.where(valid, jnp.exp(log * steps), 0.0) / math.sqrt(KH)
-
-
-def dot_tn(a, b):
-    return lax.dot_general(a, b, (((0,), (0,)), ((), ())), preferred_element_type=f32)
 
 
 def col_blocks(w):
@@ -1080,15 +1104,17 @@
     vec = jnp.pad(vec, ((0, 3), (0, 128 - shard)))
     qko_blk = first_exchange(wq, wk, wo, 1)
     qko = dp_gather(qko_blk.reshape(TP * shard, 4 * KH), n)
-    tok_all, vec_all, wd_all = second_exchange(n, after(tokens, qko_blk), vec, wd, 2)
-    gu_in = jnp.concatenate([ff_blocks(wg), ff_blocks(wu)], axis=2)
-    vs_blk, gu_blk = third_exchange(after(wv, tok_all), ws, gu_in, 3)
-    vs = dp_gather(vs_blk.reshape(TP * shard, 2 * VH), n)
-    gu = dp_gather(gu_blk.reshape(TP * shard, 2 * dp * unit), n)
+    tok_all, vec_all = second_exchange(n, after(tokens, qko_blk), vec, 2)
     gain1f, bias1f, gain2f, bias2f = (
         vec_all[:, :, i, :shard].reshape(1, d) for i in range(4)
     )
     vec2 = jnp.concatenate([gain2f, bias2f], axis=0)
+    gu_in = jnp.concatenate([ff_blocks(wg), ff_blocks(wu)], axis=2)
+    vs_blk, gu_blk, normed = third_exchange(wv, ws, gu_in, tok_all, gain1f, bias1f, 3)
+    vs = dp_gather(vs_blk.reshape(TP * shard, 2 * VH), n)
+    gu = dp_gather(gu_blk.reshape(TP * shard, 2 * dp * unit), n)
+    down = dp_gather(wd, n)
+
     mine = lax.dynamic_slice_in_dim(vec_all, lax.div(me, TP), 1, 0)[0, :, 4, :3]
     order = jnp.arange(TP, dtype=jnp.int32)
     pick = (order[None, :] == (order[:, None] ^ head)).astype(f32)
@@ -1097,35 +1123,30 @@
     cosine, sine = rotary_tables(offset)
     mask = decay_mask(segment, offset, head)
 
-    normed = norm_rows(tok_all, gain1f, bias1f)
-    q_rot, k_rot, scores, qk = rotated_and_scores(normed, qko, cosine, sine, mask)
-    cot_all, out_blk, wd_all = fourth_exchange(
-        n, after(cot, scores), qko.reshape(n, shard, 4 * KH), 2 * KH, wd, wd_all, 4
+    cot_all, out_blk, q_rot, k_rot, scores, qk = fourth_exchange(
+        n, cot, qko.reshape(n, shard, 4 * KH), normed, cosine, sine, mask, 4
     )
     out_blk = out_blk.reshape(TP, VH, d // TP)
-    down = wd_all.reshape(dp * wd.shape[0], d)
+    qk = qk.reshape(d, 2 * KH)
     v_low, mixed, retained, swish_in, middle, normed2 = forward_exchange(
         normed, vs, scores, out_blk, tokens, vec2, 5
     )
     hidden, act, slope = hidden_units(normed2, gu)
-    normed2 = normed2.reshape(TP * rows, d)
-    normed = normed.reshape(TP * rows, d)
-    down_grad = dot_tn(hidden.reshape(TP * rows, dp * unit), cot_all.reshape(TP * rows, d)).astype(bf)
+    down_grad = row_product(hidden, cot_all)
     g_down = dp_reduce(down_grad, n)
 
     g_fs = hidden_back(cot_all, down, act, slope)
-    gu_grad = dot_tn(normed2, g_fs.reshape(TP * rows, 2 * dp * unit)).astype(bf)
+    gu_grad = row_product(normed2, g_fs)
     g_gu = dp_reduce(gu_grad, n)
     g_middle, g_low, sums2 = backward_exchange(g_fs, gu, middle, cot, vec2, 6)
 
     g_retained, g_swish = gate_back(g_low, out_blk, retained, swish_in)
-    g_low = g_low.reshape(TP * rows, d)
-    swish_grad = dot_tn(normed, g_swish.reshape(TP * rows, VH)).astype(bf)
+    swish_grad = row_product(normed, g_swish)
     g_swi = dp_reduce(swish_grad, n)
-    out_grad = dot_tn(mixed.reshape(TP * rows, VH), g_low).astype(bf)
+    out_grad = row_product(mixed, g_low)
     out_grad = plane_a2a(col_blocks(out_grad), n)
     g_qkv = scores_back(scores, mask, q_rot, k_rot, v_low, g_retained, cosine, sine)
-    qkv_grad = dot_tn(normed, g_qkv.reshape(TP * rows, 2 * KH + VH)).astype(bf)
+    qkv_grad = row_product(normed, g_qkv)
     g_qkv_own = dp_reduce(qkv_grad, n)
     g_out = dp_reduce(out_grad, n)
     grad_tokens, ffn, g_vecs = last_exchange(

time: 783 us -> 763 us (0.974)
  matrix products: 55.5 us -> 0 us
  Pallas kernels: 521 us -> 573 us
  waiting for transfers between devices: 88 us -> 60.3 us
  local copies, waits for them, and re-layouts: 14.5 us -> 29.6 us
    pallas_call x3 -> x6, Pallas kernels: 42.8 us -> 100 us  [the longest x5 74 us: row_product(): pl.pallas_call(product_kernel, grid=(m // tile,), out_shape=SDS((m, width...]
    dot_general x5 -> x0, matrix products: 55.5 us -> none  [dot_tn(): lax.dot_general(a, b, (((0,), (0,)), ((), ())), preferred_element_type=f32)]
    reduce_scatter x5, waiting for transfers between devices: 73.9 us -> 56.8 us  [dp_reduce(): lax.psum_scatter(x, AXIS, scatter_dimension=0, tiled=True, axis_index_gro...]
    unnamed x45 -> x67, local copies, waits for them, and re-layouts: 8.24 us -> 24.3 us
    all_gather x3 -> x4, waiting for transfers between devices: 13.3 us -> 2.22 us  [dp_gather(): lax.all_gather(x, AXIS, axis=0, tiled=True, axis_index_groups=dp_groups(n))]
    pallas_call x4, Pallas kernels: 158 us -> 150 us  [exchange_call(): pl.pallas_call(kernel, out_shape=outs, in_specs=specs or [VMEM] * len(arg...]
  transfers between devices with their start and end apart: 10 -> 11, of which waited for: 3 -> 3; matrix products, arithmetic and copies ran while one was open for 9% -> 3% of each run, Pallas kernels for 49% -> 56%
where the time goes in v6:
time: 763 us; the launch traced here: 759 us
  Pallas kernels  573 us (75%)
  waiting for transfers between devices  60.3 us (8%)
  blocking collectives  56.6 us (7%)
  local copies, waits for them, and re-layouts  29.6 us (4%)
  between operations  14.4 us (2%)
  other arithmetic  13.9 us (2%)
  starting transfers between devices  11 us (1%)
    pallas_call x4, Pallas kernels, exchange_call(): pl.pallas_call(kernel, out_shape=outs, in_specs=specs or [VMEM] * len(arg...  150 us
    pallas_call x1, Pallas kernels, forward_exchange(): pl.pallas_call(forward_kernel, out_shape=tuple((SDS(*b) for b in blocks))...  105 us
    pallas_call x1, Pallas kernels, last_exchange(): pl.pallas_call(functools.partial(last_kernel, n), out_shape=(SDS((r, c),...  90.5 us
    pallas_call x1, Pallas kernels, backward_exchange(): pl.pallas_call(backward_kernel, out_shape=(SDS((r, c), f32), SDS((TP, r,...  84.2 us
    pallas_call x5, Pallas kernels, row_product(): pl.pallas_call(product_kernel, grid=(m // tile,), out_shape=SDS((m, width...  74 us
    reduce_scatter x5, waiting for transfers between devices, dp_reduce(): lax.psum_scatter(x, AXIS, scatter_dimension=0, tiled=True, axis_index_gro...  56.8 us
    all_to_all x3, blocking collectives, plane_a2a(): lax.all_to_all(x, AXIS, 0, 0, axis_index_groups=tp_groups(n), tiled=True)  56.6 us
    pallas_call x1, Pallas kernels, gate_back(): pl.pallas_call(gate_back_kernel, grid=(TP // 2,), out_shape=(SDS(ret.shap...  26.3 us
  transfers between devices with their start and end apart: 11, of which 3 were waited for; matrix products, arithmetic and copies ran while one was open for 3% of the time, Pallas kernels for 56%

profile of v6, /device:TPU:14, one launch (start us, length us, event | category | flops | bytes accessed | tf_op | source)
XLA Modules:
  0.0 759.3 jit_solution(6769115066890839657)
XLA Ops:
  10.2 15.4 %shard_map.254 = bf16[8,64,1024]{2,1,0:T(8,128)(2,1)} custom-call(bf16[64,2048]{1,0:T(8,128)(2,1)S(1)} %copy-done.19, bf16[64,2048]{1,0:T(8,128)(2,1)S(1)} %copy-done.20, bf16[128,2048]{1,0:T(8,128)(2,1)S(1)} %copy-done.18), custom_call_target="tpu_custom_call" | custom-call | tf_op jit(solution)/shard_map/pallas_call | solution.py:143
  28.1 41.8 %shard_map.255 = (bf16[8,256,2048]{2,1,0:T(8,128)(2,1)S(1)}, f32[4,8,8,128]{3,2,1,0:T(8,128)S(1)}) custom-call(bf16[256,2048]{1,0:T(8,128)(2,1)S(1)} %copy-done.4, f32[8,128]{1,0:T(8,128)S(1)} %pad.9.vec), custom_call_target="tpu_custom_call" | custom-call | tf_op jit(solution)/shard_map/pallas_call | solution.py:143
  78.1 26.4 %shard_map.256 = (bf16[8,64,1024]{2,1,0:T(8,128)(2,1)}, bf16[8,64,1024]{2,1,0:T(8,128)(2,1)}, bf16[8,256,2048]{2,1,0:T(8,128)(2,1)S(1)}) custom-call(bf16[64,4096]{1,0:T(8,128)(2,1)S(1)} %copy-done.16, bf16[64,4096]{1,0:T(8,128)(2,1)S(1)} %copy-done.17, bf16[8,64,1024]{2,1,0:T(8,128)(2,1)S(1)} %pad_maximum_fusion.gu, bf16[8,256,2048]{2,1,0:T(8,128)(2,1)S(1)} %copy-done.7, ...), custom_call_target="tpu_custom_call" | custom-call | tf_op jit(solution)/shard_map/pallas_call | solution.py:143
  110.6 5.3 multiply_sine_fusion
  120.1 66.1 %shard_map.257 = (bf16[8,256,2048]{2,1,0:T(8,128)(2,1)}, bf16[8,4,2,64,256]{4,3,2,1,0:T(8,128)(2,1)S(1)}, bf16[8,256,256]{2,1,0:T(8,128)(2,1)S(1)}, bf16[8,256,2...) custom-call(bf16[256,2048]{1,0:T(8,128)(2,1)S(1)} %copy-done.8, ...), custom_call_target="tpu_custom_call" | custom-call | tf_op jit(solution)/shard_map/pallas_call | solution.py:143
  191.8 104.6 %forward_exchange.1 = (bf16[8,256,512]{2,1,0:T(8,128)(2,1)}, bf16[8,256,512]{2,1,0:T(8,128)(2,1)}, f32[8,256,512]{2,1,0:T(8,128)}, f32[8,256,512]{2,1,0:T(8,128)...) custom-call(bf16[8,256,2048]{2,1,0:T(8,128)(2,1)} %copy-done, bf16[2048,1024]{1,0:T(8,128)(2,1)} %all-gather.5.cloned.1.call-done.wvs, ...), custom_call_target="tpu_custom_call" | custom-call | tf_op jit(solution)/shard_map/forward_exchange/pallas_call | solution.py:603
  296.5 15.8 %hidden_units.1 = (bf16[8,256,512]{2,1,0:T(8,128)(2,1)}, f32[8,256,512]{2,1,0:T(8,128)}, f32[8,256,512]{2,1,0:T(8,128)}) custom-call(bf16[8,256,2048]{2,1,0:T(8,128)(2,1)} %get-tuple-element.60.x.a, bf16[2048,1024]{1,0:T(8,128)(2,1)} %all-gather.11.cloned.1.call-done.gu.w), custom_call_target="tpu_custom_call" | custom-call | flops 8589934592 | bytes 25165824 | tf_op jit(solution)/shard_map/hidden_units/pallas_call | solution.py:683
  314.4 11.8 %hidden_back.1.a.b = bf16[8,256,1024]{2,1,0:T(8,128)(2,1)} custom-call(bf16[8,256,2048]{2,1,0:T(8,128)(2,1)} %get-tuple-element.59.cot.b, bf16[512,2048]{1,0:T(8,128)(2,1)} %all-gather.9.cloned.1.call-done.down.w2, f32[8,256,512]{2,1,0:T(8,128)} %get-tuple-element.62.act, f32[8,256,512]{2,1,0:T(8,128)} %get-tuple-element.63.slope), custom_call_target="tpu_custom_call" | custom-call | flops 4294967296 | bytes 25165824 | tf_op jit(solution)/shard_map/hidden_back/pallas_call | solution.py:720
  326.2 84.2 %backward_exchange.1 = (f32[256,2048]{1,0:T(8,128)}, bf16[8,256,2048]{2,1,0:T(8,128)(2,1)}, f32[2,2048]{1,0:T(2,128)S(1)}) custom-call(bf16[8,256,1024]{2,1,0:T(8,128)(2,1)} %hidden_back.1.a.b, bf16[2048,1024]{1,0:T(8,128)(2,1)} %all-gather.11.cloned.1.call-done.gu.w, f32[256,2048]{1,0:T(8,128)} %get-tuple-element.55.mid, bf16[256,2048]{1,0:T(8,128)(2,1)S(1)} %copy-done.9, ...), custom_call_target="tpu_custom_call" | custom-call | tf_op jit(solution)/shard_map/backward_exchange/pallas_call | solution.py:772
  411.0 26.3 %gate_back.1 = (bf16[8,256,512]{2,1,0:T(8,128)(2,1)}, bf16[8,256,512]{2,1,0:T(8,128)(2,1)}) custom-call(bf16[8,256,2048]{2,1,0:T(8,128)(2,1)} %get-tuple-element.64.g_low.b, bf16[8,512,256]{2,1,0:T(8,128)(2,1)} %bitcast.56, f32[8,256,512]{2,1,0:T(8,128)} %get-tuple-element.65.ret, f32[8,256,512]{2,1,0:T(8,128)} %get-tuple-element.66.swi), custom_call_target="tpu_custom_call" | custom-call | flops 4294967296 | bytes 23068672 | tf_op jit(solution)/shard_map/gate_back/pallas_call | solution.py:946
  437.3 11.4 %row_product.6 = bf16[2048,512]{1,0:T(8,128)(2,1)} custom-call(bf16[8,256,2048]{2,1,0:T(8,128)(2,1)} %copy-done, bf16[8,256,512]{2,1,0:T(8,128)(2,1)} %get-tuple-element.68.gs.b), custom_call_target="tpu_custom_call" | custom-call | flops 4294967296 | bytes 12582912 | tf_op jit(solution)/shard_map/row_product/pallas_call | solution.py:639
  448.8 12.9 %row_product.7 = bf16[512,2048]{1,0:T(8,128)(2,1)} custom-call(bf16[8,256,512]{2,1,0:T(8,128)(2,1)} %get-tuple-element.79.a, bf16[8,256,2048]{2,1,0:T(8,128)(2,1)} %get-tuple-element.64.g_low.b), custom_call_target="tpu_custom_call" | custom-call | flops 4294967296 | bytes 12582912 | tf_op jit(solution)/shard_map/row_product/pallas_call | solution.py:639
  463.5 28.8 %all_to_all.45 = bf16[8,512,256]{2,1,0:T(8,128)(2,1)} all-to-all(bf16[8,512,256]{2,1,0:T(8,128)(2,1)S(1)} %bitcast.59), channel_id=1, replica_groups={{0,1,2,3,4,5,6,7},{8,9,10,11,12,13,14,15},{16,17,18,19,20,21,22,23},{24..., dimensions={0} | all-to-all | bytes 4194304 | tf_op jit(solution)/shard_map/all_to_all | solution.py:1012
  492.4 18.3 %row_product.8 = bf16[2048,1024]{1,0:T(8,128)(2,1)} custom-call(bf16[8,256,2048]{2,1,0:T(8,128)(2,1)} %get-tuple-element.60.x.a, bf16[8,256,1024]{2,1,0:T(8,128)(2,1)} %hidden_back.1.a.b), custom_call_target="tpu_custom_call" | custom-call | flops 8589934592 | bytes 16777216 | tf_op jit(solution)/shard_map/row_product/pallas_call | solution.py:639
  510.8 10.1 %scores_back.1.gqkv.b = bf16[8,256,1024]{2,1,0:T(8,128)(2,1)} custom-call(bf16[8,256,256]{2,1,0:T(8,128)(2,1)} %copy-done.10, f32[8,256,256]{2,1,0:T(8,128)} %copy-done.1, bf16[8,256,256]{2,1,0:T(8,128)(2,1)} %copy-done.14, bf16[8,256,256]{2,1,0:T(8,128)(2,1)} %copy-done.15, bf16[8,256,512]{2,1,0:T(8,128)(2,1)} %get-tuple-element.58.v, ...), custom_call_target="tpu_custom_call" | custom-call | flops 1610612736 | bytes 16777216 | tf_op jit(solution)/shard_map/scores_back/pallas_call | solution.py:989
  520.9 18.4 %row_product.5 = bf16[2048,1024]{1,0:T(8,128)(2,1)} custom-call(bf16[8,256,2048]{2,1,0:T(8,128)(2,1)} %copy-done, bf16[8,256,1024]{2,1,0:T(8,128)(2,1)} %scores_back.1.gqkv.b), custom_call_target="tpu_custom_call" | custom-call | flops 8589934592 | bytes 16777216 | tf_op jit(solution)/shard_map/row_product/pallas_call | solution.py:639
  539.4 12.9 %row_product.9 = bf16[512,2048]{1,0:T(8,128)(2,1)} custom-call(bf16[8,256,512]{2,1,0:T(8,128)(2,1)} %get-tuple-element.70.a2.a, bf16[8,256,2048]{2,1,0:T(8,128)(2,1)} %get-tuple-element.59.cot.b), custom_call_target="tpu_custom_call" | custom-call | flops 4294967296 | bytes 12582912 | tf_op jit(solution)/shard_map/row_product/pallas_call | solution.py:639
  552.3 14.0 %all_to_all.46.x = bf16[8,64,512]{2,1,0:T(8,128)(2,1)} all-to-all(bf16[8,64,512]{2,1,0:T(8,128)(2,1)} %bitcast.70), channel_id=1, replica_groups={{0,1,2,3,4,5,6,7},{8,9,10,11,12,13,14,15},{16,17,18,19,20,21,22,23},{24..., dimensions={0} | all-to-all | bytes 1048576 | tf_op jit(solution)/shard_map/all_to_all | solution.py:1012
  566.3 13.8 %all_to_all.47.x = bf16[8,128,256]{2,1,0:T(8,128)(2,1)} all-to-all(bf16[8,128,256]{2,1,0:T(8,128)(2,1)} %bitcast.71), channel_id=1, replica_groups={{0,1,2,3,4,5,6,7},{8,9,10,11,12,13,14,15},{16,17,18,19,20,21,22,23},{24..., dimensions={0} | all-to-all | bytes 1048576 | tf_op jit(solution)/shard_map/all_to_all | solution.py:1012
  580.2 36.5 %reduce-scatter.12.cloned.1.call-done = bf16[512,1024]{1,0:T(8,128)(2,1)} async-done(((bf16[2048,1024]{1,0:T(8,128)(2,1)}), bf16[512,1024]{1,0:T(8,128)(2,1)}) %reduce-scatter.12.cloned.1.call-update) | async-done | bytes 1048592 | tf_op jit(solution)/shard_map/reduce_scatter | solution.py:1020
  616.6 4.7 all-to-all-start.4
  621.3 90.5 %last_exchange.1 = (f32[256,2048]{1,0:T(8,128)}, f32[256,2048]{1,0:T(8,128)}, f32[8,512]{1,0:T(8,128)}) custom-call(bf16[8,256,1024]{2,1,0:T(8,128)(2,1)} %scores_back.1.gqkv.b, bf16[8,256,512]{2,1,0:T(8,128)(2,1)} %get-tuple-element.68.gs.b, bf16[2048,512]{1,0:T(8,128)(2,1)} %bitcast.57, bf16[2048,1024]{1,0:T(8,128)(2,1)} %all-gather.5.cloned.1.call-done.wvs, ...), custom_call_target="tpu_custom_call" | custom-call | tf_op jit(solution)/shard_map/last_exchange/pallas_call | solution.py:883
  711.9 6.0 all-to-all-start
  722.7 20.3 %reduce-scatter.14.cloned.1.call-done = bf16[128,2048]{1,0:T(8,128)(2,1)} async-done(((bf16[512,2048]{1,0:T(8,128)(2,1)}), bf16[128,2048]{1,0:T(8,128)(2,1)}) %reduce-scatter.14.cloned.1.call-update) | async-done | bytes 524304 | tf_op jit(solution)/shard_map/reduce_scatter | solution.py:1020
  (133 shorter events, 48.4 us)
Async XLA Ops:
  7.2 109.6 %all-gather.7.cloned.1.call-start = ((), (), s32[]{:S(2)}) async-start(), calls=%async_computation.11 | async-start | bytes 5242880 | tf_op jit(solution)/shard_map/all_gather | solution.py:1016
  10.2 15.5 %copy-start.25 = (bf16[64,4096]{1,0:T(8,128)(2,1)S(1)}, bf16[64,4096]{1,0:T(8,128)(2,1)}, u32[]{:S(2)}) copy-start(bf16[64,4096]{1,0:T(8,128)(2,1)} %param.26) | copy-start | bytes 1572868
  25.6 166.2 %all-gather.5.cloned.1.call-start = ((), (), s32[]{:S(2)}) async-start(), calls=%async_computation.10 | async-start | bytes 5242880 | tf_op jit(solution)/shard_map/all_gather | solution.py:1016
  27.0 47.8 %copy-start.16 = (bf16[64,4096]{1,0:T(8,128)(2,1)S(1)}, bf16[64,4096]{1,0:T(8,128)(2,1)}, u32[]{:S(2)}) copy-start(bf16[64,4096]{1,0:T(8,128)(2,1)} %wv.1) | copy-start | bytes 1572868
  27.0 47.8 %copy-start.17 = (bf16[64,4096]{1,0:T(8,128)(2,1)S(1)}, bf16[64,4096]{1,0:T(8,128)(2,1)}, u32[]{:S(2)}) copy-start(bf16[64,4096]{1,0:T(8,128)(2,1)} %ws.1) | copy-start | bytes 1572868
  69.9 3.3 copy-start.6
  73.5 31.1 %copy-start.22 = (f32[1,2048]{1,0:T(1,128)}, f32[1,2048]{1,0:T(1,128)S(1)}, u32[]{:S(2)}) copy-start(f32[1,2048]{1,0:T(1,128)S(1)} %reshape_squeeze.12.gain) | copy-start | bytes 24580
  74.7 3.4 copy-start.7
  107.9 188.6 %all-gather.11.cloned.1.call-start = ((), (), s32[]{:S(2)}) async-start(), calls=%async_computation.13 | async-start | bytes 5242880 | tf_op jit(solution)/shard_map/all_gather | solution.py:1016
  108.6 205.8 %all-gather.9.cloned.1.call-start = ((), (), s32[]{:S(2)}) async-start(), calls=%async_computation.12 | async-start | bytes 2621440 | tf_op jit(solution)/shard_map/all_gather | solution.py:1016
  109.2 443.1 %reduce-scatter.8.cloned.1.call-start = ((), (), s32[]{:S(2)}) async-start(), calls=%async_computation.15 | async-start | bytes 2621440 | tf_op jit(solution)/shard_map/reduce_scatter | solution.py:1020
  115.9 70.2 %copy-start.2 = (f32[8,256,128]{2,1,0:T(8,128)}, f32[8,256,128]{2,1,0:T(8,128)S(1)}, u32[]{:S(2)}) copy-start(f32[8,256,128]{2,1,0:T(8,128)S(1)} %get-tuple-element.86.sine) | copy-start | bytes 3145732
  116.7 69.4 %copy-start.1 = (f32[8,256,256]{2,1,0:T(8,128)}, f32[8,256,256]{2,1,0:T(8,128)S(1)}, u32[]{:S(2)}) copy-start(f32[8,256,256]{2,1,0:T(8,128)S(1)} %fusion.4.mask) | copy-start | bytes 6291460
  314.4 11.8 %copy-start.9 = (bf16[256,2048]{1,0:T(8,128)(2,1)S(1)}, bf16[256,2048]{1,0:T(8,128)(2,1)}, u32[]{:S(2)}) copy-start(bf16[256,2048]{1,0:T(8,128)(2,1)} %cot.3) | copy-start | bytes 3145732
  314.4 11.8 %copy-start.21 = (f32[2,2048]{1,0:T(2,128)S(1)}, f32[2,2048]{1,0:T(2,128)}, u32[]{:S(2)}) copy-start(f32[2,2048]{1,0:T(2,128)} %pad_maximum_fusion.1.vec) | copy-start | bytes 49156
  448.8 117.5 %reduce-scatter.10.cloned.1.call-start = ((), (), s32[]{:S(2)}) async-start(), calls=%async_computation.16 | async-start | bytes 2621440 | tf_op jit(solution)/shard_map/reduce_scatter | solution.py:1020
  492.3 124.3 %reduce-scatter.12.cloned.1.call-start = ((), (), s32[]{:S(2)}) async-start(), calls=%async_computation.17 | async-start | bytes 5242880 | tf_op jit(solution)/shard_map/reduce_scatter | solution.py:1020
  510.8 201.1 %reduce-scatter.6.cloned.1.call-start = ((), (), s32[]{:S(2)}) async-start(), calls=%async_computation.14 | async-start | bytes 5242880 | tf_op jit(solution)/shard_map/reduce_scatter | solution.py:1020
  539.3 203.6 %reduce-scatter.14.cloned.1.call-start = ((), (), s32[]{:S(2)}) async-start(), calls=%async_computation.18 | async-start | bytes 2621440 | tf_op jit(solution)/shard_map/reduce_scatter | solution.py:1020
  616.6 95.2 %all-to-all-start.4 = ((bf16[8,64,1024]{2,1,0:T(8,128)(2,1)}), bf16[8,64,1024]{2,1,0:T(8,128)(2,1)}, u32[]{:S(2)}, u32[]{:S(2)}) async-start(bf16[8,64,1024]{2,1,0:T(8,128)(2,1)} %bitcast.67), calls=%async_computation.8 | async-start | bytes 2097152 | tf_op jit(solution)/shard_map/all_to_all | solution.py:1012
  711.9 38.1 %all-to-all-start = ((bf16[8,64,1024]{2,1,0:T(8,128)(2,1)}), bf16[8,64,1024]{2,1,0:T(8,128)(2,1)S(1)}, u32[]{:S(2)}, u32[]{:S(2)}) async-start(bf16[8,64,1024]{2,1,0:T(8,128)(2,1)} %bitcast.66), calls=%async_computation.1 | async-start | bytes 2097152 | tf_op jit(solution)/shard_map/all_to_all | solution.py:1012
  719.2 25.9 %copy-start.11 = (bf16[8,64,512]{2,1,0:T(8,128)(2,1)S(1)}, bf16[8,64,512]{2,1,0:T(8,128)(2,1)}, u32[]{:S(2)}) copy-start(bf16[8,64,512]{2,1,0:T(8,128)(2,1)} %all_to_all.46.x) | copy-start | bytes 1572868
  722.7 23.4 %copy-start.12 = (bf16[8,128,256]{2,1,0:T(8,128)(2,1)S(1)}, bf16[8,128,256]{2,1,0:T(8,128)(2,1)}, u32[]{:S(2)}) copy-start(bf16[8,128,256]{2,1,0:T(8,128)(2,1)} %all_to_all.47.x) | copy-start | bytes 1572868
  747.2 4.2 copy-start.24
  (19 other events, 28.6 us)
Sparse Core Ops, SparseCore 0:
  25.8 79.3 all-gather.6
  108.0 78.7 all-gather.4
  188.4 79.2 all-gather.10
  269.1 45.2 all-gather.8
  448.9 43.5 reduce-scatter.7
  494.6 42.8 reduce-scatter.9
  539.8 76.8 reduce-scatter.11
  618.9 78.6 reduce-scatter.5
  699.9 42.9 reduce-scatter.13

commit v7 on v6

--- a/solution.py
+++ b/solution.py
@@ -349,7 +349,7 @@
     def __init__(self, product, bufs, sems, base, peer, prepare=None, enter=None):
         self.product, self.prepare, self.sems, self.base = product, prepare, sems, base
         self.enter = enter
-        self.po, self.pe, self.rc, self.sb, self.xr, self.yr = bufs
+        self.po, self.pe, self.rc, self.sb, self.ring = bufs
         self.pc, self.px, self.py = peer(1), peer(2), peer(4)
         self.q = self.pe.shape[1] // 4
         self.sent, self.core, self.got = [], {}, ({}, {})
@@ -371,44 +371,50 @@
             self.enter = None
         self.core[i] = self.send(self.po.at[i], self.rc.at[i], self.pc, i)
 
-    def add(self, c, i, lower, out, more=None):
+    def add(self, halves, i, lower, out, more=None):
         step = 16
-
-        @pl.loop(0, self.q // step)
+        steps = self.q // step
+        first, count = halves
+
+        @pl.loop(first * steps, (first + count) * steps)
         def _(j):
-            there = pl.ds(pl.multiple_of(j * step, step), step)
-            here = pl.ds(pl.multiple_of(j * step + (2 * c + lower) * self.q, step), step)
+            c = lax.div(j, steps)
+            there = pl.ds(pl.multiple_of(lax.rem(j, steps) * step, step), step)
+            here = pl.ds(
+                pl.multiple_of(lax.rem(j, steps) * step + (2 * c + lower) * self.q, step), step
+            )
             total = self.pe[i, here, :].astype(f32) + self.rc[i, here, :].astype(f32)
             if more is not None:
-                total = total + more[there, :].astype(f32)
+                total = total + self.ring[more, c, 0, there, :].astype(f32)
             self.sb[c, out, there, :] = total.astype(bf)
 
     def link(self, c, slot, name, ring, at, dev):
         self.got[c][name] = self.send(
-            self.sb.at[c, slot], ring.at[c, at], dev, 4 + 6 * c + slot
+            self.sb.at[c, slot], self.ring.at[ring, c, at], dev, 4 + 6 * c + slot
         )
 
-    def six(self, c):
-        self.add(c, 3, 0, 0)
-        self.link(c, 0, "x6", self.xr, 0, self.px)
-        self.add(c, 3, 1, 1)
-        self.link(c, 1, "y6", self.yr, 0, self.py)
-
-    def two(self, c):
-        self.add(c, 1, 0, 2)
-        self.link(c, 2, "x2", self.xr, 1, self.px)
-
-    def four(self, c):
-        self.add(c, 2, 1, 3)
-        self.link(c, 3, "y4", self.yr, 1, self.py)
+    def both(self, slot, name, i, lower, ring, at, dev):
+        self.add((0, 2), i, lower, slot)
+        for c in (0, 1):
+            self.link(c, slot, name, ring, at, dev)
+
+    def six(self):
+        self.both(0, "x6", 3, 0, 0, 0, self.px)
+        self.both(1, "y6", 3, 1, 1, 0, self.py)
+
+    def two(self):
+        self.both(2, "x2", 1, 0, 0, 1, self.px)
+
+    def four(self):
+        self.both(3, "y4", 2, 1, 1, 1, self.py)
 
     def onward(self, c):
         self.got[c]["x6"].wait_recv()
-        self.add(c, 2, 0, 4, self.xr.at[c, 0])
-        self.link(c, 4, "y4b", self.yr, 2, self.py)
+        self.add((c, 1), 2, 0, 4, 0)
+        self.link(c, 4, "y4b", 1, 2, self.py)
         self.got[c]["y6"].wait_recv()
-        self.add(c, 1, 1, 5, self.yr.at[c, 0])
-        self.link(c, 5, "x2b", self.xr, 2, self.px)
+        self.add((c, 1), 1, 1, 5, 1)
+        self.link(c, 5, "x2b", 0, 2, self.px)
 
     def run(self):
         self.ready(3)
@@ -419,8 +425,7 @@
             if self.prepare is None:
                 self.pair(following)
             self.core[now].wait_recv()
-            for c in (0, 1):
-                stage(c)
+            stage()
             if self.prepare is not None:
                 self.pair(following)
         for c in (0, 1):
@@ -431,20 +436,20 @@
             self.core[0].wait_recv()
         for name in ("x2", "y4", "y4b", "x2b"):
             self.got[c][name].wait_recv()
-        for lower in (0, 1):
-            near, far = (self.yr, self.xr) if lower else (self.xr, self.yr)
-
-            @pl.loop(0, self.q // step)
-            def _(j, lower=lower, near=near, far=far):
-                there = pl.ds(pl.multiple_of(j * step, step), step)
-                here = pl.ds(pl.multiple_of(j * step + (2 * c + lower) * self.q, step), step)
-                body(
-                    here,
-                    self.pe[0, here, :].astype(f32)
-                    + self.rc[0, here, :].astype(f32)
-                    + near[c, 1, there, :].astype(f32)
-                    + far[c, 2, there, :].astype(f32),
-                )
+        steps = self.q // step
+
+        @pl.loop(0, 2 * steps)
+        def _(j):
+            lower = lax.div(j, steps)
+            there = pl.ds(pl.multiple_of(lax.rem(j, steps) * step, step), step)
+            here = pl.ds(pl.multiple_of(j * step + 2 * c * self.q, step), step)
+            body(
+                here,
+                self.pe[0, here, :].astype(f32)
+                + self.rc[0, here, :].astype(f32)
+                + self.ring[lower, c, 1, there, :].astype(f32)
+                + self.ring[1 - lower, c, 2, there, :].astype(f32),
+            )
 
     def finish(self):
         for copy in self.sent:
@@ -458,8 +463,7 @@
         pltpu.VMEM((4, r, c), even),
         pltpu.VMEM((4, r, c), bf),
         pltpu.VMEM((2, 6, q, c), bf),
-        pltpu.VMEM((2, 3, q, c), bf),
-        pltpu.VMEM((2, 3, q, c), bf),
+        pltpu.VMEM((2, 2, 3, q, c), bf),
     ]
 
 
@@ -513,7 +517,7 @@
 
 def forward_kernel(
     nrm, wvs, sco, w, tok, vec, v_out, mix_out, ret_out, swi_out, mid, out,
-    v_buf, mix_buf, ret_buf, swi_buf, po, pe, rc, sb, xr, yr, own, ssem, rsem, local,
+    v_buf, mix_buf, ret_buf, swi_buf, po, pe, rc, sb, ring, own, ssem, rsem, local,
 ):
     _, peer = place()
     enter = greet([peer(1), peer(2), peer(4)])
@@ -589,7 +593,7 @@
             centred * lax.rsqrt(spread + 1e-05) * vec[0:1, :] + vec[1:2, :]
         ).astype(bf)
 
-    reduce = Reduce(product, (po, pe, rc, sb, xr, yr), sems, 0, peer, prepare, enter)
+    reduce = Reduce(product, (po, pe, rc, sb, ring), sems, 0, peer, prepare, enter)
     exchange_and_gather(reduce, both_gathers(own, out, sems, local, peer), 16, body)
     for copy in kept:
         copy.wait()
@@ -620,32 +624,26 @@
     )(nrm, wvs, sco, w, tok, vec)
 
 
-def product_kernel(a, b, out, turned):
-    turned[...] = a[...].reshape(-1, a.shape[-1]).T
-    rows = turned.shape[1]
-
-    @pl.loop(0, out.shape[1] // TILE)
-    def _(j):
-        at = pl.ds(pl.multiple_of(j * TILE, TILE), TILE)
-        out[:, at] = jnp.dot(
-            turned[...], b[:, :, at].reshape(rows, TILE), preferred_element_type=f32
-        ).astype(bf)
+def product_kernel(a, b, out):
+    a, b = a[...].reshape(-1, a.shape[-1]), b[...].reshape(-1, b.shape[-1])
+    out[...] = lax.dot_general(
+        a, b, (((0,), (0,)), ((), ())), preferred_element_type=f32
+    ).astype(bf)
 
 
 def row_product(a, b):
     _, r, m = a.shape
     width = b.shape[2]
-    tile = 512 if m >= 2048 else 256
+    tile, part = 512 if m >= 2048 else 256, min(width, 1024)
     return pl.pallas_call(
         product_kernel,
-        grid=(m // tile,),
+        grid=(width // part, m // tile),
         out_shape=SDS((m, width), bf),
         in_specs=[
-            pl.BlockSpec((TP, r, tile), lambda i: (0, 0, i)),
-            pl.BlockSpec((TP, r, width), lambda i: (0, 0, 0)),
+            pl.BlockSpec((TP, r, tile), lambda j, i: (0, 0, i)),
+            pl.BlockSpec((TP, r, part), lambda j, i: (0, 0, j)),
         ],
-        out_specs=pl.BlockSpec((tile, width), lambda i: (i, 0)),
-        scratch_shapes=[pltpu.VMEM((tile, TP * r), bf)],
+        out_specs=pl.BlockSpec((tile, part), lambda j, i: (i, j)),
         compiler_params=pltpu.CompilerParams(vmem_limit_bytes=56 << 20),
         cost_estimate=pl.CostEstimate(
             flops=2 * TP * r * m * width,
@@ -737,7 +735,7 @@
 
 
 def backward_kernel(
-    a, w, mid, cot, vec, gmid, out, sums, po, pe, rc, sb, xr, yr, own, acc, ssem, rsem, local
+    a, w, mid, cot, vec, gmid, out, sums, po, pe, rc, sb, ring, own, acc, ssem, rsem, local
 ):
     _, peer = place()
     enter = greet([peer(1), peer(2), peer(4)])
@@ -759,7 +757,7 @@
         gmid[at, :] = grad
         own[at, :] = grad.astype(bf)
 
-    reduce = Reduce(times(a, w, True), (po, pe, rc, sb, xr, yr), sems, 0, peer, enter=enter)
+    reduce = Reduce(times(a, w, True), (po, pe, rc, sb, ring), sems, 0, peer, enter=enter)
     exchange_and_gather(reduce, both_gathers(own, out, sems, local, peer), 16, body)
     sums[0:1, :] = jnp.sum(acc[0], axis=0, keepdims=True)
     sums[1:2, :] = jnp.sum(acc[1], axis=0, keepdims=True)
@@ -791,7 +789,7 @@
 
 def last_kernel(
     n, gqkv, gs, wqk, wvs, a2, w2, tok, gmid, gain, sums2, gtok, ffn, vec_out,
-    po, pe, rc, sb, xr, yr, pe2, rc2, sb2, xr2, yr2, acc, vecs, near, far, part, ssem, rsem,
+    po, pe, rc, sb, ring, pe2, rc2, sb2, ring2, acc, vecs, near, far, part, ssem, rsem,
 ):
     dp = n // TP
     me, peer = place()
@@ -816,12 +814,12 @@
             even[:, at] = z[:r].astype(even.dtype)
             odd[:, at] = z[r:].astype(odd.dtype)
 
-    one = Reduce(product, (po, pe, rc, sb, xr, yr), sems, 0, peer, enter=enter)
+    one = Reduce(product, (po, pe, rc, sb, ring), sems, 0, peer, enter=enter)
     one.run()
     for copy in one.core.values():
         copy.wait_send()
     one.sent = [copy for copy in one.sent if all(copy is not c for c in one.core.values())]
-    two = Reduce(times(a2, w2, False), (po, pe2, rc2, sb2, xr2, yr2), sems, REDUCE_SEMS, peer)
+    two = Reduce(times(a2, w2, False), (po, pe2, rc2, sb2, ring2), sems, REDUCE_SEMS, peer)
     two.run()
 
     def body(at, grad):
@@ -903,8 +901,7 @@
     )(gqkv, gs, wqk, wvs, a2, w2, tok, gmid, gain, sums2)
 
 
-def gate_back_kernel(g_low, w, ret, swi, gret, gswi, whole, back):
-    two, r, _ = gret.shape
+def gate_back_kernel(g_low, w, ret, swi, gret, gswi, whole):
     cols = w.shape[2]
 
     @pl.when(pl.program_id(0) == 0)
@@ -912,49 +909,39 @@
         for j in range(w.shape[0]):
             whole[:, j * cols : (j + 1) * cols] = w[j]
 
-    back[...] = lax.dot_general(
-        g_low[...].reshape(two * r, g_low.shape[2]), whole[...], (((1,), (1,)), ((), ())),
-        preferred_element_type=f32,
+    grad = lax.dot_general(
+        g_low[0], whole[...], (((1,), (1,)), ((), ())), preferred_element_type=f32
     )
-    step = 32
-    for i in range(two):
-
-        @pl.loop(0, r // step)
-        def _(j, i=i):
-            at = pl.ds(pl.multiple_of(j * step, step), step)
-            value, gate = ret[i, at, :], swi[i, at, :]
-            grad = back[pl.ds(pl.multiple_of(i * r + j * step, step), step), :]
-            centred = value - jnp.mean(value, axis=-1, keepdims=True)
-            spread = jnp.mean(centred * centred, axis=-1, keepdims=True)
-            inv = lax.rsqrt(jnp.maximum(spread, 0.25))
-            share = 1.0 / (1.0 + jnp.exp(-gate))
-            silu = gate * share
-            gswi[i, at, :] = (
-                grad * (centred * inv) * (share * (1.0 + gate * (1.0 - share)))
-            ).astype(bf)
-            grad = grad * silu
-            pull = jnp.mean(grad * centred, axis=-1, keepdims=True)
-            pull = jnp.where(spread > 0.25, inv * inv * inv * pull, 0.0)
-            grad = grad * inv - centred * pull
-            gret[i, at, :] = (grad - jnp.mean(grad, axis=-1, keepdims=True)).astype(bf)
+    value, gate = ret[0], swi[0]
+    centred = value - jnp.mean(value, axis=-1, keepdims=True)
+    spread = jnp.mean(centred * centred, axis=-1, keepdims=True)
+    inv = lax.rsqrt(jnp.maximum(spread, 0.25))
+    share = 1.0 / (1.0 + jnp.exp(-gate))
+    silu = gate * share
+    gswi[0] = (grad * (centred * inv) * (share * (1.0 + gate * (1.0 - share)))).astype(bf)
+    grad = grad * silu
+    pull = jnp.mean(grad * centred, axis=-1, keepdims=True)
+    pull = jnp.where(spread > 0.25, inv * inv * inv * pull, 0.0)
+    grad = grad * inv - centred * pull
+    gret[0] = (grad - jnp.mean(grad, axis=-1, keepdims=True)).astype(bf)
 
 
 def gate_back(g_low, w, ret, swi):
     _, r, d = g_low.shape
     width = ret.shape[2]
-    row = pl.BlockSpec((2, r, width), lambda k: (k, 0, 0))
+    row = pl.BlockSpec((1, r, width), lambda k: (k, 0, 0))
     return pl.pallas_call(
         gate_back_kernel,
-        grid=(TP // 2,),
+        grid=(TP,),
         out_shape=(SDS(ret.shape, bf), SDS(ret.shape, bf)),
         in_specs=[
-            pl.BlockSpec((2, r, d), lambda k: (k, 0, 0)),
+            pl.BlockSpec((1, r, d), lambda k: (k, 0, 0)),
             pl.BlockSpec(w.shape, lambda k: (0, 0, 0)),
             row,
             row,
         ],
         out_specs=(row, row),
-        scratch_shapes=[pltpu.VMEM((width, d), bf), pltpu.VMEM((2 * r, width), f32)],
+        scratch_shapes=[pltpu.VMEM((width, d), bf)],
         compiler_params=pltpu.CompilerParams(vmem_limit_bytes=56 << 20),
         cost_estimate=pl.CostEstimate(
             flops=2 * TP * r * d * width, bytes_accessed=22 << 20, transcendentals=TP * r * width

time: 763 us -> 748 us (0.980)
  Pallas kernels: 573 us -> 544 us
  waiting for transfers between devices: 60.3 us -> 74.8 us
    pallas_call x6, Pallas kernels: 100 us -> 70 us  [the longest x5 56 us: row_product(): pl.pallas_call(product_kernel, grid=(width // part, m // tile), out_shape...]
    reduce_scatter x5, waiting for transfers between devices: 56.8 us -> 71.6 us  [dp_reduce(): lax.psum_scatter(x, AXIS, scatter_dimension=0, tiled=True, axis_index_gro...]
  transfers between devices with their start and end apart: 11 -> 11, of which waited for: 3 -> 3; matrix products, arithmetic and copies ran while one was open for 3% -> 3% of each run, Pallas kernels for 56% -> 55%
where the time goes in v7:
time: 748 us; the launch traced here: 744 us
  Pallas kernels  544 us (73%)
  waiting for transfers between devices  74.8 us (10%)
  blocking collectives  57.1 us (8%)
  local copies, waits for them, and re-layouts  29.5 us (4%)
  between operations  14.4 us (2%)
  other arithmetic  13.9 us (2%)
  starting transfers between devices  11 us (1%)
    pallas_call x4, Pallas kernels, exchange_call(): pl.pallas_call(kernel, out_shape=outs, in_specs=specs or [VMEM] * len(arg...  150 us
    pallas_call x1, Pallas kernels, forward_exchange(): pl.pallas_call(forward_kernel, out_shape=tuple((SDS(*b) for b in blocks))...  105 us
    pallas_call x1, Pallas kernels, last_exchange(): pl.pallas_call(functools.partial(last_kernel, n), out_shape=(SDS((r, c),...  90.9 us
    pallas_call x1, Pallas kernels, backward_exchange(): pl.pallas_call(backward_kernel, out_shape=(SDS((r, c), f32), SDS((TP, r,...  84.4 us
    reduce_scatter x5, waiting for transfers between devices, dp_reduce(): lax.psum_scatter(x, AXIS, scatter_dimension=0, tiled=True, axis_index_gro...  71.6 us
    all_to_all x3, blocking collectives, plane_a2a(): lax.all_to_all(x, AXIS, 0, 0, axis_index_groups=tp_groups(n), tiled=True)  57.1 us
    pallas_call x5, Pallas kernels, row_product(): pl.pallas_call(product_kernel, grid=(width // part, m // tile), out_shape...  56 us
    unnamed x67, local copies, waits for them, and re-layouts  24.2 us
  transfers between devices with their start and end apart: 11, of which 3 were waited for; matrix products, arithmetic and copies ran while one was open for 3% of the time, Pallas kernels for 55%

profile of v7, /device:TPU:14, one launch (start us, length us, event | category | flops | bytes accessed | tf_op | source)
XLA Modules:
  0.0 744.5 jit_solution(2143249453412217993)
XLA Ops:
  10.2 15.4 %shard_map.254 = bf16[8,64,1024]{2,1,0:T(8,128)(2,1)} custom-call(bf16[64,2048]{1,0:T(8,128)(2,1)S(1)} %copy-done.19, bf16[64,2048]{1,0:T(8,128)(2,1)S(1)} %copy-done.20, bf16[128,2048]{1,0:T(8,128)(2,1)S(1)} %copy-done.18), custom_call_target="tpu_custom_call" | custom-call | tf_op jit(solution)/shard_map/pallas_call | solution.py:143
  28.1 41.8 %shard_map.255 = (bf16[8,256,2048]{2,1,0:T(8,128)(2,1)S(1)}, f32[4,8,8,128]{3,2,1,0:T(8,128)S(1)}) custom-call(bf16[256,2048]{1,0:T(8,128)(2,1)S(1)} %copy-done.4, f32[8,128]{1,0:T(8,128)S(1)} %pad.9.vec), custom_call_target="tpu_custom_call" | custom-call | tf_op jit(solution)/shard_map/pallas_call | solution.py:143
  78.1 26.4 %shard_map.256 = (bf16[8,64,1024]{2,1,0:T(8,128)(2,1)}, bf16[8,64,1024]{2,1,0:T(8,128)(2,1)}, bf16[8,256,2048]{2,1,0:T(8,128)(2,1)S(1)}) custom-call(bf16[64,4096]{1,0:T(8,128)(2,1)S(1)} %copy-done.16, bf16[64,4096]{1,0:T(8,128)(2,1)S(1)} %copy-done.17, bf16[8,64,1024]{2,1,0:T(8,128)(2,1)S(1)} %pad_maximum_fusion.gu, bf16[8,256,2048]{2,1,0:T(8,128)(2,1)S(1)} %copy-done.7, ...), custom_call_target="tpu_custom_call" | custom-call | tf_op jit(solution)/shard_map/pallas_call | solution.py:143
  110.8 5.3 multiply_sine_fusion
  120.2 66.1 %shard_map.257 = (bf16[8,256,2048]{2,1,0:T(8,128)(2,1)}, bf16[8,4,2,64,256]{4,3,2,1,0:T(8,128)(2,1)S(1)}, bf16[8,256,256]{2,1,0:T(8,128)(2,1)S(1)}, bf16[8,256,2...) custom-call(bf16[256,2048]{1,0:T(8,128)(2,1)S(1)} %copy-done.8, ...), custom_call_target="tpu_custom_call" | custom-call | tf_op jit(solution)/shard_map/pallas_call | solution.py:143
  192.0 104.8 %forward_exchange.1 = (bf16[8,256,512]{2,1,0:T(8,128)(2,1)}, bf16[8,256,512]{2,1,0:T(8,128)(2,1)}, f32[8,256,512]{2,1,0:T(8,128)}, f32[8,256,512]{2,1,0:T(8,128)...) custom-call(bf16[8,256,2048]{2,1,0:T(8,128)(2,1)} %copy-done, bf16[2048,1024]{1,0:T(8,128)(2,1)} %all-gather.5.cloned.1.call-done.wvs, ...), custom_call_target="tpu_custom_call" | custom-call | tf_op jit(solution)/shard_map/forward_exchange/pallas_call | solution.py:607
  296.8 15.8 %hidden_units.1 = (bf16[8,256,512]{2,1,0:T(8,128)(2,1)}, f32[8,256,512]{2,1,0:T(8,128)}, f32[8,256,512]{2,1,0:T(8,128)}) custom-call(bf16[8,256,2048]{2,1,0:T(8,128)(2,1)} %get-tuple-element.60.x.a, bf16[2048,1024]{1,0:T(8,128)(2,1)} %all-gather.11.cloned.1.call-done.gu.w), custom_call_target="tpu_custom_call" | custom-call | flops 8589934592 | bytes 25165824 | tf_op jit(solution)/shard_map/hidden_units/pallas_call | solution.py:681
  314.4 11.8 %hidden_back.1.a.b = bf16[8,256,1024]{2,1,0:T(8,128)(2,1)} custom-call(bf16[8,256,2048]{2,1,0:T(8,128)(2,1)} %get-tuple-element.59.cot.b, bf16[512,2048]{1,0:T(8,128)(2,1)} %all-gather.9.cloned.1.call-done.down.w2, f32[8,256,512]{2,1,0:T(8,128)} %get-tuple-element.62.act, f32[8,256,512]{2,1,0:T(8,128)} %get-tuple-element.63.slope), custom_call_target="tpu_custom_call" | custom-call | flops 4294967296 | bytes 25165824 | tf_op jit(solution)/shard_map/hidden_back/pallas_call | solution.py:718
  326.2 84.4 %backward_exchange.1 = (f32[256,2048]{1,0:T(8,128)}, bf16[8,256,2048]{2,1,0:T(8,128)(2,1)}, f32[2,2048]{1,0:T(2,128)S(1)}) custom-call(bf16[8,256,1024]{2,1,0:T(8,128)(2,1)} %hidden_back.1.a.b, bf16[2048,1024]{1,0:T(8,128)(2,1)} %all-gather.11.cloned.1.call-done.gu.w, f32[256,2048]{1,0:T(8,128)} %get-tuple-element.55.mid, bf16[256,2048]{1,0:T(8,128)(2,1)S(1)} %copy-done.9, ...), custom_call_target="tpu_custom_call" | custom-call | tf_op jit(solution)/shard_map/backward_exchange/pallas_call | solution.py:770
  411.2 14.0 %gate_back.1 = (bf16[8,256,512]{2,1,0:T(8,128)(2,1)}, bf16[8,256,512]{2,1,0:T(8,128)(2,1)}) custom-call(bf16[8,256,2048]{2,1,0:T(8,128)(2,1)} %get-tuple-element.64.g_low.b, bf16[8,512,256]{2,1,0:T(8,128)(2,1)} %bitcast.56, f32[8,256,512]{2,1,0:T(8,128)} %get-tuple-element.65.ret, f32[8,256,512]{2,1,0:T(8,128)} %get-tuple-element.66.swi), custom_call_target="tpu_custom_call" | custom-call | flops 4294967296 | bytes 23068672 | tf_op jit(solution)/shard_map/gate_back/pallas_call | solution.py:933
  425.2 8.8 %row_product.6 = bf16[2048,512]{1,0:T(8,128)(2,1)} custom-call(bf16[8,256,2048]{2,1,0:T(8,128)(2,1)} %copy-done, bf16[8,256,512]{2,1,0:T(8,128)(2,1)} %get-tuple-element.68.gs.b), custom_call_target="tpu_custom_call" | custom-call | flops 4294967296 | bytes 12582912 | tf_op jit(solution)/shard_map/row_product/pallas_call | solution.py:638
  434.0 10.1 %row_product.7 = bf16[512,2048]{1,0:T(8,128)(2,1)} custom-call(bf16[8,256,512]{2,1,0:T(8,128)(2,1)} %get-tuple-element.79.a, bf16[8,256,2048]{2,1,0:T(8,128)(2,1)} %get-tuple-element.64.g_low.b), custom_call_target="tpu_custom_call" | custom-call | flops 4294967296 | bytes 12582912 | tf_op jit(solution)/shard_map/row_product/pallas_call | solution.py:638
  445.9 29.5 %all_to_all.45 = bf16[8,512,256]{2,1,0:T(8,128)(2,1)} all-to-all(bf16[8,512,256]{2,1,0:T(8,128)(2,1)S(1)} %bitcast.59), channel_id=1, replica_groups={{0,1,2,3,4,5,6,7},{8,9,10,11,12,13,14,15},{16,17,18,19,20,21,22,23},{24..., dimensions={0} | all-to-all | bytes 4194304 | tf_op jit(solution)/shard_map/all_to_all | solution.py:999
  475.5 13.4 %row_product.8 = bf16[2048,1024]{1,0:T(8,128)(2,1)} custom-call(bf16[8,256,2048]{2,1,0:T(8,128)(2,1)} %get-tuple-element.60.x.a, bf16[8,256,1024]{2,1,0:T(8,128)(2,1)} %hidden_back.1.a.b), custom_call_target="tpu_custom_call" | custom-call | flops 8589934592 | bytes 16777216 | tf_op jit(solution)/shard_map/row_product/pallas_call | solution.py:638
  489.0 10.2 %scores_back.1.gqkv.b = bf16[8,256,1024]{2,1,0:T(8,128)(2,1)} custom-call(bf16[8,256,256]{2,1,0:T(8,128)(2,1)} %copy-done.10, f32[8,256,256]{2,1,0:T(8,128)} %copy-done.1, bf16[8,256,256]{2,1,0:T(8,128)(2,1)} %copy-done.14, bf16[8,256,256]{2,1,0:T(8,128)(2,1)} %copy-done.15, bf16[8,256,512]{2,1,0:T(8,128)(2,1)} %get-tuple-element.58.v, ...), custom_call_target="tpu_custom_call" | custom-call | flops 1610612736 | bytes 16777216 | tf_op jit(solution)/shard_map/scores_back/pallas_call | solution.py:976
  499.1 13.5 %row_product.5 = bf16[2048,1024]{1,0:T(8,128)(2,1)} custom-call(bf16[8,256,2048]{2,1,0:T(8,128)(2,1)} %copy-done, bf16[8,256,1024]{2,1,0:T(8,128)(2,1)} %scores_back.1.gqkv.b), custom_call_target="tpu_custom_call" | custom-call | flops 8589934592 | bytes 16777216 | tf_op jit(solution)/shard_map/row_product/pallas_call | solution.py:638
  512.7 10.2 %row_product.9 = bf16[512,2048]{1,0:T(8,128)(2,1)} custom-call(bf16[8,256,512]{2,1,0:T(8,128)(2,1)} %get-tuple-element.70.a2.a, bf16[8,256,2048]{2,1,0:T(8,128)(2,1)} %get-tuple-element.59.cot.b), custom_call_target="tpu_custom_call" | custom-call | flops 4294967296 | bytes 12582912 | tf_op jit(solution)/shard_map/row_product/pallas_call | solution.py:638
  522.9 13.7 %all_to_all.46.x = bf16[8,64,512]{2,1,0:T(8,128)(2,1)} all-to-all(bf16[8,64,512]{2,1,0:T(8,128)(2,1)} %bitcast.70), channel_id=1, replica_groups={{0,1,2,3,4,5,6,7},{8,9,10,11,12,13,14,15},{16,17,18,19,20,21,22,23},{24..., dimensions={0} | all-to-all | bytes 1048576 | tf_op jit(solution)/shard_map/all_to_all | solution.py:999
  536.6 13.8 %all_to_all.47.x = bf16[8,128,256]{2,1,0:T(8,128)(2,1)} all-to-all(bf16[8,128,256]{2,1,0:T(8,128)(2,1)} %bitcast.71), channel_id=1, replica_groups={{0,1,2,3,4,5,6,7},{8,9,10,11,12,13,14,15},{16,17,18,19,20,21,22,23},{24..., dimensions={0} | all-to-all | bytes 1048576 | tf_op jit(solution)/shard_map/all_to_all | solution.py:999
  550.5 51.4 %reduce-scatter.12.cloned.1.call-done = bf16[512,1024]{1,0:T(8,128)(2,1)} async-done(((bf16[2048,1024]{1,0:T(8,128)(2,1)}), bf16[512,1024]{1,0:T(8,128)(2,1)}) %reduce-scatter.12.cloned.1.call-update) | async-done | bytes 1048592 | tf_op jit(solution)/shard_map/reduce_scatter | solution.py:1007
  601.8 4.7 all-to-all-start.4
  606.5 90.9 %last_exchange.1 = (f32[256,2048]{1,0:T(8,128)}, f32[256,2048]{1,0:T(8,128)}, f32[8,512]{1,0:T(8,128)}) custom-call(bf16[8,256,1024]{2,1,0:T(8,128)(2,1)} %scores_back.1.gqkv.b, bf16[8,256,512]{2,1,0:T(8,128)(2,1)} %get-tuple-element.68.gs.b, bf16[2048,512]{1,0:T(8,128)(2,1)} %bitcast.57, bf16[2048,1024]{1,0:T(8,128)(2,1)} %all-gather.5.cloned.1.call-done.wvs, ...), custom_call_target="tpu_custom_call" | custom-call | tf_op jit(solution)/shard_map/last_exchange/pallas_call | solution.py:881
  697.4 5.7 all-to-all-start
  708.0 20.2 %reduce-scatter.14.cloned.1.call-done = bf16[128,2048]{1,0:T(8,128)(2,1)} async-done(((bf16[512,2048]{1,0:T(8,128)(2,1)}), bf16[128,2048]{1,0:T(8,128)(2,1)}) %reduce-scatter.14.cloned.1.call-update) | async-done | bytes 524304 | tf_op jit(solution)/shard_map/reduce_scatter | solution.py:1007
  (133 shorter events, 48.2 us)
Async XLA Ops:
  7.2 109.8 %all-gather.7.cloned.1.call-start = ((), (), s32[]{:S(2)}) async-start(), calls=%async_computation.11 | async-start | bytes 5242880 | tf_op jit(solution)/shard_map/all_gather | solution.py:1003
  10.2 15.5 %copy-start.25 = (bf16[64,4096]{1,0:T(8,128)(2,1)S(1)}, bf16[64,4096]{1,0:T(8,128)(2,1)}, u32[]{:S(2)}) copy-start(bf16[64,4096]{1,0:T(8,128)(2,1)} %param.26) | copy-start | bytes 1572868
  25.6 166.3 %all-gather.5.cloned.1.call-start = ((), (), s32[]{:S(2)}) async-start(), calls=%async_computation.10 | async-start | bytes 5242880 | tf_op jit(solution)/shard_map/all_gather | solution.py:1003
  27.0 47.8 %copy-start.16 = (bf16[64,4096]{1,0:T(8,128)(2,1)S(1)}, bf16[64,4096]{1,0:T(8,128)(2,1)}, u32[]{:S(2)}) copy-start(bf16[64,4096]{1,0:T(8,128)(2,1)} %wv.1) | copy-start | bytes 1572868
  27.0 47.8 %copy-start.17 = (bf16[64,4096]{1,0:T(8,128)(2,1)S(1)}, bf16[64,4096]{1,0:T(8,128)(2,1)}, u32[]{:S(2)}) copy-start(bf16[64,4096]{1,0:T(8,128)(2,1)} %ws.1) | copy-start | bytes 1572868
  69.9 3.3 copy-start.6
  73.5 31.1 %copy-start.22 = (f32[1,2048]{1,0:T(1,128)}, f32[1,2048]{1,0:T(1,128)S(1)}, u32[]{:S(2)}) copy-start(f32[1,2048]{1,0:T(1,128)S(1)} %reshape_squeeze.12.gain) | copy-start | bytes 24580
  74.7 3.4 copy-start.7
  107.9 188.9 %all-gather.11.cloned.1.call-start = ((), (), s32[]{:S(2)}) async-start(), calls=%async_computation.13 | async-start | bytes 5242880 | tf_op jit(solution)/shard_map/all_gather | solution.py:1003
  108.6 205.8 %all-gather.9.cloned.1.call-start = ((), (), s32[]{:S(2)}) async-start(), calls=%async_computation.12 | async-start | bytes 2621440 | tf_op jit(solution)/shard_map/all_gather | solution.py:1003
  109.2 413.7 %reduce-scatter.8.cloned.1.call-start = ((), (), s32[]{:S(2)}) async-start(), calls=%async_computation.15 | async-start | bytes 2621440 | tf_op jit(solution)/shard_map/reduce_scatter | solution.py:1007
  116.1 70.2 %copy-start.2 = (f32[8,256,128]{2,1,0:T(8,128)}, f32[8,256,128]{2,1,0:T(8,128)S(1)}, u32[]{:S(2)}) copy-start(f32[8,256,128]{2,1,0:T(8,128)S(1)} %get-tuple-element.86.sine) | copy-start | bytes 3145732
  116.9 69.4 %copy-start.1 = (f32[8,256,256]{2,1,0:T(8,128)}, f32[8,256,256]{2,1,0:T(8,128)S(1)}, u32[]{:S(2)}) copy-start(f32[8,256,256]{2,1,0:T(8,128)S(1)} %fusion.4.mask) | copy-start | bytes 6291460
  314.4 11.8 %copy-start.9 = (bf16[256,2048]{1,0:T(8,128)(2,1)S(1)}, bf16[256,2048]{1,0:T(8,128)(2,1)}, u32[]{:S(2)}) copy-start(bf16[256,2048]{1,0:T(8,128)(2,1)} %cot.3) | copy-start | bytes 3145732
  314.4 11.8 %copy-start.21 = (f32[2,2048]{1,0:T(2,128)S(1)}, f32[2,2048]{1,0:T(2,128)}, u32[]{:S(2)}) copy-start(f32[2,2048]{1,0:T(2,128)} %pad_maximum_fusion.1.vec) | copy-start | bytes 49156
  434.0 102.6 %reduce-scatter.10.cloned.1.call-start = ((), (), s32[]{:S(2)}) async-start(), calls=%async_computation.16 | async-start | bytes 2621440 | tf_op jit(solution)/shard_map/reduce_scatter | solution.py:1007
  475.4 126.4 %reduce-scatter.12.cloned.1.call-start = ((), (), s32[]{:S(2)}) async-start(), calls=%async_computation.17 | async-start | bytes 5242880 | tf_op jit(solution)/shard_map/reduce_scatter | solution.py:1007
  488.9 208.5 %reduce-scatter.6.cloned.1.call-start = ((), (), s32[]{:S(2)}) async-start(), calls=%async_computation.14 | async-start | bytes 5242880 | tf_op jit(solution)/shard_map/reduce_scatter | solution.py:1007
  512.6 215.6 %reduce-scatter.14.cloned.1.call-start = ((), (), s32[]{:S(2)}) async-start(), calls=%async_computation.18 | async-start | bytes 2621440 | tf_op jit(solution)/shard_map/reduce_scatter | solution.py:1007
  601.8 95.6 %all-to-all-start.4 = ((bf16[8,64,1024]{2,1,0:T(8,128)(2,1)}), bf16[8,64,1024]{2,1,0:T(8,128)(2,1)}, u32[]{:S(2)}, u32[]{:S(2)}) async-start(bf16[8,64,1024]{2,1,0:T(8,128)(2,1)} %bitcast.67), calls=%async_computation.8 | async-start | bytes 2097152 | tf_op jit(solution)/shard_map/all_to_all | solution.py:999
  697.4 37.8 %all-to-all-start = ((bf16[8,64,1024]{2,1,0:T(8,128)(2,1)}), bf16[8,64,1024]{2,1,0:T(8,128)(2,1)S(1)}, u32[]{:S(2)}, u32[]{:S(2)}) async-start(bf16[8,64,1024]{2,1,0:T(8,128)(2,1)} %bitcast.66), calls=%async_computation.1 | async-start | bytes 2097152 | tf_op jit(solution)/shard_map/all_to_all | solution.py:999
  704.5 25.8 %copy-start.11 = (bf16[8,64,512]{2,1,0:T(8,128)(2,1)S(1)}, bf16[8,64,512]{2,1,0:T(8,128)(2,1)}, u32[]{:S(2)}) copy-start(bf16[8,64,512]{2,1,0:T(8,128)(2,1)} %all_to_all.46.x) | copy-start | bytes 1572868
  708.0 23.3 %copy-start.12 = (bf16[8,128,256]{2,1,0:T(8,128)(2,1)S(1)}, bf16[8,128,256]{2,1,0:T(8,128)(2,1)}, u32[]{:S(2)}) copy-start(bf16[8,128,256]{2,1,0:T(8,128)(2,1)} %all_to_all.47.x) | copy-start | bytes 1572868
  732.4 4.2 copy-start.24
  (19 other events, 28.6 us)
Sparse Core Ops, SparseCore 0:
  25.8 79.3 all-gather.6
  108.0 78.7 all-gather.4
  188.4 79.2 all-gather.10
  269.1 45.2 all-gather.8
  434.1 43.5 reduce-scatter.7
  479.8 42.8 reduce-scatter.9
  525.0 76.7 reduce-scatter.11
  604.1 78.6 reduce-scatter.5
  685.1 42.9 reduce-scatter.13

commit v8 on v7

--- a/solution.py
+++ b/solution.py
@@ -342,7 +342,7 @@
 
 
 REDUCE_SEMS = 16
-TILE = 256
+WIDE = 1024
 
 
 class Reduce:
@@ -350,26 +350,21 @@
         self.product, self.prepare, self.sems, self.base = product, prepare, sems, base
         self.enter = enter
         self.po, self.pe, self.rc, self.sb, self.ring = bufs
-        self.pc, self.px, self.py = peer(1), peer(2), peer(4)
+        self.pc = peer(1)
+        px, py = peer(2), peer(4)
+        self.slots = ((0, 0, px), (1, 0, py), (0, 1, px), (1, 1, py), (1, 2, py), (0, 2, px))
         self.q = self.pe.shape[1] // 4
-        self.sent, self.core, self.got = [], {}, ({}, {})
-
-    def send(self, src, dst, dev, i):
-        copy = remote(src, dst, self.sems, self.base + i, dev)
-        copy.start()
-        self.sent.append(copy)
-        return copy
-
-    def ready(self, i):
-        if self.prepare is not None:
-            self.prepare(2 * i)
-
-    def pair(self, i):
-        self.product(i, self.po.at[i], self.pe.at[i])
-        if self.enter is not None:
-            self.enter()
-            self.enter = None
-        self.core[i] = self.send(self.po.at[i], self.rc.at[i], self.pc, i)
+        self.waiting = True
+
+    def core(self, i):
+        return remote(self.po.at[i], self.rc.at[i], self.sems, self.base + i, self.pc)
+
+    def link(self, c, slot):
+        axis, at, dev = self.slots[slot]
+        return remote(
+            self.sb.at[c, slot], self.ring.at[axis, c, at], self.sems,
+            self.base + 4 + 6 * c + slot, dev,
+        )
 
     def add(self, halves, i, lower, out, more=None):
         step = 16
@@ -388,58 +383,63 @@
                 total = total + self.ring[more, c, 0, there, :].astype(f32)
             self.sb[c, out, there, :] = total.astype(bf)
 
-    def link(self, c, slot, name, ring, at, dev):
-        self.got[c][name] = self.send(
-            self.sb.at[c, slot], self.ring.at[ring, c, at], dev, 4 + 6 * c + slot
-        )
-
-    def both(self, slot, name, i, lower, ring, at, dev):
+    def both(self, slot, i, lower):
         self.add((0, 2), i, lower, slot)
         for c in (0, 1):
-            self.link(c, slot, name, ring, at, dev)
+            self.link(c, slot).start()
 
     def six(self):
-        self.both(0, "x6", 3, 0, 0, 0, self.px)
-        self.both(1, "y6", 3, 1, 1, 0, self.py)
+        self.core(3).wait_recv()
+        self.both(0, 3, 0)
+        self.both(1, 3, 1)
 
     def two(self):
-        self.both(2, "x2", 1, 0, 0, 1, self.px)
+        self.core(1).wait_recv()
+        self.both(2, 1, 0)
 
     def four(self):
-        self.both(3, "y4", 2, 1, 1, 1, self.py)
+        self.core(2).wait_recv()
+        self.both(3, 2, 1)
 
     def onward(self, c):
-        self.got[c]["x6"].wait_recv()
+        self.link(c, 0).wait_recv()
         self.add((c, 1), 2, 0, 4, 0)
-        self.link(c, 4, "y4b", 1, 2, self.py)
-        self.got[c]["y6"].wait_recv()
+        self.link(c, 4).start()
+        self.link(c, 1).wait_recv()
         self.add((c, 1), 1, 1, 5, 1)
-        self.link(c, 5, "x2b", 0, 2, self.px)
+        self.link(c, 5).start()
+
+    def pair(self, it, i):
+        self.product(it, i, self.po.at[i], self.pe.at[i])
+        self.core(i).start()
 
     def run(self):
-        self.ready(3)
-        self.pair(3)
-        stages = ((1, 3, self.six), (2, 1, self.two), (0, 2, self.four))
-        for following, now, stage in stages:
-            self.ready(following)
-            if self.prepare is None:
-                self.pair(following)
-            self.core[now].wait_recv()
-            stage()
+        if self.enter is not None:
+            self.enter()
+
+        @pl.loop(0, 4)
+        def _(it):
+            i = pair_at(it)
             if self.prepare is not None:
-                self.pair(following)
+                self.prepare(it, i)
+            else:
+                self.pair(it, i)
+            for k, stage in ((1, self.six), (2, self.two), (3, self.four)):
+                pl.when(it == k)(stage)
+            if self.prepare is not None:
+                self.pair(it, i)
+
         for c in (0, 1):
             self.onward(c)
 
-    def rows(self, c, step, body):
+    def rows(self, c, step, body, unroll=2):
         if c == 0:
-            self.core[0].wait_recv()
-        for name in ("x2", "y4", "y4b", "x2b"):
-            self.got[c][name].wait_recv()
+            self.core(0).wait_recv()
+        for slot in (2, 3, 4, 5):
+            self.link(c, slot).wait_recv()
         steps = self.q // step
 
-        @pl.loop(0, 2 * steps)
-        def _(j):
+        def some(j, _):
             lower = lax.div(j, steps)
             there = pl.ds(pl.multiple_of(lax.rem(j, steps) * step, step), step)
             here = pl.ds(pl.multiple_of(j * step + 2 * c * self.q, step), step)
@@ -450,10 +450,46 @@
                 + self.ring[lower, c, 1, there, :].astype(f32)
                 + self.ring[1 - lower, c, 2, there, :].astype(f32),
             )
+            return 0
+
+        lax.fori_loop(0, 2 * steps, some, 0, unroll=unroll)
+
+    def core_sent(self):
+        for i in range(4):
+            self.core(i).wait_send()
+        self.waiting = False
 
     def finish(self):
-        for copy in self.sent:
-            copy.wait_send()
+        if self.waiting:
+            self.core_sent()
+        for c in (0, 1):
+            for slot in range(6):
+                self.link(c, slot).wait_send()
+
+
+def pair_at(it):
+    return it + 3 * (1 - lax.div(it + 2, 3)) - 3 * lax.div(it, 3)
+
+
+class Load:
+    def __init__(self, sems):
+        self.sems, self.count = sems, 0
+
+    def whole(self, src, dst):
+        copy = pltpu.make_async_copy(src, dst, self.sems.at[self.count])
+        self.count += 1
+        copy.start()
+        return copy.wait
+
+    def paired(self, src, dst):
+        base = self.count
+        self.count += 4
+
+        def piece(i):
+            two = pl.ds(2 * i, 2)
+            return pltpu.make_async_copy(src.at[two], dst.at[two], self.sems.at[base + i])
+
+        return piece
 
 
 def reduce_scratch(r, c, even=f32):
@@ -472,13 +508,14 @@
     return a[pl.ds(2 * i, two)].reshape(two * r, k)
 
 
-def times(a, w, nt):
-    def product(i, odd, even):
+def times(a, w, nt, arrive):
+    def product(it, i, odd, even):
         r = a.shape[1]
-
-        @pl.loop(0, even.shape[1] // TILE)
+        arrive(it, i)
+
+        @pl.loop(0, even.shape[1] // WIDE)
         def _(j):
-            at = pl.ds(pl.multiple_of(j * TILE, TILE), TILE)
+            at = pl.ds(pl.multiple_of(j * WIDE, WIDE), WIDE)
             x = rows_of_pair(a, i)
             if nt:
                 y = lax.dot_general(
@@ -492,8 +529,10 @@
     return product
 
 
-def exchange_and_gather(reduce, gathers, step, body):
+def exchange_and_gather(reduce, gathers, step, body, arrivals):
     reduce.run()
+    for arrive in arrivals:
+        arrive()
     for c in (0, 1):
         reduce.rows(c, step, body)
         gathers[c].start()
@@ -516,43 +555,47 @@
 
 
 def forward_kernel(
-    nrm, wvs, sco, w, tok, vec, v_out, mix_out, ret_out, swi_out, mid, out,
-    v_buf, mix_buf, ret_buf, swi_buf, po, pe, rc, sb, ring, own, ssem, rsem, local,
+    nrm_in, wvs_in, sco, w_in, tok_in, vec, v_out, mix_out, ret_out, swi_out, mid, out,
+    nrm, wvs, w, tok, v_buf, mix_buf, ret_buf, swi_buf, po, pe, rc, sb, ring, own,
+    ssem, rsem, local, load,
 ):
     _, peer = place()
     enter = greet([peer(1), peer(2), peer(4)])
     sems = (ssem, rsem)
     r, width = v_buf.shape[1:]
-    kept = []
-
-    def prepare(first):
+    loads = Load(load)
+    nrm_piece = loads.paired(nrm_in, nrm)
+    nrm_piece(3).start()
+    wvs_here = loads.whole(wvs_in, wvs)
+    w_here = loads.whole(w_in, w)
+    for i in (1, 2, 0):
+        nrm_piece(i).start()
+    tok_here = loads.whole(tok_in, tok)
+    kept = ((v_buf, v_out), (mix_buf, mix_out), (ret_buf, ret_out), (swi_buf, swi_out))
+
+    def keep(i):
+        two = pl.ds(2 * i, 2)
+        return [
+            pltpu.make_async_copy(src.at[two], dst.at[two], local.at[2 + 4 * i + j])
+            for j, (src, dst) in enumerate(kept)
+        ]
+
+    def prepare(it, i):
+        first = 2 * i
         two = pl.ds(first, 2)
+        pl.when(it == 0)(wvs_here)
+        nrm_piece(i).wait()
         x = nrm[two].reshape(2 * r, nrm.shape[2])
-
-        tiles = width // TILE
-
-        @pl.loop(0, 2 * tiles)
-        def _(j):
-            at = pl.ds(pl.multiple_of(j * TILE, TILE), TILE)
-            y = jnp.dot(x, wvs[:, at], preferred_element_type=f32)
-            y = y.reshape(2, r, TILE)
-
-            @pl.when(j < tiles)
-            def _():
-                v_buf[two, :, at] = y.astype(bf)
-
-            @pl.when(j >= tiles)
-            def _():
-                swi_buf[two, :, pl.ds(pl.multiple_of(j * TILE - width, TILE), TILE)] = y
-
-        @pl.loop(0, 2 * tiles)
-        def _(j):
-            k = first + lax.div(j, tiles)
-            at = pl.ds(pl.multiple_of(lax.rem(j, tiles) * TILE, TILE), TILE)
-            ret_buf[k, :, at] = jnp.dot(sco[k], v_buf[k, :, at], preferred_element_type=f32)
-
-        @pl.loop(0, 2 * r // 32)
-        def _(j):
+        v = jnp.dot(x, wvs[:, :width], preferred_element_type=f32).astype(bf)
+        v_buf[two] = v.reshape(2, r, width)
+        for k in (0, 1):
+            ret_buf[first + k] = jnp.dot(
+                sco[first + k], v[k * r : (k + 1) * r], preferred_element_type=f32
+            )
+        s = jnp.dot(x, wvs[:, width:], preferred_element_type=f32)
+        swi_buf[two] = s.reshape(2, r, width)
+
+        def gated(j, _):
             k = first + lax.div(j, r // 32)
             at = pl.ds(pl.multiple_of(lax.rem(j, r // 32) * 32, 32), 32)
             value = ret_buf[k, at, :]
@@ -563,25 +606,24 @@
             mix_buf[k, at, :] = (
                 gate * (centred * lax.rsqrt(jnp.maximum(spread, 0.25)))
             ).astype(bf)
-
-        for i, (src, dst) in enumerate(
-            ((v_buf, v_out), (mix_buf, mix_out), (ret_buf, ret_out), (swi_buf, swi_out))
-        ):
-            copy = pltpu.make_async_copy(
-                src.at[two], dst.at[two], local.at[2 + 2 * first + i]
-            )
+            return 0
+
+        lax.fori_loop(0, 2 * r // 32, gated, 0, unroll=4)
+        for copy in keep(i):
             copy.start()
-            kept.append(copy)
-
-    def product(i, odd, even):
+
+    def product(it, i, odd, even):
         step = w.shape[2]
-
-        @pl.loop(0, w.shape[0])
-        def _(j):
+        pl.when(it == 0)(w_here)
+
+        def columns(j, _):
             at = pl.ds(pl.multiple_of(j * step, step), step)
             y = jnp.dot(rows_of_pair(mix_buf, i), w[j], preferred_element_type=f32)
             even[:, at] = y[:r].astype(even.dtype)
             odd[:, at] = y[r:].astype(odd.dtype)
+            return 0
+
+        lax.fori_loop(0, w.shape[0], columns, 0, unroll=4)
 
     def body(at, value):
         value = value + tok[at, :].astype(f32)
@@ -594,9 +636,10 @@
         ).astype(bf)
 
     reduce = Reduce(product, (po, pe, rc, sb, ring), sems, 0, peer, prepare, enter)
-    exchange_and_gather(reduce, both_gathers(own, out, sems, local, peer), 16, body)
-    for copy in kept:
-        copy.wait()
+    exchange_and_gather(reduce, both_gathers(own, out, sems, local, peer), 16, body, (tok_here,))
+    for i in range(4):
+        for copy in keep(i):
+            copy.wait()
 
 
 def forward_exchange(nrm, wvs, sco, w, tok, vec, cid):
@@ -607,15 +650,17 @@
     return pl.pallas_call(
         forward_kernel,
         out_shape=tuple(SDS(*b) for b in blocks) + (SDS((r, d), f32), SDS((TP, r, d), bf)),
-        in_specs=[VMEM] * 6,
+        in_specs=[ANY, ANY, VMEM, ANY, ANY, VMEM],
         out_specs=(ANY,) * 4 + (VMEM, ANY),
-        scratch_shapes=[pltpu.VMEM(*b) for b in blocks]
+        scratch_shapes=[pltpu.VMEM(x.shape, x.dtype) for x in (nrm, wvs, w, tok)]
+        + [pltpu.VMEM(*b) for b in blocks]
         + reduce_scratch(r, d)
         + [
             pltpu.VMEM((r, d), bf),
             pltpu.SemaphoreType.DMA((count,)),
             pltpu.SemaphoreType.DMA((count,)),
             pltpu.SemaphoreType.DMA((18,)),
+            pltpu.SemaphoreType.DMA((7,)),
         ],
         compiler_params=pltpu.CompilerParams(
             collective_id=cid, has_side_effects=True, vmem_limit_bytes=60 << 20
@@ -735,11 +780,24 @@
 
 
 def backward_kernel(
-    a, w, mid, cot, vec, gmid, out, sums, po, pe, rc, sb, ring, own, acc, ssem, rsem, local
+    a_in, w_in, mid_in, cot_in, vec, gmid, out, sums,
+    a, w, mid, cot, po, pe, rc, sb, ring, own, acc, ssem, rsem, local, load,
 ):
     _, peer = place()
     enter = greet([peer(1), peer(2), peer(4)])
     sems = (ssem, rsem)
+    loads = Load(load)
+    piece = loads.paired(a_in, a)
+    piece(3).start()
+    w_here = loads.whole(w_in, w)
+    for i in (1, 2, 0):
+        piece(i).start()
+    arrivals = (loads.whole(mid_in, mid), loads.whole(cot_in, cot))
+
+    def arrive(it, i):
+        pl.when(it == 0)(w_here)
+        piece(i).wait()
+
     acc[...] = jnp.zeros_like(acc)
 
     def body(at, g):
@@ -757,8 +815,10 @@
         gmid[at, :] = grad
         own[at, :] = grad.astype(bf)
 
-    reduce = Reduce(times(a, w, True), (po, pe, rc, sb, ring), sems, 0, peer, enter=enter)
-    exchange_and_gather(reduce, both_gathers(own, out, sems, local, peer), 16, body)
+    reduce = Reduce(
+        times(a, w, True, arrive), (po, pe, rc, sb, ring), sems, 0, peer, enter=enter
+    )
+    exchange_and_gather(reduce, both_gathers(own, out, sems, local, peer), 16, body, arrivals)
     sums[0:1, :] = jnp.sum(acc[0], axis=0, keepdims=True)
     sums[1:2, :] = jnp.sum(acc[1], axis=0, keepdims=True)
 
@@ -770,15 +830,17 @@
     return pl.pallas_call(
         backward_kernel,
         out_shape=(SDS((r, c), f32), SDS((TP, r, c), bf), SDS((2, c), f32)),
-        in_specs=[VMEM] * 5,
+        in_specs=[ANY] * 4 + [VMEM],
         out_specs=(VMEM, ANY, VMEM),
-        scratch_shapes=reduce_scratch(r, c)
+        scratch_shapes=[pltpu.VMEM(x.shape, x.dtype) for x in (a, w, mid, cot)]
+        + reduce_scratch(r, c)
         + [
             pltpu.VMEM((r, c), bf),
             pltpu.VMEM((2, 16, c), f32),
             pltpu.SemaphoreType.DMA((count,)),
             pltpu.SemaphoreType.DMA((count,)),
             pltpu.SemaphoreType.DMA((2,)),
+            pltpu.SemaphoreType.DMA((7,)),
         ],
         compiler_params=pltpu.CompilerParams(
             collective_id=cid, has_side_effects=True, vmem_limit_bytes=52 << 20
@@ -788,8 +850,9 @@
 
 
 def last_kernel(
-    n, gqkv, gs, wqk, wvs, a2, w2, tok, gmid, gain, sums2, gtok, ffn, vec_out,
-    po, pe, rc, sb, ring, pe2, rc2, sb2, ring2, acc, vecs, near, far, part, ssem, rsem,
+    n, gqkv_in, gs_in, wqk_in, wvs_in, a2_in, w2_in, tok_in, gmid_in, gain, sums2,
+    gtok, ffn, vec_out, gqkv, gs, wqk, wvs, a2, w2, tok, gmid,
+    po, pe, rc, sb, ring, pe2, rc2, sb2, ring2, acc, vecs, near, far, part, ssem, rsem, load,
 ):
     dp = n // TP
     me, peer = place()
@@ -798,16 +861,37 @@
     others = [lax.rem(me + TP * j, n) for j in range(1, dp)]
     enter = greet([peer(k) for k in range(1, TP)] + others)
     sems = (ssem, rsem)
+    loads = Load(load)
+    pieces = loads.paired(gqkv_in, gqkv), loads.paired(gs_in, gs)
+    for piece in pieces:
+        piece(3).start()
+    weights = loads.whole(wqk_in, wqk), loads.whole(wvs_in, wvs)
+    for i in (1, 2, 0):
+        for piece in pieces:
+            piece(i).start()
+    second = loads.whole(a2_in, a2), loads.whole(w2_in, w2)
+    arrivals = loads.whole(tok_in, tok), loads.whole(gmid_in, gmid)
+
+    def all_here(waits):
+        def wait():
+            for one in waits:
+                one()
+
+        return wait
+
     acc[...] = jnp.zeros_like(acc)
     nt = (((1,), (1,)), ((), ()))
 
-    def product(i, odd, even):
+    def product(it, i, odd, even):
         r, qk, v = gqkv.shape[1], wqk.shape[1], gs.shape[2]
+        pl.when(it == 0)(all_here(weights))
+        for piece in pieces:
+            piece(i).wait()
         x, y = rows_of_pair(gqkv, i), rows_of_pair(gs, i)
 
-        @pl.loop(0, even.shape[1] // TILE)
+        @pl.loop(0, even.shape[1] // WIDE)
         def _(j):
-            at = pl.ds(pl.multiple_of(j * TILE, TILE), TILE)
+            at = pl.ds(pl.multiple_of(j * WIDE, WIDE), WIDE)
             z = lax.dot_general(x[:, :qk], wqk[at, :], nt, preferred_element_type=f32)
             z += lax.dot_general(x[:, qk:], wvs[at, :v], nt, preferred_element_type=f32)
             z += lax.dot_general(y, wvs[at, v:], nt, preferred_element_type=f32)
@@ -816,10 +900,12 @@
 
     one = Reduce(product, (po, pe, rc, sb, ring), sems, 0, peer, enter=enter)
     one.run()
-    for copy in one.core.values():
-        copy.wait_send()
-    one.sent = [copy for copy in one.sent if all(copy is not c for c in one.core.values())]
-    two = Reduce(times(a2, w2, False), (po, pe2, rc2, sb2, ring2), sems, REDUCE_SEMS, peer)
+    one.core_sent()
+
+    def arrive(it, _):
+        pl.when(it == 0)(all_here(second))
+
+    two = Reduce(times(a2, w2, False, arrive), (po, pe2, rc2, sb2, ring2), sems, REDUCE_SEMS, peer)
     two.run()
 
     def body(at, grad):
@@ -835,6 +921,7 @@
         mean_gh = jnp.mean(scaled * hat, axis=-1, keepdims=True)
         gtok[at, :] = gmid[at, :] + inv * (scaled - mean_g - hat * mean_gh)
 
+    all_here(arrivals)()
     for c in (0, 1):
         one.rows(c, 16, body)
     vecs[...] = jnp.zeros_like(vecs)
@@ -881,9 +968,12 @@
     return pl.pallas_call(
         functools.partial(last_kernel, n),
         out_shape=(SDS((r, c), f32), SDS((r, c), f32), SDS((8, width), f32)),
-        in_specs=[VMEM] * 10,
+        in_specs=[ANY] * 8 + [VMEM] * 2,
         out_specs=(VMEM,) * 3,
-        scratch_shapes=reduce_scratch(r, c)
+        scratch_shapes=[
+            pltpu.VMEM(x.shape, x.dtype) for x in (gqkv, gs, wqk, wvs, a2, w2, tok, gmid)
+        ]
+        + reduce_scratch(r, c)
         + reduce_scratch(r, c, bf)[1:]
         + [
             pltpu.VMEM((2, 16, c), f32),
@@ -893,6 +983,7 @@
             pltpu.VMEM((8, width), f32),
             pltpu.SemaphoreType.DMA((count,)),
             pltpu.SemaphoreType.DMA((count,)),
+            pltpu.SemaphoreType.DMA((14,)),
         ],
         compiler_params=pltpu.CompilerParams(
             collective_id=cid, has_side_effects=True, vmem_limit_bytes=ALL_VMEM

time: 748 us -> 745 us (level)
  Pallas kernels: 544 us -> 517 us
  waiting for transfers between devices: 74.8 us -> 98.2 us
    all_gather x4, waiting for transfers between devices: 1.87 us -> 19.6 us  [dp_gather(): lax.all_gather(x, AXIS, axis=0, tiled=True, axis_index_groups=dp_groups(n))]
    pallas_call x1, Pallas kernels: 105 us -> 87.1 us  [forward_exchange(): pl.pallas_call(forward_kernel, out_shape=tuple((SDS(*b) for b in blocks))...]
  transfers between devices with their start and end apart: 11 -> 11, of which waited for: 3 -> 3; matrix products, arithmetic and copies ran while one was open for 3% -> 3% of each run, Pallas kernels for 55% -> 52%
where the time goes in v8:
time: 745 us; the launch traced here: 741 us
  Pallas kernels  517 us (69%)
  waiting for transfers between devices  98.2 us (13%)
  blocking collectives  56.6 us (8%)
  local copies, waits for them, and re-layouts  29.5 us (4%)
  between operations  14.4 us (2%)
  other arithmetic  13.9 us (2%)
  starting transfers between devices  11 us (1%)
    pallas_call x4, Pallas kernels, exchange_call(): pl.pallas_call(kernel, out_shape=outs, in_specs=specs or [VMEM] * len(arg...  150 us
    pallas_call x1, Pallas kernels, forward_exchange(): pl.pallas_call(forward_kernel, out_shape=tuple((SDS(*b) for b in blocks))...  87.1 us
    pallas_call x1, Pallas kernels, last_exchange(): pl.pallas_call(functools.partial(last_kernel, n), out_shape=(SDS((r, c),...  84.9 us
    pallas_call x1, Pallas kernels, backward_exchange(): pl.pallas_call(backward_kernel, out_shape=(SDS((r, c), f32), SDS((TP, r,...  81.1 us
    reduce_scatter x5, waiting for transfers between devices, dp_reduce(): lax.psum_scatter(x, AXIS, scatter_dimension=0, tiled=True, axis_index_gro...  77.3 us
    all_to_all x3, blocking collectives, plane_a2a(): lax.all_to_all(x, AXIS, 0, 0, axis_index_groups=tp_groups(n), tiled=True)  56.6 us
    pallas_call x5, Pallas kernels, row_product(): pl.pallas_call(product_kernel, grid=(width // part, m // tile), out_shape...  56.3 us
    unnamed x67, local copies, waits for them, and re-layouts  24.2 us
  transfers between devices with their start and end apart: 11, of which 3 were waited for; matrix products, arithmetic and copies ran while one was open for 3% of the time, Pallas kernels for 52%

profile of v8, /device:TPU:14, one launch (start us, length us, event | category | flops | bytes accessed | tf_op | source)
XLA Modules:
  0.0 740.8 jit_solution(6746127749193812944)
XLA Ops:
  10.2 15.4 %shard_map.254 = bf16[8,64,1024]{2,1,0:T(8,128)(2,1)} custom-call(bf16[64,2048]{1,0:T(8,128)(2,1)S(1)} %copy-done.19, bf16[64,2048]{1,0:T(8,128)(2,1)S(1)} %copy-done.20, bf16[128,2048]{1,0:T(8,128)(2,1)S(1)} %copy-done.18), custom_call_target="tpu_custom_call" | custom-call | tf_op jit(solution)/shard_map/pallas_call | solution.py:143
  28.1 41.8 %shard_map.255 = (bf16[8,256,2048]{2,1,0:T(8,128)(2,1)S(1)}, f32[4,8,8,128]{3,2,1,0:T(8,128)S(1)}) custom-call(bf16[256,2048]{1,0:T(8,128)(2,1)S(1)} %copy-done.4, f32[8,128]{1,0:T(8,128)S(1)} %pad.9.vec), custom_call_target="tpu_custom_call" | custom-call | tf_op jit(solution)/shard_map/pallas_call | solution.py:143
  78.1 26.4 %shard_map.256 = (bf16[8,64,1024]{2,1,0:T(8,128)(2,1)}, bf16[8,64,1024]{2,1,0:T(8,128)(2,1)}, bf16[8,256,2048]{2,1,0:T(8,128)(2,1)S(1)}) custom-call(bf16[64,4096]{1,0:T(8,128)(2,1)S(1)} %copy-done.16, bf16[64,4096]{1,0:T(8,128)(2,1)S(1)} %copy-done.17, bf16[8,64,1024]{2,1,0:T(8,128)(2,1)S(1)} %pad_maximum_fusion.gu, bf16[8,256,2048]{2,1,0:T(8,128)(2,1)S(1)} %copy-done.7, ...), custom_call_target="tpu_custom_call" | custom-call | tf_op jit(solution)/shard_map/pallas_call | solution.py:143
  110.8 5.3 multiply_sine_fusion
  120.2 66.1 %shard_map.257 = (bf16[8,256,2048]{2,1,0:T(8,128)(2,1)}, bf16[8,4,2,64,256]{4,3,2,1,0:T(8,128)(2,1)S(1)}, bf16[8,256,256]{2,1,0:T(8,128)(2,1)S(1)}, bf16[8,256,2...) custom-call(bf16[256,2048]{1,0:T(8,128)(2,1)S(1)} %copy-done.8, ...), custom_call_target="tpu_custom_call" | custom-call | tf_op jit(solution)/shard_map/pallas_call | solution.py:143
  192.0 87.1 %forward_exchange.1 = (bf16[8,256,512]{2,1,0:T(8,128)(2,1)}, bf16[8,256,512]{2,1,0:T(8,128)(2,1)}, f32[8,256,512]{2,1,0:T(8,128)}, f32[8,256,512]{2,1,0:T(8,128)...) custom-call(bf16[8,256,2048]{2,1,0:T(8,128)(2,1)} %copy-done, ...), custom_call_target="tpu_custom_call" | custom-call | tf_op jit(solution)/shard_map/forward_exchange/pallas_call | solution.py:650
  279.1 15.7 %hidden_units.1 = (bf16[8,256,512]{2,1,0:T(8,128)(2,1)}, f32[8,256,512]{2,1,0:T(8,128)}, f32[8,256,512]{2,1,0:T(8,128)}) custom-call(bf16[8,256,2048]{2,1,0:T(8,128)(2,1)} %get-tuple-element.60.x.a, bf16[2048,1024]{1,0:T(8,128)(2,1)} %all-gather.11.cloned.1.call-done.gu.w_in), custom_call_target="tpu_custom_call" | custom-call | flops 8589934592 | bytes 25165824 | tf_op jit(solution)/shard_map/hidden_units/pallas_call | solution.py:726
  294.9 19.5 %all-gather.9.cloned.1.call-done.down.w2_in = bf16[512,2048]{1,0:T(8,128)(2,1)} async-done(((bf16[128,2048]{1,0:T(8,128)(2,1)}), bf16[512,2048]{1,0:T(8,128)(2,1)}) %all-gather.9.cloned.1.call-update) | async-done | bytes 2097168 | tf_op jit(solution)/shard_map/all_gather | solution.py:1094
  314.4 11.8 %hidden_back.1.a_in.b = bf16[8,256,1024]{2,1,0:T(8,128)(2,1)} custom-call(bf16[8,256,2048]{2,1,0:T(8,128)(2,1)} %get-tuple-element.59.cot.b, bf16[512,2048]{1,0:T(8,128)(2,1)} %all-gather.9.cloned.1.call-done.down.w2_in, f32[8,256,512]{2,1,0:T(8,128)} %get-tuple-element.62.act, f32[8,256,512]{2,1,0:T(8,128)} %get-tuple-element.63.slope), custom_call_target="tpu_custom_call" | custom-call | flops 4294967296 | bytes 25165824 | tf_op jit(solution)/shard_map/hidden_back/pallas_call | solution.py:763
  326.2 81.1 %backward_exchange.1 = (f32[256,2048]{1,0:T(8,128)}, bf16[8,256,2048]{2,1,0:T(8,128)(2,1)}, f32[2,2048]{1,0:T(2,128)S(1)}) custom-call(bf16[8,256,1024]{2,1,0:T(8,128)(2,1)} %hidden_back.1.a_in.b, bf16[2048,1024]{1,0:T(8,128)(2,1)} %all-gather.11.cloned.1.call-done.gu.w_in, f32[256,2048]{1,0:T(8,128)} %get-tuple-element.55.mid_in, ...), custom_call_target="tpu_custom_call" | custom-call | tf_op jit(solution)/shard_map/backward_exchange/pallas_call | solution.py:830
  407.9 14.0 %gate_back.1 = (bf16[8,256,512]{2,1,0:T(8,128)(2,1)}, bf16[8,256,512]{2,1,0:T(8,128)(2,1)}) custom-call(bf16[8,256,2048]{2,1,0:T(8,128)(2,1)} %get-tuple-element.64.g_low.b, bf16[8,512,256]{2,1,0:T(8,128)(2,1)} %bitcast.56, f32[8,256,512]{2,1,0:T(8,128)} %get-tuple-element.65.ret, f32[8,256,512]{2,1,0:T(8,128)} %get-tuple-element.66.swi), custom_call_target="tpu_custom_call" | custom-call | flops 4294967296 | bytes 23068672 | tf_op jit(solution)/shard_map/gate_back/pallas_call | solution.py:1024
  421.9 9.0 %row_product.6 = bf16[2048,512]{1,0:T(8,128)(2,1)} custom-call(bf16[8,256,2048]{2,1,0:T(8,128)(2,1)} %copy-done, bf16[8,256,512]{2,1,0:T(8,128)(2,1)} %get-tuple-element.68.gs_in.b), custom_call_target="tpu_custom_call" | custom-call | flops 4294967296 | bytes 12582912 | tf_op jit(solution)/shard_map/row_product/pallas_call | solution.py:683
  431.0 10.2 %row_product.7 = bf16[512,2048]{1,0:T(8,128)(2,1)} custom-call(bf16[8,256,512]{2,1,0:T(8,128)(2,1)} %get-tuple-element.79.a, bf16[8,256,2048]{2,1,0:T(8,128)(2,1)} %get-tuple-element.64.g_low.b), custom_call_target="tpu_custom_call" | custom-call | flops 4294967296 | bytes 12582912 | tf_op jit(solution)/shard_map/row_product/pallas_call | solution.py:683
  442.9 29.1 %all_to_all.45 = bf16[8,512,256]{2,1,0:T(8,128)(2,1)} all-to-all(bf16[8,512,256]{2,1,0:T(8,128)(2,1)S(1)} %bitcast.59), channel_id=1, replica_groups={{0,1,2,3,4,5,6,7},{8,9,10,11,12,13,14,15},{16,17,18,19,20,21,22,23},{24..., dimensions={0} | all-to-all | bytes 4194304 | tf_op jit(solution)/shard_map/all_to_all | solution.py:1090
  472.1 13.4 %row_product.8 = bf16[2048,1024]{1,0:T(8,128)(2,1)} custom-call(bf16[8,256,2048]{2,1,0:T(8,128)(2,1)} %get-tuple-element.60.x.a, bf16[8,256,1024]{2,1,0:T(8,128)(2,1)} %hidden_back.1.a_in.b), custom_call_target="tpu_custom_call" | custom-call | flops 8589934592 | bytes 16777216 | tf_op jit(solution)/shard_map/row_product/pallas_call | solution.py:683
  485.5 10.2 %scores_back.1.gqkv_in.b = bf16[8,256,1024]{2,1,0:T(8,128)(2,1)} custom-call(bf16[8,256,256]{2,1,0:T(8,128)(2,1)} %copy-done.10, f32[8,256,256]{2,1,0:T(8,128)} %copy-done.1, bf16[8,256,256]{2,1,0:T(8,128)(2,1)} %copy-done.14, bf16[8,256,256]{2,1,0:T(8,128)(2,1)} %copy-done.15, bf16[8,256,512]{2,1,0:T(8,128)(2,1)} %get-tuple-element.58.v, ...), custom_call_target="tpu_custom_call" | custom-call | flops 1610612736 | bytes 16777216 | tf_op jit(solution)/shard_map/scores_back/pallas_call | solution.py:1067
  495.7 13.5 %row_product.5 = bf16[2048,1024]{1,0:T(8,128)(2,1)} custom-call(bf16[8,256,2048]{2,1,0:T(8,128)(2,1)} %copy-done, bf16[8,256,1024]{2,1,0:T(8,128)(2,1)} %scores_back.1.gqkv_in.b), custom_call_target="tpu_custom_call" | custom-call | flops 8589934592 | bytes 16777216 | tf_op jit(solution)/shard_map/row_product/pallas_call | solution.py:683
  509.3 10.2 %row_product.9 = bf16[512,2048]{1,0:T(8,128)(2,1)} custom-call(bf16[8,256,512]{2,1,0:T(8,128)(2,1)} %get-tuple-element.70.a2_in.a, bf16[8,256,2048]{2,1,0:T(8,128)(2,1)} %get-tuple-element.59.cot.b), custom_call_target="tpu_custom_call" | custom-call | flops 4294967296 | bytes 12582912 | tf_op jit(solution)/shard_map/row_product/pallas_call | solution.py:683
  519.5 13.7 %all_to_all.46.x = bf16[8,64,512]{2,1,0:T(8,128)(2,1)} all-to-all(bf16[8,64,512]{2,1,0:T(8,128)(2,1)} %bitcast.70), channel_id=1, replica_groups={{0,1,2,3,4,5,6,7},{8,9,10,11,12,13,14,15},{16,17,18,19,20,21,22,23},{24..., dimensions={0} | all-to-all | bytes 1048576 | tf_op jit(solution)/shard_map/all_to_all | solution.py:1090
  533.2 13.8 %all_to_all.47.x = bf16[8,128,256]{2,1,0:T(8,128)(2,1)} all-to-all(bf16[8,128,256]{2,1,0:T(8,128)(2,1)} %bitcast.71), channel_id=1, replica_groups={{0,1,2,3,4,5,6,7},{8,9,10,11,12,13,14,15},{16,17,18,19,20,21,22,23},{24..., dimensions={0} | all-to-all | bytes 1048576 | tf_op jit(solution)/shard_map/all_to_all | solution.py:1090
  547.0 51.2 %reduce-scatter.12.cloned.1.call-done = bf16[512,1024]{1,0:T(8,128)(2,1)} async-done(((bf16[2048,1024]{1,0:T(8,128)(2,1)}), bf16[512,1024]{1,0:T(8,128)(2,1)}) %reduce-scatter.12.cloned.1.call-update) | async-done | bytes 1048592 | tf_op jit(solution)/shard_map/reduce_scatter | solution.py:1098
  602.9 84.9 %last_exchange.1 = (f32[256,2048]{1,0:T(8,128)}, f32[256,2048]{1,0:T(8,128)}, f32[8,512]{1,0:T(8,128)}) custom-call(bf16[8,256,1024]{2,1,0:T(8,128)(2,1)} %scores_back.1.gqkv_in.b, bf16[8,256,512]{2,1,0:T(8,128)(2,1)} %get-tuple-element.68.gs_in.b, bf16[2048,512]{1,0:T(8,128)(2,1)} %bitcast.57, bf16[2048,1024]{1,0:T(8,128)(2,1)} %all-gather.5.cloned.1.call-done.wvs_in, ...), custom_call_target="tpu_custom_call" | custom-call | tf_op jit(solution)/shard_map/last_exchange/pallas_call | solution.py:968
  687.8 5.7 all-to-all-start
  698.4 26.1 %reduce-scatter.14.cloned.1.call-done = bf16[128,2048]{1,0:T(8,128)(2,1)} async-done(((bf16[512,2048]{1,0:T(8,128)(2,1)}), bf16[128,2048]{1,0:T(8,128)(2,1)}) %reduce-scatter.14.cloned.1.call-update) | async-done | bytes 524304 | tf_op jit(solution)/shard_map/reduce_scatter | solution.py:1098
  (133 shorter events, 51.0 us)
Async XLA Ops:
  7.2 109.8 %all-gather.7.cloned.1.call-start = ((), (), s32[]{:S(2)}) async-start(), calls=%async_computation.11 | async-start | bytes 5242880 | tf_op jit(solution)/shard_map/all_gather | solution.py:1094
  10.2 15.5 %copy-start.25 = (bf16[64,4096]{1,0:T(8,128)(2,1)S(1)}, bf16[64,4096]{1,0:T(8,128)(2,1)}, u32[]{:S(2)}) copy-start(bf16[64,4096]{1,0:T(8,128)(2,1)} %param.26) | copy-start | bytes 1572868
  25.6 166.3 %all-gather.5.cloned.1.call-start = ((), (), s32[]{:S(2)}) async-start(), calls=%async_computation.10 | async-start | bytes 5242880 | tf_op jit(solution)/shard_map/all_gather | solution.py:1094
  27.0 47.8 %copy-start.16 = (bf16[64,4096]{1,0:T(8,128)(2,1)S(1)}, bf16[64,4096]{1,0:T(8,128)(2,1)}, u32[]{:S(2)}) copy-start(bf16[64,4096]{1,0:T(8,128)(2,1)} %wv.1) | copy-start | bytes 1572868
  27.0 47.8 %copy-start.17 = (bf16[64,4096]{1,0:T(8,128)(2,1)S(1)}, bf16[64,4096]{1,0:T(8,128)(2,1)}, u32[]{:S(2)}) copy-start(bf16[64,4096]{1,0:T(8,128)(2,1)} %ws.1) | copy-start | bytes 1572868
  69.9 3.3 copy-start.6
  73.5 31.1 %copy-start.22 = (f32[1,2048]{1,0:T(1,128)}, f32[1,2048]{1,0:T(1,128)S(1)}, u32[]{:S(2)}) copy-start(f32[1,2048]{1,0:T(1,128)S(1)} %reshape_squeeze.12.gain) | copy-start | bytes 24580
  74.7 3.4 copy-start.7
  107.9 171.2 %all-gather.11.cloned.1.call-start = ((), (), s32[]{:S(2)}) async-start(), calls=%async_computation.13 | async-start | bytes 5242880 | tf_op jit(solution)/shard_map/all_gather | solution.py:1094
  108.6 205.8 %all-gather.9.cloned.1.call-start = ((), (), s32[]{:S(2)}) async-start(), calls=%async_computation.12 | async-start | bytes 2621440 | tf_op jit(solution)/shard_map/all_gather | solution.py:1094
  109.2 410.3 %reduce-scatter.8.cloned.1.call-start = ((), (), s32[]{:S(2)}) async-start(), calls=%async_computation.15 | async-start | bytes 2621440 | tf_op jit(solution)/shard_map/reduce_scatter | solution.py:1098
  116.1 70.2 %copy-start.2 = (f32[8,256,128]{2,1,0:T(8,128)}, f32[8,256,128]{2,1,0:T(8,128)S(1)}, u32[]{:S(2)}) copy-start(f32[8,256,128]{2,1,0:T(8,128)S(1)} %get-tuple-element.86.sine) | copy-start | bytes 3145732
  116.9 69.4 %copy-start.1 = (f32[8,256,256]{2,1,0:T(8,128)}, f32[8,256,256]{2,1,0:T(8,128)S(1)}, u32[]{:S(2)}) copy-start(f32[8,256,256]{2,1,0:T(8,128)S(1)} %fusion.4.mask) | copy-start | bytes 6291460
  314.4 11.8 %copy-start.9 = (bf16[256,2048]{1,0:T(8,128)(2,1)S(1)}, bf16[256,2048]{1,0:T(8,128)(2,1)}, u32[]{:S(2)}) copy-start(bf16[256,2048]{1,0:T(8,128)(2,1)} %cot_in.1) | copy-start | bytes 3145732
  314.4 11.8 %copy-start.21 = (f32[2,2048]{1,0:T(2,128)S(1)}, f32[2,2048]{1,0:T(2,128)}, u32[]{:S(2)}) copy-start(f32[2,2048]{1,0:T(2,128)} %pad_maximum_fusion.1.vec) | copy-start | bytes 49156
  430.9 102.3 %reduce-scatter.10.cloned.1.call-start = ((), (), s32[]{:S(2)}) async-start(), calls=%async_computation.16 | async-start | bytes 2621440 | tf_op jit(solution)/shard_map/reduce_scatter | solution.py:1098
  472.0 126.2 %reduce-scatter.12.cloned.1.call-start = ((), (), s32[]{:S(2)}) async-start(), calls=%async_computation.17 | async-start | bytes 5242880 | tf_op jit(solution)/shard_map/reduce_scatter | solution.py:1098
  485.5 202.3 %reduce-scatter.6.cloned.1.call-start = ((), (), s32[]{:S(2)}) async-start(), calls=%async_computation.14 | async-start | bytes 5242880 | tf_op jit(solution)/shard_map/reduce_scatter | solution.py:1098
  509.2 215.3 %reduce-scatter.14.cloned.1.call-start = ((), (), s32[]{:S(2)}) async-start(), calls=%async_computation.18 | async-start | bytes 2621440 | tf_op jit(solution)/shard_map/reduce_scatter | solution.py:1098
  598.2 89.6 %all-to-all-start.4 = ((bf16[8,64,1024]{2,1,0:T(8,128)(2,1)}), bf16[8,64,1024]{2,1,0:T(8,128)(2,1)}, u32[]{:S(2)}, u32[]{:S(2)}) async-start(bf16[8,64,1024]{2,1,0:T(8,128)(2,1)} %bitcast.67), calls=%async_computation.8 | async-start | bytes 2097152 | tf_op jit(solution)/shard_map/all_to_all | solution.py:1090
  687.8 43.7 %all-to-all-start = ((bf16[8,64,1024]{2,1,0:T(8,128)(2,1)}), bf16[8,64,1024]{2,1,0:T(8,128)(2,1)S(1)}, u32[]{:S(2)}, u32[]{:S(2)}) async-start(bf16[8,64,1024]{2,1,0:T(8,128)(2,1)} %bitcast.66), calls=%async_computation.1 | async-start | bytes 2097152 | tf_op jit(solution)/shard_map/all_to_all | solution.py:1090
  694.9 31.8 %copy-start.11 = (bf16[8,64,512]{2,1,0:T(8,128)(2,1)S(1)}, bf16[8,64,512]{2,1,0:T(8,128)(2,1)}, u32[]{:S(2)}) copy-start(bf16[8,64,512]{2,1,0:T(8,128)(2,1)} %all_to_all.46.x) | copy-start | bytes 1572868
  698.4 29.3 %copy-start.12 = (bf16[8,128,256]{2,1,0:T(8,128)(2,1)S(1)}, bf16[8,128,256]{2,1,0:T(8,128)(2,1)}, u32[]{:S(2)}) copy-start(bf16[8,128,256]{2,1,0:T(8,128)(2,1)} %all_to_all.47.x) | copy-start | bytes 1572868
  728.7 4.2 copy-start.24
  (19 other events, 28.6 us)
Sparse Core Ops, SparseCore 0:
  25.8 79.3 all-gather.6
  108.0 78.7 all-gather.4
  188.4 79.2 all-gather.10
  269.1 45.2 all-gather.8
  431.1 42.9 reduce-scatter.7
  476.2 42.8 reduce-scatter.9
  521.4 76.7 reduce-scatter.11
  600.5 78.6 reduce-scatter.5
  681.5 42.9 reduce-scatter.13

commit v9 on v8

--- a/solution.py
+++ b/solution.py
@@ -9,6 +9,7 @@
 from jax.sharding import PartitionSpec as P
 
 
+HEADS = 8
 KH = 256
 VH = 512
 TP = 8
@@ -1000,33 +1001,36 @@
         for j in range(w.shape[0]):
             whole[:, j * cols : (j + 1) * cols] = w[j]
 
-    grad = lax.dot_general(
-        g_low[0], whole[...], (((1,), (1,)), ((), ())), preferred_element_type=f32
+    two, r, _ = gret.shape
+    grads = lax.dot_general(
+        g_low[...].reshape(two * r, g_low.shape[2]), whole[...], (((1,), (1,)), ((), ())),
+        preferred_element_type=f32,
     )
-    value, gate = ret[0], swi[0]
-    centred = value - jnp.mean(value, axis=-1, keepdims=True)
-    spread = jnp.mean(centred * centred, axis=-1, keepdims=True)
-    inv = lax.rsqrt(jnp.maximum(spread, 0.25))
-    share = 1.0 / (1.0 + jnp.exp(-gate))
-    silu = gate * share
-    gswi[0] = (grad * (centred * inv) * (share * (1.0 + gate * (1.0 - share)))).astype(bf)
-    grad = grad * silu
-    pull = jnp.mean(grad * centred, axis=-1, keepdims=True)
-    pull = jnp.where(spread > 0.25, inv * inv * inv * pull, 0.0)
-    grad = grad * inv - centred * pull
-    gret[0] = (grad - jnp.mean(grad, axis=-1, keepdims=True)).astype(bf)
+    for i in range(two):
+        grad, value, gate = grads[i * r : (i + 1) * r], ret[i], swi[i]
+        centred = value - jnp.mean(value, axis=-1, keepdims=True)
+        spread = jnp.mean(centred * centred, axis=-1, keepdims=True)
+        inv = lax.rsqrt(jnp.maximum(spread, 0.25))
+        share = 1.0 / (1.0 + jnp.exp(-gate))
+        silu = gate * share
+        gswi[i] = (grad * (centred * inv) * (share * (1.0 + gate * (1.0 - share)))).astype(bf)
+        grad = grad * silu
+        pull = jnp.mean(grad * centred, axis=-1, keepdims=True)
+        pull = jnp.where(spread > 0.25, inv * inv * inv * pull, 0.0)
+        grad = grad * inv - centred * pull
+        gret[i] = (grad - jnp.mean(grad, axis=-1, keepdims=True)).astype(bf)
 
 
 def gate_back(g_low, w, ret, swi):
     _, r, d = g_low.shape
     width = ret.shape[2]
-    row = pl.BlockSpec((1, r, width), lambda k: (k, 0, 0))
+    row = pl.BlockSpec((2, r, width), lambda k: (k, 0, 0))
     return pl.pallas_call(
         gate_back_kernel,
-        grid=(TP,),
+        grid=(TP // 2,),
         out_shape=(SDS(ret.shape, bf), SDS(ret.shape, bf)),
         in_specs=[
-            pl.BlockSpec((1, r, d), lambda k: (k, 0, 0)),
+            pl.BlockSpec((2, r, d), lambda k: (k, 0, 0)),
             pl.BlockSpec(w.shape, lambda k: (0, 0, 0)),
             row,
             row,
@@ -1088,6 +1092,22 @@
 
 def plane_a2a(x, n):
     return lax.all_to_all(x, AXIS, 0, 0, axis_index_groups=tp_groups(n), tiled=True)
+
+
+def spread_rows(x, n):
+    rows = x.shape[0] // 4
+    t = lax.rem(lax.axis_index(AXIS), TP)
+    got = []
+    for m in range(4):
+        chunk = lax.dynamic_slice_in_dim(x, lax.rem(lax.div(t, 2) + m, 4) * rows, rows, 0)
+        pairs = [
+            (g * TP + h, g * TP + 4 * (h % 2) + (h // 2 + m) % 4)
+            for g in range(n // TP)
+            for h in range(TP)
+        ]
+        got.append(lax.ppermute(chunk, AXIS, pairs))
+    turned = jnp.concatenate(got[::-1] * 2, axis=0)
+    return lax.dynamic_slice_in_dim(turned, (3 - lax.rem(t, 4)) * rows, 4 * rows, 0)
 
 
 def dp_gather(x, n):
@@ -1222,7 +1242,11 @@
     swish_grad = row_product(normed, g_swish)
     g_swi = dp_reduce(swish_grad, n)
     out_grad = row_product(mixed, g_low)
-    out_grad = plane_a2a(col_blocks(out_grad), n)
+    spread = wo.shape[0] * HEADS == VH * 2
+    if spread:
+        out_grad = spread_rows(out_grad, n)
+    else:
+        out_grad = plane_a2a(col_blocks(out_grad), n)
     g_qkv = scores_back(scores, mask, q_rot, k_rot, v_low, g_retained, cosine, sine)
     qkv_grad = row_product(normed, g_qkv)
     g_qkv_own = dp_reduce(qkv_grad, n)
@@ -1240,8 +1264,11 @@
     (grad_s,) = join(g_swi.reshape(TP, shard, VH), (VH,))
     g_qkv_own = plane_a2a(g_qkv_own, n)
     grad_q, grad_k, grad_v = join(g_qkv_own.reshape(TP, shard, 2 * KH + VH), (KH, KH, VH))
-    g_out = plane_a2a(g_out, n)
-    (grad_o,) = join(g_out.reshape(TP, wo.shape[0], d // TP), (d // TP,))
+    if spread:
+        grad_o = g_out.astype(f32)
+    else:
+        g_out = plane_a2a(g_out, n)
+        (grad_o,) = join(g_out.reshape(TP, wo.shape[0], d // TP), (d // TP,))
     return (
         layer_out, grad_tokens, g_vecs[0], g_vecs[1], grad_q, grad_k, grad_v, grad_s, grad_o,
         g_vecs[2], g_vecs[3], grad_g, grad_u, grad_d,

time: 745 us -> 743 us (level)
  blocking collectives: 56.6 us -> 13 us
  waiting for transfers between devices: 98.2 us -> 126 us
  starting transfers between devices: 11 us -> 21 us
    all_to_all x3 -> x1, blocking collectives: 56.6 us -> 13 us  [plane_a2a(): lax.all_to_all(x, AXIS, 0, 0, axis_index_groups=tp_groups(n), tiled=True)]
    ppermute x0 -> x4, waiting for transfers between devices: none -> 17.9 us  [spread_rows(): got.append(lax.ppermute(chunk, AXIS, pairs))]
    ppermute x0 -> x4, starting transfers between devices: none -> 10.1 us  [spread_rows(): got.append(lax.ppermute(chunk, AXIS, pairs))]
    reduce_scatter x5, waiting for transfers between devices: 77.3 us -> 86.9 us  [dp_reduce(): lax.psum_scatter(x, AXIS, scatter_dimension=0, tiled=True, axis_index_gro...]
    unnamed x67 -> x68, local copies, waits for them, and re-layouts: 24.2 us -> 26.4 us
  transfers between devices with their start and end apart: 11 -> 15, of which waited for: 3 -> 6; matrix products, arithmetic and copies ran while one was open for 3% -> 4% of each run, Pallas kernels for 52% -> 52%
where the time goes in v9:
time: 743 us; the launch traced here: 739 us
  Pallas kernels  515 us (69%)
  waiting for transfers between devices  126 us (17%)
  local copies, waits for them, and re-layouts  33.9 us (5%)
  starting transfers between devices  21 us (3%)
  other arithmetic  16 us (2%)
  between operations  14.6 us (2%)
  blocking collectives  13 us (2%)
    pallas_call x4, Pallas kernels, exchange_call(): pl.pallas_call(kernel, out_shape=outs, in_specs=specs or [VMEM] * len(arg...  150 us
    pallas_call x1, Pallas kernels, forward_exchange(): pl.pallas_call(forward_kernel, out_shape=tuple((SDS(*b) for b in blocks))...  87.1 us
    reduce_scatter x5, waiting for transfers between devices, dp_reduce(): lax.psum_scatter(x, AXIS, scatter_dimension=0, tiled=True, axis_index_gro...  86.9 us
    pallas_call x1, Pallas kernels, last_exchange(): pl.pallas_call(functools.partial(last_kernel, n), out_shape=(SDS((r, c),...  84.8 us
    pallas_call x1, Pallas kernels, backward_exchange(): pl.pallas_call(backward_kernel, out_shape=(SDS((r, c), f32), SDS((TP, r,...  81.1 us
    pallas_call x5, Pallas kernels, row_product(): pl.pallas_call(product_kernel, grid=(width // part, m // tile), out_shape...  56.5 us
    unnamed x68, local copies, waits for them, and re-layouts  26.4 us
    all_gather x4, waiting for transfers between devices, dp_gather(): lax.all_gather(x, AXIS, axis=0, tiled=True, axis_index_groups=dp_groups(n))  19.5 us
  transfers between devices with their start and end apart: 15, of which 6 were waited for; matrix products, arithmetic and copies ran while one was open for 4% of the time, Pallas kernels for 52%

profile of v9, /device:TPU:14, one launch (start us, length us, event | category | flops | bytes accessed | tf_op | source)
XLA Modules:
  0.0 738.7 jit_solution(8370338101909388882)
XLA Ops:
  10.2 15.4 %shard_map.254 = bf16[8,64,1024]{2,1,0:T(8,128)(2,1)} custom-call(bf16[64,2048]{1,0:T(8,128)(2,1)S(1)} %copy-done.18, bf16[64,2048]{1,0:T(8,128)(2,1)S(1)} %copy-done.19, bf16[128,2048]{1,0:T(8,128)(2,1)S(1)} %copy-done.17), custom_call_target="tpu_custom_call" | custom-call | tf_op jit(solution)/shard_map/pallas_call | solution.py:144
  29.9 41.8 %shard_map.255 = (bf16[8,256,2048]{2,1,0:T(8,128)(2,1)S(1)}, f32[4,8,8,128]{3,2,1,0:T(8,128)S(1)}) custom-call(bf16[256,2048]{1,0:T(8,128)(2,1)S(1)} %copy-done.4, f32[8,128]{1,0:T(8,128)S(1)} %pad.9.vec), custom_call_target="tpu_custom_call" | custom-call | tf_op jit(solution)/shard_map/pallas_call | solution.py:144
  80.0 26.4 %shard_map.256 = (bf16[8,64,1024]{2,1,0:T(8,128)(2,1)}, bf16[8,64,1024]{2,1,0:T(8,128)(2,1)}, bf16[8,256,2048]{2,1,0:T(8,128)(2,1)S(1)}) custom-call(bf16[64,4096]{1,0:T(8,128)(2,1)S(1)} %copy-done.15, bf16[64,4096]{1,0:T(8,128)(2,1)S(1)} %copy-done.16, bf16[8,64,1024]{2,1,0:T(8,128)(2,1)S(1)} %pad_maximum_fusion.gu, bf16[8,256,2048]{2,1,0:T(8,128)(2,1)S(1)} %copy-done.7, ...), custom_call_target="tpu_custom_call" | custom-call | tf_op jit(solution)/shard_map/pallas_call | solution.py:144
  112.4 5.3 multiply_sine_fusion
  121.8 66.1 %shard_map.257 = (bf16[8,256,2048]{2,1,0:T(8,128)(2,1)}, bf16[8,4,2,64,256]{4,3,2,1,0:T(8,128)(2,1)S(1)}, bf16[8,256,256]{2,1,0:T(8,128)(2,1)S(1)}, bf16[8,256,2...) custom-call(bf16[256,2048]{1,0:T(8,128)(2,1)S(1)} %copy-done.8, ...), custom_call_target="tpu_custom_call" | custom-call | tf_op jit(solution)/shard_map/pallas_call | solution.py:144
  193.6 87.1 %forward_exchange.1 = (bf16[8,256,512]{2,1,0:T(8,128)(2,1)}, bf16[8,256,512]{2,1,0:T(8,128)(2,1)}, f32[8,256,512]{2,1,0:T(8,128)}, f32[8,256,512]{2,1,0:T(8,128)...) custom-call(bf16[8,256,2048]{2,1,0:T(8,128)(2,1)} %copy-done, ...), custom_call_target="tpu_custom_call" | custom-call | tf_op jit(solution)/shard_map/forward_exchange/pallas_call | solution.py:651
  280.8 15.8 %hidden_units.1 = (bf16[8,256,512]{2,1,0:T(8,128)(2,1)}, f32[8,256,512]{2,1,0:T(8,128)}, f32[8,256,512]{2,1,0:T(8,128)}) custom-call(bf16[8,256,2048]{2,1,0:T(8,128)(2,1)} %get-tuple-element.60.x.a, bf16[2048,1024]{1,0:T(8,128)(2,1)} %all-gather.11.cloned.1.call-done.gu.w_in), custom_call_target="tpu_custom_call" | custom-call | flops 8589934592 | bytes 25165824 | tf_op jit(solution)/shard_map/hidden_units/pallas_call | solution.py:727
  296.5 19.4 %all-gather.9.cloned.1.call-done.down.w2_in = bf16[512,2048]{1,0:T(8,128)(2,1)} async-done(((bf16[128,2048]{1,0:T(8,128)(2,1)}), bf16[512,2048]{1,0:T(8,128)(2,1)}) %all-gather.9.cloned.1.call-update) | async-done | bytes 2097168 | tf_op jit(solution)/shard_map/all_gather | solution.py:1114
  316.0 11.7 %hidden_back.1.a_in.b = bf16[8,256,1024]{2,1,0:T(8,128)(2,1)} custom-call(bf16[8,256,2048]{2,1,0:T(8,128)(2,1)} %get-tuple-element.59.cot.b, bf16[512,2048]{1,0:T(8,128)(2,1)} %all-gather.9.cloned.1.call-done.down.w2_in, f32[8,256,512]{2,1,0:T(8,128)} %get-tuple-element.62.act, f32[8,256,512]{2,1,0:T(8,128)} %get-tuple-element.63.slope), custom_call_target="tpu_custom_call" | custom-call | flops 4294967296 | bytes 25165824 | tf_op jit(solution)/shard_map/hidden_back/pallas_call | solution.py:764
  327.7 81.1 %backward_exchange.1 = (f32[256,2048]{1,0:T(8,128)}, bf16[8,256,2048]{2,1,0:T(8,128)(2,1)}, f32[2,2048]{1,0:T(2,128)S(1)}) custom-call(bf16[8,256,1024]{2,1,0:T(8,128)(2,1)} %hidden_back.1.a_in.b, bf16[2048,1024]{1,0:T(8,128)(2,1)} %all-gather.11.cloned.1.call-done.gu.w_in, f32[256,2048]{1,0:T(8,128)} %get-tuple-element.55.mid_in, ...), custom_call_target="tpu_custom_call" | custom-call | tf_op jit(solution)/shard_map/backward_exchange/pallas_call | solution.py:831
  409.5 12.6 %gate_back.1 = (bf16[8,256,512]{2,1,0:T(8,128)(2,1)}, bf16[8,256,512]{2,1,0:T(8,128)(2,1)}) custom-call(bf16[8,256,2048]{2,1,0:T(8,128)(2,1)} %get-tuple-element.64.g_low.b, bf16[8,512,256]{2,1,0:T(8,128)(2,1)} %bitcast.47, f32[8,256,512]{2,1,0:T(8,128)} %get-tuple-element.65.ret, f32[8,256,512]{2,1,0:T(8,128)} %get-tuple-element.66.swi), custom_call_target="tpu_custom_call" | custom-call | flops 4294967296 | bytes 23068672 | tf_op jit(solution)/shard_map/gate_back/pallas_call | solution.py:1028
  422.1 9.0 %row_product.6 = bf16[2048,512]{1,0:T(8,128)(2,1)} custom-call(bf16[8,256,2048]{2,1,0:T(8,128)(2,1)} %copy-done, bf16[8,256,512]{2,1,0:T(8,128)(2,1)} %get-tuple-element.68.gs_in.b), custom_call_target="tpu_custom_call" | custom-call | flops 4294967296 | bytes 12582912 | tf_op jit(solution)/shard_map/row_product/pallas_call | solution.py:684
  431.2 13.4 %row_product.8 = bf16[2048,1024]{1,0:T(8,128)(2,1)} custom-call(bf16[8,256,2048]{2,1,0:T(8,128)(2,1)} %get-tuple-element.60.x.a, bf16[8,256,1024]{2,1,0:T(8,128)(2,1)} %hidden_back.1.a_in.b), custom_call_target="tpu_custom_call" | custom-call | flops 8589934592 | bytes 16777216 | tf_op jit(solution)/shard_map/row_product/pallas_call | solution.py:684
  444.6 10.1 %scores_back.1.gqkv_in.b = bf16[8,256,1024]{2,1,0:T(8,128)(2,1)} custom-call(bf16[8,256,256]{2,1,0:T(8,128)(2,1)} %copy-done.10, f32[8,256,256]{2,1,0:T(8,128)} %copy-done.1, bf16[8,256,256]{2,1,0:T(8,128)(2,1)} %copy-done.13, bf16[8,256,256]{2,1,0:T(8,128)(2,1)} %copy-done.14, bf16[8,256,512]{2,1,0:T(8,128)(2,1)} %get-tuple-element.58.v, ...), custom_call_target="tpu_custom_call" | custom-call | flops 1610612736 | bytes 16777216 | tf_op jit(solution)/shard_map/scores_back/pallas_call | solution.py:1071
  454.8 13.4 %row_product.5 = bf16[2048,1024]{1,0:T(8,128)(2,1)} custom-call(bf16[8,256,2048]{2,1,0:T(8,128)(2,1)} %copy-done, bf16[8,256,1024]{2,1,0:T(8,128)(2,1)} %scores_back.1.gqkv_in.b), custom_call_target="tpu_custom_call" | custom-call | flops 8589934592 | bytes 16777216 | tf_op jit(solution)/shard_map/row_product/pallas_call | solution.py:684
  468.2 10.2 %row_product.9 = bf16[512,2048]{1,0:T(8,128)(2,1)} custom-call(bf16[8,256,512]{2,1,0:T(8,128)(2,1)} %get-tuple-element.70.a2_in.a, bf16[8,256,2048]{2,1,0:T(8,128)(2,1)} %get-tuple-element.59.cot.b), custom_call_target="tpu_custom_call" | custom-call | flops 4294967296 | bytes 12582912 | tf_op jit(solution)/shard_map/row_product/pallas_call | solution.py:684
  478.5 10.5 %row_product.7 = bf16[512,2048]{1,0:T(8,128)(2,1)} custom-call(bf16[8,256,512]{2,1,0:T(8,128)(2,1)} %get-tuple-element.79.a, bf16[8,256,2048]{2,1,0:T(8,128)(2,1)} %get-tuple-element.64.g_low.b), custom_call_target="tpu_custom_call" | custom-call | flops 4294967296 | bytes 12582912 | tf_op jit(solution)/shard_map/row_product/pallas_call | solution.py:684
  503.6 15.9 %collective-permute-done.1 = bf16[128,2048]{1,0:T(8,128)(2,1)S(1)} collective-permute-done((bf16[128,2048]{1,0:T(8,128)(2,1)S(1)}, bf16[128,2048]{1,0:T(8,128)(2,1)S(1)}, u32[]{:S(2)}, u32[]{:S(2)}) %collective-permute-start.1) | collective-permute-done | bytes 524320 | tf_op jit(solution)/shard_map/ppermute | solution.py:1108
  521.4 13.0 %all_to_all.27.x = bf16[8,64,512]{2,1,0:T(8,128)(2,1)} all-to-all(bf16[8,64,512]{2,1,0:T(8,128)(2,1)} %bitcast.58), channel_id=1, replica_groups={{0,1,2,3,4,5,6,7},{8,9,10,11,12,13,14,15},{16,17,18,19,20,21,22,23},{24..., dimensions={0} | all-to-all | bytes 1048576 | tf_op jit(solution)/shard_map/all_to_all | solution.py:1094
  534.5 18.8 %reduce-scatter.12.cloned.1.call-done = bf16[512,1024]{1,0:T(8,128)(2,1)} async-done(((bf16[2048,1024]{1,0:T(8,128)(2,1)}), bf16[512,1024]{1,0:T(8,128)(2,1)}) %reduce-scatter.12.cloned.1.call-update) | async-done | bytes 1048592 | tf_op jit(solution)/shard_map/reduce_scatter | solution.py:1118
  558.0 84.8 %last_exchange.1 = (f32[256,2048]{1,0:T(8,128)}, f32[256,2048]{1,0:T(8,128)}, f32[8,512]{1,0:T(8,128)}) custom-call(bf16[8,256,1024]{2,1,0:T(8,128)(2,1)} %scores_back.1.gqkv_in.b, bf16[8,256,512]{2,1,0:T(8,128)(2,1)} %get-tuple-element.68.gs_in.b, bf16[2048,512]{1,0:T(8,128)(2,1)} %bitcast.48, bf16[2048,1024]{1,0:T(8,128)(2,1)} %all-gather.5.cloned.1.call-done.wvs_in, ...), custom_call_target="tpu_custom_call" | custom-call | tf_op jit(solution)/shard_map/last_exchange/pallas_call | solution.py:969
  642.8 5.9 all-to-all-start
  653.4 26.1 %reduce-scatter.14.cloned.1.call-done = bf16[128,2048]{1,0:T(8,128)(2,1)} async-done(((bf16[512,2048]{1,0:T(8,128)(2,1)}), bf16[128,2048]{1,0:T(8,128)(2,1)}) %reduce-scatter.14.cloned.1.call-update) | async-done | bytes 524304 | tf_op jit(solution)/shard_map/reduce_scatter | solution.py:1118
  682.7 42.0 %reduce-scatter.10.cloned.1.call-done = bf16[128,2048]{1,0:T(8,128)(2,1)} async-done(((bf16[512,2048]{1,0:T(8,128)(2,1)}), bf16[128,2048]{1,0:T(8,128)(2,1)}) %reduce-scatter.10.cloned.1.call-update) | async-done | bytes 524304 | tf_op jit(solution)/shard_map/reduce_scatter | solution.py:1118
  (142 shorter events, 68.2 us)
Async XLA Ops:
  7.2 111.4 %all-gather.7.cloned.1.call-start = ((), (), s32[]{:S(2)}) async-start(), calls=%async_computation.9 | async-start | bytes 5242880 | tf_op jit(solution)/shard_map/all_gather | solution.py:1114
  25.7 167.9 %all-gather.5.cloned.1.call-start = ((), (), s32[]{:S(2)}) async-start(), calls=%async_computation.8 | async-start | bytes 5242880 | tf_op jit(solution)/shard_map/all_gather | solution.py:1114
  27.0 49.5 %copy-start.15 = (bf16[64,4096]{1,0:T(8,128)(2,1)S(1)}, bf16[64,4096]{1,0:T(8,128)(2,1)}, u32[]{:S(2)}) copy-start(bf16[64,4096]{1,0:T(8,128)(2,1)} %wv.1) | copy-start | bytes 1572868
  27.0 49.5 %copy-start.16 = (bf16[64,4096]{1,0:T(8,128)(2,1)S(1)}, bf16[64,4096]{1,0:T(8,128)(2,1)}, u32[]{:S(2)}) copy-start(bf16[64,4096]{1,0:T(8,128)(2,1)} %ws.1) | copy-start | bytes 1572868
  75.3 31.1 %copy-start.21 = (f32[1,2048]{1,0:T(1,128)}, f32[1,2048]{1,0:T(1,128)S(1)}, u32[]{:S(2)}) copy-start(f32[1,2048]{1,0:T(1,128)S(1)} %reshape_squeeze.12.gain) | copy-start | bytes 24580
  109.7 171.0 %all-gather.11.cloned.1.call-start = ((), (), s32[]{:S(2)}) async-start(), calls=%async_computation.11 | async-start | bytes 5242880 | tf_op jit(solution)/shard_map/all_gather | solution.py:1114
  110.4 205.5 %all-gather.9.cloned.1.call-start = ((), (), s32[]{:S(2)}) async-start(), calls=%async_computation.10 | async-start | bytes 2621440 | tf_op jit(solution)/shard_map/all_gather | solution.py:1114
  111.0 410.4 %reduce-scatter.8.cloned.1.call-start = ((), (), s32[]{:S(2)}) async-start(), calls=%async_computation.13 | async-start | bytes 2621440 | tf_op jit(solution)/shard_map/reduce_scatter | solution.py:1118
  117.8 70.2 %copy-start.2 = (f32[8,256,128]{2,1,0:T(8,128)}, f32[8,256,128]{2,1,0:T(8,128)S(1)}, u32[]{:S(2)}) copy-start(f32[8,256,128]{2,1,0:T(8,128)S(1)} %get-tuple-element.90.sine) | copy-start | bytes 3145732
  118.6 69.4 %copy-start.1 = (f32[8,256,256]{2,1,0:T(8,128)}, f32[8,256,256]{2,1,0:T(8,128)S(1)}, u32[]{:S(2)}) copy-start(f32[8,256,256]{2,1,0:T(8,128)S(1)} %fusion.4.mask) | copy-start | bytes 6291460
  316.0 11.8 %copy-start.9 = (bf16[256,2048]{1,0:T(8,128)(2,1)S(1)}, bf16[256,2048]{1,0:T(8,128)(2,1)}, u32[]{:S(2)}) copy-start(bf16[256,2048]{1,0:T(8,128)(2,1)} %cot_in.1) | copy-start | bytes 3145732
  316.0 11.8 %copy-start.20 = (f32[2,2048]{1,0:T(2,128)S(1)}, f32[2,2048]{1,0:T(2,128)}, u32[]{:S(2)}) copy-start(f32[2,2048]{1,0:T(2,128)} %pad_maximum_fusion.1.vec) | copy-start | bytes 49156
  431.1 122.1 %reduce-scatter.12.cloned.1.call-start = ((), (), s32[]{:S(2)}) async-start(), calls=%async_computation.15 | async-start | bytes 5242880 | tf_op jit(solution)/shard_map/reduce_scatter | solution.py:1118
  444.6 198.2 %reduce-scatter.6.cloned.1.call-start = ((), (), s32[]{:S(2)}) async-start(), calls=%async_computation.12 | async-start | bytes 5242880 | tf_op jit(solution)/shard_map/reduce_scatter | solution.py:1118
  468.2 211.4 %reduce-scatter.14.cloned.1.call-start = ((), (), s32[]{:S(2)}) async-start(), calls=%async_computation.16 | async-start | bytes 2621440 | tf_op jit(solution)/shard_map/reduce_scatter | solution.py:1118
  478.4 246.3 %reduce-scatter.10.cloned.1.call-start = ((), (), s32[]{:S(2)}) async-start(), calls=%async_computation.14 | async-start | bytes 2621440 | tf_op jit(solution)/shard_map/reduce_scatter | solution.py:1118
  491.5 12.0 %collective-permute-start = (bf16[128,2048]{1,0:T(8,128)(2,1)}, bf16[128,2048]{1,0:T(8,128)(2,1)S(1)}, u32[]{:S(2)}, u32[]{:S(2)}) collective-permute-start(bf16[128,2048]{1,0:T(8,128)(2,1)} %get-tuple-element.89), channel_id=1, source_target_pairs={{0,3},{1,7},{2,0},{3,4},{4,1},{5,5},{6,2},{7,6},{8,11},{9,15},{10,... | collective-permute-start | bytes 1572872 | tf_op jit(solution)/shard_map/ppermute | solution.py:1108
  494.6 25.0 %collective-permute-start.1 = (bf16[128,2048]{1,0:T(8,128)(2,1)S(1)}, bf16[128,2048]{1,0:T(8,128)(2,1)S(1)}, u32[]{:S(2)}, u32[]{:S(2)}) collective-permute-start(bf16[128,2048]{1,0:T(8,128)(2,1)S(1)} %get-tuple-element.88), channel_id=1, source_target_pairs={{0,2},{1,6},{2,3},{3,7},{4,0},{5,4},{6,1},{7,5},{8,10},{9,14},{10,... | collective-permute-start | bytes 1572872 | tf_op jit(solution)/shard_map/ppermute | solution.py:1108
  496.1 23.5 %collective-permute-start.2 = (bf16[128,2048]{1,0:T(8,128)(2,1)S(1)}, bf16[128,2048]{1,0:T(8,128)(2,1)S(1)}, u32[]{:S(2)}, u32[]{:S(2)}) collective-permute-start(bf16[128,2048]{1,0:T(8,128)(2,1)S(1)} %get-tuple-element.87), channel_id=1, source_target_pairs={{0,1},{1,5},{2,2},{3,6},{4,3},{5,7},{6,0},{7,4},{8,9},{9,13},{10,1... | collective-permute-start | bytes 1572872 | tf_op jit(solution)/shard_map/ppermute | solution.py:1108
  498.6 21.1 %collective-permute-start.3 = (bf16[128,2048]{1,0:T(8,128)(2,1)S(1)}, bf16[128,2048]{1,0:T(8,128)(2,1)S(1)}, u32[]{:S(2)}, u32[]{:S(2)}) collective-permute-start(bf16[128,2048]{1,0:T(8,128)(2,1)S(1)} %get-tuple-element.86), channel_id=1, source_target_pairs={{0,0},{1,4},{2,1},{3,5},{4,2},{5,6},{6,3},{7,7},{8,8},{9,12},{10,9... | collective-permute-start | bytes 1572872 | tf_op jit(solution)/shard_map/ppermute | solution.py:1108
  553.3 89.5 %all-to-all-start.2 = ((bf16[8,64,1024]{2,1,0:T(8,128)(2,1)}), bf16[8,64,1024]{2,1,0:T(8,128)(2,1)}, u32[]{:S(2)}, u32[]{:S(2)}) async-start(bf16[8,64,1024]{2,1,0:T(8,128)(2,1)} %bitcast.55), calls=%async_computation.6 | async-start | bytes 2097152 | tf_op jit(solution)/shard_map/all_to_all | solution.py:1094
  642.8 38.8 %copy-start.11 = (bf16[8,64,512]{2,1,0:T(8,128)(2,1)S(1)}, bf16[8,64,512]{2,1,0:T(8,128)(2,1)}, u32[]{:S(2)}) copy-start(bf16[8,64,512]{2,1,0:T(8,128)(2,1)} %all_to_all.27.x) | copy-start | bytes 1572868
  642.8 86.6 %all-to-all-start = ((bf16[8,64,1024]{2,1,0:T(8,128)(2,1)}), bf16[8,64,1024]{2,1,0:T(8,128)(2,1)S(1)}, u32[]{:S(2)}, u32[]{:S(2)}) async-start(bf16[8,64,1024]{2,1,0:T(8,128)(2,1)} %bitcast.54), calls=%async_computation.1 | async-start | bytes 2097152 | tf_op jit(solution)/shard_map/all_to_all | solution.py:1094
  682.7 48.2 %copy-start.23 = (f32[256,2048]{1,0:T(8,128)S(1)}, f32[256,2048]{1,0:T(8,128)}, u32[]{:S(2)}) copy-start(f32[256,2048]{1,0:T(8,128)} %get-tuple-element.117) | copy-start | bytes 6291460
  (20 other events, 47.5 us)
Sparse Core Ops, SparseCore 0:
  25.8 79.3 all-gather.6
  109.8 78.5 all-gather.4
  190.0 79.2 all-gather.10
  270.6 45.2 all-gather.8
  431.3 42.9 reduce-scatter.7
  476.4 76.8 reduce-scatter.11
  555.6 78.6 reduce-scatter.5
  636.6 42.8 reduce-scatter.13
  681.8 42.8 reduce-scatter.9

commit v10 on v9

--- a/solution.py
+++ b/solution.py
@@ -157,25 +157,33 @@
     )(*args)
 
 
-def first_kernel(wq, wk, wo, out, ssem, rsem, local):
+def first_kernel(n, wq, wk, wo, wd, out, wd_out, ssem, rsem, local):
     me, peer = place()
-    t = lax.rem(me, TP)
-    meet([peer(k) for k in range(1, TP)])
+    t, g = lax.rem(me, TP), lax.div(me, TP)
+    others = others_along(n)
+    meet([peer(k) for k in range(1, TP)] + others)
     sems = (ssem, rsem)
     shard, cq, co = wq.shape[0], wq.shape[1] // TP, wo.shape[1] // TP
     low, high = pl.ds(0, shard), pl.ds(shard, shard)
+    along = [remote(wd, wd_out.at[g], sems, 28 + j, dev) for j, dev in enumerate(others)]
+    for copy in along:
+        copy.start()
+    keep = pltpu.make_async_copy(wd, wd_out.at[g], local.at[4])
+    keep.start()
     finish([
         send_columns(wq, out, cq, 0, sems, 0, local.at[0], t, peer),
         send_columns(wk, out, cq, cq, sems, 7, local.at[1], t, peer),
         send_columns(wo, out, co, 2 * cq, sems, 14, local.at[2], t, peer, low),
         send_columns(wo, out, co, 2 * cq + co, sems, 21, local.at[3], t, peer, high),
+        (along, keep),
     ])
 
 
-def first_exchange(wq, wk, wo, cid):
+def first_exchange(n, wq, wk, wo, wd, cid):
     width = 2 * wq.shape[1] // TP + 2 * wo.shape[1] // TP
-    outs = (SDS((TP, wq.shape[0], width), bf),)
-    return exchange_call(first_kernel, outs, (wq, wk, wo), 28, 4, cid)[0]
+    outs = (SDS((TP, wq.shape[0], width), bf), SDS((n // TP,) + wd.shape, bf))
+    kernel = functools.partial(first_kernel, n)
+    return exchange_call(kernel, outs, (wq, wk, wo, wd), 28 + n // TP, 5, cid)
 
 
 def others_along(n):
@@ -741,9 +749,16 @@
     )(x, gu)
 
 
-def hidden_back_kernel(cot, down, act, slope, out):
+def hidden_back_kernel(cot, d0, d1, act, slope, out, down):
     width = act.shape[2]
     step = 256
+    early, rows = d0.shape[1], d0.shape[1] + d1.shape[1]
+
+    @pl.when(pl.program_id(0) == 0)
+    def _():
+        for g in range(d0.shape[0]):
+            down[g * rows : g * rows + early] = d0[g]
+            down[g * rows + early : (g + 1) * rows] = d1[g]
 
     @pl.loop(0, width // step)
     def _(j):
@@ -757,7 +772,7 @@
         out[:, :, behind] = (grad * act[:, :, at]).astype(bf)
 
 
-def hidden_back(cot, down, act, slope):
+def hidden_back(cot, d0, d1, act, slope):
     _, r, d = cot.shape
     width = act.shape[2]
     row = pl.BlockSpec((2, r, width), lambda k: (k, 0, 0))
@@ -767,17 +782,19 @@
         out_shape=SDS((TP, r, 2 * width), bf),
         in_specs=[
             pl.BlockSpec((2, r, d), lambda k: (k, 0, 0)),
-            pl.BlockSpec(down.shape, lambda k: (0, 0)),
+            pl.BlockSpec(d0.shape, lambda k: (0, 0, 0)),
+            pl.BlockSpec(d1.shape, lambda k: (0, 0, 0)),
             row,
             row,
         ],
+        scratch_shapes=[pltpu.VMEM((width, d), bf)],
         out_specs=pl.BlockSpec((2, r, 2 * width), lambda k: (k, 0, 0)),
         compiler_params=pltpu.CompilerParams(vmem_limit_bytes=56 << 20),
         cost_estimate=pl.CostEstimate(
             flops=2 * TP * r * d * width, bytes_accessed=24 << 20, transcendentals=0
         ),
         name="hidden_back",
-    )(cot, down, act, slope)
+    )(cot, d0, d1, act, slope)
 
 
 def backward_kernel(
@@ -851,7 +868,7 @@
 
 
 def last_kernel(
-    n, gqkv_in, gs_in, wqk_in, wvs_in, a2_in, w2_in, tok_in, gmid_in, gain, sums2,
+    n, gqkv_in, gs_in, wqk_in, wvs_in, a2_in, d0, d1, tok_in, gmid_in, gain, sums2,
     gtok, ffn, vec_out, gqkv, gs, wqk, wvs, a2, w2, tok, gmid,
     po, pe, rc, sb, ring, pe2, rc2, sb2, ring2, acc, vecs, near, far, part, ssem, rsem, load,
 ):
@@ -870,7 +887,11 @@
     for i in (1, 2, 0):
         for piece in pieces:
             piece(i).start()
-    second = loads.whole(a2_in, a2), loads.whole(w2_in, w2)
+    second = [loads.whole(a2_in, a2)]
+    early, rows = d0.shape[1], d0.shape[1] + d1.shape[1]
+    for k in range(dp):
+        second.append(loads.whole(d0.at[k], w2.at[pl.ds(k * rows, early)]))
+        second.append(loads.whole(d1.at[k], w2.at[pl.ds(k * rows + early, rows - early)]))
     arrivals = loads.whole(tok_in, tok), loads.whole(gmid_in, gmid)
 
     def all_here(waits):
@@ -960,19 +981,20 @@
     two.finish()
 
 
-def last_exchange(n, gqkv, gs, wqk, wvs, a2, w2, tok, gmid, gain, sums2, cid):
+def last_exchange(n, gqkv, gs, wqk, wvs, a2, d0, d1, tok, gmid, gain, sums2, cid):
     dp = n // TP
     _, r, _ = a2.shape
-    c = w2.shape[1]
+    c = d0.shape[2]
     width = c // dp
     count = 2 * REDUCE_SEMS + dp + TP
     return pl.pallas_call(
         functools.partial(last_kernel, n),
         out_shape=(SDS((r, c), f32), SDS((r, c), f32), SDS((8, width), f32)),
-        in_specs=[ANY] * 8 + [VMEM] * 2,
+        in_specs=[ANY] * 9 + [VMEM] * 2,
         out_specs=(VMEM,) * 3,
         scratch_shapes=[
-            pltpu.VMEM(x.shape, x.dtype) for x in (gqkv, gs, wqk, wvs, a2, w2, tok, gmid)
+            pltpu.VMEM(x.shape, x.dtype)
+            for x in (gqkv, gs, wqk, wvs, a2, SDS((a2.shape[2], c), bf), tok, gmid)
         ]
         + reduce_scratch(r, c)
         + reduce_scratch(r, c, bf)[1:]
@@ -984,13 +1006,13 @@
             pltpu.VMEM((8, width), f32),
             pltpu.SemaphoreType.DMA((count,)),
             pltpu.SemaphoreType.DMA((count,)),
-            pltpu.SemaphoreType.DMA((14,)),
+            pltpu.SemaphoreType.DMA((13 + 2 * dp,)),
         ],
         compiler_params=pltpu.CompilerParams(
             collective_id=cid, has_side_effects=True, vmem_limit_bytes=ALL_VMEM
         ),
         name="last_exchange",
-    )(gqkv, gs, wqk, wvs, a2, w2, tok, gmid, gain, sums2)
+    )(gqkv, gs, wqk, wvs, a2, d0, d1, tok, gmid, gain, sums2)
 
 
 def gate_back_kernel(g_low, w, ret, swi, gret, gswi, whole):
@@ -1082,6 +1104,61 @@
     )(*arrays)
 
 
+def spread_kernel(a, b, out, turned, made, ssem, rsem, local):
+    me, peer = place()
+    t = lax.rem(me, TP)
+    first = me - t
+    place_of, low = lax.div(t, 2), lax.rem(t, 2)
+    sems = (ssem, rsem)
+    enter = greet([peer(k) for k in range(1, TP)])
+    turned[...] = a[...].reshape(-1, a.shape[2]).T
+    rows, tile = out.shape[1], 512
+    enter()
+    copies = []
+    for j in range(out.shape[2] // tile):
+        at = pl.ds(j * tile, tile)
+        made[:, at] = jnp.dot(
+            turned[...], b[:, :, at].reshape(turned.shape[1], tile), preferred_element_type=f32
+        ).astype(bf)
+        for m in range(4):
+            chunk = lax.rem(place_of + m, 4)
+            dev = first + 4 * low + chunk
+            src = made.at[pl.ds(pl.multiple_of(chunk * rows, rows), rows), at]
+            dst = out.at[place_of, :, at]
+            i = 4 * j + m
+            away = remote(src, dst, sems, i, dev)
+            here = pltpu.make_async_copy(src, dst, local.at[i])
+            pl.when(dev != me)(away.start)
+            pl.when(dev == me)(here.start)
+            copies.append((dev, away, here))
+    for dev, away, here in copies:
+        pl.when(dev != me)(away.wait)
+        pl.when(dev == me)(here.wait)
+
+
+def spread_product(a, b, cid):
+    _, r, m = a.shape
+    width = b.shape[2]
+    count = 4 * (width // 512)
+    return pl.pallas_call(
+        spread_kernel,
+        out_shape=SDS((4, m // 4, width), bf),
+        in_specs=[VMEM, VMEM],
+        out_specs=ANY,
+        scratch_shapes=[
+            pltpu.VMEM((m, TP * r), bf),
+            pltpu.VMEM((m, width), bf),
+            pltpu.SemaphoreType.DMA((count,)),
+            pltpu.SemaphoreType.DMA((count,)),
+            pltpu.SemaphoreType.DMA((count,)),
+        ],
+        compiler_params=pltpu.CompilerParams(
+            collective_id=cid, has_side_effects=True, vmem_limit_bytes=32 << 20
+        ),
+        name="spread_product",
+    )(a, b)
+
+
 def tp_groups(n):
     return [[g * TP + t for t in range(TP)] for g in range(n // TP)]
 
@@ -1092,22 +1169,6 @@
 
 def plane_a2a(x, n):
     return lax.all_to_all(x, AXIS, 0, 0, axis_index_groups=tp_groups(n), tiled=True)
-
-
-def spread_rows(x, n):
-    rows = x.shape[0] // 4
-    t = lax.rem(lax.axis_index(AXIS), TP)
-    got = []
-    for m in range(4):
-        chunk = lax.dynamic_slice_in_dim(x, lax.rem(lax.div(t, 2) + m, 4) * rows, rows, 0)
-        pairs = [
-            (g * TP + h, g * TP + 4 * (h % 2) + (h // 2 + m) % 4)
-            for g in range(n // TP)
-            for h in range(TP)
-        ]
-        got.append(lax.ppermute(chunk, AXIS, pairs))
-    turned = jnp.concatenate(got[::-1] * 2, axis=0)
-    return lax.dynamic_slice_in_dim(turned, (3 - lax.rem(t, 4)) * rows, 4 * rows, 0)
 
 
 def dp_gather(x, n):
@@ -1200,7 +1261,8 @@
     lens = jnp.pad(lengths[0].astype(f32), (0, shard - lengths.shape[1]))
     vec = jnp.stack([v.astype(f32) for v in (gain1, bias1, gain2, bias2)] + [lens])
     vec = jnp.pad(vec, ((0, 3), (0, 128 - shard)))
-    qko_blk = first_exchange(wq, wk, wo, 1)
+    early = max(16, wd.shape[0] // 4)
+    qko_blk, d0 = first_exchange(n, wq, wk, wo, wd[:early], 1)
     qko = dp_gather(qko_blk.reshape(TP * shard, 4 * KH), n)
     tok_all, vec_all = second_exchange(n, after(tokens, qko_blk), vec, 2)
     gain1f, bias1f, gain2f, bias2f = (
@@ -1211,7 +1273,7 @@
     vs_blk, gu_blk, normed = third_exchange(wv, ws, gu_in, tok_all, gain1f, bias1f, 3)
     vs = dp_gather(vs_blk.reshape(TP * shard, 2 * VH), n)
     gu = dp_gather(gu_blk.reshape(TP * shard, 2 * dp * unit), n)
-    down = dp_gather(wd, n)
+    down = d0, dp_gather(wd[early:], n).reshape(dp, wd.shape[0] - early, d)
 
     mine = lax.dynamic_slice_in_dim(vec_all, lax.div(me, TP), 1, 0)[0, :, 4, :3]
     order = jnp.arange(TP, dtype=jnp.int32)
@@ -1233,7 +1295,7 @@
     down_grad = row_product(hidden, cot_all)
     g_down = dp_reduce(down_grad, n)
 
-    g_fs = hidden_back(cot_all, down, act, slope)
+    g_fs = hidden_back(cot_all, *down, act, slope)
     gu_grad = row_product(normed2, g_fs)
     g_gu = dp_reduce(gu_grad, n)
     g_middle, g_low, sums2 = backward_exchange(g_fs, gu, middle, cot, vec2, 6)
@@ -1241,18 +1303,18 @@
     g_retained, g_swish = gate_back(g_low, out_blk, retained, swish_in)
     swish_grad = row_product(normed, g_swish)
     g_swi = dp_reduce(swish_grad, n)
-    out_grad = row_product(mixed, g_low)
     spread = wo.shape[0] * HEADS == VH * 2
     if spread:
-        out_grad = spread_rows(out_grad, n)
+        out_grad = spread_product(mixed, g_low, 8).reshape(VH, d)
     else:
+        out_grad = row_product(mixed, g_low)
         out_grad = plane_a2a(col_blocks(out_grad), n)
     g_qkv = scores_back(scores, mask, q_rot, k_rot, v_low, g_retained, cosine, sine)
     qkv_grad = row_product(normed, g_qkv)
     g_qkv_own = dp_reduce(qkv_grad, n)
     g_out = dp_reduce(out_grad, n)
     grad_tokens, ffn, g_vecs = last_exchange(
-        n, g_qkv, g_swish, qk, vs, hidden, down, tokens, g_middle, gain1f, sums2, 7
+        n, g_qkv, g_swish, qk, vs, hidden, *down, tokens, g_middle, gain1f, sums2, 7
     )
     layer_out = (middle + ffn).astype(bf)
 

time: 743 us -> 736 us (level)
  Pallas kernels: 515 us -> 531 us
  waiting for transfers between devices: 126 us -> 110 us
  starting transfers between devices: 21 us -> 11.1 us
    pallas_call x0 -> x1, Pallas kernels: none -> 26.3 us  [spread_product(): pl.pallas_call(spread_kernel, out_shape=SDS((4, m // 4, width), bf), in_s...]
    ppermute x4 -> x0, waiting for transfers between devices: 17.9 us -> none  [spread_rows(): got.append(lax.ppermute(chunk, AXIS, pairs))]
    reduce_scatter x5, waiting for transfers between devices: 86.9 us -> 97.8 us  [dp_reduce(): lax.psum_scatter(x, AXIS, scatter_dimension=0, tiled=True, axis_index_gro...]
    pallas_call x5 -> x4, Pallas kernels: 56.5 us -> 45.6 us  [row_product(): pl.pallas_call(product_kernel, grid=(width // part, m // tile), out_shape...]
    ppermute x4 -> x0, starting transfers between devices: 10.1 us -> none  [spread_rows(): got.append(lax.ppermute(chunk, AXIS, pairs))]
    all_gather x4, waiting for transfers between devices: 19.5 us -> 11.5 us  [dp_gather(): lax.all_gather(x, AXIS, axis=0, tiled=True, axis_index_groups=dp_groups(n))]
    unnamed x68 -> x75, local copies, waits for them, and re-layouts: 26.4 us -> 30.9 us
  transfers between devices with their start and end apart: 15 -> 11, of which waited for: 6 -> 4; matrix products, arithmetic and copies ran while one was open for 4% -> 3% of each run, Pallas kernels for 52% -> 55%
where the time goes in v10:
time: 736 us; the launch traced here: 732 us
  Pallas kernels  531 us (72%)
  waiting for transfers between devices  110 us (15%)
  local copies, waits for them, and re-layouts  36.1 us (5%)
  other arithmetic  15.3 us (2%)
  blocking collectives  14.4 us (2%)
  between operations  14.4 us (2%)
  starting transfers between devices  11.1 us (2%)
    pallas_call x4, Pallas kernels, exchange_call(): pl.pallas_call(kernel, out_shape=outs, in_specs=specs or [VMEM] * len(arg...  150 us
    reduce_scatter x5, waiting for transfers between devices, dp_reduce(): lax.psum_scatter(x, AXIS, scatter_dimension=0, tiled=True, axis_index_gro...  97.8 us
    pallas_call x1, Pallas kernels, forward_exchange(): pl.pallas_call(forward_kernel, out_shape=tuple((SDS(*b) for b in blocks))...  87.1 us
    pallas_call x1, Pallas kernels, last_exchange(): pl.pallas_call(functools.partial(last_kernel, n), out_shape=(SDS((r, c),...  84.9 us
    pallas_call x1, Pallas kernels, backward_exchange(): pl.pallas_call(backward_kernel, out_shape=(SDS((r, c), f32), SDS((TP, r,...  81.1 us
    pallas_call x4, Pallas kernels, row_product(): pl.pallas_call(product_kernel, grid=(width // part, m // tile), out_shape...  45.6 us
    unnamed x75, local copies, waits for them, and re-layouts  30.9 us
    pallas_call x1, Pallas kernels, spread_product(): pl.pallas_call(spread_kernel, out_shape=SDS((4, m // 4, width), bf), in_s...  26.3 us
  transfers between devices with their start and end apart: 11, of which 4 were waited for; matrix products, arithmetic and copies ran while one was open for 3% of the time, Pallas kernels for 55%

profile of v10, /device:TPU:14, one launch (start us, length us, event | category | flops | bytes accessed | tf_op | source)
XLA Modules:
  0.0 732.3 jit_solution(1208036173844743992)
XLA Ops:
  11.1 15.7 %shard_map.254 = (bf16[8,64,1024]{2,1,0:T(8,128)(2,1)}, bf16[4,32,2048]{2,1,0:T(8,128)(2,1)S(1)}) custom-call(bf16[64,2048]{1,0:T(8,128)(2,1)S(1)} %copy-done.21, bf16[64,2048]{1,0:T(8,128)(2,1)S(1)} %copy-done.22, bf16[128,2048]{1,0:T(8,128)(2,1)S(1)} %copy-done.20, bf16[32,2048]{1,0:T(8,128)(2,1)S(1)} %slice.33.wd), custom_call_target="tpu_custom_call" | custom-call | tf_op jit(solution)/shard_map/pallas_call | solution.py:144
  30.1 41.8 %shard_map.255 = (bf16[8,256,2048]{2,1,0:T(8,128)(2,1)S(1)}, f32[4,8,8,128]{3,2,1,0:T(8,128)S(1)}) custom-call(bf16[256,2048]{1,0:T(8,128)(2,1)S(1)} %copy-done.5, f32[8,128]{1,0:T(8,128)S(1)} %pad.9.vec), custom_call_target="tpu_custom_call" | custom-call | tf_op jit(solution)/shard_map/pallas_call | solution.py:144
  80.1 26.4 %shard_map.256 = (bf16[8,64,1024]{2,1,0:T(8,128)(2,1)}, bf16[8,64,1024]{2,1,0:T(8,128)(2,1)}, bf16[8,256,2048]{2,1,0:T(8,128)(2,1)S(1)}) custom-call(bf16[64,4096]{1,0:T(8,128)(2,1)S(1)} %copy-done.18, bf16[64,4096]{1,0:T(8,128)(2,1)S(1)} %copy-done.19, bf16[8,64,1024]{2,1,0:T(8,128)(2,1)S(1)} %pad_maximum_fusion.gu, bf16[8,256,2048]{2,1,0:T(8,128)(2,1)S(1)} %copy-done.8, ...), custom_call_target="tpu_custom_call" | custom-call | tf_op jit(solution)/shard_map/pallas_call | solution.py:144
  113.3 5.3 multiply_sine_fusion
  122.6 66.3 %shard_map.257 = (bf16[8,256,2048]{2,1,0:T(8,128)(2,1)}, bf16[8,4,2,64,256]{4,3,2,1,0:T(8,128)(2,1)S(1)}, bf16[8,256,256]{2,1,0:T(8,128)(2,1)S(1)}, bf16[8,256,2...) custom-call(bf16[256,2048]{1,0:T(8,128)(2,1)S(1)} %copy-done.9, ...), custom_call_target="tpu_custom_call" | custom-call | tf_op jit(solution)/shard_map/pallas_call | solution.py:144
  194.5 87.1 %forward_exchange.1 = (bf16[8,256,512]{2,1,0:T(8,128)(2,1)}, bf16[8,256,512]{2,1,0:T(8,128)(2,1)}, f32[8,256,512]{2,1,0:T(8,128)}, f32[8,256,512]{2,1,0:T(8,128)...) custom-call(bf16[8,256,2048]{2,1,0:T(8,128)(2,1)} %copy-done, ...), custom_call_target="tpu_custom_call" | custom-call | tf_op jit(solution)/shard_map/forward_exchange/pallas_call | solution.py:659
  281.7 15.7 %hidden_units.1 = (bf16[8,256,512]{2,1,0:T(8,128)(2,1)}, f32[8,256,512]{2,1,0:T(8,128)}, f32[8,256,512]{2,1,0:T(8,128)}) custom-call(bf16[8,256,2048]{2,1,0:T(8,128)(2,1)} %get-tuple-element.64.x.a, bf16[2048,1024]{1,0:T(8,128)(2,1)} %all-gather.11.cloned.1.call-done.gu.w_in), custom_call_target="tpu_custom_call" | custom-call | flops 8589934592 | bytes 25165824 | tf_op jit(solution)/shard_map/hidden_units/pallas_call | solution.py:735
  297.4 11.4 %all-gather.9.cloned.1.call-done = bf16[384,2048]{1,0:T(8,128)(2,1)} async-done(((bf16[96,2048]{1,0:T(8,128)(2,1)}), bf16[384,2048]{1,0:T(8,128)(2,1)}) %all-gather.9.cloned.1.call-update) | async-done | bytes 1572880 | tf_op jit(solution)/shard_map/all_gather | solution.py:1175
  308.8 11.9 %hidden_back.1.a_in.b = bf16[8,256,1024]{2,1,0:T(8,128)(2,1)} custom-call(bf16[8,256,2048]{2,1,0:T(8,128)(2,1)} %get-tuple-element.62.cot.b, bf16[4,32,2048]{2,1,0:T(8,128)(2,1)} %copy-done.15, bf16[4,96,2048]{2,1,0:T(8,128)(2,1)} %bitcast.51, f32[8,256,512]{2,1,0:T(8,128)} %get-tuple-element.66.act, f32[8,256,512]{2,1,0:T(8,128)} %get-tuple-element.67.slope), custom_call_target="tpu_custom_call" | custom-call | flops 4294967296 | bytes 25165824 | tf_op jit(solution)/shard_map/hidden_back/pallas_call | solution.py:779
  320.7 81.1 %backward_exchange.1 = (f32[256,2048]{1,0:T(8,128)}, bf16[8,256,2048]{2,1,0:T(8,128)(2,1)}, f32[2,2048]{1,0:T(2,128)S(1)}) custom-call(bf16[8,256,1024]{2,1,0:T(8,128)(2,1)} %hidden_back.1.a_in.b, bf16[2048,1024]{1,0:T(8,128)(2,1)} %all-gather.11.cloned.1.call-done.gu.w_in, f32[256,2048]{1,0:T(8,128)} %get-tuple-element.58.mid_in, ...), custom_call_target="tpu_custom_call" | custom-call | tf_op jit(solution)/shard_map/backward_exchange/pallas_call | solution.py:848
  402.4 12.6 %gate_back.1 = (bf16[8,256,512]{2,1,0:T(8,128)(2,1)}, bf16[8,256,512]{2,1,0:T(8,128)(2,1)}) custom-call(bf16[8,256,2048]{2,1,0:T(8,128)(2,1)} %get-tuple-element.68.g_low.b, bf16[8,512,256]{2,1,0:T(8,128)(2,1)} %bitcast.49, f32[8,256,512]{2,1,0:T(8,128)} %get-tuple-element.69.ret, f32[8,256,512]{2,1,0:T(8,128)} %get-tuple-element.70.swi), custom_call_target="tpu_custom_call" | custom-call | flops 4294967296 | bytes 23068672 | tf_op jit(solution)/shard_map/gate_back/pallas_call | solution.py:1050
  415.1 8.8 %row_product.5 = bf16[2048,512]{1,0:T(8,128)(2,1)} custom-call(bf16[8,256,2048]{2,1,0:T(8,128)(2,1)} %copy-done, bf16[8,256,512]{2,1,0:T(8,128)(2,1)} %get-tuple-element.72.gs_in.b), custom_call_target="tpu_custom_call" | custom-call | flops 4294967296 | bytes 12582912 | tf_op jit(solution)/shard_map/row_product/pallas_call | solution.py:692
  423.9 13.3 %row_product.6 = bf16[2048,1024]{1,0:T(8,128)(2,1)} custom-call(bf16[8,256,2048]{2,1,0:T(8,128)(2,1)} %get-tuple-element.64.x.a, bf16[8,256,1024]{2,1,0:T(8,128)(2,1)} %hidden_back.1.a_in.b), custom_call_target="tpu_custom_call" | custom-call | flops 8589934592 | bytes 16777216 | tf_op jit(solution)/shard_map/row_product/pallas_call | solution.py:692
  437.3 10.1 %scores_back.1.gqkv_in.b = bf16[8,256,1024]{2,1,0:T(8,128)(2,1)} custom-call(bf16[8,256,256]{2,1,0:T(8,128)(2,1)} %copy-done.11, f32[8,256,256]{2,1,0:T(8,128)} %copy-done.2, bf16[8,256,256]{2,1,0:T(8,128)(2,1)} %copy-done.16, bf16[8,256,256]{2,1,0:T(8,128)(2,1)} %copy-done.17, bf16[8,256,512]{2,1,0:T(8,128)(2,1)} %get-tuple-element.61.v, ...), custom_call_target="tpu_custom_call" | custom-call | flops 1610612736 | bytes 16777216 | tf_op jit(solution)/shard_map/scores_back/pallas_call | solution.py:1093
  447.5 13.3 %row_product.4 = bf16[2048,1024]{1,0:T(8,128)(2,1)} custom-call(bf16[8,256,2048]{2,1,0:T(8,128)(2,1)} %copy-done, bf16[8,256,1024]{2,1,0:T(8,128)(2,1)} %scores_back.1.gqkv_in.b), custom_call_target="tpu_custom_call" | custom-call | flops 8589934592 | bytes 16777216 | tf_op jit(solution)/shard_map/row_product/pallas_call | solution.py:692
  460.9 10.2 %row_product.7 = bf16[512,2048]{1,0:T(8,128)(2,1)} custom-call(bf16[8,256,512]{2,1,0:T(8,128)(2,1)} %get-tuple-element.74.a2_in.a, bf16[8,256,2048]{2,1,0:T(8,128)(2,1)} %get-tuple-element.62.cot.b), custom_call_target="tpu_custom_call" | custom-call | flops 4294967296 | bytes 12582912 | tf_op jit(solution)/shard_map/row_product/pallas_call | solution.py:692
  476.8 26.3 %spread_product.1 = bf16[4,128,2048]{2,1,0:T(8,128)(2,1)} custom-call(bf16[8,256,512]{2,1,0:T(8,128)(2,1)S(1)} %copy-done.13, bf16[8,256,2048]{2,1,0:T(8,128)(2,1)S(1)} %copy-done.1), custom_call_target="tpu_custom_call" | custom-call | tf_op jit(solution)/shard_map/spread_product/pallas_call | solution.py:1143
  503.2 14.4 %all_to_all.27.x = bf16[8,64,512]{2,1,0:T(8,128)(2,1)} all-to-all(bf16[8,64,512]{2,1,0:T(8,128)(2,1)} %bitcast.62), channel_id=1, replica_groups={{0,1,2,3,4,5,6,7},{8,9,10,11,12,13,14,15},{16,17,18,19,20,21,22,23},{24..., dimensions={0} | all-to-all | bytes 1048576 | tf_op jit(solution)/shard_map/all_to_all | solution.py:1171
  517.6 28.1 %reduce-scatter.12.cloned.1.call-done = bf16[512,1024]{1,0:T(8,128)(2,1)} async-done(((bf16[2048,1024]{1,0:T(8,128)(2,1)}), bf16[512,1024]{1,0:T(8,128)(2,1)}) %reduce-scatter.12.cloned.1.call-update) | async-done | bytes 1048592 | tf_op jit(solution)/shard_map/reduce_scatter | solution.py:1179
  545.6 4.7 all-to-all-start.2
  550.3 84.9 %last_exchange.1 = (f32[256,2048]{1,0:T(8,128)}, f32[256,2048]{1,0:T(8,128)}, f32[8,512]{1,0:T(8,128)}) custom-call(bf16[8,256,1024]{2,1,0:T(8,128)(2,1)} %scores_back.1.gqkv_in.b, bf16[8,256,512]{2,1,0:T(8,128)(2,1)} %get-tuple-element.72.gs_in.b, bf16[2048,512]{1,0:T(8,128)(2,1)} %bitcast.50, bf16[2048,1024]{1,0:T(8,128)(2,1)} %all-gather.5.cloned.1.call-done.wvs_in, ...), custom_call_target="tpu_custom_call" | custom-call | tf_op jit(solution)/shard_map/last_exchange/pallas_call | solution.py:990
  635.3 5.9 all-to-all-start
  645.2 26.7 %reduce-scatter.14.cloned.1.call-done = bf16[128,2048]{1,0:T(8,128)(2,1)} async-done(((bf16[512,2048]{1,0:T(8,128)(2,1)}), bf16[128,2048]{1,0:T(8,128)(2,1)}) %reduce-scatter.14.cloned.1.call-update) | async-done | bytes 524304 | tf_op jit(solution)/shard_map/reduce_scatter | solution.py:1179
  674.0 43.0 %reduce-scatter.10.cloned.1.call-done = bf16[128,2048]{1,0:T(8,128)(2,1)} async-done(((bf16[512,2048]{1,0:T(8,128)(2,1)}), bf16[128,2048]{1,0:T(8,128)(2,1)}) %reduce-scatter.10.cloned.1.call-update) | async-done | bytes 524304 | tf_op jit(solution)/shard_map/reduce_scatter | solution.py:1179
  (140 shorter events, 52.8 us)
Async XLA Ops:
  7.2 112.2 %all-gather.7.cloned.1.call-start = ((), (), s32[]{:S(2)}) async-start(), calls=%async_computation.9 | async-start | bytes 5242880 | tf_op jit(solution)/shard_map/all_gather | solution.py:1175
  11.1 16.6 %copy-start.29 = (bf16[64,4096]{1,0:T(8,128)(2,1)S(1)}, bf16[64,4096]{1,0:T(8,128)(2,1)}, u32[]{:S(2)}) copy-start(bf16[64,4096]{1,0:T(8,128)(2,1)} %param.26) | copy-start | bytes 1572868
  27.6 166.9 %all-gather.5.cloned.1.call-start = ((), (), s32[]{:S(2)}) async-start(), calls=%async_computation.8 | async-start | bytes 5242880 | tf_op jit(solution)/shard_map/all_gather | solution.py:1175
  28.9 47.8 %copy-start.18 = (bf16[64,4096]{1,0:T(8,128)(2,1)S(1)}, bf16[64,4096]{1,0:T(8,128)(2,1)}, u32[]{:S(2)}) copy-start(bf16[64,4096]{1,0:T(8,128)(2,1)} %wv.1) | copy-start | bytes 1572868
  28.9 47.8 %copy-start.19 = (bf16[64,4096]{1,0:T(8,128)(2,1)S(1)}, bf16[64,4096]{1,0:T(8,128)(2,1)}, u32[]{:S(2)}) copy-start(bf16[64,4096]{1,0:T(8,128)(2,1)} %ws.1) | copy-start | bytes 1572868
  75.4 31.1 %copy-start.24 = (f32[1,2048]{1,0:T(1,128)}, f32[1,2048]{1,0:T(1,128)S(1)}, u32[]{:S(2)}) copy-start(f32[1,2048]{1,0:T(1,128)S(1)} %reshape_squeeze.12.gain) | copy-start | bytes 24580
  76.7 3.4 copy-start.8
  109.8 171.9 %all-gather.11.cloned.1.call-start = ((), (), s32[]{:S(2)}) async-start(), calls=%async_computation.11 | async-start | bytes 5242880 | tf_op jit(solution)/shard_map/all_gather | solution.py:1175
  110.6 198.3 %all-gather.9.cloned.1.call-start = ((), (), s32[]{:S(2)}) async-start(), calls=%async_computation.10 | async-start | bytes 1966080 | tf_op jit(solution)/shard_map/all_gather | solution.py:1175
  111.7 391.5 %reduce-scatter.8.cloned.1.call-start = ((), (), s32[]{:S(2)}) async-start(), calls=%async_computation.13 | async-start | bytes 2621440 | tf_op jit(solution)/shard_map/reduce_scatter | solution.py:1179
  118.6 70.3 %copy-start.3 = (f32[8,256,128]{2,1,0:T(8,128)}, f32[8,256,128]{2,1,0:T(8,128)S(1)}, u32[]{:S(2)}) copy-start(f32[8,256,128]{2,1,0:T(8,128)S(1)} %get-tuple-element.90.sine) | copy-start | bytes 3145732
  119.4 69.5 %copy-start.2 = (f32[8,256,256]{2,1,0:T(8,128)}, f32[8,256,256]{2,1,0:T(8,128)S(1)}, u32[]{:S(2)}) copy-start(f32[8,256,256]{2,1,0:T(8,128)S(1)} %fusion.4.mask) | copy-start | bytes 6291460
  308.8 11.9 %copy-start.10 = (bf16[256,2048]{1,0:T(8,128)(2,1)S(1)}, bf16[256,2048]{1,0:T(8,128)(2,1)}, u32[]{:S(2)}) copy-start(bf16[256,2048]{1,0:T(8,128)(2,1)} %cot_in.1) | copy-start | bytes 3145732
  308.8 11.9 %copy-start.23 = (f32[2,2048]{1,0:T(2,128)S(1)}, f32[2,2048]{1,0:T(2,128)}, u32[]{:S(2)}) copy-start(f32[2,2048]{1,0:T(2,128)} %pad_maximum_fusion.1.vec) | copy-start | bytes 49156
  423.9 121.8 %reduce-scatter.12.cloned.1.call-start = ((), (), s32[]{:S(2)}) async-start(), calls=%async_computation.15 | async-start | bytes 5242880 | tf_op jit(solution)/shard_map/reduce_scatter | solution.py:1179
  437.3 198.0 %reduce-scatter.6.cloned.1.call-start = ((), (), s32[]{:S(2)}) async-start(), calls=%async_computation.12 | async-start | bytes 5242880 | tf_op jit(solution)/shard_map/reduce_scatter | solution.py:1179
  460.8 211.1 %reduce-scatter.14.cloned.1.call-start = ((), (), s32[]{:S(2)}) async-start(), calls=%async_computation.16 | async-start | bytes 2621440 | tf_op jit(solution)/shard_map/reduce_scatter | solution.py:1179
  471.1 246.0 %reduce-scatter.10.cloned.1.call-start = ((), (), s32[]{:S(2)}) async-start(), calls=%async_computation.14 | async-start | bytes 2621440 | tf_op jit(solution)/shard_map/reduce_scatter | solution.py:1179
  472.6 4.1 copy-start.1
  545.6 89.6 %all-to-all-start.2 = ((bf16[8,64,1024]{2,1,0:T(8,128)(2,1)}), bf16[8,64,1024]{2,1,0:T(8,128)(2,1)}, u32[]{:S(2)}, u32[]{:S(2)}) async-start(bf16[8,64,1024]{2,1,0:T(8,128)(2,1)} %bitcast.59), calls=%async_computation.6 | async-start | bytes 2097152 | tf_op jit(solution)/shard_map/all_to_all | solution.py:1171
  635.2 7.2 copy-start.26
  635.3 87.8 %all-to-all-start = ((bf16[8,64,1024]{2,1,0:T(8,128)(2,1)}), bf16[8,64,1024]{2,1,0:T(8,128)(2,1)S(1)}, u32[]{:S(2)}, u32[]{:S(2)}) async-start(bf16[8,64,1024]{2,1,0:T(8,128)(2,1)} %bitcast.58), calls=%async_computation.1 | async-start | bytes 2097152 | tf_op jit(solution)/shard_map/all_to_all | solution.py:1171
  645.2 74.0 %copy-start.12 = (bf16[8,64,512]{2,1,0:T(8,128)(2,1)S(1)}, bf16[8,64,512]{2,1,0:T(8,128)(2,1)}, u32[]{:S(2)}) copy-start(bf16[8,64,512]{2,1,0:T(8,128)(2,1)} %all_to_all.27.x) | copy-start | bytes 1572868
  720.2 4.2 copy-start.27
  (23 other events, 35.3 us)
Sparse Core Ops, SparseCore 0:
  27.7 79.3 all-gather.6
  110.0 78.9 all-gather.4
  190.5 79.1 all-gather.10
  271.7 37.0 all-gather.8
  424.0 42.6 reduce-scatter.7
  468.8 76.7 reduce-scatter.11
  547.9 78.6 reduce-scatter.5
  629.0 42.9 reduce-scatter.13
  674.2 42.8 reduce-scatter.9

commit v11 on v10

--- a/solution.py
+++ b/solution.py
@@ -165,6 +165,7 @@
     sems = (ssem, rsem)
     shard, cq, co = wq.shape[0], wq.shape[1] // TP, wo.shape[1] // TP
     low, high = pl.ds(0, shard), pl.ds(shard, shard)
+    wd = wd.at[pl.ds(0, wd_out.shape[1])]
     along = [remote(wd, wd_out.at[g], sems, 28 + j, dev) for j, dev in enumerate(others)]
     for copy in along:
         copy.start()
@@ -179,9 +180,9 @@
     ])
 
 
-def first_exchange(n, wq, wk, wo, wd, cid):
+def first_exchange(n, wq, wk, wo, wd, early, cid):
     width = 2 * wq.shape[1] // TP + 2 * wo.shape[1] // TP
-    outs = (SDS((TP, wq.shape[0], width), bf), SDS((n // TP,) + wd.shape, bf))
+    outs = (SDS((TP, wq.shape[0], width), bf), SDS((n // TP, early, wd.shape[1]), bf))
     kernel = functools.partial(first_kernel, n)
     return exchange_call(kernel, outs, (wq, wk, wo, wd), 28 + n // TP, 5, cid)
 
@@ -632,7 +633,7 @@
             odd[:, at] = y[r:].astype(odd.dtype)
             return 0
 
-        lax.fori_loop(0, w.shape[0], columns, 0, unroll=4)
+        lax.fori_loop(0, w.shape[0], columns, 0, unroll=2)
 
     def body(at, value):
         value = value + tok[at, :].astype(f32)
@@ -751,7 +752,7 @@
 
 def hidden_back_kernel(cot, d0, d1, act, slope, out, down):
     width = act.shape[2]
-    step = 256
+    step = 512
     early, rows = d0.shape[1], d0.shape[1] + d1.shape[1]
 
     @pl.when(pl.program_id(0) == 0)
@@ -868,8 +869,8 @@
 
 
 def last_kernel(
-    n, gqkv_in, gs_in, wqk_in, wvs_in, a2_in, d0, d1, tok_in, gmid_in, gain, sums2,
-    gtok, ffn, vec_out, gqkv, gs, wqk, wvs, a2, w2, tok, gmid,
+    n, gqkv_in, gs_in, wqk_in, wvs_in, a2_in, d0, d1, tok_in, gain, sums2,
+    gtok, ffn, vec_out, gqkv, gs, wqk, wvs, a2, w2, tok,
     po, pe, rc, sb, ring, pe2, rc2, sb2, ring2, acc, vecs, near, far, part, ssem, rsem, load,
 ):
     dp = n // TP
@@ -892,7 +893,7 @@
     for k in range(dp):
         second.append(loads.whole(d0.at[k], w2.at[pl.ds(k * rows, early)]))
         second.append(loads.whole(d1.at[k], w2.at[pl.ds(k * rows + early, rows - early)]))
-    arrivals = loads.whole(tok_in, tok), loads.whole(gmid_in, gmid)
+    arrivals = (loads.whole(tok_in, tok),)
 
     def all_here(waits):
         def wait():
@@ -941,7 +942,7 @@
         scaled = grad * gain[...]
         mean_g = jnp.mean(scaled, axis=-1, keepdims=True)
         mean_gh = jnp.mean(scaled * hat, axis=-1, keepdims=True)
-        gtok[at, :] = gmid[at, :] + inv * (scaled - mean_g - hat * mean_gh)
+        gtok[at, :] = inv * (scaled - mean_g - hat * mean_gh)
 
     all_here(arrivals)()
     for c in (0, 1):
@@ -981,7 +982,7 @@
     two.finish()
 
 
-def last_exchange(n, gqkv, gs, wqk, wvs, a2, d0, d1, tok, gmid, gain, sums2, cid):
+def last_exchange(n, gqkv, gs, wqk, wvs, a2, d0, d1, tok, gain, sums2, cid):
     dp = n // TP
     _, r, _ = a2.shape
     c = d0.shape[2]
@@ -990,11 +991,11 @@
     return pl.pallas_call(
         functools.partial(last_kernel, n),
         out_shape=(SDS((r, c), f32), SDS((r, c), f32), SDS((8, width), f32)),
-        in_specs=[ANY] * 9 + [VMEM] * 2,
+        in_specs=[ANY] * 8 + [VMEM] * 2,
         out_specs=(VMEM,) * 3,
         scratch_shapes=[
             pltpu.VMEM(x.shape, x.dtype)
-            for x in (gqkv, gs, wqk, wvs, a2, SDS((a2.shape[2], c), bf), tok, gmid)
+            for x in (gqkv, gs, wqk, wvs, a2, SDS((a2.shape[2], c), bf), tok)
         ]
         + reduce_scratch(r, c)
         + reduce_scratch(r, c, bf)[1:]
@@ -1006,13 +1007,13 @@
             pltpu.VMEM((8, width), f32),
             pltpu.SemaphoreType.DMA((count,)),
             pltpu.SemaphoreType.DMA((count,)),
-            pltpu.SemaphoreType.DMA((13 + 2 * dp,)),
+            pltpu.SemaphoreType.DMA((12 + 2 * dp,)),
         ],
         compiler_params=pltpu.CompilerParams(
             collective_id=cid, has_side_effects=True, vmem_limit_bytes=ALL_VMEM
         ),
         name="last_exchange",
-    )(gqkv, gs, wqk, wvs, a2, d0, d1, tok, gmid, gain, sums2)
+    )(gqkv, gs, wqk, wvs, a2, d0, d1, tok, gain, sums2)
 
 
 def gate_back_kernel(g_low, w, ret, swi, gret, gswi, whole):
@@ -1104,36 +1105,55 @@
     )(*arrays)
 
 
-def spread_kernel(a, b, out, turned, made, ssem, rsem, local):
+def spread_kernel(a_in, b_in, out, a, b, turned, made, ssem, rsem, local, load):
     me, peer = place()
     t = lax.rem(me, TP)
-    first = me - t
     place_of, low = lax.div(t, 2), lax.rem(t, 2)
     sems = (ssem, rsem)
     enter = greet([peer(k) for k in range(1, TP)])
-    turned[...] = a[...].reshape(-1, a.shape[2]).T
     rows, tile = out.shape[1], 512
-    enter()
-    copies = []
-    for j in range(out.shape[2] // tile):
-        at = pl.ds(j * tile, tile)
-        made[:, at] = jnp.dot(
-            turned[...], b[:, :, at].reshape(turned.shape[1], tile), preferred_element_type=f32
-        ).astype(bf)
+    tiles = out.shape[2] // tile
+
+    def columns(j):
+        return pl.ds(pl.multiple_of(j * tile, tile), tile)
+
+    def piece(j):
+        return pltpu.make_async_copy(
+            b_in.at[:, :, columns(j)], b.at[:, :, columns(j)], load.at[1 + j]
+        )
+
+    def sends(j, act):
         for m in range(4):
             chunk = lax.rem(place_of + m, 4)
-            dev = first + 4 * low + chunk
-            src = made.at[pl.ds(pl.multiple_of(chunk * rows, rows), rows), at]
-            dst = out.at[place_of, :, at]
+            dev = me - t + 4 * low + chunk
+            src = made.at[pl.ds(pl.multiple_of(chunk * rows, rows), rows), columns(j)]
+            dst = out.at[place_of, :, columns(j)]
             i = 4 * j + m
             away = remote(src, dst, sems, i, dev)
             here = pltpu.make_async_copy(src, dst, local.at[i])
-            pl.when(dev != me)(away.start)
-            pl.when(dev == me)(here.start)
-            copies.append((dev, away, here))
-    for dev, away, here in copies:
-        pl.when(dev != me)(away.wait)
-        pl.when(dev == me)(here.wait)
+            pl.when(dev != me)(getattr(away, act))
+            pl.when(dev == me)(getattr(here, act))
+
+    whole = pltpu.make_async_copy(a_in, a, load.at[0])
+    whole.start()
+    for j in range(tiles):
+        piece(j).start()
+    whole.wait()
+    turned[...] = a[...].reshape(-1, a.shape[2]).T
+    enter()
+
+    @pl.loop(0, tiles)
+    def _(j):
+        piece(j).wait()
+        made[:, columns(j)] = jnp.dot(
+            turned[...], b[:, :, columns(j)].reshape(turned.shape[1], tile),
+            preferred_element_type=f32,
+        ).astype(bf)
+        sends(j, "start")
+
+    @pl.loop(0, tiles)
+    def _(j):
+        sends(j, "wait")
 
 
 def spread_product(a, b, cid):
@@ -1143,17 +1163,20 @@
     return pl.pallas_call(
         spread_kernel,
         out_shape=SDS((4, m // 4, width), bf),
-        in_specs=[VMEM, VMEM],
+        in_specs=[ANY, ANY],
         out_specs=ANY,
         scratch_shapes=[
+            pltpu.VMEM(a.shape, bf),
+            pltpu.VMEM(b.shape, bf),
             pltpu.VMEM((m, TP * r), bf),
             pltpu.VMEM((m, width), bf),
             pltpu.SemaphoreType.DMA((count,)),
             pltpu.SemaphoreType.DMA((count,)),
             pltpu.SemaphoreType.DMA((count,)),
+            pltpu.SemaphoreType.DMA((1 + width // 512,)),
         ],
         compiler_params=pltpu.CompilerParams(
-            collective_id=cid, has_side_effects=True, vmem_limit_bytes=32 << 20
+            collective_id=cid, has_side_effects=True, vmem_limit_bytes=ALL_VMEM
         ),
         name="spread_product",
     )(a, b)
@@ -1262,7 +1285,7 @@
     vec = jnp.stack([v.astype(f32) for v in (gain1, bias1, gain2, bias2)] + [lens])
     vec = jnp.pad(vec, ((0, 3), (0, 128 - shard)))
     early = max(16, wd.shape[0] // 4)
-    qko_blk, d0 = first_exchange(n, wq, wk, wo, wd[:early], 1)
+    qko_blk, d0 = first_exchange(n, wq, wk, wo, wd, early, 1)
     qko = dp_gather(qko_blk.reshape(TP * shard, 4 * KH), n)
     tok_all, vec_all = second_exchange(n, after(tokens, qko_blk), vec, 2)
     gain1f, bias1f, gain2f, bias2f = (
@@ -1313,9 +1336,10 @@
     qkv_grad = row_product(normed, g_qkv)
     g_qkv_own = dp_reduce(qkv_grad, n)
     g_out = dp_reduce(out_grad, n)
-    grad_tokens, ffn, g_vecs = last_exchange(
-        n, g_qkv, g_swish, qk, vs, hidden, *down, tokens, g_middle, gain1f, sums2, 7
+    grad_part, ffn, g_vecs = last_exchange(
+        n, g_qkv, g_swish, qk, vs, hidden, *down, tokens, gain1f, sums2, 7
     )
+    grad_tokens = g_middle + grad_part
     layer_out = (middle + ffn).astype(bf)
 
     g_vecs = lax.dynamic_slice_in_dim(g_vecs, head * shard, shard, 1)

time: 736 us -> 734 us (level)
    unnamed x75 -> x70, local copies, waits for them, and re-layouts: 30.9 us -> 25 us
where the time goes in v11:
time: 734 us; the launch traced here: 730 us
  Pallas kernels  532 us (72%)
  waiting for transfers between devices  110 us (15%)
  local copies, waits for them, and re-layouts  29.3 us (4%)
  other arithmetic  19.3 us (3%)
  blocking collectives  14.7 us (2%)
  between operations  14.4 us (2%)
  starting transfers between devices  11.1 us (2%)
    pallas_call x4, Pallas kernels, exchange_call(): pl.pallas_call(kernel, out_shape=outs, in_specs=specs or [VMEM] * len(arg...  150 us
    reduce_scatter x5, waiting for transfers between devices, dp_reduce(): lax.psum_scatter(x, AXIS, scatter_dimension=0, tiled=True, axis_index_gro...  98.1 us
    pallas_call x1, Pallas kernels, forward_exchange(): pl.pallas_call(forward_kernel, out_shape=tuple((SDS(*b) for b in blocks))...  87.4 us
    pallas_call x1, Pallas kernels, last_exchange(): pl.pallas_call(functools.partial(last_kernel, n), out_shape=(SDS((r, c),...  84.9 us
    pallas_call x1, Pallas kernels, backward_exchange(): pl.pallas_call(backward_kernel, out_shape=(SDS((r, c), f32), SDS((TP, r,...  81.1 us
    pallas_call x4, Pallas kernels, row_product(): pl.pallas_call(product_kernel, grid=(width // part, m // tile), out_shape...  45.7 us
    pallas_call x1, Pallas kernels, spread_product(): pl.pallas_call(spread_kernel, out_shape=SDS((4, m // 4, width), bf), in_s...  27.5 us
    unnamed x70, local copies, waits for them, and re-layouts  25 us
  transfers between devices with their start and end apart: 11, of which 4 were waited for; matrix products, arithmetic and copies ran while one was open for 3% of the time, Pallas kernels for 55%

profile of v11, /device:TPU:14, one launch (start us, length us, event | category | flops | bytes accessed | tf_op | source)
XLA Modules:
  0.0 730.5 jit_solution(18086095349452754661)
XLA Ops:
  11.2 15.7 %shard_map.254 = (bf16[8,64,1024]{2,1,0:T(8,128)(2,1)}, bf16[4,32,2048]{2,1,0:T(8,128)(2,1)S(1)}) custom-call(bf16[64,2048]{1,0:T(8,128)(2,1)S(1)} %copy-done.21, bf16[64,2048]{1,0:T(8,128)(2,1)S(1)} %copy-done.22, bf16[128,2048]{1,0:T(8,128)(2,1)S(1)} %copy-done.18, bf16[128,2048]{1,0:T(8,128)(2,1)S(1)} %copy-done.14), custom_call_target="tpu_custom_call" | custom-call | tf_op jit(solution)/shard_map/pallas_call | solution.py:144
  30.2 41.8 %shard_map.255 = (bf16[8,256,2048]{2,1,0:T(8,128)(2,1)S(1)}, f32[4,8,8,128]{3,2,1,0:T(8,128)S(1)}) custom-call(bf16[256,2048]{1,0:T(8,128)(2,1)S(1)} %copy-done.2, f32[8,128]{1,0:T(8,128)S(1)} %pad.9.vec), custom_call_target="tpu_custom_call" | custom-call | tf_op jit(solution)/shard_map/pallas_call | solution.py:144
  80.2 26.4 %shard_map.256 = (bf16[8,64,1024]{2,1,0:T(8,128)(2,1)}, bf16[8,64,1024]{2,1,0:T(8,128)(2,1)}, bf16[8,256,2048]{2,1,0:T(8,128)(2,1)S(1)}) custom-call(bf16[64,4096]{1,0:T(8,128)(2,1)S(1)} %copy-done.19, bf16[64,4096]{1,0:T(8,128)(2,1)S(1)} %copy-done.20, bf16[8,64,1024]{2,1,0:T(8,128)(2,1)S(1)} %pad_maximum_fusion.gu, bf16[8,256,2048]{2,1,0:T(8,128)(2,1)S(1)} %copy-done.7, ...), custom_call_target="tpu_custom_call" | custom-call | tf_op jit(solution)/shard_map/pallas_call | solution.py:144
  113.4 5.3 multiply_sine_fusion
  122.8 66.3 %shard_map.257 = (bf16[8,256,2048]{2,1,0:T(8,128)(2,1)}, bf16[8,4,2,64,256]{4,3,2,1,0:T(8,128)(2,1)S(1)}, bf16[8,256,256]{2,1,0:T(8,128)(2,1)S(1)}, bf16[8,256,2...) custom-call(bf16[256,2048]{1,0:T(8,128)(2,1)S(1)} %copy-done.8, ...), custom_call_target="tpu_custom_call" | custom-call | tf_op jit(solution)/shard_map/pallas_call | solution.py:144
  194.7 87.4 %forward_exchange.1 = (bf16[8,256,512]{2,1,0:T(8,128)(2,1)}, bf16[8,256,512]{2,1,0:T(8,128)(2,1)}, f32[8,256,512]{2,1,0:T(8,128)}, f32[8,256,512]{2,1,0:T(8,128)...) custom-call(bf16[8,256,2048]{2,1,0:T(8,128)(2,1)} %copy-done, ...), custom_call_target="tpu_custom_call" | custom-call | tf_op jit(solution)/shard_map/forward_exchange/pallas_call | solution.py:660
  282.2 15.8 %hidden_units.1 = (bf16[8,256,512]{2,1,0:T(8,128)(2,1)}, f32[8,256,512]{2,1,0:T(8,128)}, f32[8,256,512]{2,1,0:T(8,128)}) custom-call(bf16[8,256,2048]{2,1,0:T(8,128)(2,1)} %get-tuple-element.64.x.a, bf16[2048,1024]{1,0:T(8,128)(2,1)} %all-gather.11.cloned.1.call-done.gu.w_in), custom_call_target="tpu_custom_call" | custom-call | flops 8589934592 | bytes 25165824 | tf_op jit(solution)/shard_map/hidden_units/pallas_call | solution.py:736
  297.9 11.1 %all-gather.9.cloned.1.call-done = bf16[384,2048]{1,0:T(8,128)(2,1)} async-done(((bf16[96,2048]{1,0:T(8,128)(2,1)}), bf16[384,2048]{1,0:T(8,128)(2,1)}) %all-gather.9.cloned.1.call-update) | async-done | bytes 1572880 | tf_op jit(solution)/shard_map/all_gather | solution.py:1198
  309.0 11.3 %hidden_back.1.a_in.b = bf16[8,256,1024]{2,1,0:T(8,128)(2,1)} custom-call(bf16[8,256,2048]{2,1,0:T(8,128)(2,1)} %get-tuple-element.62.cot.b, bf16[4,32,2048]{2,1,0:T(8,128)(2,1)} %copy-done.12, bf16[4,96,2048]{2,1,0:T(8,128)(2,1)} %bitcast.52, f32[8,256,512]{2,1,0:T(8,128)} %get-tuple-element.66.act, f32[8,256,512]{2,1,0:T(8,128)} %get-tuple-element.67.slope), custom_call_target="tpu_custom_call" | custom-call | flops 4294967296 | bytes 25165824 | tf_op jit(solution)/shard_map/hidden_back/pallas_call | solution.py:780
  320.3 81.1 %backward_exchange.1 = (f32[256,2048]{1,0:T(8,128)}, bf16[8,256,2048]{2,1,0:T(8,128)(2,1)}, f32[2,2048]{1,0:T(2,128)S(1)}) custom-call(bf16[8,256,1024]{2,1,0:T(8,128)(2,1)} %hidden_back.1.a_in.b, bf16[2048,1024]{1,0:T(8,128)(2,1)} %all-gather.11.cloned.1.call-done.gu.w_in, f32[256,2048]{1,0:T(8,128)} %get-tuple-element.58.mid_in, ...), custom_call_target="tpu_custom_call" | custom-call | tf_op jit(solution)/shard_map/backward_exchange/pallas_call | solution.py:849
  402.0 12.6 %gate_back.1 = (bf16[8,256,512]{2,1,0:T(8,128)(2,1)}, bf16[8,256,512]{2,1,0:T(8,128)(2,1)}) custom-call(bf16[8,256,2048]{2,1,0:T(8,128)(2,1)} %get-tuple-element.68.g_low.b_in, bf16[8,512,256]{2,1,0:T(8,128)(2,1)} %bitcast.49, f32[8,256,512]{2,1,0:T(8,128)} %get-tuple-element.69.ret, f32[8,256,512]{2,1,0:T(8,128)} %get-tuple-element.70.swi), custom_call_target="tpu_custom_call" | custom-call | flops 4294967296 | bytes 23068672 | tf_op jit(solution)/shard_map/gate_back/pallas_call | solution.py:1051
  414.6 8.8 %row_product.5 = bf16[2048,512]{1,0:T(8,128)(2,1)} custom-call(bf16[8,256,2048]{2,1,0:T(8,128)(2,1)} %copy-done, bf16[8,256,512]{2,1,0:T(8,128)(2,1)} %get-tuple-element.72.gs_in.b), custom_call_target="tpu_custom_call" | custom-call | flops 4294967296 | bytes 12582912 | tf_op jit(solution)/shard_map/row_product/pallas_call | solution.py:693
  423.5 13.4 %row_product.6 = bf16[2048,1024]{1,0:T(8,128)(2,1)} custom-call(bf16[8,256,2048]{2,1,0:T(8,128)(2,1)} %get-tuple-element.64.x.a, bf16[8,256,1024]{2,1,0:T(8,128)(2,1)} %hidden_back.1.a_in.b), custom_call_target="tpu_custom_call" | custom-call | flops 8589934592 | bytes 16777216 | tf_op jit(solution)/shard_map/row_product/pallas_call | solution.py:693
  436.9 10.1 %scores_back.1.gqkv_in.b = bf16[8,256,1024]{2,1,0:T(8,128)(2,1)} custom-call(bf16[8,256,256]{2,1,0:T(8,128)(2,1)} %copy-done.10, f32[8,256,256]{2,1,0:T(8,128)} %copy-done.1, bf16[8,256,256]{2,1,0:T(8,128)(2,1)} %copy-done.16, bf16[8,256,256]{2,1,0:T(8,128)(2,1)} %copy-done.17, bf16[8,256,512]{2,1,0:T(8,128)(2,1)} %get-tuple-element.61.v, ...), custom_call_target="tpu_custom_call" | custom-call | flops 1610612736 | bytes 16777216 | tf_op jit(solution)/shard_map/scores_back/pallas_call | solution.py:1094
  447.1 13.3 %row_product.4 = bf16[2048,1024]{1,0:T(8,128)(2,1)} custom-call(bf16[8,256,2048]{2,1,0:T(8,128)(2,1)} %copy-done, bf16[8,256,1024]{2,1,0:T(8,128)(2,1)} %scores_back.1.gqkv_in.b), custom_call_target="tpu_custom_call" | custom-call | flops 8589934592 | bytes 16777216 | tf_op jit(solution)/shard_map/row_product/pallas_call | solution.py:693
  460.5 10.2 %row_product.7 = bf16[512,2048]{1,0:T(8,128)(2,1)} custom-call(bf16[8,256,512]{2,1,0:T(8,128)(2,1)} %get-tuple-element.74.a2_in.a, bf16[8,256,2048]{2,1,0:T(8,128)(2,1)} %get-tuple-element.62.cot.b), custom_call_target="tpu_custom_call" | custom-call | flops 4294967296 | bytes 12582912 | tf_op jit(solution)/shard_map/row_product/pallas_call | solution.py:693
  470.7 27.5 %spread_product.1 = bf16[4,128,2048]{2,1,0:T(8,128)(2,1)} custom-call(bf16[8,256,512]{2,1,0:T(8,128)(2,1)} %get-tuple-element.83.a_in, bf16[8,256,2048]{2,1,0:T(8,128)(2,1)} %get-tuple-element.68.g_low.b_in), custom_call_target="tpu_custom_call" | custom-call | tf_op jit(solution)/shard_map/spread_product/pallas_call | solution.py:1163
  498.2 14.7 %all_to_all.27.x = bf16[8,64,512]{2,1,0:T(8,128)(2,1)} all-to-all(bf16[8,64,512]{2,1,0:T(8,128)(2,1)} %bitcast.63), channel_id=1, replica_groups={{0,1,2,3,4,5,6,7},{8,9,10,11,12,13,14,15},{16,17,18,19,20,21,22,23},{24..., dimensions={0} | all-to-all | bytes 1048576 | tf_op jit(solution)/shard_map/all_to_all | solution.py:1194
  513.0 32.3 %reduce-scatter.12.cloned.1.call-done = bf16[512,1024]{1,0:T(8,128)(2,1)} async-done(((bf16[2048,1024]{1,0:T(8,128)(2,1)}), bf16[512,1024]{1,0:T(8,128)(2,1)}) %reduce-scatter.12.cloned.1.call-update) | async-done | bytes 1048592 | tf_op jit(solution)/shard_map/reduce_scatter | solution.py:1202
  545.2 4.7 all-to-all-start.2
  550.0 84.9 %last_exchange.1 = (f32[256,2048]{1,0:T(8,128)}, f32[256,2048]{1,0:T(8,128)}, f32[8,512]{1,0:T(8,128)}) custom-call(bf16[8,256,1024]{2,1,0:T(8,128)(2,1)} %scores_back.1.gqkv_in.b, bf16[8,256,512]{2,1,0:T(8,128)(2,1)} %get-tuple-element.72.gs_in.b, bf16[2048,512]{1,0:T(8,128)(2,1)} %bitcast.50, bf16[2048,1024]{1,0:T(8,128)(2,1)} %all-gather.5.cloned.1.call-done.wvs_in, ...), custom_call_target="tpu_custom_call" | custom-call | tf_op jit(solution)/shard_map/last_exchange/pallas_call | solution.py:991
  638.8 5.8 all-to-all-start
  648.8 22.7 %reduce-scatter.14.cloned.1.call-done = bf16[128,2048]{1,0:T(8,128)(2,1)} async-done(((bf16[512,2048]{1,0:T(8,128)(2,1)}), bf16[128,2048]{1,0:T(8,128)(2,1)}) %reduce-scatter.14.cloned.1.call-update) | async-done | bytes 524304 | tf_op jit(solution)/shard_map/reduce_scatter | solution.py:1202
  673.6 43.1 %reduce-scatter.10.cloned.1.call-done = bf16[128,2048]{1,0:T(8,128)(2,1)} async-done(((bf16[512,2048]{1,0:T(8,128)(2,1)}), bf16[128,2048]{1,0:T(8,128)(2,1)}) %reduce-scatter.10.cloned.1.call-update) | async-done | bytes 524304 | tf_op jit(solution)/shard_map/reduce_scatter | solution.py:1202
  (135 shorter events, 49.8 us)
Async XLA Ops:
  7.2 112.4 %all-gather.7.cloned.1.call-start = ((), (), s32[]{:S(2)}) async-start(), calls=%async_computation.9 | async-start | bytes 5242880 | tf_op jit(solution)/shard_map/all_gather | solution.py:1198
  11.2 16.6 %copy-start.27 = (bf16[64,4096]{1,0:T(8,128)(2,1)S(1)}, bf16[64,4096]{1,0:T(8,128)(2,1)}, u32[]{:S(2)}) copy-start(bf16[64,4096]{1,0:T(8,128)(2,1)} %param.26) | copy-start | bytes 1572868
  27.7 167.0 %all-gather.5.cloned.1.call-start = ((), (), s32[]{:S(2)}) async-start(), calls=%async_computation.8 | async-start | bytes 5242880 | tf_op jit(solution)/shard_map/all_gather | solution.py:1198
  29.0 47.8 %copy-start.19 = (bf16[64,4096]{1,0:T(8,128)(2,1)S(1)}, bf16[64,4096]{1,0:T(8,128)(2,1)}, u32[]{:S(2)}) copy-start(bf16[64,4096]{1,0:T(8,128)(2,1)} %wv.1) | copy-start | bytes 1572868
  29.1 47.8 %copy-start.20 = (bf16[64,4096]{1,0:T(8,128)(2,1)S(1)}, bf16[64,4096]{1,0:T(8,128)(2,1)}, u32[]{:S(2)}) copy-start(bf16[64,4096]{1,0:T(8,128)(2,1)} %ws.1) | copy-start | bytes 1572868
  72.0 3.3 copy-start.6
  75.6 31.1 %copy-start.24 = (f32[1,2048]{1,0:T(1,128)}, f32[1,2048]{1,0:T(1,128)S(1)}, u32[]{:S(2)}) copy-start(f32[1,2048]{1,0:T(1,128)S(1)} %reshape_squeeze.12.gain) | copy-start | bytes 24580
  76.8 3.4 copy-start.7
  106.7 3.3 copy-start
  110.0 172.2 %all-gather.11.cloned.1.call-start = ((), (), s32[]{:S(2)}) async-start(), calls=%async_computation.11 | async-start | bytes 5242880 | tf_op jit(solution)/shard_map/all_gather | solution.py:1198
  110.7 198.3 %all-gather.9.cloned.1.call-start = ((), (), s32[]{:S(2)}) async-start(), calls=%async_computation.10 | async-start | bytes 1966080 | tf_op jit(solution)/shard_map/all_gather | solution.py:1198
  111.8 386.4 %reduce-scatter.8.cloned.1.call-start = ((), (), s32[]{:S(2)}) async-start(), calls=%async_computation.13 | async-start | bytes 2621440 | tf_op jit(solution)/shard_map/reduce_scatter | solution.py:1202
  118.7 70.3 %copy-start.3 = (f32[8,256,128]{2,1,0:T(8,128)}, f32[8,256,128]{2,1,0:T(8,128)S(1)}, u32[]{:S(2)}) copy-start(f32[8,256,128]{2,1,0:T(8,128)S(1)} %get-tuple-element.90.sine) | copy-start | bytes 3145732
  119.5 69.5 %copy-start.1 = (f32[8,256,256]{2,1,0:T(8,128)}, f32[8,256,256]{2,1,0:T(8,128)S(1)}, u32[]{:S(2)}) copy-start(f32[8,256,256]{2,1,0:T(8,128)S(1)} %fusion.4.mask) | copy-start | bytes 6291460
  309.0 11.3 %copy-start.9 = (bf16[256,2048]{1,0:T(8,128)(2,1)S(1)}, bf16[256,2048]{1,0:T(8,128)(2,1)}, u32[]{:S(2)}) copy-start(bf16[256,2048]{1,0:T(8,128)(2,1)} %cot_in.1) | copy-start | bytes 3145732
  309.0 11.3 %copy-start.23 = (f32[2,2048]{1,0:T(2,128)S(1)}, f32[2,2048]{1,0:T(2,128)}, u32[]{:S(2)}) copy-start(f32[2,2048]{1,0:T(2,128)} %pad_maximum_fusion.1.vec) | copy-start | bytes 49156
  423.5 121.8 %reduce-scatter.12.cloned.1.call-start = ((), (), s32[]{:S(2)}) async-start(), calls=%async_computation.15 | async-start | bytes 5242880 | tf_op jit(solution)/shard_map/reduce_scatter | solution.py:1202
  436.9 201.9 %reduce-scatter.6.cloned.1.call-start = ((), (), s32[]{:S(2)}) async-start(), calls=%async_computation.12 | async-start | bytes 5242880 | tf_op jit(solution)/shard_map/reduce_scatter | solution.py:1202
  460.4 211.1 %reduce-scatter.14.cloned.1.call-start = ((), (), s32[]{:S(2)}) async-start(), calls=%async_computation.16 | async-start | bytes 2621440 | tf_op jit(solution)/shard_map/reduce_scatter | solution.py:1202
  470.7 246.1 %reduce-scatter.10.cloned.1.call-start = ((), (), s32[]{:S(2)}) async-start(), calls=%async_computation.14 | async-start | bytes 2621440 | tf_op jit(solution)/shard_map/reduce_scatter | solution.py:1202
  545.2 93.6 %all-to-all-start.2 = ((bf16[8,64,1024]{2,1,0:T(8,128)(2,1)}), bf16[8,64,1024]{2,1,0:T(8,128)(2,1)}, u32[]{:S(2)}, u32[]{:S(2)}) async-start(bf16[8,64,1024]{2,1,0:T(8,128)(2,1)} %bitcast.60), calls=%async_computation.6 | async-start | bytes 2097152 | tf_op jit(solution)/shard_map/all_to_all | solution.py:1194
  638.8 7.1 copy-start.26
  638.8 83.7 %all-to-all-start = ((bf16[8,64,1024]{2,1,0:T(8,128)(2,1)}), bf16[8,64,1024]{2,1,0:T(8,128)(2,1)S(1)}, u32[]{:S(2)}, u32[]{:S(2)}) async-start(bf16[8,64,1024]{2,1,0:T(8,128)(2,1)} %bitcast.59), calls=%async_computation.1 | async-start | bytes 2097152 | tf_op jit(solution)/shard_map/all_to_all | solution.py:1194
  648.8 70.0 %copy-start.13 = (bf16[8,64,512]{2,1,0:T(8,128)(2,1)S(1)}, bf16[8,64,512]{2,1,0:T(8,128)(2,1)}, u32[]{:S(2)}) copy-start(bf16[8,64,512]{2,1,0:T(8,128)(2,1)} %all_to_all.27.x) | copy-start | bytes 1572868
  (21 other events, 28.2 us)
Sparse Core Ops, SparseCore 0:
  27.8 79.3 all-gather.6
  110.1 78.9 all-gather.4
  190.6 79.2 all-gather.10
  271.9 37.0 all-gather.8
  423.6 42.6 reduce-scatter.7
  468.4 76.8 reduce-scatter.11
  547.5 78.6 reduce-scatter.5
  628.6 42.9 reduce-scatter.13
  673.8 42.8 reduce-scatter.9

commit v12 on v11

--- a/solution.py
+++ b/solution.py
@@ -184,7 +184,10 @@
     width = 2 * wq.shape[1] // TP + 2 * wo.shape[1] // TP
     outs = (SDS((TP, wq.shape[0], width), bf), SDS((n // TP, early, wd.shape[1]), bf))
     kernel = functools.partial(first_kernel, n)
-    return exchange_call(kernel, outs, (wq, wk, wo, wd), 28 + n // TP, 5, cid)
+    return exchange_call(
+        kernel, outs, (wq, wk, wo, wd), 28 + n // TP, 5, cid,
+        specs=[ANY] * 4, vmem=ALL_VMEM,
+    )
 
 
 def others_along(n):
@@ -1236,21 +1239,21 @@
 
 def join_kernel(widths, parts, x, *outs):
     at = 0
-    for out, width in zip(outs, widths):
-        piece = width // parts
+    for out, width, count in zip(outs, widths, parts):
+        piece = width // count
         for t in range(TP):
-            for p in range(parts):
+            for p in range(count):
                 to = (p * TP + t) * piece
                 out[:, to : to + piece] = x[t, :, at + p * piece : at + (p + 1) * piece].astype(f32)
         at += width
 
 
-def join(x, widths, parts=1):
+def join(x, widths, parts):
     r = x.shape[1]
-    if any(width // parts % 128 for width in widths):
+    if any(width // count % 128 for width, count in zip(widths, parts)):
         made, at = [], 0
-        for width in widths:
-            part = x[:, :, at : at + width].reshape(TP, r, parts, width // parts)
+        for width, count in zip(widths, parts):
+            part = x[:, :, at : at + width].reshape(TP, r, count, width // count)
             made.append(part.transpose(1, 2, 0, 3).reshape(r, TP * width).astype(f32))
             at += width
         return made
@@ -1259,7 +1262,7 @@
         out_shape=tuple(SDS((r, TP * width), f32) for width in widths),
         in_specs=[VMEM],
         out_specs=tuple(VMEM for _ in widths),
-        compiler_params=pltpu.CompilerParams(vmem_limit_bytes=8 << 20),
+        compiler_params=pltpu.CompilerParams(vmem_limit_bytes=10 << 20),
         cost_estimate=pl.CostEstimate(flops=0, bytes_accessed=6 * x.size, transcendentals=0),
         name="join",
     )(x)
@@ -1344,17 +1347,17 @@
 
     g_vecs = lax.dynamic_slice_in_dim(g_vecs, head * shard, shard, 1)
     grad_d = g_down.astype(f32)
-    g_gu = plane_a2a(g_gu, n)
-    grad_g, grad_u = join(g_gu.reshape(TP, shard, 2 * dp * unit), (dp * unit,) * 2, dp)
-    g_swi = plane_a2a(g_swi, n)
-    (grad_s,) = join(g_swi.reshape(TP, shard, VH), (VH,))
+    g_gs = plane_a2a(jnp.concatenate([g_gu, g_swi], axis=1), n)
+    grad_g, grad_u, grad_s = join(
+        g_gs.reshape(TP, shard, 2 * dp * unit + VH), (dp * unit, dp * unit, VH), (dp, dp, 1)
+    )
     g_qkv_own = plane_a2a(g_qkv_own, n)
-    grad_q, grad_k, grad_v = join(g_qkv_own.reshape(TP, shard, 2 * KH + VH), (KH, KH, VH))
+    grad_q, grad_k, grad_v = join(g_qkv_own.reshape(TP, shard, 2 * KH + VH), (KH, KH, VH), (1, 1, 1))
     if spread:
         grad_o = g_out.astype(f32)
     else:
         g_out = plane_a2a(g_out, n)
-        (grad_o,) = join(g_out.reshape(TP, wo.shape[0], d // TP), (d // TP,))
+        (grad_o,) = join(g_out.reshape(TP, wo.shape[0], d // TP), (d // TP,), (1,))
     return (
         layer_out, grad_tokens, g_vecs[0], g_vecs[1], grad_q, grad_k, grad_v, grad_s, grad_o,
         g_vecs[2], g_vecs[3], grad_g, grad_u, grad_d,

time: 734 us -> 761 us (1.037)
  waiting for transfers between devices: 110 us -> 149 us
  blocking collectives: 14.7 us -> 0 us
    reduce_scatter x5, waiting for transfers between devices: 98.1 us -> 137 us  [dp_reduce(): lax.psum_scatter(x, AXIS, scatter_dimension=0, tiled=True, axis_index_gro...]
    all_to_all x1 -> x0, blocking collectives: 14.7 us -> none  [plane_a2a(): lax.all_to_all(x, AXIS, 0, 0, axis_index_groups=tp_groups(n), tiled=True)]
    unnamed x70 -> x62, local copies, waits for them, and re-layouts: 25 us -> 21.9 us
  transfers between devices with their start and end apart: 11 -> 11, of which waited for: 4 -> 4; matrix products, arithmetic and copies ran while one was open for 3% -> 3% of each run, Pallas kernels for 55% -> 51%
where the time goes in v12:
time: 761 us; the launch traced here: 757 us
  Pallas kernels  537 us (71%)
  waiting for transfers between devices  149 us (20%)
  local copies, waits for them, and re-layouts  26.2 us (3%)
  other arithmetic  20.5 us (3%)
  between operations  14.4 us (2%)
  starting transfers between devices  9.53 us (1%)
    pallas_call x4, Pallas kernels, exchange_call(): pl.pallas_call(kernel, out_shape=outs, in_specs=specs or [VMEM] * len(arg...  150 us
    reduce_scatter x5, waiting for transfers between devices, dp_reduce(): lax.psum_scatter(x, AXIS, scatter_dimension=0, tiled=True, axis_index_gro...  137 us
    pallas_call x1, Pallas kernels, last_exchange(): pl.pallas_call(functools.partial(last_kernel, n), out_shape=(SDS((r, c),...  90.1 us
    pallas_call x1, Pallas kernels, forward_exchange(): pl.pallas_call(forward_kernel, out_shape=tuple((SDS(*b) for b in blocks))...  87.4 us
    pallas_call x1, Pallas kernels, backward_exchange(): pl.pallas_call(backward_kernel, out_shape=(SDS((r, c), f32), SDS((TP, r,...  81.1 us
    pallas_call x4, Pallas kernels, row_product(): pl.pallas_call(product_kernel, grid=(width // part, m // tile), out_shape...  46 us
    pallas_call x1, Pallas kernels, spread_product(): pl.pallas_call(spread_kernel, out_shape=SDS((4, m // 4, width), bf), in_s...  27.4 us
    unnamed x62, local copies, waits for them, and re-layouts  21.9 us
  transfers between devices with their start and end apart: 11, of which 4 were waited for; matrix products, arithmetic and copies ran while one was open for 3% of the time, Pallas kernels for 51%

profile of v12, /device:TPU:14, one launch (start us, length us, event | category | flops | bytes accessed | tf_op | source)
XLA Modules:
  0.0 756.7 jit_solution(8570641917110552590)
XLA Ops:
  7.2 15.9 %shard_map.254 = (bf16[8,64,1024]{2,1,0:T(8,128)(2,1)}, bf16[4,32,2048]{2,1,0:T(8,128)(2,1)}) custom-call(bf16[64,2048]{1,0:T(8,128)(2,1)} %wq.1, bf16[64,2048]{1,0:T(8,128)(2,1)} %wk.1, bf16[128,2048]{1,0:T(8,128)(2,1)} %wo.1, bf16[128,2048]{1,0:T(8,128)(2,1)} %wd.1), custom_call_target="tpu_custom_call" | custom-call | tf_op jit(solution)/shard_map/pallas_call | solution.py:144
  26.3 41.7 %shard_map.255 = (bf16[8,256,2048]{2,1,0:T(8,128)(2,1)S(1)}, f32[4,8,8,128]{3,2,1,0:T(8,128)S(1)}) custom-call(bf16[256,2048]{1,0:T(8,128)(2,1)S(1)} %copy-done.2, f32[8,128]{1,0:T(8,128)S(1)} %pad.9.vec), custom_call_target="tpu_custom_call" | custom-call | tf_op jit(solution)/shard_map/pallas_call | solution.py:144
  76.3 26.4 %shard_map.256 = (bf16[8,64,1024]{2,1,0:T(8,128)(2,1)}, bf16[8,64,1024]{2,1,0:T(8,128)(2,1)}, bf16[8,256,2048]{2,1,0:T(8,128)(2,1)S(1)}) custom-call(bf16[64,4096]{1,0:T(8,128)(2,1)S(1)} %copy-done.16, bf16[64,4096]{1,0:T(8,128)(2,1)S(1)} %copy-done.17, bf16[8,64,1024]{2,1,0:T(8,128)(2,1)S(1)} %pad_maximum_fusion.1.gu, bf16[8,256,2048]{2,1,0:T(8,128)(2,1)S(1)} %copy-done.7, ...), custom_call_target="tpu_custom_call" | custom-call | tf_op jit(solution)/shard_map/pallas_call | solution.py:144
  109.4 5.3 multiply_sine_fusion
  118.8 66.2 %shard_map.257 = (bf16[8,256,2048]{2,1,0:T(8,128)(2,1)}, bf16[8,4,2,64,256]{4,3,2,1,0:T(8,128)(2,1)S(1)}, bf16[8,256,256]{2,1,0:T(8,128)(2,1)S(1)}, bf16[8,256,2...) custom-call(bf16[256,2048]{1,0:T(8,128)(2,1)S(1)} %copy-done.10, ...), custom_call_target="tpu_custom_call" | custom-call | tf_op jit(solution)/shard_map/pallas_call | solution.py:144
  190.7 87.4 %forward_exchange.1 = (bf16[8,256,512]{2,1,0:T(8,128)(2,1)}, bf16[8,256,512]{2,1,0:T(8,128)(2,1)}, f32[8,256,512]{2,1,0:T(8,128)}, f32[8,256,512]{2,1,0:T(8,128)...) custom-call(bf16[8,256,2048]{2,1,0:T(8,128)(2,1)} %copy-done, ...), custom_call_target="tpu_custom_call" | custom-call | tf_op jit(solution)/shard_map/forward_exchange/pallas_call | solution.py:663
  278.1 15.7 %hidden_units.1 = (bf16[8,256,512]{2,1,0:T(8,128)(2,1)}, f32[8,256,512]{2,1,0:T(8,128)}, f32[8,256,512]{2,1,0:T(8,128)}) custom-call(bf16[8,256,2048]{2,1,0:T(8,128)(2,1)} %get-tuple-element.65.x.a, bf16[2048,1024]{1,0:T(8,128)(2,1)} %all-gather.11.cloned.1.call-done.gu.w_in), custom_call_target="tpu_custom_call" | custom-call | flops 8589934592 | bytes 25165824 | tf_op jit(solution)/shard_map/hidden_units/pallas_call | solution.py:739
  293.8 11.2 %all-gather.9.cloned.1.call-done = bf16[384,2048]{1,0:T(8,128)(2,1)} async-done(((bf16[96,2048]{1,0:T(8,128)(2,1)}), bf16[384,2048]{1,0:T(8,128)(2,1)}) %all-gather.9.cloned.1.call-update) | async-done | bytes 1572880 | tf_op jit(solution)/shard_map/all_gather | solution.py:1201
  305.1 11.3 %hidden_back.1.a_in.b = bf16[8,256,1024]{2,1,0:T(8,128)(2,1)} custom-call(bf16[8,256,2048]{2,1,0:T(8,128)(2,1)} %get-tuple-element.63.cot.b, bf16[4,32,2048]{2,1,0:T(8,128)(2,1)} %get-tuple-element.64.d0, bf16[4,96,2048]{2,1,0:T(8,128)(2,1)} %bitcast.51, f32[8,256,512]{2,1,0:T(8,128)} %get-tuple-element.67.act, f32[8,256,512]{2,1,0:T(8,128)} %get-tuple-element.68.slope), custom_call_target="tpu_custom_call" | custom-call | flops 4294967296 | bytes 25165824 | tf_op jit(solution)/shard_map/hidden_back/pallas_call | solution.py:783
  316.4 81.1 %backward_exchange.1 = (f32[256,2048]{1,0:T(8,128)}, bf16[8,256,2048]{2,1,0:T(8,128)(2,1)}, f32[2,2048]{1,0:T(2,128)S(1)}) custom-call(bf16[8,256,1024]{2,1,0:T(8,128)(2,1)} %hidden_back.1.a_in.b, bf16[2048,1024]{1,0:T(8,128)(2,1)} %all-gather.11.cloned.1.call-done.gu.w_in, f32[256,2048]{1,0:T(8,128)} %get-tuple-element.59.mid_in, ...), custom_call_target="tpu_custom_call" | custom-call | tf_op jit(solution)/shard_map/backward_exchange/pallas_call | solution.py:852
  398.1 12.6 %gate_back.1 = (bf16[8,256,512]{2,1,0:T(8,128)(2,1)}, bf16[8,256,512]{2,1,0:T(8,128)(2,1)}) custom-call(bf16[8,256,2048]{2,1,0:T(8,128)(2,1)} %get-tuple-element.69.g_low.b_in, bf16[8,512,256]{2,1,0:T(8,128)(2,1)} %bitcast.48, f32[8,256,512]{2,1,0:T(8,128)} %get-tuple-element.70.ret, f32[8,256,512]{2,1,0:T(8,128)} %get-tuple-element.71.swi), custom_call_target="tpu_custom_call" | custom-call | flops 4294967296 | bytes 23068672 | tf_op jit(solution)/shard_map/gate_back/pallas_call | solution.py:1054
  410.7 10.1 %scores_back.1.gqkv_in.b = bf16[8,256,1024]{2,1,0:T(8,128)(2,1)} custom-call(bf16[8,256,256]{2,1,0:T(8,128)(2,1)} %copy-done.12, f32[8,256,256]{2,1,0:T(8,128)} %copy-done.1, bf16[8,256,256]{2,1,0:T(8,128)(2,1)} %copy-done.14, bf16[8,256,256]{2,1,0:T(8,128)(2,1)} %copy-done.15, bf16[8,256,512]{2,1,0:T(8,128)(2,1)} %get-tuple-element.62.v, ...), custom_call_target="tpu_custom_call" | custom-call | flops 1610612736 | bytes 16777216 | tf_op jit(solution)/shard_map/scores_back/pallas_call | solution.py:1097
  420.8 13.3 %row_product.4 = bf16[2048,1024]{1,0:T(8,128)(2,1)} custom-call(bf16[8,256,2048]{2,1,0:T(8,128)(2,1)} %copy-done, bf16[8,256,1024]{2,1,0:T(8,128)(2,1)} %scores_back.1.gqkv_in.b), custom_call_target="tpu_custom_call" | custom-call | flops 8589934592 | bytes 16777216 | tf_op jit(solution)/shard_map/row_product/pallas_call | solution.py:696
  434.2 9.2 %row_product.6 = bf16[2048,512]{1,0:T(8,128)(2,1)} custom-call(bf16[8,256,2048]{2,1,0:T(8,128)(2,1)} %copy-done, bf16[8,256,512]{2,1,0:T(8,128)(2,1)} %get-tuple-element.73.gs_in.b), custom_call_target="tpu_custom_call" | custom-call | flops 4294967296 | bytes 12582912 | tf_op jit(solution)/shard_map/row_product/pallas_call | solution.py:696
  443.4 13.4 %row_product.5 = bf16[2048,1024]{1,0:T(8,128)(2,1)} custom-call(bf16[8,256,2048]{2,1,0:T(8,128)(2,1)} %get-tuple-element.65.x.a, bf16[8,256,1024]{2,1,0:T(8,128)(2,1)} %hidden_back.1.a_in.b), custom_call_target="tpu_custom_call" | custom-call | flops 8589934592 | bytes 16777216 | tf_op jit(solution)/shard_map/row_product/pallas_call | solution.py:696
  456.9 10.1 %row_product.7 = bf16[512,2048]{1,0:T(8,128)(2,1)} custom-call(bf16[8,256,512]{2,1,0:T(8,128)(2,1)} %get-tuple-element.75.a2_in.a, bf16[8,256,2048]{2,1,0:T(8,128)(2,1)} %get-tuple-element.63.cot.b), custom_call_target="tpu_custom_call" | custom-call | flops 4294967296 | bytes 12582912 | tf_op jit(solution)/shard_map/row_product/pallas_call | solution.py:696
  467.1 27.4 %spread_product.1 = bf16[4,128,2048]{2,1,0:T(8,128)(2,1)} custom-call(bf16[8,256,512]{2,1,0:T(8,128)(2,1)} %get-tuple-element.85.a_in, bf16[8,256,2048]{2,1,0:T(8,128)(2,1)} %get-tuple-element.69.g_low.b_in), custom_call_target="tpu_custom_call" | custom-call | tf_op jit(solution)/shard_map/spread_product/pallas_call | solution.py:1166
  494.5 16.4 %reduce-scatter.6.cloned.1.call-done = bf16[512,1024]{1,0:T(8,128)(2,1)} async-done(((bf16[2048,1024]{1,0:T(8,128)(2,1)}), bf16[512,1024]{1,0:T(8,128)(2,1)}) %reduce-scatter.6.cloned.1.call-update) | async-done | bytes 1048592 | tf_op jit(solution)/shard_map/reduce_scatter | solution.py:1205
  510.9 4.2 all-to-all-start
  515.1 41.9 %reduce-scatter.10.cloned.1.call-done = bf16[512,512]{1,0:T(8,128)(2,1)} async-done(((bf16[2048,512]{1,0:T(8,128)(2,1)}), bf16[512,512]{1,0:T(8,128)(2,1)}) %reduce-scatter.10.cloned.1.call-update) | async-done | bytes 524304 | tf_op jit(solution)/shard_map/reduce_scatter | solution.py:1205
  557.0 79.1 %reduce-scatter.8.cloned.1.call-done = bf16[512,1024]{1,0:T(8,128)(2,1)} async-done(((bf16[2048,1024]{1,0:T(8,128)(2,1)}), bf16[512,1024]{1,0:T(8,128)(2,1)}) %reduce-scatter.8.cloned.1.call-update) | async-done | bytes 1048592 | tf_op jit(solution)/shard_map/reduce_scatter | solution.py:1205
  639.7 4.8 all-to-all-start.1
  644.5 90.1 %last_exchange.1 = (f32[256,2048]{1,0:T(8,128)}, f32[256,2048]{1,0:T(8,128)}, f32[8,512]{1,0:T(8,128)}) custom-call(bf16[8,256,1024]{2,1,0:T(8,128)(2,1)} %scores_back.1.gqkv_in.b, bf16[8,256,512]{2,1,0:T(8,128)(2,1)} %get-tuple-element.73.gs_in.b, bf16[2048,512]{1,0:T(8,128)(2,1)} %bitcast.49, bf16[2048,1024]{1,0:T(8,128)(2,1)} %all-gather.5.cloned.1.call-done.wvs_in, ...), custom_call_target="tpu_custom_call" | custom-call | tf_op jit(solution)/shard_map/last_exchange/pallas_call | solution.py:994
  734.7 4.0 add.28
  (126 shorter events, 43.4 us)
Async XLA Ops:
  7.2 108.4 %all-gather.7.cloned.1.call-start = ((), (), s32[]{:S(2)}) async-start(), calls=%async_computation.8 | async-start | bytes 5242880 | tf_op jit(solution)/shard_map/all_gather | solution.py:1201
  23.1 167.6 %all-gather.5.cloned.1.call-start = ((), (), s32[]{:S(2)}) async-start(), calls=%async_computation.7 | async-start | bytes 5242880 | tf_op jit(solution)/shard_map/all_gather | solution.py:1201
  25.2 47.7 %copy-start.16 = (bf16[64,4096]{1,0:T(8,128)(2,1)S(1)}, bf16[64,4096]{1,0:T(8,128)(2,1)}, u32[]{:S(2)}) copy-start(bf16[64,4096]{1,0:T(8,128)(2,1)} %wv.1) | copy-start | bytes 1572868
  25.2 47.7 %copy-start.17 = (bf16[64,4096]{1,0:T(8,128)(2,1)S(1)}, bf16[64,4096]{1,0:T(8,128)(2,1)}, u32[]{:S(2)}) copy-start(bf16[64,4096]{1,0:T(8,128)(2,1)} %ws.1) | copy-start | bytes 1572868
  68.1 3.3 copy-start.6
  71.6 31.1 %copy-start.19 = (f32[1,2048]{1,0:T(1,128)}, f32[1,2048]{1,0:T(1,128)S(1)}, u32[]{:S(2)}) copy-start(f32[1,2048]{1,0:T(1,128)S(1)} %reshape_squeeze.12.gain) | copy-start | bytes 24580
  72.9 3.4 copy-start.7
  102.7 3.2 copy-start
  106.0 172.1 %all-gather.11.cloned.1.call-start = ((), (), s32[]{:S(2)}) async-start(), calls=%async_computation.10 | async-start | bytes 5242880 | tf_op jit(solution)/shard_map/all_gather | solution.py:1201
  106.8 198.3 %all-gather.9.cloned.1.call-start = ((), (), s32[]{:S(2)}) async-start(), calls=%async_computation.9 | async-start | bytes 1966080 | tf_op jit(solution)/shard_map/all_gather | solution.py:1201
  107.8 403.1 %reduce-scatter.6.cloned.1.call-start = ((), (), s32[]{:S(2)}) async-start(), calls=%async_computation.11 | async-start | bytes 5242880 | tf_op jit(solution)/shard_map/reduce_scatter | solution.py:1205
  114.7 70.3 %copy-start.3 = (f32[8,256,128]{2,1,0:T(8,128)}, f32[8,256,128]{2,1,0:T(8,128)S(1)}, u32[]{:S(2)}) copy-start(f32[8,256,128]{2,1,0:T(8,128)S(1)} %get-tuple-element.92.sine) | copy-start | bytes 3145732
  115.5 69.5 %copy-start.1 = (f32[8,256,256]{2,1,0:T(8,128)}, f32[8,256,256]{2,1,0:T(8,128)S(1)}, u32[]{:S(2)}) copy-start(f32[8,256,256]{2,1,0:T(8,128)S(1)} %fusion.4.mask) | copy-start | bytes 6291460
  305.0 11.3 %copy-start.11 = (bf16[256,2048]{1,0:T(8,128)(2,1)S(1)}, bf16[256,2048]{1,0:T(8,128)(2,1)}, u32[]{:S(2)}) copy-start(bf16[256,2048]{1,0:T(8,128)(2,1)} %cot_in.1) | copy-start | bytes 3145732
  305.1 11.3 %copy-start.18 = (f32[2,2048]{1,0:T(2,128)S(1)}, f32[2,2048]{1,0:T(2,128)}, u32[]{:S(2)}) copy-start(f32[2,2048]{1,0:T(2,128)} %pad_maximum_fusion.2.vec) | copy-start | bytes 49156
  434.1 122.8 %reduce-scatter.10.cloned.1.call-start = ((), (), s32[]{:S(2)}) async-start(), calls=%async_computation.13 | async-start | bytes 2621440 | tf_op jit(solution)/shard_map/reduce_scatter | solution.py:1205
  443.4 192.7 %reduce-scatter.8.cloned.1.call-start = ((), (), s32[]{:S(2)}) async-start(), calls=%async_computation.12 | async-start | bytes 5242880 | tf_op jit(solution)/shard_map/reduce_scatter | solution.py:1205
  456.8 284.4 %reduce-scatter.14.cloned.1.call-start = ((), (), s32[]{:S(2)}) async-start(), calls=%async_computation.15 | async-start | bytes 2621440 | tf_op jit(solution)/shard_map/reduce_scatter | solution.py:1205
  467.0 276.4 %reduce-scatter.12.cloned.1.call-start = ((), (), s32[]{:S(2)}) async-start(), calls=%async_computation.14 | async-start | bytes 2621440 | tf_op jit(solution)/shard_map/reduce_scatter | solution.py:1205
  510.9 127.9 %all-to-all-start = ((bf16[8,64,1024]{2,1,0:T(8,128)(2,1)}), bf16[8,64,1024]{2,1,0:T(8,128)(2,1)S(1)}, u32[]{:S(2)}, u32[]{:S(2)}) async-start(bf16[8,64,1024]{2,1,0:T(8,128)(2,1)} %bitcast.59), calls=%async_computation.1 | async-start | bytes 2097152 | tf_op jit(solution)/shard_map/all_to_all | solution.py:1197
  639.7 107.2 %all-to-all-start.1 = ((bf16[8,64,1536]{2,1,0:T(8,128)(2,1)}), bf16[8,64,1536]{2,1,0:T(8,128)(2,1)}, u32[]{:S(2)}, u32[]{:S(2)}) async-start(bf16[8,64,1536]{2,1,0:T(8,128)(2,1)} %bitcast.19), calls=%async_computation.4 | async-start | bytes 3145728 | tf_op jit(solution)/shard_map/all_to_all | solution.py:1197
  734.6 5.3 copy-start.21
  734.7 5.3 copy-start.22
  741.2 4.3 copy-start.9
  (17 other events, 23.0 us)
Sparse Core Ops, SparseCore 0:
  23.3 79.2 all-gather.6
  106.1 78.9 all-gather.4
  186.7 79.2 all-gather.10
  267.9 37.0 all-gather.8
  434.3 76.5 reduce-scatter.5
  513.6 43.3 reduce-scatter.9
  559.3 76.7 reduce-scatter.7
  638.4 43.3 reduce-scatter.13
  684.0 44.2 reduce-scatter.11
